TPU v7x, 128 devices: a whole 4x4x4 slice. The times are simulated.
128 devices in a mesh: seq: 64 (over y, z_hi, x, core), tp: 2 (over z_lo).
Axes of the slice: x: 4, y: 4, z: 4 (z_hi: 2, z_lo: 2; z = z_hi * 2 + z_lo), core: 2. Of those that a mesh axis runs over, the one named last changes fastest.
Arguments:
- query_rows: bfloat16 [8192, 2048], P('seq', 'tp'), may hold values from -350 to 350
- key_rows: bfloat16 [8192, 512], P('seq', 'tp'), may hold values from -6 to 6
- stored_value_rows: bfloat16 [8192, 512], P('seq', 'tp'), may hold values from -6 to 6
- output_grad: bfloat16 [8192, 2048], P('seq', 'tp'), may hold values from -96 to 96
- layer_input: bfloat16 [8192, 4096], P('seq', 'tp'), may hold values from -16 to 16
- key_matrix: bfloat16 [4096, 512], P(None, 'tp'), may hold values from -0.09375 to 0.09375
- value_matrix: bfloat16 [4096, 512], P(None, 'tp'), may hold values from -0.09375 to 0.09375
- run_placement: int32 [64, 64], replicated, may hold values from 0 to 63, as said below
Outputs:
- query_grad: bfloat16 [8192, 2048], P('seq', 'tp')
- input_grad: bfloat16 [8192, 4096], P('seq', 'tp')
- key_weight_grad: float32 [4096, 512], P('seq', 'tp')
- value_weight_grad: float32 [4096, 512], P('seq', 'tp')
Inputs may be any that keep to these rules, and one draw needn't show every extreme that they name: `run_placement`: row j gives, for each storing index d of seq, the slot within sequence block j of the 2 consecutive positions that d holds; every row is a permutation of 0 to 63.
All inputs are finite; a program needn't handle non-finite values.
Results may differ from a plain program's by a relative error of at most 0.0081.
Values may be sent and summed in bfloat16 or wider, within the bound.
No kernel may reach another device: no remote copies, remote signals or barrier semaphores. Data moves between devices by JAX's collectives and lax.ppermute only.
A program may use at most 128 MiB of HBM per device.

v0:
```python
import math

import jax
import jax.numpy as jnp
from jax import lax
from jax.experimental import pallas as pl
from jax.experimental.pallas import tpu as pltpu
from jax.sharding import Mesh
from jax.sharding import PartitionSpec as P


HEAD = 128
WINDOW = 4096
GROUP = 4
TOK = 128
SEQ = ("y", "z", "x", "c")
BF = jnp.bfloat16
F32 = jnp.float32
NEG = -1e30

PARTS = 4
T = TOK // PARTS
KSLOTS = 16
QSLOTS = 8
KR = KSLOTS * T
QR = QSLOTS * GROUP * T
SPAN = PARTS // 2
SCALE = 1.0 / math.sqrt(HEAD)
SCORE2 = SCALE * math.log2(math.e)
VMEM_LIMIT = 60 * 1024 * 1024


def moved(array, axis, by):
    n = lax.axis_size(axis)
    return lax.ppermute(array, axis, [(i, (i + by) % n) for i in range(n)])


def nt(a, b):
    return lax.dot_general(a, b, (((1,), (1,)), ((), ())), preferred_element_type=F32)


def nn(a, b):
    return lax.dot_general(a, b, (((1,), (0,)), ((), ())), preferred_element_type=F32)


def load_parts(kv_refs, qg_refs, kpos_ref, ks, vs, qs, gs, kposb):
    for part in range(PARTS):
        tok = slice(part * T, (part + 1) * T)
        for a in range(2):
            rows = slice(a * 8 * T, (a + 1) * 8 * T)
            ks[part, rows, :] = kv_refs[a][:, :, tok, :HEAD].reshape(8 * T, HEAD)
            vs[part, rows, :] = kv_refs[a][:, :, tok, HEAD:].reshape(8 * T, HEAD)
        for h in range(GROUP):
            for s in range(4):
                row = (h * QSLOTS + s * 2) * T
                qs[part, row : row + 2 * T, :] = qg_refs[s][:, tok, h * HEAD : (h + 1) * HEAD].reshape(2 * T, HEAD)
                col = (GROUP + h) * HEAD
                gs[part, row : row + 2 * T, :] = qg_refs[s][:, tok, col : col + HEAD].reshape(2 * T, HEAD)
    for slot in range(KSLOTS):
        column = jnp.broadcast_to(kpos_ref[slot : slot + 1, :], (TOK, 128)).T
        for part in range(PARTS):
            kposb[part, slot * T : (slot + 1) * T, :] = column[part * T : (part + 1) * T, :]


def masked_scores(delta, i, ip, ks, qs, kposb, qpos_ref):
    s = nt(ks[ip], qs[i]) * SCORE2
    if delta == 0 or delta == SPAN:
        kp = jnp.concatenate([kposb[ip]] * (QR // 128), axis=1)
        qp = qpos_ref[i]
        valid = (kp <= qp) if delta == 0 else (kp > qp - float(WINDOW))
        s = jnp.where(valid, s, NEG)
    return s


def stats_kernel(*refs):
    kv_refs, qg_refs = refs[0:2], refs[2:6]
    kpos_ref, qpos_ref = refs[6:8]
    out_refs = refs[8:12]
    ks, vs, qs, gs, kposb, ms, ls, ws = refs[12:]
    load_parts(kv_refs, qg_refs, kpos_ref, ks, vs, qs, gs, kposb)
    ms[...] = jnp.full(ms.shape, NEG, F32)
    ls[...] = jnp.zeros(ls.shape, F32)
    ws[...] = jnp.zeros(ws.shape, F32)
    for delta in range(SPAN + 1):

        def body(i, carry, delta=delta):
            ip = i - delta
            s = masked_scores(delta, i, ip, ks, qs, kposb, qpos_ref).reshape(KR // 8, 8, QR)
            dp = nt(vs[ip], gs[i]).reshape(KR // 8, 8, QR)
            old = ms[i]
            new = jnp.maximum(old, jnp.max(s, axis=0))
            e = jnp.exp2(s - new[None])
            fade = jnp.exp2(old - new)
            ls[i] = ls[i] * fade + jnp.sum(e, axis=0)
            ws[i] = ws[i] * fade + jnp.sum(e * dp, axis=0)
            ms[i] = new
            return carry

        lax.fori_loop(delta, PARTS, body, 0)
    rows = []
    for i in range(PARTS):
        m8 = ms[i]
        top = jnp.max(m8, axis=0, keepdims=True)
        fade = jnp.exp2(m8 - top)
        total = jnp.sum(ls[i] * fade, axis=0, keepdims=True)
        weighted = jnp.sum(ws[i] * fade, axis=0, keepdims=True)
        rows += [top, total, weighted, jnp.zeros((1, QR), F32)]
    stats = jnp.concatenate(rows, axis=0)
    per_head = QSLOTS * T
    for o in range(4):
        for h in range(GROUP):
            cols = slice(h * per_head, (h + 1) * per_head)
            piece = stats[:, cols]
            out_refs[o][:, cols] = pltpu.roll(piece, o * 2 * T, 1) if o else piece


def grads_kernel(*refs):
    kv_refs, qg_refs = refs[0:2], refs[2:6]
    kpos_ref, qpos_ref = refs[6:8]
    st_refs = refs[8:12]
    dkv_refs, dq_refs = refs[12:14], refs[14:18]
    ks, vs, qs, gs, kposb, kt, dks, dvs, dqt, lse, mean = refs[18:]
    load_parts(kv_refs, qg_refs, kpos_ref, ks, vs, qs, gs, kposb)
    for part in range(PARTS):
        kt[part] = ks[part].T
        st = [r[part * 4 : part * 4 + 3, :] for r in st_refs]
        top = jnp.maximum(jnp.maximum(st[0][0:1], st[1][0:1]), jnp.maximum(st[2][0:1], st[3][0:1]))
        fade = [jnp.exp2(a[0:1] - top) for a in st]
        total = sum(a[1:2] * f for a, f in zip(st, fade))
        lse[part] = top + jnp.log2(total)
        mean[part] = sum(a[2:3] * f for a, f in zip(st, fade)) / total
    for delta in range(SPAN + 1):

        def body(i, carry, delta=delta):
            ip = i - delta
            q, g = qs[i], gs[i]
            p = jnp.exp2(masked_scores(delta, i, ip, ks, qs, kposb, qpos_ref) - lse[i])
            ds = (p * (nt(vs[ip], g) - mean[i])).astype(BF)
            p = p.astype(BF)
            dk, dv, dq = nn(ds, q), nn(p, g), nn(kt[ip], ds)
            if delta == 0:
                dks[ip], dvs[ip], dqt[i] = dk, dv, dq
            else:
                dks[ip] += dk
                dvs[ip] += dv
                dqt[i] += dq
            return carry

        lax.fori_loop(delta, PARTS, body, 0)
    for part in range(PARTS):
        tok = slice(part * T, (part + 1) * T)
        for a in range(2):
            rows = slice(a * 8 * T, (a + 1) * 8 * T)
            dkv_refs[a][:, :, tok, :HEAD] = (dks[part, rows, :] * SCALE).astype(BF).reshape(4, 2, T, HEAD)
            dkv_refs[a][:, :, tok, HEAD:] = dvs[part, rows, :].astype(BF).reshape(4, 2, T, HEAD)
        dq = dqt[part].T * SCALE
        for h in range(GROUP):
            for s in range(4):
                row = (h * QSLOTS + s * 2) * T
                piece = dq[row : row + 2 * T, :].reshape(2, T, HEAD)
                dq_refs[s][:, tok, h * HEAD : (h + 1) * HEAD] = piece.astype(dq_refs[s].dtype)


def common_scratch():
    return [
        pltpu.VMEM((PARTS, KR, HEAD), BF),
        pltpu.VMEM((PARTS, KR, HEAD), BF),
        pltpu.VMEM((PARTS, QR, HEAD), BF),
        pltpu.VMEM((PARTS, QR, HEAD), BF),
        pltpu.VMEM((PARTS, KR, 128), F32),
    ]


def run_stats(kvs, qgs, kpos, qpos):
    return pl.pallas_call(
        stats_kernel,
        out_shape=[jax.ShapeDtypeStruct((PARTS * 4, QR), F32)] * 4,
        scratch_shapes=common_scratch() + [pltpu.VMEM((PARTS, 8, QR), F32)] * 3,
        compiler_params=pltpu.CompilerParams(vmem_limit_bytes=VMEM_LIMIT),
        cost_estimate=pl.CostEstimate(flops=6_000_000_000, bytes_accessed=3_000_000, transcendentals=5_000_000),
        name="stats",
    )(*kvs, *qgs, kpos, qpos)


def run_grads(kvs, qgs, kpos, qpos, sts):
    dkv = jax.ShapeDtypeStruct((4, 2, TOK, 2 * HEAD), BF)
    dq = [jax.ShapeDtypeStruct((2, TOK, GROUP * HEAD), F32 if s == 0 else BF) for s in range(4)]
    out = pl.pallas_call(
        grads_kernel,
        out_shape=[dkv, dkv] + dq,
        scratch_shapes=common_scratch()
        + [
            pltpu.VMEM((PARTS, HEAD, KR), BF),
            pltpu.VMEM((PARTS, KR, HEAD), F32),
            pltpu.VMEM((PARTS, KR, HEAD), F32),
            pltpu.VMEM((PARTS, HEAD, QR), F32),
            pltpu.VMEM((PARTS, 1, QR), F32),
            pltpu.VMEM((PARTS, 1, QR), F32),
        ],
        compiler_params=pltpu.CompilerParams(vmem_limit_bytes=VMEM_LIMIT),
        cost_estimate=pl.CostEstimate(flops=12_000_000_000, bytes_accessed=6_000_000, transcendentals=5_000_000),
        name="grads",
    )(*kvs, *qgs, kpos, qpos, *sts)
    return out[0:2], out[2:6]


def pack_kernel(at_ref, q_ref, g_ref, k_ref, v_ref, kv_own, qg_own, kv_send, qg_send):
    wide = GROUP * HEAD
    mine = at_ref[0]
    for which, kv, qg in ((mine, kv_own.at[0], qg_own.at[0]), (1 - mine, kv_send, qg_send)):
        cols = pl.ds(pl.multiple_of(which * wide, 128), wide)
        small = pl.ds(pl.multiple_of(which * HEAD, 128), HEAD)
        kv[:, :HEAD] = k_ref[:, small]
        kv[:, HEAD:] = v_ref[:, small]
        qg[:, :wide] = q_ref[:, cols]
        qg[:, wide:] = g_ref[:, cols]
    kv_own[1] = kv_send[...]
    qg_own[1] = qg_send[...]


def run_pack(at, q, g, k, v):
    kv, qg = (TOK, 2 * HEAD), (TOK, 2 * GROUP * HEAD)
    vmem = pl.BlockSpec(memory_space=pltpu.VMEM)
    return pl.pallas_call(
        pack_kernel,
        out_shape=[jax.ShapeDtypeStruct(a, BF) for a in ((2, *kv), (2, *qg), kv, qg)],
        in_specs=[pl.BlockSpec(memory_space=pltpu.SMEM)] + [vmem] * 4,
        name="pack",
    )(at, q, g, k, v)


def columns_kernel(at_ref, in_ref, *out_refs):
    for o in range(4):
        target = (at_ref[1] + o) % 4
        for n in range(4):
            cols = pl.ds(pl.multiple_of(n * 4 * HEAD + target * HEAD, 128), HEAD)
            out_refs[o][:, n * HEAD : (n + 1) * HEAD] = in_ref[:, cols]


def run_columns(at, layer_input):
    return pl.pallas_call(
        columns_kernel,
        out_shape=[jax.ShapeDtypeStruct((TOK, 4 * HEAD), BF)] * 4,
        in_specs=[pl.BlockSpec(memory_space=pltpu.SMEM), pl.BlockSpec(memory_space=pltpu.VMEM)],
        name="columns",
    )(at, layer_input)


def finish_kernel(in_ref, k_ref, v_ref):
    for h in range(2):
        total = in_ref[h].astype(F32)
        for n in range(1, 8):
            total = total + in_ref[2 * n + h].astype(F32)
        k_ref[:, h * HEAD : (h + 1) * HEAD] = total[:, :HEAD]
        v_ref[:, h * HEAD : (h + 1) * HEAD] = total[:, HEAD:]


def run_finish(got):
    out = jax.ShapeDtypeStruct((HEAD // 2, 2 * HEAD), F32)
    return pl.pallas_call(finish_kernel, out_shape=[out, out], name="finish")(got)


def positions(run_placement, y, z, x, c):
    def device(yy, zz, xx, cc):
        return (((yy % 4) * 2 + zz % 2) * 4 + xx % 4) * 2 + cc % 2

    a, b, e = jnp.meshgrid(jnp.arange(2), jnp.arange(4), jnp.arange(2), indexing="ij")
    keys = device(y, z + a, x + b, c + e).reshape(KSLOTS)
    a, e = jnp.meshgrid(jnp.arange(4), jnp.arange(2), indexing="ij")
    queries = device(y + a, z, x, c + e).reshape(QSLOTS)
    index = jnp.concatenate([keys, queries]).astype(jnp.int32)
    pick = (index[:, None] == jnp.arange(64, dtype=jnp.int32)[None, :]).astype(BF)
    slots = nt(pick, run_placement.astype(BF)).astype(BF)
    lane = jnp.arange(TOK, dtype=jnp.int32)
    spread = jnp.where(lane[None, :] // 2 == jnp.arange(64, dtype=jnp.int32)[:, None], 2.0, 0.0).astype(BF)
    pos = nn(slots, spread) + ((lane // 2) * TOK + lane % 2).astype(F32)[None, :]
    kpos = pos[:KSLOTS]
    qpos = pos[KSLOTS:].reshape(QSLOTS, PARTS, T).transpose(1, 0, 2).reshape(PARTS, 1, 1, QSLOTS * T)
    qpos = jnp.broadcast_to(qpos, (PARTS, 1, GROUP, QSLOTS * T)).reshape(PARTS, 1, QR)
    return kpos, qpos


def own_first(c, mine, other, axis):
    return jnp.where(c == 0, jnp.concatenate([mine, other], axis), jnp.concatenate([other, mine], axis))


def after(array, *gates):
    return lax.optimization_barrier((array, *gates))[0]


def step(query_rows, key_rows, value_rows, output_grad, layer_input, key_matrix, value_matrix, run_placement):
    y, z, x, c, t = (lax.axis_index(a) for a in ("y", "z", "x", "c", "tp"))
    at = jnp.stack([c, x]).astype(jnp.int32)
    kv_pair, qg_pair, kv_send, qg_send = run_pack(at, query_rows, output_grad, key_rows, value_rows)
    kv_own = kv_pair.at[1].set(moved(kv_send, "c", 1))
    qg_own = qg_pair.at[1].set(moved(qg_send, "c", 1))
    kpos, qpos = positions(run_placement, y, z, x, c)
    kv_row = jnp.stack([kv_own] + [moved(kv_own, "x", -o) for o in (1, 2, 3)])
    qgs = [qg_own] + [moved(qg_own, "y", -o) for o in (1, 2, 3)]
    kvs = [kv_row, moved(kv_row, "z", 1)]

    half = key_matrix.shape[0] // 2
    cuts = [lax.dynamic_slice_in_dim(after(m, kv_row), (1 - t) * half, half, 0) for m in (key_matrix, value_matrix)]
    m_far = moved(jnp.where(c == 0, *cuts), "tp", 1)
    x_pieces = run_columns(at, after(layer_input, kv_row))
    kpos = after(kpos, *x_pieces)

    sts = run_stats(kvs, qgs, kpos, qpos)
    sts = [sts[0]] + [moved(sts[o], "y", -o) for o in (1, 2, 3)]
    x_half = jnp.stack([x_pieces[0]] + [moved(x_pieces[4 - o], "x", -o) for o in (1, 2, 3)])
    dkvs, dqs = run_grads(kvs, qgs, kpos, qpos, sts)

    def total_of(own, arrived):
        total = own.astype(F32)
        for a in arrived:
            total = total + a.astype(F32)
        return total.astype(BF)

    dkv_row = total_of(dkvs[0], [moved(dkvs[1], "z", 1)])
    dq = total_of(dqs[0], [moved(dqs[o], "y", o) for o in (1, 2, 3)])
    x_other = moved(x_half, "tp", 1)
    x_here = jnp.where(t == 0, jnp.concatenate([x_half, x_other], 2), jnp.concatenate([x_other, x_half], 2))
    x_all = jnp.stack([x_here, moved(x_here, "c", 1)], axis=1)
    m_core = moved(m_far, "c", 1)
    k_far = jnp.where(c == 0, m_far, m_core)
    v_far = jnp.where(c == 0, m_core, m_far)

    dkv = total_of(dkv_row[0], [moved(dkv_row[o], "x", o) for o in (1, 2, 3)])
    dkv_all = jnp.stack([dkv] + [moved(dkv, "x", -o) for o in (1, 2, 3)])
    dkv_far = moved(dkv[1], "c", 1)
    k_here = own_first(c, dkv[0, :, :HEAD], dkv_far[:, :HEAD], 1)
    v_here = own_first(c, dkv[0, :, HEAD:], dkv_far[:, HEAD:], 1)
    kv_here = jnp.concatenate([k_here, v_here], 1)
    kv_there = moved(kv_here, "tp", 1)

    query_grad = own_first(c, dq[0], moved(dq[1], "c", 1), 1)

    tokens = 8 * TOK
    weight = lax.dot_general(
        x_all.reshape(tokens, 8 * HEAD),
        dkv_all.reshape(tokens, 2 * HEAD),
        (((0,), (0,)), ((), ())),
        preferred_element_type=F32,
    )
    pieces = weight.astype(BF).reshape(16, HEAD // 2, 2 * HEAD)
    got = lax.all_to_all(pieces, ("y", "z", "c"), 0, 0, tiled=True)
    key_weight, value_weight = run_finish(got)

    km = lax.dynamic_slice_in_dim(key_matrix, t * half, half, 0)
    vm = lax.dynamic_slice_in_dim(value_matrix, t * half, half, 0)
    wide = 2 * HEAD
    total = nt(kv_here[:, :wide], km) + nt(kv_here[:, wide:], vm)
    input_grad = (total + nt(kv_there[:, :wide], k_far) + nt(kv_there[:, wide:], v_far)).astype(BF)
    return (query_grad, input_grad, key_weight, value_weight)


def solution(mesh):
    torus = Mesh(mesh.devices.reshape(4, 2, 4, 2, mesh.shape["tp"]), ("y", "z", "x", "c", "tp"))
    return jax.shard_map(
        step,
        mesh=torus,
        in_specs=(P(SEQ, "tp"),) * 5 + (P(None, "tp"),) * 2 + (P(),),
        out_specs=(P(SEQ, "tp"),) * 4,
        check_vma=False,
    )
```

profile of v0, /device:TPU:1, one launch (start us, length us, event | category | flops | bytes accessed | tf_op | source)
XLA Modules:
  0.0 171.7 jit_solution(6996946203270725343)
XLA Ops:
  1.2 2.0 %pack.1 = (bf16[2,128,256]{2,1,0:T(8,128)(2,1)}, bf16[2,128,1024]{2,1,0:T(8,128)(2,1)}, bf16[128,256]{1,0:T(8,128)(2,1)}, bf16[128,1024]{1,0:T(8,128)(2,1)}) custom-call(s32[2]{0:T(128)} %pad_add_fusion.at_ref, bf16[128,1024]{1,0:T(8,128)(2,1)} %q_ref.1, bf16[128,1024]{1,0:T(8,128)(2,1)} %g_ref.1, bf16[128,256]{1,0:T(8,128)(2,1)} %k_ref.1, ...), custom_call_target="tpu_custom_call" | custom-call | tf_op jit(solution)/shard_map/pack/pallas_call | solution.py:224
  3.3 1.4 collective-permute-start
  6.4 1.3 collective-permute-start.3
  7.7 2.5 %collective-permute-start.2 = (bf16[2,128,256]{2,1,0:T(8,128)(2,1)}, bf16[2,128,256]{2,1,0:T(8,128)(2,1)S(1)}, u32[]{:S(2)}, u32[]{:S(2)}) collective-permute-start(bf16[2,128,256]{2,1,0:T(8,128)(2,1)} %bitcast_dynamic-update-slice_fusion.1), channel_id=1, source_target_pairs={{0,8},{4,12},{8,0},{12,4},{1,9},{5,13},{9,1},{13,5},{2,10},{6,14},... | collective-permute-start | bytes 393224 | tf_op jit(solution)/shard_map/ppermute | solution.py:35
  10.2 1.2 collective-permute-start.1
  11.3 1.2 collective-permute-done.3
  12.5 3.9 %collective-permute-done.2 = bf16[2,128,256]{2,1,0:T(8,128)(2,1)S(1)} collective-permute-done((bf16[2,128,256]{2,1,0:T(8,128)(2,1)}, bf16[2,128,256]{2,1,0:T(8,128)(2,1)S(1)}, u32[]{:S(2)}, u32[]{:S(2)}) %collective-permute-start.2) | collective-permute-done | bytes 131104 | tf_op jit(solution)/shard_map/ppermute | solution.py:35
  16.4 1.0 pad_maximum_fusion.1.refs_0_
  17.4 3.7 %collective-permute-start.4 = (bf16[4,2,128,256]{3,2,1,0:T(8,128)(2,1)S(1)}, bf16[4,2,128,256]{3,2,1,0:T(8,128)(2,1)S(1)}, u32[]{:S(2)}, u32[]{:S(2)}) collective-permute-start(bf16[4,2,128,256]{3,2,1,0:T(8,128)(2,1)S(1)} %pad_maximum_fusion.1.refs_0_), channel_id=1, source_target_pairs={{0,16},{16,0},{1,17},{17,1},{2,18},{18,2},{3,19},{19,3},{4,20},{20... | collective-permute-start | bytes 1572872 | tf_op jit(solution)/shard_map/ppermute | solution.py:35
  21.1 0.7 bitcast_dynamic-update-slice_fusion.refs_2_
  21.8 2.7 %collective-permute-start.6 = (bf16[2,128,1024]{2,1,0:T(8,128)(2,1)}, bf16[2,128,1024]{2,1,0:T(8,128)(2,1)S(1)}, u32[]{:S(2)}, u32[]{:S(2)}) collective-permute-start(bf16[2,128,1024]{2,1,0:T(8,128)(2,1)} %bitcast_dynamic-update-slice_fusion.refs_2_), channel_id=1, source_target_pairs={{0,96},{32,0},{64,32},{96,64},{1,97},{33,1},{65,33},{97,65},{2,98}... | collective-permute-start | bytes 1572872 | tf_op jit(solution)/shard_map/ppermute | solution.py:35
  24.9 0.7 collective-permute-start.8
  27.4 2.0 %columns.1 = (bf16[128,512]{1,0:T(8,128)(2,1)}, bf16[128,512]{1,0:T(8,128)(2,1)}, bf16[128,512]{1,0:T(8,128)(2,1)}, bf16[128,512]{1,0:T(8,128)(2,1)}) custom-call(s32[2]{0:T(128)} %pad_add_fusion.at_ref, bf16[128,2048]{1,0:T(8,128)(2,1)} %in_ref), custom_call_target="tpu_custom_call" | custom-call | tf_op jit(solution)/shard_map/columns/pallas_call | solution.py:241
  29.4 1.1 collective-permute-start.26
  30.5 1.7 collective-permute-done.4.refs_1_
  32.2 1.9 %collective-permute-start.25 = (bf16[128,512]{1,0:T(8,128)(2,1)}, bf16[128,512]{1,0:T(8,128)(2,1)S(1)}, u32[]{:S(2)}, u32[]{:S(2)}) collective-permute-start(bf16[128,512]{1,0:T(8,128)(2,1)} %get-tuple-element.59), channel_id=1, source_target_pairs={{0,8},{4,12},{8,0},{12,4},{1,9},{5,13},{9,1},{13,5},{2,10},{6,14},... | collective-permute-start | bytes 393224 | tf_op jit(solution)/shard_map/ppermute | solution.py:35
  34.1 1.6 collective-permute-done.6.refs_3_
  35.7 2.3 %collective-permute-start.24 = (bf16[128,512]{1,0:T(8,128)(2,1)}, bf16[128,512]{1,0:T(8,128)(2,1)S(1)}, u32[]{:S(2)}, u32[]{:S(2)}) collective-permute-start(bf16[128,512]{1,0:T(8,128)(2,1)} %get-tuple-element.60), channel_id=1, source_target_pairs={{0,12},{4,0},{8,4},{12,8},{1,13},{5,1},{9,5},{13,9},{2,14},{6,2},{... | collective-permute-start | bytes 393224 | tf_op jit(solution)/shard_map/ppermute | solution.py:35
  38.1 13.3 %collective-permute-done.8.refs_5_ = bf16[2,128,1024]{2,1,0:T(8,128)(2,1)S(1)} collective-permute-done((bf16[2,128,1024]{2,1,0:T(8,128)(2,1)}, bf16[2,128,1024]{2,1,0:T(8,128)(2,1)S(1)}, u32[]{:S(2)}, u32[]{:S(2)}) %collective-permute-start.8) | collective-permute-done | bytes 524320 | tf_op jit(solution)/shard_map/ppermute | solution.py:35
  51.4 0.8 copy-done.9
  52.2 10.8 %stats.1 = (f32[16,1024]{1,0:T(8,128)}, f32[16,1024]{1,0:T(8,128)}, f32[16,1024]{1,0:T(8,128)}, f32[16,1024]{1,0:T(8,128)}) custom-call(bf16[4,2,128,256]{3,2,1,0:T(8,128)(2,1)} %copy-done.5, bf16[4,2,128,256]{3,2,1,0:T(8,128)(2,1)} %copy-done.6, bf16[2,128,1024]{2,1,0:T(8,128)(2,1)} %bitcast_dynamic-update-slice_fusion.refs_2_, ...), custom_call_target="tpu_custom_call" | custom-call | flops 6000000000 | bytes 3000000 | tf_op jit(solution)/shard_map/stats/pallas_call | solution.py:175
  63.4 1.1 collective-permute-start.11
  64.5 1.0 collective-permute-start.27
  65.5 0.8 collective-permute-done.9.refs_9_
  66.3 1.6 collective-permute-done.10.refs_10_
  67.8 0.8 collective-permute-done.11.refs_11_
  69.3 17.9 %grads.1 = (bf16[4,2,128,256]{3,2,1,0:T(8,128)(2,1)}, bf16[4,2,128,256]{3,2,1,0:T(8,128)(2,1)}, f32[2,128,512]{2,1,0:T(8,128)}, bf16[2,128,512]{2,1,0:T(8,128)(2...) custom-call(bf16[4,2,128,256]{3,2,1,0:T(8,128)(2,1)} %copy-done.5, bf16[4,2,128,256]{3,2,1,0:T(8,128)(2,1)} %copy-done.6, ...), custom_call_target="tpu_custom_call" | custom-call | flops 12000000000 | bytes 6000000 | tf_op jit(solution)/shard_map/grads/pallas_call | solution.py:188
  87.2 1.5 collective-permute-start.14
  88.8 1.3 collective-permute-start.13
  90.1 1.8 %dynamic-slice_select_fusion = bf16[2048,256]{1,0:T(8,128)(2,1)S(1)} fusion(bf16[4096,256]{1,0:T(8,128)(2,1)} %param.18, s32[]{:T(128)S(6)} %select_n.157, bf16[4096,256]{1,0:T(8,128)(2,1)} %param.17, pred[]{:T(512)S(6)} %eq.50), kind=kLoop, calls=%fused_computation.16 | loop fusion | flops 524288 | bytes 3145733 | tf_op jit(solution)/shard_map/jit(_where)/select_n | solution.py:304
  92.0 0.8 collective-permute-start.22
  92.8 1.0 collective-permute-start.16
  94.1 1.7 %collective-permute-done.13 = bf16[2,128,512]{2,1,0:T(8,128)(2,1)S(1)} collective-permute-done((bf16[2,128,512]{2,1,0:T(8,128)(2,1)}, bf16[2,128,512]{2,1,0:T(8,128)(2,1)S(1)}, u32[]{:S(2)}, u32[]{:S(2)}) %collective-permute-start.13) | collective-permute-done | bytes 262176 | tf_op jit(solution)/shard_map/ppermute | solution.py:35
  95.8 7.0 %collective-permute-done.12 = bf16[2,128,512]{2,1,0:T(8,128)(2,1)S(1)} collective-permute-done((bf16[2,128,512]{2,1,0:T(8,128)(2,1)}, bf16[2,128,512]{2,1,0:T(8,128)(2,1)S(1)}, u32[]{:S(2)}, u32[]{:S(2)}) %collective-permute-start.12) | collective-permute-done | bytes 262176 | tf_op jit(solution)/shard_map/ppermute | solution.py:35
  102.9 2.1 %collective-permute-start.15 = (bf16[128,512]{1,0:T(8,128)(2,1)S(1)}, bf16[128,512]{1,0:T(8,128)(2,1)S(1)}, u32[]{:S(2)}, u32[]{:S(2)}) collective-permute-start(bf16[128,512]{1,0:T(8,128)(2,1)S(1)} %get-tuple-element.82), channel_id=1, source_target_pairs={{0,2},{2,0},{1,3},{3,1},{4,6},{6,4},{5,7},{7,5},{8,10},{10,8},{9,1... | collective-permute-start | bytes 393224 | tf_op jit(solution)/shard_map/ppermute | solution.py:35
  105.1 18.5 %collective-permute-done.16 = bf16[4,2,128,256]{3,2,1,0:T(8,128)(2,1)S(1)} collective-permute-done((bf16[4,2,128,256]{3,2,1,0:T(8,128)(2,1)S(1)}, bf16[4,2,128,256]{3,2,1,0:T(8,128)(2,1)S(1)}, u32[]{:S(2)}, u32[]{:S(2)}) %collective-permute-start.16) | collective-permute-done | bytes 524320 | tf_op jit(solution)/shard_map/ppermute | solution.py:35
  123.8 4.1 %collective-permute-start.19 = (bf16[2,128,256]{2,1,0:T(8,128)(2,1)S(1)}, bf16[2,128,256]{2,1,0:T(8,128)(2,1)S(1)}, u32[]{:S(2)}, u32[]{:S(2)}) collective-permute-start(bf16[2,128,256]{2,1,0:T(8,128)(2,1)S(1)} %get-tuple-element.79), channel_id=1, source_target_pairs={{0,12},{4,0},{8,4},{12,8},{1,13},{5,1},{9,5},{13,9},{2,14},{6,2},{... | collective-permute-start | bytes 393224 | tf_op jit(solution)/shard_map/ppermute | solution.py:35
  129.0 4.2 %collective-permute-start.28 = (bf16[4,128,1024]{2,1,0:T(8,128)(2,1)S(1)}, bf16[4,128,1024]{2,1,0:T(8,128)(2,1)S(1)}, u32[]{:S(2)}, u32[]{:S(2)}) collective-permute-start(bf16[4,128,1024]{2,1,0:T(8,128)(2,1)S(1)} %maximum_select_fusion.1), channel_id=1, source_target_pairs={{0,2},{2,0},{1,3},{3,1},{4,6},{6,4},{5,7},{7,5},{8,10},{10,8},{9,1... | collective-permute-start | bytes 3145736 | tf_op jit(solution)/shard_map/ppermute | solution.py:35
  133.3 0.8 maximum_select_fusion.2
  134.7 5.0 %collective-permute-start.20 = (bf16[128,256]{1,0:T(8,128)(2,1)S(1)}, bf16[128,256]{1,0:T(8,128)(2,1)S(1)}, u32[]{:S(2)}, u32[]{:S(2)}) collective-permute-start(bf16[128,256]{1,0:T(8,128)(2,1)S(1)} %slice_bitcast_fusion.6), channel_id=1, source_target_pairs={{0,2},{2,0},{1,3},{3,1},{4,6},{6,4},{5,7},{7,5},{8,10},{10,8},{9,1... | collective-permute-start | bytes 196616 | tf_op jit(solution)/shard_map/ppermute | solution.py:35
  139.8 1.5 collective-permute-start.30
  141.2 1.3 collective-permute-start.29
  143.6 5.2 %collective-permute-done.31 = bf16[2,128,256]{2,1,0:T(8,128)(2,1)S(1)} collective-permute-done((bf16[2,128,256]{2,1,0:T(8,128)(2,1)S(1)}, bf16[2,128,256]{2,1,0:T(8,128)(2,1)S(1)}, u32[]{:S(2)}, u32[]{:S(2)}) %collective-permute-start.31) | collective-permute-done | bytes 131104 | tf_op jit(solution)/shard_map/ppermute | solution.py:35
  149.1 1.6 fusion.7
  150.7 7.9 %all-to-all-start = ((bf16[16,64,256]{2,1,0:T(8,128)(2,1)}), bf16[16,64,256]{2,1,0:T(8,128)(2,1)}, u32[]{:S(2)}, u32[]{:S(2)}) async-start(bf16[16,64,256]{2,1,0:T(8,128)(2,1)} %bitcast.65), calls=%async_computation | async-start | bytes 1048576 | tf_op jit(solution)/shard_map/all_to_all | solution.py:346
  159.1 1.3 fusion.1
  160.4 9.5 %all-to-all-done.in_ref = bf16[16,64,256]{2,1,0:T(8,128)(2,1)} async-done(((bf16[16,64,256]{2,1,0:T(8,128)(2,1)}), bf16[16,64,256]{2,1,0:T(8,128)(2,1)}, u32[]{:S(2)}, u32[]{:S(2)}) %all-to-all-start) | async-done | bytes 524320 | tf_op jit(solution)/shard_map/all_to_all | solution.py:346
  169.9 1.7 %finish.1 = (f32[64,256]{1,0:T(8,128)}, f32[64,256]{1,0:T(8,128)}) custom-call(bf16[16,64,256]{2,1,0:T(8,128)(2,1)} %all-to-all-done.in_ref), custom_call_target="tpu_custom_call" | custom-call | tf_op jit(solution)/shard_map/finish/pallas_call | solution.py:260
  (104 shorter events, 10.0 us)
Async XLA Ops:
  0.6 25.1 %copy-start.14 = (s32[64,64]{1,0:T(8,128)S(1)}, s32[64,64]{1,0:T(8,128)}, u32[]{:S(2)}) copy-start(s32[64,64]{1,0:T(8,128)} %param.19) | copy-start | bytes 49156
  3.3 2.5 %collective-permute-start = (bf16[128,256]{1,0:T(8,128)(2,1)}, bf16[128,256]{1,0:T(8,128)(2,1)S(1)}, u32[]{:S(2)}, u32[]{:S(2)}) collective-permute-start(bf16[128,256]{1,0:T(8,128)(2,1)} %get-tuple-element.53), channel_id=1, source_target_pairs={{0,2},{2,0},{1,3},{3,1},{4,6},{6,4},{5,7},{7,5},{8,10},{10,8},{9,1... | collective-permute-start | bytes 196616 | tf_op jit(solution)/shard_map/ppermute | solution.py:35
  4.7 16.4 %collective-permute-start.5 = (bf16[128,1024]{1,0:T(8,128)(2,1)}, bf16[128,1024]{1,0:T(8,128)(2,1)S(1)}, u32[]{:S(2)}, u32[]{:S(2)}) collective-permute-start(bf16[128,1024]{1,0:T(8,128)(2,1)} %get-tuple-element.55), channel_id=1, source_target_pairs={{0,2},{2,0},{1,3},{3,1},{4,6},{6,4},{5,7},{7,5},{8,10},{10,8},{9,1... | collective-permute-start | bytes 786440 | tf_op jit(solution)/shard_map/ppermute | solution.py:35
  6.4 6.1 %collective-permute-start.3 = (bf16[2,128,256]{2,1,0:T(8,128)(2,1)}, bf16[2,128,256]{2,1,0:T(8,128)(2,1)S(1)}, u32[]{:S(2)}, u32[]{:S(2)}) collective-permute-start(bf16[2,128,256]{2,1,0:T(8,128)(2,1)} %bitcast_dynamic-update-slice_fusion.1), channel_id=1, source_target_pairs={{0,4},{4,8},{8,12},{12,0},{1,5},{5,9},{9,13},{13,1},{2,6},{6,10},{... | collective-permute-start | bytes 393224 | tf_op jit(solution)/shard_map/ppermute | solution.py:35
  7.7 8.7 %collective-permute-start.2 = (bf16[2,128,256]{2,1,0:T(8,128)(2,1)}, bf16[2,128,256]{2,1,0:T(8,128)(2,1)S(1)}, u32[]{:S(2)}, u32[]{:S(2)}) collective-permute-start(bf16[2,128,256]{2,1,0:T(8,128)(2,1)} %bitcast_dynamic-update-slice_fusion.1), channel_id=1, source_target_pairs={{0,8},{4,12},{8,0},{12,4},{1,9},{5,13},{9,1},{13,5},{2,10},{6,14},... | collective-permute-start | bytes 393224 | tf_op jit(solution)/shard_map/ppermute | solution.py:35
  10.2 6.3 %collective-permute-start.1 = (bf16[2,128,256]{2,1,0:T(8,128)(2,1)}, bf16[2,128,256]{2,1,0:T(8,128)(2,1)S(1)}, u32[]{:S(2)}, u32[]{:S(2)}) collective-permute-start(bf16[2,128,256]{2,1,0:T(8,128)(2,1)} %bitcast_dynamic-update-slice_fusion.1), channel_id=1, source_target_pairs={{0,12},{4,0},{8,4},{12,8},{1,13},{5,1},{9,5},{13,9},{2,14},{6,2},{... | collective-permute-start | bytes 393224 | tf_op jit(solution)/shard_map/ppermute | solution.py:35
  17.4 33.9 %copy-start.5 = (bf16[4,2,128,256]{3,2,1,0:T(8,128)(2,1)}, bf16[4,2,128,256]{3,2,1,0:T(8,128)(2,1)S(1)}, u32[]{:S(2)}) copy-start(bf16[4,2,128,256]{3,2,1,0:T(8,128)(2,1)S(1)} %pad_maximum_fusion.1.refs_0_) | copy-start | bytes 1572868
  17.4 14.8 %collective-permute-start.4 = (bf16[4,2,128,256]{3,2,1,0:T(8,128)(2,1)S(1)}, bf16[4,2,128,256]{3,2,1,0:T(8,128)(2,1)S(1)}, u32[]{:S(2)}, u32[]{:S(2)}) collective-permute-start(bf16[4,2,128,256]{3,2,1,0:T(8,128)(2,1)S(1)} %pad_maximum_fusion.1.refs_0_), channel_id=1, source_target_pairs={{0,16},{16,0},{1,17},{17,1},{2,18},{18,2},{3,19},{19,3},{4,20},{20... | collective-permute-start | bytes 1572872 | tf_op jit(solution)/shard_map/ppermute | solution.py:35
  21.8 13.9 %collective-permute-start.6 = (bf16[2,128,1024]{2,1,0:T(8,128)(2,1)}, bf16[2,128,1024]{2,1,0:T(8,128)(2,1)S(1)}, u32[]{:S(2)}, u32[]{:S(2)}) collective-permute-start(bf16[2,128,1024]{2,1,0:T(8,128)(2,1)} %bitcast_dynamic-update-slice_fusion.refs_2_), channel_id=1, source_target_pairs={{0,96},{32,0},{64,32},{96,64},{1,97},{33,1},{65,33},{97,65},{2,98}... | collective-permute-start | bytes 1572872 | tf_op jit(solution)/shard_map/ppermute | solution.py:35
  24.5 13.5 %collective-permute-start.7 = (bf16[2,128,1024]{2,1,0:T(8,128)(2,1)}, bf16[2,128,1024]{2,1,0:T(8,128)(2,1)S(1)}, u32[]{:S(2)}, u32[]{:S(2)}) collective-permute-start(bf16[2,128,1024]{2,1,0:T(8,128)(2,1)} %bitcast_dynamic-update-slice_fusion.refs_2_), channel_id=1, source_target_pairs={{0,64},{32,96},{64,0},{96,32},{1,65},{33,97},{65,1},{97,33},{2,66}... | collective-permute-start | bytes 1572872 | tf_op jit(solution)/shard_map/ppermute | solution.py:35
  24.9 26.4 %collective-permute-start.8 = (bf16[2,128,1024]{2,1,0:T(8,128)(2,1)}, bf16[2,128,1024]{2,1,0:T(8,128)(2,1)S(1)}, u32[]{:S(2)}, u32[]{:S(2)}) collective-permute-start(bf16[2,128,1024]{2,1,0:T(8,128)(2,1)} %bitcast_dynamic-update-slice_fusion.refs_2_), channel_id=1, source_target_pairs={{0,32},{32,64},{64,96},{96,0},{1,33},{33,65},{65,97},{97,1},{2,34}... | collective-permute-start | bytes 1572872 | tf_op jit(solution)/shard_map/ppermute | solution.py:35
  29.4 34.0 %collective-permute-start.26 = (bf16[128,512]{1,0:T(8,128)(2,1)}, bf16[128,512]{1,0:T(8,128)(2,1)S(1)}, u32[]{:S(2)}, u32[]{:S(2)}) collective-permute-start(bf16[128,512]{1,0:T(8,128)(2,1)} %get-tuple-element.58), channel_id=1, source_target_pairs={{0,4},{4,8},{8,12},{12,0},{1,5},{5,9},{9,13},{13,1},{2,6},{6,10},{... | collective-permute-start | bytes 393224 | tf_op jit(solution)/shard_map/ppermute | solution.py:35
  30.5 33.9 %copy-start.4 = (bf16[128,512]{1,0:T(8,128)(2,1)S(1)}, bf16[128,512]{1,0:T(8,128)(2,1)}, u32[]{:S(2)}) copy-start(bf16[128,512]{1,0:T(8,128)(2,1)} %get-tuple-element.57) | copy-start | bytes 393220
  32.2 19.2 %copy-start.6 = (bf16[4,2,128,256]{3,2,1,0:T(8,128)(2,1)}, bf16[4,2,128,256]{3,2,1,0:T(8,128)(2,1)S(1)}, u32[]{:S(2)}) copy-start(bf16[4,2,128,256]{3,2,1,0:T(8,128)(2,1)S(1)} %collective-permute-done.4.refs_1_) | copy-start | bytes 1572868
  32.2 32.2 %collective-permute-start.25 = (bf16[128,512]{1,0:T(8,128)(2,1)}, bf16[128,512]{1,0:T(8,128)(2,1)S(1)}, u32[]{:S(2)}, u32[]{:S(2)}) collective-permute-start(bf16[128,512]{1,0:T(8,128)(2,1)} %get-tuple-element.59), channel_id=1, source_target_pairs={{0,8},{4,12},{8,0},{12,4},{1,9},{5,13},{9,1},{13,5},{2,10},{6,14},... | collective-permute-start | bytes 393224 | tf_op jit(solution)/shard_map/ppermute | solution.py:35
  35.7 15.6 %copy-start.7 = (bf16[2,128,1024]{2,1,0:T(8,128)(2,1)}, bf16[2,128,1024]{2,1,0:T(8,128)(2,1)S(1)}, u32[]{:S(2)}) copy-start(bf16[2,128,1024]{2,1,0:T(8,128)(2,1)S(1)} %collective-permute-done.6.refs_3_) | copy-start | bytes 1572868
  35.7 28.7 %collective-permute-start.24 = (bf16[128,512]{1,0:T(8,128)(2,1)}, bf16[128,512]{1,0:T(8,128)(2,1)S(1)}, u32[]{:S(2)}, u32[]{:S(2)}) collective-permute-start(bf16[128,512]{1,0:T(8,128)(2,1)} %get-tuple-element.60), channel_id=1, source_target_pairs={{0,12},{4,0},{8,4},{12,8},{1,13},{5,1},{9,5},{13,9},{2,14},{6,2},{... | collective-permute-start | bytes 393224 | tf_op jit(solution)/shard_map/ppermute | solution.py:35
  38.1 13.3 %copy-start.8 = (bf16[2,128,1024]{2,1,0:T(8,128)(2,1)}, bf16[2,128,1024]{2,1,0:T(8,128)(2,1)S(1)}, u32[]{:S(2)}) copy-start(bf16[2,128,1024]{2,1,0:T(8,128)(2,1)S(1)} %collective-permute-done.7.refs_4_) | copy-start | bytes 1572868
  51.4 0.8 copy-start.9
  62.9 3.3 %collective-permute-start.9 = (f32[16,1024]{1,0:T(8,128)}, f32[16,1024]{1,0:T(8,128)S(1)}, u32[]{:S(2)}, u32[]{:S(2)}) collective-permute-start(f32[16,1024]{1,0:T(8,128)} %get-tuple-element.63), channel_id=1, source_target_pairs={{0,96},{32,0},{64,32},{96,64},{1,97},{33,1},{65,33},{97,65},{2,98}... | collective-permute-start | bytes 196616 | tf_op jit(solution)/shard_map/ppermute | solution.py:35
  62.9 4.9 %collective-permute-start.10 = (f32[16,1024]{1,0:T(8,128)}, f32[16,1024]{1,0:T(8,128)S(1)}, u32[]{:S(2)}, u32[]{:S(2)}) collective-permute-start(f32[16,1024]{1,0:T(8,128)} %get-tuple-element.64), channel_id=1, source_target_pairs={{0,64},{32,96},{64,0},{96,32},{1,65},{33,97},{65,1},{97,33},{2,66}... | collective-permute-start | bytes 196616 | tf_op jit(solution)/shard_map/ppermute | solution.py:35
  63.4 5.3 %collective-permute-start.11 = (f32[16,1024]{1,0:T(8,128)}, f32[16,1024]{1,0:T(8,128)S(1)}, u32[]{:S(2)}, u32[]{:S(2)}) collective-permute-start(f32[16,1024]{1,0:T(8,128)} %get-tuple-element.65), channel_id=1, source_target_pairs={{0,32},{32,64},{64,96},{96,0},{1,33},{33,65},{65,97},{97,1},{2,34}... | collective-permute-start | bytes 196616 | tf_op jit(solution)/shard_map/ppermute | solution.py:35
  64.5 28.3 %collective-permute-start.27 = (bf16[4,128,512]{2,1,0:T(8,128)(2,1)S(1)}, bf16[4,128,512]{2,1,0:T(8,128)(2,1)S(1)}, u32[]{:S(2)}, u32[]{:S(2)}) collective-permute-start(bf16[4,128,512]{2,1,0:T(8,128)(2,1)S(1)} %get-tuple-element.77), channel_id=1, source_target_pairs={{0,1},{1,0},{2,3},{3,2},{4,5},{5,4},{6,7},{7,6},{8,9},{9,8},{10,11... | collective-permute-start | bytes 1572872 | tf_op jit(solution)/shard_map/ppermute | solution.py:35
  66.3 2.4 %copy-start.11 = (f32[16,1024]{1,0:T(8,128)}, f32[16,1024]{1,0:T(8,128)S(1)}, u32[]{:S(2)}) copy-start(f32[16,1024]{1,0:T(8,128)S(1)} %collective-permute-done.9.refs_9_) | copy-start | bytes 196612
  67.8 0.8 copy-start.12
  68.7 0.6 copy-start.13
  87.2 5.5 %copy-start.10 = (bf16[4,2,128,256]{3,2,1,0:T(8,128)(2,1)S(1)}, bf16[4,2,128,256]{3,2,1,0:T(8,128)(2,1)}, u32[]{:S(2)}) copy-start(bf16[4,2,128,256]{3,2,1,0:T(8,128)(2,1)} %get-tuple-element.71) | copy-start | bytes 1572868
  87.2 6.8 %collective-permute-start.14 = (bf16[2,128,512]{2,1,0:T(8,128)(2,1)}, bf16[2,128,512]{2,1,0:T(8,128)(2,1)S(1)}, u32[]{:S(2)}, u32[]{:S(2)}) collective-permute-start(bf16[2,128,512]{2,1,0:T(8,128)(2,1)} %get-tuple-element.69), channel_id=1, source_target_pairs={{0,96},{32,0},{64,32},{96,64},{1,97},{33,1},{65,33},{97,65},{2,98}... | collective-permute-start | bytes 786440 | tf_op jit(solution)/shard_map/ppermute | solution.py:35
  88.8 7.0 %collective-permute-start.13 = (bf16[2,128,512]{2,1,0:T(8,128)(2,1)}, bf16[2,128,512]{2,1,0:T(8,128)(2,1)S(1)}, u32[]{:S(2)}, u32[]{:S(2)}) collective-permute-start(bf16[2,128,512]{2,1,0:T(8,128)(2,1)} %get-tuple-element.68), channel_id=1, source_target_pairs={{0,64},{32,96},{64,0},{96,32},{1,65},{33,97},{65,1},{97,33},{2,66}... | collective-permute-start | bytes 786440 | tf_op jit(solution)/shard_map/ppermute | solution.py:35
  90.1 12.7 %copy-start.3 = (f32[2,128,512]{2,1,0:T(8,128)S(1)}, f32[2,128,512]{2,1,0:T(8,128)}, u32[]{:S(2)}) copy-start(f32[2,128,512]{2,1,0:T(8,128)} %get-tuple-element.66) | copy-start | bytes 1572868
  90.1 12.7 %collective-permute-start.12 = (bf16[2,128,512]{2,1,0:T(8,128)(2,1)}, bf16[2,128,512]{2,1,0:T(8,128)(2,1)S(1)}, u32[]{:S(2)}, u32[]{:S(2)}) collective-permute-start(bf16[2,128,512]{2,1,0:T(8,128)(2,1)} %get-tuple-element.67), channel_id=1, source_target_pairs={{0,32},{32,64},{64,96},{96,0},{1,33},{33,65},{65,97},{97,1},{2,34}... | collective-permute-start | bytes 786440 | tf_op jit(solution)/shard_map/ppermute | solution.py:35
  92.0 41.2 %collective-permute-start.22 = (bf16[2048,256]{1,0:T(8,128)(2,1)S(1)}, bf16[2048,256]{1,0:T(8,128)(2,1)S(1)}, u32[]{:S(2)}, u32[]{:S(2)}) collective-permute-start(bf16[2048,256]{1,0:T(8,128)(2,1)S(1)} %dynamic-slice_select_fusion), channel_id=1, source_target_pairs={{0,1},{1,0},{2,3},{3,2},{4,5},{5,4},{6,7},{7,6},{8,9},{9,8},{10,11... | collective-permute-start | bytes 3145736 | tf_op jit(solution)/shard_map/ppermute | solution.py:35
  92.8 30.8 %copy-start.2 = (bf16[4,2,128,256]{3,2,1,0:T(8,128)(2,1)S(1)}, bf16[4,2,128,256]{3,2,1,0:T(8,128)(2,1)}, u32[]{:S(2)}) copy-start(bf16[4,2,128,256]{3,2,1,0:T(8,128)(2,1)} %get-tuple-element.70) | copy-start | bytes 1572868
  92.8 30.8 %collective-permute-start.16 = (bf16[4,2,128,256]{3,2,1,0:T(8,128)(2,1)S(1)}, bf16[4,2,128,256]{3,2,1,0:T(8,128)(2,1)S(1)}, u32[]{:S(2)}, u32[]{:S(2)}) collective-permute-start(bf16[4,2,128,256]{3,2,1,0:T(8,128)(2,1)S(1)} %copy-done.10), channel_id=1, source_target_pairs={{0,16},{16,0},{1,17},{17,1},{2,18},{18,2},{3,19},{19,3},{4,20},{20... | collective-permute-start | bytes 1572872 | tf_op jit(solution)/shard_map/ppermute | solution.py:35
  102.9 26.0 %collective-permute-start.15 = (bf16[128,512]{1,0:T(8,128)(2,1)S(1)}, bf16[128,512]{1,0:T(8,128)(2,1)S(1)}, u32[]{:S(2)}, u32[]{:S(2)}) collective-permute-start(bf16[128,512]{1,0:T(8,128)(2,1)S(1)} %get-tuple-element.82), channel_id=1, source_target_pairs={{0,2},{2,0},{1,3},{3,1},{4,6},{6,4},{5,7},{7,5},{8,10},{10,8},{9,1... | collective-permute-start | bytes 393224 | tf_op jit(solution)/shard_map/ppermute | solution.py:35
  123.8 18.8 %copy-start = (bf16[4096,256]{1,0:T(8,128)(2,1)S(1)}, bf16[4096,256]{1,0:T(8,128)(2,1)}, u32[]{:S(2)}) copy-start(bf16[4096,256]{1,0:T(8,128)(2,1)} %param.18) | copy-start | bytes 6291460
  123.8 10.3 %collective-permute-start.19 = (bf16[2,128,256]{2,1,0:T(8,128)(2,1)S(1)}, bf16[2,128,256]{2,1,0:T(8,128)(2,1)S(1)}, u32[]{:S(2)}, u32[]{:S(2)}) collective-permute-start(bf16[2,128,256]{2,1,0:T(8,128)(2,1)S(1)} %get-tuple-element.79), channel_id=1, source_target_pairs={{0,12},{4,0},{8,4},{12,8},{1,13},{5,1},{9,5},{13,9},{2,14},{6,2},{... | collective-permute-start | bytes 393224 | tf_op jit(solution)/shard_map/ppermute | solution.py:35
  127.9 6.2 %collective-permute-start.18 = (bf16[2,128,256]{2,1,0:T(8,128)(2,1)S(1)}, bf16[2,128,256]{2,1,0:T(8,128)(2,1)S(1)}, u32[]{:S(2)}, u32[]{:S(2)}) collective-permute-start(bf16[2,128,256]{2,1,0:T(8,128)(2,1)S(1)} %get-tuple-element.80), channel_id=1, source_target_pairs={{0,8},{4,12},{8,0},{12,4},{1,9},{5,13},{9,1},{13,5},{2,10},{6,14},... | collective-permute-start | bytes 393224 | tf_op jit(solution)/shard_map/ppermute | solution.py:35
  128.5 6.2 %collective-permute-start.17 = (bf16[2,128,256]{2,1,0:T(8,128)(2,1)S(1)}, bf16[2,128,256]{2,1,0:T(8,128)(2,1)S(1)}, u32[]{:S(2)}, u32[]{:S(2)}) collective-permute-start(bf16[2,128,256]{2,1,0:T(8,128)(2,1)S(1)} %get-tuple-element.78), channel_id=1, source_target_pairs={{0,4},{4,8},{8,12},{12,0},{1,5},{5,9},{9,13},{13,1},{2,6},{6,10},{... | collective-permute-start | bytes 393224 | tf_op jit(solution)/shard_map/ppermute | solution.py:35
  128.9 14.1 %copy-start.1 = (bf16[4096,256]{1,0:T(8,128)(2,1)S(1)}, bf16[4096,256]{1,0:T(8,128)(2,1)}, u32[]{:S(2)}) copy-start(bf16[4096,256]{1,0:T(8,128)(2,1)} %param.17) | copy-start | bytes 6291460
  129.0 20.1 %collective-permute-start.28 = (bf16[4,128,1024]{2,1,0:T(8,128)(2,1)S(1)}, bf16[4,128,1024]{2,1,0:T(8,128)(2,1)S(1)}, u32[]{:S(2)}, u32[]{:S(2)}) collective-permute-start(bf16[4,128,1024]{2,1,0:T(8,128)(2,1)S(1)} %maximum_select_fusion.1), channel_id=1, source_target_pairs={{0,2},{2,0},{1,3},{3,1},{4,6},{6,4},{5,7},{7,5},{8,10},{10,8},{9,1... | collective-permute-start | bytes 3145736 | tf_op jit(solution)/shard_map/ppermute | solution.py:35
  133.2 25.4 %collective-permute-start.23 = (bf16[2048,256]{1,0:T(8,128)(2,1)S(1)}, bf16[2048,256]{1,0:T(8,128)(2,1)S(1)}, u32[]{:S(2)}, u32[]{:S(2)}) collective-permute-start(bf16[2048,256]{1,0:T(8,128)(2,1)S(1)} %collective-permute-done.22), channel_id=1, source_target_pairs={{0,2},{2,0},{1,3},{3,1},{4,6},{6,4},{5,7},{7,5},{8,10},{10,8},{9,1... | collective-permute-start | bytes 3145736 | tf_op jit(solution)/shard_map/ppermute | solution.py:35
  134.7 6.5 %collective-permute-start.20 = (bf16[128,256]{1,0:T(8,128)(2,1)S(1)}, bf16[128,256]{1,0:T(8,128)(2,1)S(1)}, u32[]{:S(2)}, u32[]{:S(2)}) collective-permute-start(bf16[128,256]{1,0:T(8,128)(2,1)S(1)} %slice_bitcast_fusion.6), channel_id=1, source_target_pairs={{0,2},{2,0},{1,3},{3,1},{4,6},{6,4},{5,7},{7,5},{8,10},{10,8},{9,1... | collective-permute-start | bytes 196616 | tf_op jit(solution)/shard_map/ppermute | solution.py:35
  139.8 9.0 %collective-permute-start.31 = (bf16[2,128,256]{2,1,0:T(8,128)(2,1)S(1)}, bf16[2,128,256]{2,1,0:T(8,128)(2,1)S(1)}, u32[]{:S(2)}, u32[]{:S(2)}) collective-permute-start(bf16[2,128,256]{2,1,0:T(8,128)(2,1)S(1)} %fusion.27), channel_id=1, source_target_pairs={{0,4},{4,8},{8,12},{12,0},{1,5},{5,9},{9,13},{13,1},{2,6},{6,10},{... | collective-permute-start | bytes 393224 | tf_op jit(solution)/shard_map/ppermute | solution.py:35
  139.8 9.0 %collective-permute-start.30 = (bf16[2,128,256]{2,1,0:T(8,128)(2,1)S(1)}, bf16[2,128,256]{2,1,0:T(8,128)(2,1)S(1)}, u32[]{:S(2)}, u32[]{:S(2)}) collective-permute-start(bf16[2,128,256]{2,1,0:T(8,128)(2,1)S(1)} %fusion.27), channel_id=1, source_target_pairs={{0,8},{4,12},{8,0},{12,4},{1,9},{5,13},{9,1},{13,5},{2,10},{6,14},... | collective-permute-start | bytes 393224 | tf_op jit(solution)/shard_map/ppermute | solution.py:35
  141.2 7.9 %collective-permute-start.29 = (bf16[2,128,256]{2,1,0:T(8,128)(2,1)S(1)}, bf16[2,128,256]{2,1,0:T(8,128)(2,1)S(1)}, u32[]{:S(2)}, u32[]{:S(2)}) collective-permute-start(bf16[2,128,256]{2,1,0:T(8,128)(2,1)S(1)} %fusion.27), channel_id=1, source_target_pairs={{0,12},{4,0},{8,4},{12,8},{1,13},{5,1},{9,5},{13,9},{2,14},{6,2},{... | collective-permute-start | bytes 393224 | tf_op jit(solution)/shard_map/ppermute | solution.py:35
  148.8 9.9 %collective-permute-start.21 = (bf16[128,512]{1,0:T(8,128)(2,1)S(1)}, bf16[128,512]{1,0:T(8,128)(2,1)S(1)}, u32[]{:S(2)}, u32[]{:S(2)}) collective-permute-start(bf16[128,512]{1,0:T(8,128)(2,1)S(1)} %pad_maximum_fusion.3), channel_id=1, source_target_pairs={{0,1},{1,0},{2,3},{3,2},{4,5},{5,4},{6,7},{7,6},{8,9},{9,8},{10,11... | collective-permute-start | bytes 393224 | tf_op jit(solution)/shard_map/ppermute | solution.py:35
  150.7 19.3 %all-to-all-start = ((bf16[16,64,256]{2,1,0:T(8,128)(2,1)}), bf16[16,64,256]{2,1,0:T(8,128)(2,1)}, u32[]{:S(2)}, u32[]{:S(2)}) async-start(bf16[16,64,256]{2,1,0:T(8,128)(2,1)} %bitcast.65), calls=%async_computation | async-start | bytes 1048576 | tf_op jit(solution)/shard_map/all_to_all | solution.py:346
where the time goes:
time: 172 us
  waiting for transfers between devices  68.1 us (40%)
  starting transfers between devices  53.2 us (31%)
  Pallas kernels  34.5 us (20%)
  other arithmetic  5.43 us (3%)
  local copies, waits for them, and re-layouts  4.92 us (3%)
  matrix products  4.63 us (3%)
    ppermute x32, waiting for transfers between devices, moved(): return lax.ppermute(array, axis, [(i, (i + by) % n) for i in range(n)])  58.6 us
    ppermute x32, starting transfers between devices, moved(): return lax.ppermute(array, axis, [(i, (i + by) % n) for i in range(n)])  45.2 us
    pallas_call x1, Pallas kernels, run_grads(): pl.pallas_call(grads_kernel, out_shape=[dkv, dkv] + dq, scratch_shapes=co...  17.9 us
    pallas_call x1, Pallas kernels, run_stats(): pl.pallas_call(stats_kernel, out_shape=[jax.ShapeDtypeStruct((PARTS * 4,...  10.8 us
    all_to_all x1, waiting for transfers between devices, step(): got = lax.all_to_all(pieces, ('y', 'z', 'c'), 0, 0, tiled=True)  9.5 us
    all_to_all x1, starting transfers between devices, step(): got = lax.all_to_all(pieces, ('y', 'z', 'c'), 0, 0, tiled=True)  7.95 us
  transfers between devices with their start and end apart: 33, of which 17 were waited for; matrix products, arithmetic and copies ran while one was open for 8% of the time, Pallas kernels for 18%

commit v1 on v0

--- a/solution.py
+++ b/solution.py
@@ -46,10 +46,10 @@
 def load_parts(kv_refs, qg_refs, kpos_ref, ks, vs, qs, gs, kposb):
     for part in range(PARTS):
         tok = slice(part * T, (part + 1) * T)
-        for a in range(2):
-            rows = slice(a * 8 * T, (a + 1) * 8 * T)
-            ks[part, rows, :] = kv_refs[a][:, :, tok, :HEAD].reshape(8 * T, HEAD)
-            vs[part, rows, :] = kv_refs[a][:, :, tok, HEAD:].reshape(8 * T, HEAD)
+        for b in range(4):
+            rows = slice(b * 4 * T, (b + 1) * 4 * T)
+            ks[part, rows, :] = kv_refs[b][:, :, tok, :HEAD].reshape(4 * T, HEAD)
+            vs[part, rows, :] = kv_refs[b][:, :, tok, HEAD:].reshape(4 * T, HEAD)
         for h in range(GROUP):
             for s in range(4):
                 row = (h * QSLOTS + s * 2) * T
@@ -73,10 +73,10 @@
 
 
 def stats_kernel(*refs):
-    kv_refs, qg_refs = refs[0:2], refs[2:6]
-    kpos_ref, qpos_ref = refs[6:8]
-    out_refs = refs[8:12]
-    ks, vs, qs, gs, kposb, ms, ls, ws = refs[12:]
+    kv_refs, qg_refs = refs[0:4], refs[4:8]
+    kpos_ref, qpos_ref = refs[8:10]
+    out_refs = refs[10:14]
+    ks, vs, qs, gs, kposb, ms, ls, ws = refs[14:]
     load_parts(kv_refs, qg_refs, kpos_ref, ks, vs, qs, gs, kposb)
     ms[...] = jnp.full(ms.shape, NEG, F32)
     ls[...] = jnp.zeros(ls.shape, F32)
@@ -115,11 +115,11 @@
 
 
 def grads_kernel(*refs):
-    kv_refs, qg_refs = refs[0:2], refs[2:6]
-    kpos_ref, qpos_ref = refs[6:8]
-    st_refs = refs[8:12]
-    dkv_refs, dq_refs = refs[12:14], refs[14:18]
-    ks, vs, qs, gs, kposb, kt, dks, dvs, dqt, lse, mean = refs[18:]
+    kv_refs, qg_refs = refs[0:4], refs[4:8]
+    kpos_ref, qpos_ref = refs[8:10]
+    st_refs = refs[10:14]
+    dkv_refs, dq_refs = refs[14:16], refs[16:20]
+    ks, vs, qs, gs, kposb, kt, dks, dvs, dqt, lse, mean = refs[20:]
     load_parts(kv_refs, qg_refs, kpos_ref, ks, vs, qs, gs, kposb)
     for part in range(PARTS):
         kt[part] = ks[part].T
@@ -149,10 +149,11 @@
         lax.fori_loop(delta, PARTS, body, 0)
     for part in range(PARTS):
         tok = slice(part * T, (part + 1) * T)
-        for a in range(2):
-            rows = slice(a * 8 * T, (a + 1) * 8 * T)
-            dkv_refs[a][:, :, tok, :HEAD] = (dks[part, rows, :] * SCALE).astype(BF).reshape(4, 2, T, HEAD)
-            dkv_refs[a][:, :, tok, HEAD:] = dvs[part, rows, :].astype(BF).reshape(4, 2, T, HEAD)
+        for b in range(4):
+            for a in range(2):
+                rows = slice((b * 4 + a * 2) * T, (b * 4 + a * 2 + 2) * T)
+                dkv_refs[a][b, :, tok, :HEAD] = (dks[part, rows, :] * SCALE).astype(BF).reshape(2, T, HEAD)
+                dkv_refs[a][b, :, tok, HEAD:] = dvs[part, rows, :].astype(BF).reshape(2, T, HEAD)
         dq = dqt[part].T * SCALE
         for h in range(GROUP):
             for s in range(4):
@@ -229,21 +230,24 @@
     )(at, q, g, k, v)
 
 
-def columns_kernel(at_ref, in_ref, *out_refs):
-    for o in range(4):
-        target = (at_ref[1] + o) % 4
-        for n in range(4):
-            cols = pl.ds(pl.multiple_of(n * 4 * HEAD + target * HEAD, 128), HEAD)
-            out_refs[o][:, n * HEAD : (n + 1) * HEAD] = in_ref[:, cols]
-
-
-def run_columns(at, layer_input):
+def columns_kernel(at_ref, mine_ref, far_ref, *out_refs):
+    for ref, half in ((mine_ref, at_ref[2]), (far_ref, 1 - at_ref[2])):
+        for o in range(4):
+            target = (at_ref[1] + o) % 4
+            for n in range(4):
+                src = pl.ds(pl.multiple_of(n * 4 * HEAD + target * HEAD, 128), HEAD)
+                dst = pl.ds(pl.multiple_of(half * 4 * HEAD + n * HEAD, 128), HEAD)
+                out_refs[o][:, dst] = ref[:, src]
+
+
+def run_columns(at, mine, far):
+    vmem = pl.BlockSpec(memory_space=pltpu.VMEM)
     return pl.pallas_call(
         columns_kernel,
-        out_shape=[jax.ShapeDtypeStruct((TOK, 4 * HEAD), BF)] * 4,
-        in_specs=[pl.BlockSpec(memory_space=pltpu.SMEM), pl.BlockSpec(memory_space=pltpu.VMEM)],
+        out_shape=[jax.ShapeDtypeStruct((TOK, 8 * HEAD), BF)] * 4,
+        in_specs=[pl.BlockSpec(memory_space=pltpu.SMEM), vmem, vmem],
         name="columns",
-    )(at, layer_input)
+    )(at, mine, far)
 
 
 def finish_kernel(in_ref, k_ref, v_ref):
@@ -264,7 +268,7 @@
     def device(yy, zz, xx, cc):
         return (((yy % 4) * 2 + zz % 2) * 4 + xx % 4) * 2 + cc % 2
 
-    a, b, e = jnp.meshgrid(jnp.arange(2), jnp.arange(4), jnp.arange(2), indexing="ij")
+    b, a, e = jnp.meshgrid(jnp.arange(4), jnp.arange(2), jnp.arange(2), indexing="ij")
     keys = device(y, z + a, x + b, c + e).reshape(KSLOTS)
     a, e = jnp.meshgrid(jnp.arange(4), jnp.arange(2), indexing="ij")
     queries = device(y + a, z, x, c + e).reshape(QSLOTS)
@@ -290,24 +294,25 @@
 
 def step(query_rows, key_rows, value_rows, output_grad, layer_input, key_matrix, value_matrix, run_placement):
     y, z, x, c, t = (lax.axis_index(a) for a in ("y", "z", "x", "c", "tp"))
-    at = jnp.stack([c, x]).astype(jnp.int32)
+    at = jnp.stack([c, x, t]).astype(jnp.int32)
+    x_far = moved(layer_input, "tp", 1)
     kv_pair, qg_pair, kv_send, qg_send = run_pack(at, query_rows, output_grad, key_rows, value_rows)
+    qg_own = qg_pair.at[1].set(moved(qg_send, "c", 1))
     kv_own = kv_pair.at[1].set(moved(kv_send, "c", 1))
-    qg_own = qg_pair.at[1].set(moved(qg_send, "c", 1))
+    qgs = [qg_own] + [moved(qg_own, "y", -o) for o in (1, 2, 3)]
+    kv_both = jnp.stack([kv_own, moved(kv_own, "z", 1)])
+    kvs = [kv_both] + [moved(kv_both, "x", -o) for o in (1, 2, 3)]
     kpos, qpos = positions(run_placement, y, z, x, c)
-    kv_row = jnp.stack([kv_own] + [moved(kv_own, "x", -o) for o in (1, 2, 3)])
-    qgs = [qg_own] + [moved(qg_own, "y", -o) for o in (1, 2, 3)]
-    kvs = [kv_row, moved(kv_row, "z", 1)]
 
     half = key_matrix.shape[0] // 2
-    cuts = [lax.dynamic_slice_in_dim(after(m, kv_row), (1 - t) * half, half, 0) for m in (key_matrix, value_matrix)]
+    cuts = [lax.dynamic_slice_in_dim(after(m, kv_both), (1 - t) * half, half, 0) for m in (key_matrix, value_matrix)]
+    x_pieces = run_columns(at, after(layer_input, kv_both), x_far)
+    x_here = jnp.stack([x_pieces[0]] + [moved(x_pieces[4 - o], "x", -o) for o in (1, 2, 3)])
     m_far = moved(jnp.where(c == 0, *cuts), "tp", 1)
-    x_pieces = run_columns(at, after(layer_input, kv_row))
     kpos = after(kpos, *x_pieces)
 
     sts = run_stats(kvs, qgs, kpos, qpos)
     sts = [sts[0]] + [moved(sts[o], "y", -o) for o in (1, 2, 3)]
-    x_half = jnp.stack([x_pieces[0]] + [moved(x_pieces[4 - o], "x", -o) for o in (1, 2, 3)])
     dkvs, dqs = run_grads(kvs, qgs, kpos, qpos, sts)
 
     def total_of(own, arrived):
@@ -318,8 +323,6 @@
 
     dkv_row = total_of(dkvs[0], [moved(dkvs[1], "z", 1)])
     dq = total_of(dqs[0], [moved(dqs[o], "y", o) for o in (1, 2, 3)])
-    x_other = moved(x_half, "tp", 1)
-    x_here = jnp.where(t == 0, jnp.concatenate([x_half, x_other], 2), jnp.concatenate([x_other, x_half], 2))
     x_all = jnp.stack([x_here, moved(x_here, "c", 1)], axis=1)
     m_core = moved(m_far, "c", 1)
     k_far = jnp.where(c == 0, m_far, m_core)

time: 172 us -> 167 us (0.971)
  starting transfers between devices: 53.2 us -> 49 us
    ppermute x32, starting transfers between devices: 45.2 us -> 39.6 us  [moved(): return lax.ppermute(array, axis, [(i, (i + by) % n) for i in range(n)])]
  transfers between devices with their start and end apart: 33 -> 33, of which waited for: 17 -> 14; matrix products, arithmetic and copies ran while one was open for 8% -> 8% of each run, Pallas kernels for 18% -> 2%
where the time goes in v1:
time: 167 us
  waiting for transfers between devices  66.8 us (40%)
  starting transfers between devices  49 us (29%)
  Pallas kernels  35.2 us (21%)
  matrix products  5.38 us (3%)
  local copies, waits for them, and re-layouts  4.98 us (3%)
  other arithmetic  4.62 us (3%)
    ppermute x32, waiting for transfers between devices, moved(): return lax.ppermute(array, axis, [(i, (i + by) % n) for i in range(n)])  57.3 us
    ppermute x32, starting transfers between devices, moved(): return lax.ppermute(array, axis, [(i, (i + by) % n) for i in range(n)])  39.6 us
    pallas_call x1, Pallas kernels, run_grads(): pl.pallas_call(grads_kernel, out_shape=[dkv, dkv] + dq, scratch_shapes=co...  18.1 us
    pallas_call x1, Pallas kernels, run_stats(): pl.pallas_call(stats_kernel, out_shape=[jax.ShapeDtypeStruct((PARTS * 4,...  10.8 us
    all_to_all x1, waiting for transfers between devices, step(): got = lax.all_to_all(pieces, ('y', 'z', 'c'), 0, 0, tiled=True)  9.5 us
    all_to_all x1, starting transfers between devices, step(): got = lax.all_to_all(pieces, ('y', 'z', 'c'), 0, 0, tiled=True)  9.37 us
  transfers between devices with their start and end apart: 33, of which 14 were waited for; matrix products, arithmetic and copies ran while one was open for 8% of the time, Pallas kernels for 2%

profile of v1, /device:TPU:1, one launch (start us, length us, event | category | flops | bytes accessed | tf_op | source)
XLA Modules:
  0.0 166.9 jit_solution(3164350934339529572)
XLA Ops:
  0.6 0.7 pad_add_fusion.at_ref
  1.3 2.0 %pack.1 = (bf16[2,128,256]{2,1,0:T(8,128)(2,1)}, bf16[2,128,1024]{2,1,0:T(8,128)(2,1)}, bf16[128,256]{1,0:T(8,128)(2,1)}, bf16[128,1024]{1,0:T(8,128)(2,1)}) custom-call(s32[3]{0:T(128)} %pad_add_fusion.at_ref, bf16[128,1024]{1,0:T(8,128)(2,1)} %q_ref.1, bf16[128,1024]{1,0:T(8,128)(2,1)} %g_ref.1, bf16[128,256]{1,0:T(8,128)(2,1)} %k_ref.1, ...), custom_call_target="tpu_custom_call" | custom-call | tf_op jit(solution)/shard_map/pack/pallas_call | solution.py:225
  3.3 1.4 collective-permute-start
  4.8 1.7 %collective-permute-start.9 = (bf16[128,2048]{1,0:T(8,128)(2,1)}, bf16[128,2048]{1,0:T(8,128)(2,1)S(1)}, u32[]{:S(2)}, u32[]{:S(2)}) collective-permute-start(bf16[128,2048]{1,0:T(8,128)(2,1)} %mine_ref), channel_id=1, source_target_pairs={{0,1},{1,0},{2,3},{3,2},{4,5},{5,4},{6,7},{7,6},{8,9},{9,8},{10,11... | collective-permute-start | bytes 1572872 | tf_op jit(solution)/shard_map/ppermute | solution.py:35
  7.0 0.6 bitcast_dynamic-update-slice_fusion.1
  7.6 3.3 %collective-permute-start.1 = (bf16[2,128,256]{2,1,0:T(8,128)(2,1)}, bf16[2,128,256]{2,1,0:T(8,128)(2,1)S(1)}, u32[]{:S(2)}, u32[]{:S(2)}) collective-permute-start(bf16[2,128,256]{2,1,0:T(8,128)(2,1)} %bitcast_dynamic-update-slice_fusion.1), channel_id=1, source_target_pairs={{0,16},{16,0},{1,17},{17,1},{2,18},{18,2},{3,19},{19,3},{4,20},{20... | collective-permute-start | bytes 393224 | tf_op jit(solution)/shard_map/ppermute | solution.py:35
  11.2 13.3 %collective-permute-done.1 = bf16[2,128,256]{2,1,0:T(8,128)(2,1)S(1)} collective-permute-done((bf16[2,128,256]{2,1,0:T(8,128)(2,1)}, bf16[2,128,256]{2,1,0:T(8,128)(2,1)S(1)}, u32[]{:S(2)}, u32[]{:S(2)}) %collective-permute-start.1) | collective-permute-done | bytes 131104 | tf_op jit(solution)/shard_map/ppermute | solution.py:35
  24.5 0.9 pad_maximum_fusion.2.refs_0_
  25.4 2.5 %collective-permute-start.2 = (bf16[2,2,128,256]{3,2,1,0:T(8,128)(2,1)S(1)}, bf16[2,2,128,256]{3,2,1,0:T(8,128)(2,1)S(1)}, u32[]{:S(2)}, u32[]{:S(2)}) collective-permute-start(bf16[2,2,128,256]{3,2,1,0:T(8,128)(2,1)S(1)} %pad_maximum_fusion.2.refs_0_), channel_id=1, source_target_pairs={{0,12},{4,0},{8,4},{12,8},{1,13},{5,1},{9,5},{13,9},{2,14},{6,2},{... | collective-permute-start | bytes 786440 | tf_op jit(solution)/shard_map/ppermute | solution.py:35
  28.0 0.7 bitcast_dynamic-update-slice_fusion.refs_4_
  28.7 2.7 %collective-permute-start.6 = (bf16[2,128,1024]{2,1,0:T(8,128)(2,1)}, bf16[2,128,1024]{2,1,0:T(8,128)(2,1)S(1)}, u32[]{:S(2)}, u32[]{:S(2)}) collective-permute-start(bf16[2,128,1024]{2,1,0:T(8,128)(2,1)} %bitcast_dynamic-update-slice_fusion.refs_4_), channel_id=1, source_target_pairs={{0,96},{32,0},{64,32},{96,64},{1,97},{33,1},{65,33},{97,65},{2,98}... | collective-permute-start | bytes 1572872 | tf_op jit(solution)/shard_map/ppermute | solution.py:35
  31.8 0.7 collective-permute-start.8
  32.5 2.3 %collective-permute-start.3 = (bf16[2,2,128,256]{3,2,1,0:T(8,128)(2,1)S(1)}, bf16[2,2,128,256]{3,2,1,0:T(8,128)(2,1)S(1)}, u32[]{:S(2)}, u32[]{:S(2)}) collective-permute-start(bf16[2,2,128,256]{3,2,1,0:T(8,128)(2,1)S(1)} %pad_maximum_fusion.2.refs_0_), channel_id=1, source_target_pairs={{0,8},{4,12},{8,0},{12,4},{1,9},{5,13},{9,1},{13,5},{2,10},{6,14},... | collective-permute-start | bytes 786440 | tf_op jit(solution)/shard_map/ppermute | solution.py:35
  34.8 1.5 collective-permute-start.4
  36.4 1.1 convolution_add_fusion.2
  38.2 0.6 broadcast_in_dim.61.refs_9_
  38.9 2.5 %columns.1 = (bf16[128,1024]{1,0:T(8,128)(2,1)}, bf16[128,1024]{1,0:T(8,128)(2,1)}, bf16[128,1024]{1,0:T(8,128)(2,1)}, bf16[128,1024]{1,0:T(8,128)(2,1)}) custom-call(s32[3]{0:T(128)} %pad_add_fusion.at_ref, bf16[128,2048]{1,0:T(8,128)(2,1)} %mine_ref, bf16[128,2048]{1,0:T(8,128)(2,1)} %copy-done.5), custom_call_target="tpu_custom_call" | custom-call | tf_op jit(solution)/shard_map/columns/pallas_call | solution.py:245
  41.4 5.6 %collective-permute-done.4.refs_3_ = bf16[2,2,128,256]{3,2,1,0:T(8,128)(2,1)S(1)} collective-permute-done((bf16[2,2,128,256]{3,2,1,0:T(8,128)(2,1)S(1)}, bf16[2,2,128,256]{3,2,1,0:T(8,128)(2,1)S(1)}, u32[]{:S(2)}, u32[]{:S(2)}) %collective-permute-start.4) | collective-permute-done | bytes 262176 | tf_op jit(solution)/shard_map/ppermute | solution.py:35
  47.0 11.2 %collective-permute-done.8.refs_7_ = bf16[2,128,1024]{2,1,0:T(8,128)(2,1)S(1)} collective-permute-done((bf16[2,128,1024]{2,1,0:T(8,128)(2,1)}, bf16[2,128,1024]{2,1,0:T(8,128)(2,1)S(1)}, u32[]{:S(2)}, u32[]{:S(2)}) %collective-permute-start.8) | collective-permute-done | bytes 524320 | tf_op jit(solution)/shard_map/ppermute | solution.py:35
  58.3 0.8 copy-done.10
  59.1 10.8 %stats.1 = (f32[16,1024]{1,0:T(8,128)}, f32[16,1024]{1,0:T(8,128)}, f32[16,1024]{1,0:T(8,128)}, f32[16,1024]{1,0:T(8,128)}) custom-call(bf16[2,2,128,256]{3,2,1,0:T(8,128)(2,1)} %copy-done.7, bf16[2,2,128,256]{3,2,1,0:T(8,128)(2,1)} %copy-done.14, bf16[2,2,128,256]{3,2,1,0:T(8,128)(2,1)} %copy-done.15, bf16[2,2,128,256]{3,2,1,0:T(8,128)(2,1)} %copy-done.16, ...), custom_call_target="tpu_custom_call" | custom-call | flops 6000000000 | bytes 3000000 | tf_op jit(solution)/shard_map/stats/pallas_call | solution.py:176
  70.3 1.1 collective-permute-start.12
  71.3 1.9 %collective-permute-done.10.refs_11_ = f32[16,1024]{1,0:T(8,128)S(1)} collective-permute-done((f32[16,1024]{1,0:T(8,128)}, f32[16,1024]{1,0:T(8,128)S(1)}, u32[]{:S(2)}, u32[]{:S(2)}) %collective-permute-start.10) | collective-permute-done | bytes 65568 | tf_op jit(solution)/shard_map/ppermute | solution.py:35
  73.2 1.6 collective-permute-done.11.refs_12_
  74.8 0.8 collective-permute-done.12.refs_13_
  75.6 0.6 copy-done.19
  76.2 18.1 %grads.1 = (bf16[4,2,128,256]{3,2,1,0:T(8,128)(2,1)}, bf16[4,2,128,256]{3,2,1,0:T(8,128)(2,1)}, f32[2,128,512]{2,1,0:T(8,128)}, bf16[2,128,512]{2,1,0:T(8,128)(2...) custom-call(bf16[2,2,128,256]{3,2,1,0:T(8,128)(2,1)} %copy-done.7, bf16[2,2,128,256]{3,2,1,0:T(8,128)(2,1)} %copy-done.14, ...), custom_call_target="tpu_custom_call" | custom-call | flops 12000000000 | bytes 6000000 | tf_op jit(solution)/shard_map/grads/pallas_call | solution.py:189
  94.3 2.4 %collective-permute-start.15 = (bf16[2,128,512]{2,1,0:T(8,128)(2,1)}, bf16[2,128,512]{2,1,0:T(8,128)(2,1)S(1)}, u32[]{:S(2)}, u32[]{:S(2)}) collective-permute-start(bf16[2,128,512]{2,1,0:T(8,128)(2,1)} %get-tuple-element.69), channel_id=1, source_target_pairs={{0,96},{32,0},{64,32},{96,64},{1,97},{33,1},{65,33},{97,65},{2,98}... | collective-permute-start | bytes 786440 | tf_op jit(solution)/shard_map/ppermute | solution.py:35
  97.4 1.6 dynamic-slice_select_fusion
  99.1 3.9 %collective-permute-done.15 = bf16[2,128,512]{2,1,0:T(8,128)(2,1)S(1)} collective-permute-done((bf16[2,128,512]{2,1,0:T(8,128)(2,1)}, bf16[2,128,512]{2,1,0:T(8,128)(2,1)S(1)}, u32[]{:S(2)}, u32[]{:S(2)}) %collective-permute-start.15) | collective-permute-done | bytes 262176 | tf_op jit(solution)/shard_map/ppermute | solution.py:35
  103.0 1.7 %collective-permute-done.14 = bf16[2,128,512]{2,1,0:T(8,128)(2,1)S(1)} collective-permute-done((bf16[2,128,512]{2,1,0:T(8,128)(2,1)}, bf16[2,128,512]{2,1,0:T(8,128)(2,1)S(1)}, u32[]{:S(2)}, u32[]{:S(2)}) %collective-permute-start.14) | collective-permute-done | bytes 262176 | tf_op jit(solution)/shard_map/ppermute | solution.py:35
  105.2 6.7 %collective-permute-done.13 = bf16[2,128,512]{2,1,0:T(8,128)(2,1)S(1)} collective-permute-done((bf16[2,128,512]{2,1,0:T(8,128)(2,1)}, bf16[2,128,512]{2,1,0:T(8,128)(2,1)S(1)}, u32[]{:S(2)}, u32[]{:S(2)}) %collective-permute-start.13) | collective-permute-done | bytes 262176 | tf_op jit(solution)/shard_map/ppermute | solution.py:35
  112.6 3.5 %collective-permute-start.16 = (bf16[128,512]{1,0:T(8,128)(2,1)S(1)}, bf16[128,512]{1,0:T(8,128)(2,1)S(1)}, u32[]{:S(2)}, u32[]{:S(2)}) collective-permute-start(bf16[128,512]{1,0:T(8,128)(2,1)S(1)} %get-tuple-element.82), channel_id=1, source_target_pairs={{0,2},{2,0},{1,3},{3,1},{4,6},{6,4},{5,7},{7,5},{8,10},{10,8},{9,1... | collective-permute-start | bytes 393224 | tf_op jit(solution)/shard_map/ppermute | solution.py:35
  117.2 3.4 %collective-permute-done.25 = bf16[128,1024]{1,0:T(8,128)(2,1)S(1)} collective-permute-done((bf16[128,1024]{1,0:T(8,128)(2,1)S(1)}, bf16[128,1024]{1,0:T(8,128)(2,1)S(1)}, u32[]{:S(2)}, u32[]{:S(2)}) %collective-permute-start.25) | collective-permute-done | bytes 262176 | tf_op jit(solution)/shard_map/ppermute | solution.py:35
  120.8 5.4 %collective-permute-start.28 = (bf16[4,128,1024]{2,1,0:T(8,128)(2,1)S(1)}, bf16[4,128,1024]{2,1,0:T(8,128)(2,1)S(1)}, u32[]{:S(2)}, u32[]{:S(2)}) collective-permute-start(bf16[4,128,1024]{2,1,0:T(8,128)(2,1)S(1)} %get-tuple-element.77), channel_id=1, source_target_pairs={{0,2},{2,0},{1,3},{3,1},{4,6},{6,4},{5,7},{7,5},{8,10},{10,8},{9,1... | collective-permute-start | bytes 3145736 | tf_op jit(solution)/shard_map/ppermute | solution.py:35
  126.2 3.6 %collective-permute-done.23 = bf16[2048,256]{1,0:T(8,128)(2,1)S(1)} collective-permute-done((bf16[2048,256]{1,0:T(8,128)(2,1)S(1)}, bf16[2048,256]{1,0:T(8,128)(2,1)S(1)}, u32[]{:S(2)}, u32[]{:S(2)}) %collective-permute-start.23) | collective-permute-done | bytes 1048608 | tf_op jit(solution)/shard_map/ppermute | solution.py:35
  129.8 3.0 %collective-permute-start.24 = (bf16[2048,256]{1,0:T(8,128)(2,1)S(1)}, bf16[2048,256]{1,0:T(8,128)(2,1)S(1)}, u32[]{:S(2)}, u32[]{:S(2)}) collective-permute-start(bf16[2048,256]{1,0:T(8,128)(2,1)S(1)} %collective-permute-done.23), channel_id=1, source_target_pairs={{0,2},{2,0},{1,3},{3,1},{4,6},{6,4},{5,7},{7,5},{8,10},{10,8},{9,1... | collective-permute-start | bytes 3145736 | tf_op jit(solution)/shard_map/ppermute | solution.py:35
  132.8 0.8 maximum_select_fusion
  133.9 1.7 %collective-permute-start.30 = (bf16[2,128,256]{2,1,0:T(8,128)(2,1)S(1)}, bf16[2,128,256]{2,1,0:T(8,128)(2,1)S(1)}, u32[]{:S(2)}, u32[]{:S(2)}) collective-permute-start(bf16[2,128,256]{2,1,0:T(8,128)(2,1)S(1)} %fusion.27), channel_id=1, source_target_pairs={{0,8},{4,12},{8,0},{12,4},{1,9},{5,13},{9,1},{13,5},{2,10},{6,14},... | collective-permute-start | bytes 393224 | tf_op jit(solution)/shard_map/ppermute | solution.py:35
  135.6 0.9 collective-permute-start.29
  137.6 3.0 %collective-permute-done.31 = bf16[2,128,256]{2,1,0:T(8,128)(2,1)S(1)} collective-permute-done((bf16[2,128,256]{2,1,0:T(8,128)(2,1)S(1)}, bf16[2,128,256]{2,1,0:T(8,128)(2,1)S(1)}, u32[]{:S(2)}, u32[]{:S(2)}) %collective-permute-start.31) | collective-permute-done | bytes 131104 | tf_op jit(solution)/shard_map/ppermute | solution.py:35
  140.6 1.6 collective-permute-start.22
  142.3 0.7 collective-permute-done.29
  142.9 1.6 fusion.7
  144.5 9.4 %all-to-all-start = ((bf16[16,64,256]{2,1,0:T(8,128)(2,1)}), bf16[16,64,256]{2,1,0:T(8,128)(2,1)}, u32[]{:S(2)}, u32[]{:S(2)}) async-start(bf16[16,64,256]{2,1,0:T(8,128)(2,1)} %bitcast.54), calls=%async_computation | async-start | bytes 1048576 | tf_op jit(solution)/shard_map/all_to_all | solution.py:349
  154.4 1.3 fusion.1
  155.7 9.5 %all-to-all-done.in_ref = bf16[16,64,256]{2,1,0:T(8,128)(2,1)} async-done(((bf16[16,64,256]{2,1,0:T(8,128)(2,1)}), bf16[16,64,256]{2,1,0:T(8,128)(2,1)}, u32[]{:S(2)}, u32[]{:S(2)}) %all-to-all-start) | async-done | bytes 524320 | tf_op jit(solution)/shard_map/all_to_all | solution.py:349
  165.2 1.7 %finish.1 = (f32[64,256]{1,0:T(8,128)}, f32[64,256]{1,0:T(8,128)}) custom-call(bf16[16,64,256]{2,1,0:T(8,128)(2,1)} %all-to-all-done.in_ref), custom_call_target="tpu_custom_call" | custom-call | tf_op jit(solution)/shard_map/finish/pallas_call | solution.py:264
  (112 shorter events, 7.5 us)
Async XLA Ops:
  3.3 3.7 %collective-permute-start = (bf16[128,256]{1,0:T(8,128)(2,1)}, bf16[128,256]{1,0:T(8,128)(2,1)S(1)}, u32[]{:S(2)}, u32[]{:S(2)}) collective-permute-start(bf16[128,256]{1,0:T(8,128)(2,1)} %get-tuple-element.53), channel_id=1, source_target_pairs={{0,2},{2,0},{1,3},{3,1},{4,6},{6,4},{5,7},{7,5},{8,10},{10,8},{9,1... | collective-permute-start | bytes 196616 | tf_op jit(solution)/shard_map/ppermute | solution.py:35
  4.7 23.2 %collective-permute-start.5 = (bf16[128,1024]{1,0:T(8,128)(2,1)}, bf16[128,1024]{1,0:T(8,128)(2,1)S(1)}, u32[]{:S(2)}, u32[]{:S(2)}) collective-permute-start(bf16[128,1024]{1,0:T(8,128)(2,1)} %get-tuple-element.55), channel_id=1, source_target_pairs={{0,2},{2,0},{1,3},{3,1},{4,6},{6,4},{5,7},{7,5},{8,10},{10,8},{9,1... | collective-permute-start | bytes 786440 | tf_op jit(solution)/shard_map/ppermute | solution.py:35
  4.8 30.0 %collective-permute-start.9 = (bf16[128,2048]{1,0:T(8,128)(2,1)}, bf16[128,2048]{1,0:T(8,128)(2,1)S(1)}, u32[]{:S(2)}, u32[]{:S(2)}) collective-permute-start(bf16[128,2048]{1,0:T(8,128)(2,1)} %mine_ref), channel_id=1, source_target_pairs={{0,1},{1,0},{2,3},{3,2},{4,5},{5,4},{6,7},{7,6},{8,9},{9,8},{10,11... | collective-permute-start | bytes 1572872 | tf_op jit(solution)/shard_map/ppermute | solution.py:35
  7.6 16.8 %collective-permute-start.1 = (bf16[2,128,256]{2,1,0:T(8,128)(2,1)}, bf16[2,128,256]{2,1,0:T(8,128)(2,1)S(1)}, u32[]{:S(2)}, u32[]{:S(2)}) collective-permute-start(bf16[2,128,256]{2,1,0:T(8,128)(2,1)} %bitcast_dynamic-update-slice_fusion.1), channel_id=1, source_target_pairs={{0,16},{16,0},{1,17},{17,1},{2,18},{18,2},{3,19},{19,3},{4,20},{20... | collective-permute-start | bytes 393224 | tf_op jit(solution)/shard_map/ppermute | solution.py:35
  25.4 32.8 %copy-start.7 = (bf16[2,2,128,256]{3,2,1,0:T(8,128)(2,1)}, bf16[2,2,128,256]{3,2,1,0:T(8,128)(2,1)S(1)}, u32[]{:S(2)}) copy-start(bf16[2,2,128,256]{3,2,1,0:T(8,128)(2,1)S(1)} %pad_maximum_fusion.2.refs_0_) | copy-start | bytes 786436
  25.4 7.1 %collective-permute-start.2 = (bf16[2,2,128,256]{3,2,1,0:T(8,128)(2,1)S(1)}, bf16[2,2,128,256]{3,2,1,0:T(8,128)(2,1)S(1)}, u32[]{:S(2)}, u32[]{:S(2)}) collective-permute-start(bf16[2,2,128,256]{3,2,1,0:T(8,128)(2,1)S(1)} %pad_maximum_fusion.2.refs_0_), channel_id=1, source_target_pairs={{0,12},{4,0},{8,4},{12,8},{1,13},{5,1},{9,5},{13,9},{2,14},{6,2},{... | collective-permute-start | bytes 786440 | tf_op jit(solution)/shard_map/ppermute | solution.py:35
  28.7 18.3 %collective-permute-start.6 = (bf16[2,128,1024]{2,1,0:T(8,128)(2,1)}, bf16[2,128,1024]{2,1,0:T(8,128)(2,1)S(1)}, u32[]{:S(2)}, u32[]{:S(2)}) collective-permute-start(bf16[2,128,1024]{2,1,0:T(8,128)(2,1)} %bitcast_dynamic-update-slice_fusion.refs_4_), channel_id=1, source_target_pairs={{0,96},{32,0},{64,32},{96,64},{1,97},{33,1},{65,33},{97,65},{2,98}... | collective-permute-start | bytes 1572872 | tf_op jit(solution)/shard_map/ppermute | solution.py:35
  31.4 15.6 %collective-permute-start.7 = (bf16[2,128,1024]{2,1,0:T(8,128)(2,1)}, bf16[2,128,1024]{2,1,0:T(8,128)(2,1)S(1)}, u32[]{:S(2)}, u32[]{:S(2)}) collective-permute-start(bf16[2,128,1024]{2,1,0:T(8,128)(2,1)} %bitcast_dynamic-update-slice_fusion.refs_4_), channel_id=1, source_target_pairs={{0,64},{32,96},{64,0},{96,32},{1,65},{33,97},{65,1},{97,33},{2,66}... | collective-permute-start | bytes 1572872 | tf_op jit(solution)/shard_map/ppermute | solution.py:35
  31.8 26.4 %collective-permute-start.8 = (bf16[2,128,1024]{2,1,0:T(8,128)(2,1)}, bf16[2,128,1024]{2,1,0:T(8,128)(2,1)S(1)}, u32[]{:S(2)}, u32[]{:S(2)}) collective-permute-start(bf16[2,128,1024]{2,1,0:T(8,128)(2,1)} %bitcast_dynamic-update-slice_fusion.refs_4_), channel_id=1, source_target_pairs={{0,32},{32,64},{64,96},{96,0},{1,33},{33,65},{65,97},{97,1},{2,34}... | collective-permute-start | bytes 1572872 | tf_op jit(solution)/shard_map/ppermute | solution.py:35
  32.5 25.7 %copy-start.14 = (bf16[2,2,128,256]{3,2,1,0:T(8,128)(2,1)}, bf16[2,2,128,256]{3,2,1,0:T(8,128)(2,1)S(1)}, u32[]{:S(2)}) copy-start(bf16[2,2,128,256]{3,2,1,0:T(8,128)(2,1)S(1)} %collective-permute-done.2.refs_1_) | copy-start | bytes 786436
  32.5 8.9 %collective-permute-start.3 = (bf16[2,2,128,256]{3,2,1,0:T(8,128)(2,1)S(1)}, bf16[2,2,128,256]{3,2,1,0:T(8,128)(2,1)S(1)}, u32[]{:S(2)}, u32[]{:S(2)}) collective-permute-start(bf16[2,2,128,256]{3,2,1,0:T(8,128)(2,1)S(1)} %pad_maximum_fusion.2.refs_0_), channel_id=1, source_target_pairs={{0,8},{4,12},{8,0},{12,4},{1,9},{5,13},{9,1},{13,5},{2,10},{6,14},... | collective-permute-start | bytes 786440 | tf_op jit(solution)/shard_map/ppermute | solution.py:35
  34.8 12.2 %collective-permute-start.4 = (bf16[2,2,128,256]{3,2,1,0:T(8,128)(2,1)S(1)}, bf16[2,2,128,256]{3,2,1,0:T(8,128)(2,1)S(1)}, u32[]{:S(2)}, u32[]{:S(2)}) collective-permute-start(bf16[2,2,128,256]{3,2,1,0:T(8,128)(2,1)S(1)} %pad_maximum_fusion.2.refs_0_), channel_id=1, source_target_pairs={{0,4},{4,8},{8,12},{12,0},{1,5},{5,9},{9,13},{13,1},{2,6},{6,10},{... | collective-permute-start | bytes 786440 | tf_op jit(solution)/shard_map/ppermute | solution.py:35
  41.4 16.8 %copy-start.15 = (bf16[2,2,128,256]{3,2,1,0:T(8,128)(2,1)}, bf16[2,2,128,256]{3,2,1,0:T(8,128)(2,1)S(1)}, u32[]{:S(2)}) copy-start(bf16[2,2,128,256]{3,2,1,0:T(8,128)(2,1)S(1)} %collective-permute-done.3.refs_2_) | copy-start | bytes 786436
  47.0 11.2 %copy-start.16 = (bf16[2,2,128,256]{3,2,1,0:T(8,128)(2,1)}, bf16[2,2,128,256]{3,2,1,0:T(8,128)(2,1)S(1)}, u32[]{:S(2)}) copy-start(bf16[2,2,128,256]{3,2,1,0:T(8,128)(2,1)S(1)} %collective-permute-done.4.refs_3_) | copy-start | bytes 786436
  47.0 11.2 %copy-start.8 = (bf16[2,128,1024]{2,1,0:T(8,128)(2,1)}, bf16[2,128,1024]{2,1,0:T(8,128)(2,1)S(1)}, u32[]{:S(2)}) copy-start(bf16[2,128,1024]{2,1,0:T(8,128)(2,1)S(1)} %collective-permute-done.6.refs_5_) | copy-start | bytes 1572868
  47.0 11.2 %copy-start.9 = (bf16[2,128,1024]{2,1,0:T(8,128)(2,1)}, bf16[2,128,1024]{2,1,0:T(8,128)(2,1)S(1)}, u32[]{:S(2)}) copy-start(bf16[2,128,1024]{2,1,0:T(8,128)(2,1)S(1)} %collective-permute-done.7.refs_6_) | copy-start | bytes 1572868
  69.9 3.3 %collective-permute-start.10 = (f32[16,1024]{1,0:T(8,128)}, f32[16,1024]{1,0:T(8,128)S(1)}, u32[]{:S(2)}, u32[]{:S(2)}) collective-permute-start(f32[16,1024]{1,0:T(8,128)} %get-tuple-element.63), channel_id=1, source_target_pairs={{0,96},{32,0},{64,32},{96,64},{1,97},{33,1},{65,33},{97,65},{2,98}... | collective-permute-start | bytes 196616 | tf_op jit(solution)/shard_map/ppermute | solution.py:35
  69.9 4.9 %collective-permute-start.11 = (f32[16,1024]{1,0:T(8,128)}, f32[16,1024]{1,0:T(8,128)S(1)}, u32[]{:S(2)}, u32[]{:S(2)}) collective-permute-start(f32[16,1024]{1,0:T(8,128)} %get-tuple-element.64), channel_id=1, source_target_pairs={{0,64},{32,96},{64,0},{96,32},{1,65},{33,97},{65,1},{97,33},{2,66}... | collective-permute-start | bytes 196616 | tf_op jit(solution)/shard_map/ppermute | solution.py:35
  70.3 5.3 %collective-permute-start.12 = (f32[16,1024]{1,0:T(8,128)}, f32[16,1024]{1,0:T(8,128)S(1)}, u32[]{:S(2)}, u32[]{:S(2)}) collective-permute-start(f32[16,1024]{1,0:T(8,128)} %get-tuple-element.65), channel_id=1, source_target_pairs={{0,32},{32,64},{64,96},{96,0},{1,33},{33,65},{65,97},{97,1},{2,34}... | collective-permute-start | bytes 196616 | tf_op jit(solution)/shard_map/ppermute | solution.py:35
  76.2 21.2 %copy-start = (bf16[4096,256]{1,0:T(8,128)(2,1)S(1)}, bf16[4096,256]{1,0:T(8,128)(2,1)}, u32[]{:S(2)}) copy-start(bf16[4096,256]{1,0:T(8,128)(2,1)} %param.18) | copy-start | bytes 6291460
  94.3 18.1 %copy-start.4 = (f32[2,128,512]{2,1,0:T(8,128)S(1)}, f32[2,128,512]{2,1,0:T(8,128)}, u32[]{:S(2)}) copy-start(f32[2,128,512]{2,1,0:T(8,128)} %get-tuple-element.66) | copy-start | bytes 1572868
  94.3 8.7 %collective-permute-start.15 = (bf16[2,128,512]{2,1,0:T(8,128)(2,1)}, bf16[2,128,512]{2,1,0:T(8,128)(2,1)S(1)}, u32[]{:S(2)}, u32[]{:S(2)}) collective-permute-start(bf16[2,128,512]{2,1,0:T(8,128)(2,1)} %get-tuple-element.69), channel_id=1, source_target_pairs={{0,96},{32,0},{64,32},{96,64},{1,97},{33,1},{65,33},{97,65},{2,98}... | collective-permute-start | bytes 786440 | tf_op jit(solution)/shard_map/ppermute | solution.py:35
  96.7 8.0 %collective-permute-start.14 = (bf16[2,128,512]{2,1,0:T(8,128)(2,1)}, bf16[2,128,512]{2,1,0:T(8,128)(2,1)S(1)}, u32[]{:S(2)}, u32[]{:S(2)}) collective-permute-start(bf16[2,128,512]{2,1,0:T(8,128)(2,1)} %get-tuple-element.68), channel_id=1, source_target_pairs={{0,64},{32,96},{64,0},{96,32},{1,65},{33,97},{65,1},{97,33},{2,66}... | collective-permute-start | bytes 786440 | tf_op jit(solution)/shard_map/ppermute | solution.py:35
  96.8 15.1 %collective-permute-start.13 = (bf16[2,128,512]{2,1,0:T(8,128)(2,1)}, bf16[2,128,512]{2,1,0:T(8,128)(2,1)S(1)}, u32[]{:S(2)}, u32[]{:S(2)}) collective-permute-start(bf16[2,128,512]{2,1,0:T(8,128)(2,1)} %get-tuple-element.67), channel_id=1, source_target_pairs={{0,32},{32,64},{64,96},{96,0},{1,33},{33,65},{65,97},{97,1},{2,34}... | collective-permute-start | bytes 786440 | tf_op jit(solution)/shard_map/ppermute | solution.py:35
  97.3 5.6 %copy-start.13 = (bf16[128,1024]{1,0:T(8,128)(2,1)S(1)}, bf16[128,1024]{1,0:T(8,128)(2,1)}, u32[]{:S(2)}) copy-start(bf16[128,1024]{1,0:T(8,128)(2,1)} %get-tuple-element.58) | copy-start | bytes 786436
  97.3 7.3 %copy-start.12 = (bf16[128,1024]{1,0:T(8,128)(2,1)S(1)}, bf16[128,1024]{1,0:T(8,128)(2,1)}, u32[]{:S(2)}) copy-start(bf16[128,1024]{1,0:T(8,128)(2,1)} %get-tuple-element.59) | copy-start | bytes 786436
  97.3 14.5 %copy-start.11 = (bf16[128,1024]{1,0:T(8,128)(2,1)S(1)}, bf16[128,1024]{1,0:T(8,128)(2,1)}, u32[]{:S(2)}) copy-start(bf16[128,1024]{1,0:T(8,128)(2,1)} %get-tuple-element.60) | copy-start | bytes 786436
  97.3 18.8 %copy-start.3 = (bf16[4,2,128,256]{3,2,1,0:T(8,128)(2,1)S(1)}, bf16[4,2,128,256]{3,2,1,0:T(8,128)(2,1)}, u32[]{:S(2)}) copy-start(bf16[4,2,128,256]{3,2,1,0:T(8,128)(2,1)} %get-tuple-element.70) | copy-start | bytes 1572868
  97.3 15.2 %collective-permute-start.17 = (bf16[4,2,128,256]{3,2,1,0:T(8,128)(2,1)}, bf16[4,2,128,256]{3,2,1,0:T(8,128)(2,1)S(1)}, u32[]{:S(2)}, u32[]{:S(2)}) collective-permute-start(bf16[4,2,128,256]{3,2,1,0:T(8,128)(2,1)} %get-tuple-element.71), channel_id=1, source_target_pairs={{0,16},{16,0},{1,17},{17,1},{2,18},{18,2},{3,19},{19,3},{4,20},{20... | collective-permute-start | bytes 1572872 | tf_op jit(solution)/shard_map/ppermute | solution.py:35
  99.0 30.8 %collective-permute-start.23 = (bf16[2048,256]{1,0:T(8,128)(2,1)S(1)}, bf16[2048,256]{1,0:T(8,128)(2,1)S(1)}, u32[]{:S(2)}, u32[]{:S(2)}) collective-permute-start(bf16[2048,256]{1,0:T(8,128)(2,1)S(1)} %dynamic-slice_select_fusion), channel_id=1, source_target_pairs={{0,1},{1,0},{2,3},{3,2},{4,5},{5,4},{6,7},{7,6},{8,9},{9,8},{10,11... | collective-permute-start | bytes 3145736 | tf_op jit(solution)/shard_map/ppermute | solution.py:35
  103.0 13.3 %collective-permute-start.27 = (bf16[128,1024]{1,0:T(8,128)(2,1)S(1)}, bf16[128,1024]{1,0:T(8,128)(2,1)S(1)}, u32[]{:S(2)}, u32[]{:S(2)}) collective-permute-start(bf16[128,1024]{1,0:T(8,128)(2,1)S(1)} %copy-done.13), channel_id=1, source_target_pairs={{0,4},{4,8},{8,12},{12,0},{1,5},{5,9},{9,13},{13,1},{2,6},{6,10},{... | collective-permute-start | bytes 786440 | tf_op jit(solution)/shard_map/ppermute | solution.py:35
  104.7 12.3 %collective-permute-start.26 = (bf16[128,1024]{1,0:T(8,128)(2,1)S(1)}, bf16[128,1024]{1,0:T(8,128)(2,1)S(1)}, u32[]{:S(2)}, u32[]{:S(2)}) collective-permute-start(bf16[128,1024]{1,0:T(8,128)(2,1)S(1)} %copy-done.12), channel_id=1, source_target_pairs={{0,8},{4,12},{8,0},{12,4},{1,9},{5,13},{9,1},{13,5},{2,10},{6,14},... | collective-permute-start | bytes 786440 | tf_op jit(solution)/shard_map/ppermute | solution.py:35
  111.8 8.7 %collective-permute-start.25 = (bf16[128,1024]{1,0:T(8,128)(2,1)S(1)}, bf16[128,1024]{1,0:T(8,128)(2,1)S(1)}, u32[]{:S(2)}, u32[]{:S(2)}) collective-permute-start(bf16[128,1024]{1,0:T(8,128)(2,1)S(1)} %copy-done.11), channel_id=1, source_target_pairs={{0,12},{4,0},{8,4},{12,8},{1,13},{5,1},{9,5},{13,9},{2,14},{6,2},{... | collective-permute-start | bytes 786440 | tf_op jit(solution)/shard_map/ppermute | solution.py:35
  112.4 8.2 %copy-start.6 = (bf16[128,1024]{1,0:T(8,128)(2,1)S(1)}, bf16[128,1024]{1,0:T(8,128)(2,1)}, u32[]{:S(2)}) copy-start(bf16[128,1024]{1,0:T(8,128)(2,1)} %get-tuple-element.57) | copy-start | bytes 786436
  112.6 8.2 %collective-permute-start.16 = (bf16[128,512]{1,0:T(8,128)(2,1)S(1)}, bf16[128,512]{1,0:T(8,128)(2,1)S(1)}, u32[]{:S(2)}, u32[]{:S(2)}) collective-permute-start(bf16[128,512]{1,0:T(8,128)(2,1)S(1)} %get-tuple-element.82), channel_id=1, source_target_pairs={{0,2},{2,0},{1,3},{3,1},{4,6},{6,4},{5,7},{7,5},{8,10},{10,8},{9,1... | collective-permute-start | bytes 393224 | tf_op jit(solution)/shard_map/ppermute | solution.py:35
  116.3 17.3 %collective-permute-start.20 = (bf16[2,128,256]{2,1,0:T(8,128)(2,1)S(1)}, bf16[2,128,256]{2,1,0:T(8,128)(2,1)S(1)}, u32[]{:S(2)}, u32[]{:S(2)}) collective-permute-start(bf16[2,128,256]{2,1,0:T(8,128)(2,1)S(1)} %get-tuple-element.79), channel_id=1, source_target_pairs={{0,12},{4,0},{8,4},{12,8},{1,13},{5,1},{9,5},{13,9},{2,14},{6,2},{... | collective-permute-start | bytes 393224 | tf_op jit(solution)/shard_map/ppermute | solution.py:35
  116.9 16.7 %collective-permute-start.19 = (bf16[2,128,256]{2,1,0:T(8,128)(2,1)S(1)}, bf16[2,128,256]{2,1,0:T(8,128)(2,1)S(1)}, u32[]{:S(2)}, u32[]{:S(2)}) collective-permute-start(bf16[2,128,256]{2,1,0:T(8,128)(2,1)S(1)} %get-tuple-element.80), channel_id=1, source_target_pairs={{0,8},{4,12},{8,0},{12,4},{1,9},{5,13},{9,1},{13,5},{2,10},{6,14},... | collective-permute-start | bytes 393224 | tf_op jit(solution)/shard_map/ppermute | solution.py:35
  120.6 13.0 %collective-permute-start.18 = (bf16[2,128,256]{2,1,0:T(8,128)(2,1)S(1)}, bf16[2,128,256]{2,1,0:T(8,128)(2,1)S(1)}, u32[]{:S(2)}, u32[]{:S(2)}) collective-permute-start(bf16[2,128,256]{2,1,0:T(8,128)(2,1)S(1)} %get-tuple-element.78), channel_id=1, source_target_pairs={{0,4},{4,8},{8,12},{12,0},{1,5},{5,9},{9,13},{13,1},{2,6},{6,10},{... | collective-permute-start | bytes 393224 | tf_op jit(solution)/shard_map/ppermute | solution.py:35
  120.6 16.0 %copy-start.1 = (bf16[4096,256]{1,0:T(8,128)(2,1)S(1)}, bf16[4096,256]{1,0:T(8,128)(2,1)}, u32[]{:S(2)}) copy-start(bf16[4096,256]{1,0:T(8,128)(2,1)} %param.18) | copy-start | bytes 6291460
  120.8 16.3 %copy-start.2 = (bf16[4096,256]{1,0:T(8,128)(2,1)S(1)}, bf16[4096,256]{1,0:T(8,128)(2,1)}, u32[]{:S(2)}) copy-start(bf16[4096,256]{1,0:T(8,128)(2,1)} %param.17) | copy-start | bytes 6291460
  120.8 22.1 %collective-permute-start.28 = (bf16[4,128,1024]{2,1,0:T(8,128)(2,1)S(1)}, bf16[4,128,1024]{2,1,0:T(8,128)(2,1)S(1)}, u32[]{:S(2)}, u32[]{:S(2)}) collective-permute-start(bf16[4,128,1024]{2,1,0:T(8,128)(2,1)S(1)} %get-tuple-element.77), channel_id=1, source_target_pairs={{0,2},{2,0},{1,3},{3,1},{4,6},{6,4},{5,7},{7,5},{8,10},{10,8},{9,1... | collective-permute-start | bytes 3145736 | tf_op jit(solution)/shard_map/ppermute | solution.py:35
  129.8 24.1 %collective-permute-start.24 = (bf16[2048,256]{1,0:T(8,128)(2,1)S(1)}, bf16[2048,256]{1,0:T(8,128)(2,1)S(1)}, u32[]{:S(2)}, u32[]{:S(2)}) collective-permute-start(bf16[2048,256]{1,0:T(8,128)(2,1)S(1)} %collective-permute-done.23), channel_id=1, source_target_pairs={{0,2},{2,0},{1,3},{3,1},{4,6},{6,4},{5,7},{7,5},{8,10},{10,8},{9,1... | collective-permute-start | bytes 3145736 | tf_op jit(solution)/shard_map/ppermute | solution.py:35
  133.7 1.9 %collective-permute-start.21 = (bf16[128,256]{1,0:T(8,128)(2,1)S(1)}, bf16[128,256]{1,0:T(8,128)(2,1)S(1)}, u32[]{:S(2)}, u32[]{:S(2)}) collective-permute-start(bf16[128,256]{1,0:T(8,128)(2,1)S(1)} %slice_bitcast_fusion.6), channel_id=1, source_target_pairs={{0,2},{2,0},{1,3},{3,1},{4,6},{6,4},{5,7},{7,5},{8,10},{10,8},{9,1... | collective-permute-start | bytes 196616 | tf_op jit(solution)/shard_map/ppermute | solution.py:35
  133.8 6.8 %collective-permute-start.31 = (bf16[2,128,256]{2,1,0:T(8,128)(2,1)S(1)}, bf16[2,128,256]{2,1,0:T(8,128)(2,1)S(1)}, u32[]{:S(2)}, u32[]{:S(2)}) collective-permute-start(bf16[2,128,256]{2,1,0:T(8,128)(2,1)S(1)} %fusion.27), channel_id=1, source_target_pairs={{0,4},{4,8},{8,12},{12,0},{1,5},{5,9},{9,13},{13,1},{2,6},{6,10},{... | collective-permute-start | bytes 393224 | tf_op jit(solution)/shard_map/ppermute | solution.py:35
  133.9 8.4 %collective-permute-start.30 = (bf16[2,128,256]{2,1,0:T(8,128)(2,1)S(1)}, bf16[2,128,256]{2,1,0:T(8,128)(2,1)S(1)}, u32[]{:S(2)}, u32[]{:S(2)}) collective-permute-start(bf16[2,128,256]{2,1,0:T(8,128)(2,1)S(1)} %fusion.27), channel_id=1, source_target_pairs={{0,8},{4,12},{8,0},{12,4},{1,9},{5,13},{9,1},{13,5},{2,10},{6,14},... | collective-permute-start | bytes 393224 | tf_op jit(solution)/shard_map/ppermute | solution.py:35
  135.6 7.3 %collective-permute-start.29 = (bf16[2,128,256]{2,1,0:T(8,128)(2,1)S(1)}, bf16[2,128,256]{2,1,0:T(8,128)(2,1)S(1)}, u32[]{:S(2)}, u32[]{:S(2)}) collective-permute-start(bf16[2,128,256]{2,1,0:T(8,128)(2,1)S(1)} %fusion.27), channel_id=1, source_target_pairs={{0,12},{4,0},{8,4},{12,8},{1,13},{5,1},{9,5},{13,9},{2,14},{6,2},{... | collective-permute-start | bytes 393224 | tf_op jit(solution)/shard_map/ppermute | solution.py:35
  140.6 13.3 %collective-permute-start.22 = (bf16[128,512]{1,0:T(8,128)(2,1)S(1)}, bf16[128,512]{1,0:T(8,128)(2,1)S(1)}, u32[]{:S(2)}, u32[]{:S(2)}) collective-permute-start(bf16[128,512]{1,0:T(8,128)(2,1)S(1)} %pad_maximum_fusion.3), channel_id=1, source_target_pairs={{0,1},{1,0},{2,3},{3,2},{4,5},{5,4},{6,7},{7,6},{8,9},{9,8},{10,11... | collective-permute-start | bytes 393224 | tf_op jit(solution)/shard_map/ppermute | solution.py:35
  144.5 20.7 %all-to-all-start = ((bf16[16,64,256]{2,1,0:T(8,128)(2,1)}), bf16[16,64,256]{2,1,0:T(8,128)(2,1)}, u32[]{:S(2)}, u32[]{:S(2)}) async-start(bf16[16,64,256]{2,1,0:T(8,128)(2,1)} %bitcast.54), calls=%async_computation | async-start | bytes 1048576 | tf_op jit(solution)/shard_map/all_to_all | solution.py:349
  (5 other events, 8.7 us)

commit v2 on v1

--- a/solution.py
+++ b/solution.py
@@ -118,8 +118,9 @@
     kv_refs, qg_refs = refs[0:4], refs[4:8]
     kpos_ref, qpos_ref = refs[8:10]
     st_refs = refs[10:14]
-    dkv_refs, dq_refs = refs[14:16], refs[16:20]
-    ks, vs, qs, gs, kposb, kt, dks, dvs, dqt, lse, mean = refs[20:]
+    dkv_near, dkv_first, dkv_last, dq_refs = refs[14], refs[15], refs[16], refs[17:21]
+    ks, vs, qs, gs, kposb, kt, dks, dvs, dqt, lse, mean = refs[21:]
+    far = (dkv_last.at[1], dkv_first.at[0], dkv_first.at[1], dkv_last.at[0])
     load_parts(kv_refs, qg_refs, kpos_ref, ks, vs, qs, gs, kposb)
     for part in range(PARTS):
         kt[part] = ks[part].T
@@ -152,8 +153,9 @@
         for b in range(4):
             for a in range(2):
                 rows = slice((b * 4 + a * 2) * T, (b * 4 + a * 2 + 2) * T)
-                dkv_refs[a][b, :, tok, :HEAD] = (dks[part, rows, :] * SCALE).astype(BF).reshape(2, T, HEAD)
-                dkv_refs[a][b, :, tok, HEAD:] = dvs[part, rows, :].astype(BF).reshape(2, T, HEAD)
+                ref = far[b] if a else dkv_near.at[b]
+                ref[:, tok, :HEAD] = (dks[part, rows, :] * SCALE).astype(BF).reshape(2, T, HEAD)
+                ref[:, tok, HEAD:] = dvs[part, rows, :].astype(BF).reshape(2, T, HEAD)
         dq = dqt[part].T * SCALE
         for h in range(GROUP):
             for s in range(4):
@@ -184,11 +186,11 @@
 
 
 def run_grads(kvs, qgs, kpos, qpos, sts):
-    dkv = jax.ShapeDtypeStruct((4, 2, TOK, 2 * HEAD), BF)
+    dkv = [jax.ShapeDtypeStruct((n, 2, TOK, 2 * HEAD), BF) for n in (4, 2, 2)]
     dq = [jax.ShapeDtypeStruct((2, TOK, GROUP * HEAD), F32 if s == 0 else BF) for s in range(4)]
     out = pl.pallas_call(
         grads_kernel,
-        out_shape=[dkv, dkv] + dq,
+        out_shape=dkv + dq,
         scratch_shapes=common_scratch()
         + [
             pltpu.VMEM((PARTS, HEAD, KR), BF),
@@ -202,7 +204,7 @@
         cost_estimate=pl.CostEstimate(flops=12_000_000_000, bytes_accessed=6_000_000, transcendentals=5_000_000),
         name="grads",
     )(*kvs, *qgs, kpos, qpos, *sts)
-    return out[0:2], out[2:6]
+    return out[0], out[1:3], out[3:7]
 
 
 def pack_kernel(at_ref, q_ref, g_ref, k_ref, v_ref, kv_own, qg_own, kv_send, qg_send):
@@ -230,24 +232,21 @@
     )(at, q, g, k, v)
 
 
-def columns_kernel(at_ref, mine_ref, far_ref, *out_refs):
-    for ref, half in ((mine_ref, at_ref[2]), (far_ref, 1 - at_ref[2])):
-        for o in range(4):
-            target = (at_ref[1] + o) % 4
-            for n in range(4):
-                src = pl.ds(pl.multiple_of(n * 4 * HEAD + target * HEAD, 128), HEAD)
-                dst = pl.ds(pl.multiple_of(half * 4 * HEAD + n * HEAD, 128), HEAD)
-                out_refs[o][:, dst] = ref[:, src]
-
-
-def run_columns(at, mine, far):
-    vmem = pl.BlockSpec(memory_space=pltpu.VMEM)
+def columns_kernel(at_ref, in_ref, *out_refs):
+    for o in range(4):
+        target = (at_ref[1] + o) % 4
+        for n in range(4):
+            src = pl.ds(pl.multiple_of(n * 4 * HEAD + target * HEAD, 128), HEAD)
+            out_refs[o][:, n * HEAD : (n + 1) * HEAD] = in_ref[:, src]
+
+
+def run_columns(at, layer_input):
     return pl.pallas_call(
         columns_kernel,
-        out_shape=[jax.ShapeDtypeStruct((TOK, 8 * HEAD), BF)] * 4,
-        in_specs=[pl.BlockSpec(memory_space=pltpu.SMEM), vmem, vmem],
+        out_shape=[jax.ShapeDtypeStruct((TOK, 4 * HEAD), BF)] * 4,
+        in_specs=[pl.BlockSpec(memory_space=pltpu.SMEM), pl.BlockSpec(memory_space=pltpu.VMEM)],
         name="columns",
-    )(at, mine, far)
+    )(at, layer_input)
 
 
 def finish_kernel(in_ref, k_ref, v_ref):
@@ -295,7 +294,6 @@
 def step(query_rows, key_rows, value_rows, output_grad, layer_input, key_matrix, value_matrix, run_placement):
     y, z, x, c, t = (lax.axis_index(a) for a in ("y", "z", "x", "c", "tp"))
     at = jnp.stack([c, x, t]).astype(jnp.int32)
-    x_far = moved(layer_input, "tp", 1)
     kv_pair, qg_pair, kv_send, qg_send = run_pack(at, query_rows, output_grad, key_rows, value_rows)
     qg_own = qg_pair.at[1].set(moved(qg_send, "c", 1))
     kv_own = kv_pair.at[1].set(moved(kv_send, "c", 1))
@@ -306,14 +304,16 @@
 
     half = key_matrix.shape[0] // 2
     cuts = [lax.dynamic_slice_in_dim(after(m, kv_both), (1 - t) * half, half, 0) for m in (key_matrix, value_matrix)]
-    x_pieces = run_columns(at, after(layer_input, kv_both), x_far)
-    x_here = jnp.stack([x_pieces[0]] + [moved(x_pieces[4 - o], "x", -o) for o in (1, 2, 3)])
+    x_pieces = run_columns(at, after(layer_input, kv_both))
+    x_half = jnp.stack([x_pieces[0]] + [moved(x_pieces[4 - o], "x", -o) for o in (1, 2, 3)])
+    x_other = moved(x_half, "tp", 1)
+    x_here = jnp.where(t == 0, jnp.concatenate([x_half, x_other], 2), jnp.concatenate([x_other, x_half], 2))
     m_far = moved(jnp.where(c == 0, *cuts), "tp", 1)
     kpos = after(kpos, *x_pieces)
 
     sts = run_stats(kvs, qgs, kpos, qpos)
     sts = [sts[0]] + [moved(sts[o], "y", -o) for o in (1, 2, 3)]
-    dkvs, dqs = run_grads(kvs, qgs, kpos, qpos, sts)
+    dkv_near, dkv_sent, dqs = run_grads(kvs, qgs, kpos, qpos, sts)
 
     def total_of(own, arrived):
         total = own.astype(F32)
@@ -321,14 +321,18 @@
             total = total + a.astype(F32)
         return total.astype(BF)
 
-    dkv_row = total_of(dkvs[0], [moved(dkvs[1], "z", 1)])
+    first = moved(dkv_sent[0], "z", 1)
+    row1, row2 = (total_of(dkv_near[o], [first[o - 1]]) for o in (1, 2))
+    last = moved(dkv_sent[1], "z", 1)
+    near = after(dkv_near, row1)
+    row3, row0 = (total_of(near[o], [last[n]]) for n, o in enumerate((3, 0)))
     dq = total_of(dqs[0], [moved(dqs[o], "y", o) for o in (1, 2, 3)])
     x_all = jnp.stack([x_here, moved(x_here, "c", 1)], axis=1)
     m_core = moved(m_far, "c", 1)
     k_far = jnp.where(c == 0, m_far, m_core)
     v_far = jnp.where(c == 0, m_core, m_far)
 
-    dkv = total_of(dkv_row[0], [moved(dkv_row[o], "x", o) for o in (1, 2, 3)])
+    dkv = total_of(row0, [moved(row, "x", o) for o, row in ((2, row2), (1, row1), (3, row3))])
     dkv_all = jnp.stack([dkv] + [moved(dkv, "x", -o) for o in (1, 2, 3)])
     dkv_far = moved(dkv[1], "c", 1)
     k_here = own_first(c, dkv[0, :, :HEAD], dkv_far[:, :HEAD], 1)

time: 167 us -> 146 us (0.87)
  waiting for transfers between devices: 66.8 us -> 44 us
  other arithmetic: 4.62 us -> 6.7 us
    ppermute x32 -> x33, waiting for transfers between devices: 57.3 us -> 34.5 us  [moved(): return lax.ppermute(array, axis, [(i, (i + by) % n) for i in range(n)])]
    ppermute x32 -> x33, starting transfers between devices: 39.6 us -> 43.4 us  [moved(): return lax.ppermute(array, axis, [(i, (i + by) % n) for i in range(n)])]
    all_to_all x1, starting transfers between devices: 9.37 us -> 6.18 us  [step(): got = lax.all_to_all(pieces, ('y', 'z', 'c'), 0, 0, tiled=True)]
  transfers between devices with their start and end apart: 33 -> 34, of which waited for: 14 -> 12; matrix products, arithmetic and copies ran while one was open for 8% -> 10% of each run, Pallas kernels for 2% -> 21%
where the time goes in v2:
time: 146 us; the launch traced here: 145 us
  starting transfers between devices  49.6 us (34%)
  waiting for transfers between devices  44 us (30%)
  Pallas kernels  34.5 us (24%)
  other arithmetic  6.7 us (5%)
  matrix products  5.39 us (4%)
  local copies, waits for them, and re-layouts  4.04 us (3%)
    ppermute x33, starting transfers between devices, moved(): return lax.ppermute(array, axis, [(i, (i + by) % n) for i in range(n)])  43.4 us
    ppermute x33, waiting for transfers between devices, moved(): return lax.ppermute(array, axis, [(i, (i + by) % n) for i in range(n)])  34.5 us
    pallas_call x1, Pallas kernels, run_grads(): pl.pallas_call(grads_kernel, out_shape=dkv + dq, scratch_shapes=common_sc...  17.9 us
    pallas_call x1, Pallas kernels, run_stats(): pl.pallas_call(stats_kernel, out_shape=[jax.ShapeDtypeStruct((PARTS * 4,...  10.8 us
    all_to_all x1, waiting for transfers between devices, step(): got = lax.all_to_all(pieces, ('y', 'z', 'c'), 0, 0, tiled=True)  9.49 us
    all_to_all x1, starting transfers between devices, step(): got = lax.all_to_all(pieces, ('y', 'z', 'c'), 0, 0, tiled=True)  6.18 us
  transfers between devices with their start and end apart: 34, of which 12 were waited for; matrix products, arithmetic and copies ran while one was open for 10% of the time, Pallas kernels for 21%

profile of v2, /device:TPU:1, one launch (start us, length us, event | category | flops | bytes accessed | tf_op | source)
XLA Modules:
  0.0 145.2 jit_solution(21893935876270131)
XLA Ops:
  0.7 0.6 pad_add_fusion.at_ref
  1.2 2.1 %pack.1 = (bf16[2,128,256]{2,1,0:T(8,128)(2,1)}, bf16[2,128,1024]{2,1,0:T(8,128)(2,1)}, bf16[128,256]{1,0:T(8,128)(2,1)}, bf16[128,1024]{1,0:T(8,128)(2,1)}) custom-call(s32[3]{0:T(128)} %pad_add_fusion.at_ref, bf16[128,1024]{1,0:T(8,128)(2,1)} %q_ref.1, bf16[128,1024]{1,0:T(8,128)(2,1)} %g_ref.1, bf16[128,256]{1,0:T(8,128)(2,1)} %k_ref.1, ...), custom_call_target="tpu_custom_call" | custom-call | tf_op jit(solution)/shard_map/pack/pallas_call | solution.py:227
  3.3 1.4 collective-permute-start
  5.8 0.6 bitcast_dynamic-update-slice_fusion.1
  6.4 3.7 %collective-permute-start.1 = (bf16[2,128,256]{2,1,0:T(8,128)(2,1)}, bf16[2,128,256]{2,1,0:T(8,128)(2,1)S(1)}, u32[]{:S(2)}, u32[]{:S(2)}) collective-permute-start(bf16[2,128,256]{2,1,0:T(8,128)(2,1)} %bitcast_dynamic-update-slice_fusion.1), channel_id=1, source_target_pairs={{0,16},{16,0},{1,17},{17,1},{2,18},{18,2},{3,19},{19,3},{4,20},{20... | collective-permute-start | bytes 393224 | tf_op jit(solution)/shard_map/ppermute | solution.py:35
  10.2 3.7 %collective-permute-done.1 = bf16[2,128,256]{2,1,0:T(8,128)(2,1)S(1)} collective-permute-done((bf16[2,128,256]{2,1,0:T(8,128)(2,1)}, bf16[2,128,256]{2,1,0:T(8,128)(2,1)S(1)}, u32[]{:S(2)}, u32[]{:S(2)}) %collective-permute-start.1) | collective-permute-done | bytes 131104 | tf_op jit(solution)/shard_map/ppermute | solution.py:35
  13.9 1.6 %pad_maximum_fusion.2.refs_0_ = bf16[2,2,128,256]{3,2,1,0:T(8,128)(2,1)} fusion(bf16[1,2,128,256]{3,2,1,0:T(8,128)(2,1)S(1)} %bitcast.66, bf16[1,2,128,256]{3,2,1,0:T(8,128)(2,1)} %bitcast.65), kind=kLoop, calls=%fused_computation.31 | loop fusion | flops 131072 | bytes 524288 | tf_op jit(solution)/shard_map/stack | solution.py:301
  15.5 2.5 %collective-permute-start.2 = (bf16[2,2,128,256]{3,2,1,0:T(8,128)(2,1)}, bf16[2,2,128,256]{3,2,1,0:T(8,128)(2,1)S(1)}, u32[]{:S(2)}, u32[]{:S(2)}) collective-permute-start(bf16[2,2,128,256]{3,2,1,0:T(8,128)(2,1)} %pad_maximum_fusion.2.refs_0_), channel_id=1, source_target_pairs={{0,12},{4,0},{8,4},{12,8},{1,13},{5,1},{9,5},{13,9},{2,14},{6,2},{... | collective-permute-start | bytes 786440 | tf_op jit(solution)/shard_map/ppermute | solution.py:35
  18.0 0.7 bitcast_dynamic-update-slice_fusion.refs_4_
  18.7 2.7 %collective-permute-start.6 = (bf16[2,128,1024]{2,1,0:T(8,128)(2,1)}, bf16[2,128,1024]{2,1,0:T(8,128)(2,1)}, u32[]{:S(2)}, u32[]{:S(2)}) collective-permute-start(bf16[2,128,1024]{2,1,0:T(8,128)(2,1)} %bitcast_dynamic-update-slice_fusion.refs_4_), channel_id=1, source_target_pairs={{0,96},{32,0},{64,32},{96,64},{1,97},{33,1},{65,33},{97,65},{2,98}... | collective-permute-start | bytes 1572872 | tf_op jit(solution)/shard_map/ppermute | solution.py:35
  21.8 0.7 collective-permute-start.8
  23.1 0.9 collective-permute-start.4
  23.9 1.1 convolution_add_fusion.2
  25.0 0.6 slice.116.refs_8_
  25.8 0.6 broadcast_in_dim.61.refs_9_
  26.4 2.0 %columns.1 = (bf16[128,512]{1,0:T(8,128)(2,1)}, bf16[128,512]{1,0:T(8,128)(2,1)}, bf16[128,512]{1,0:T(8,128)(2,1)}, bf16[128,512]{1,0:T(8,128)(2,1)}) custom-call(s32[3]{0:T(128)} %pad_add_fusion.at_ref, bf16[128,2048]{1,0:T(8,128)(2,1)} %in_ref), custom_call_target="tpu_custom_call" | custom-call | tf_op jit(solution)/shard_map/columns/pallas_call | solution.py:244
  28.4 1.5 %dynamic-slice_select_fusion = bf16[2048,256]{1,0:T(8,128)(2,1)S(1)} fusion(bf16[4096,256]{1,0:T(8,128)(2,1)S(1)} %copy-done, s32[]{:T(128)S(6)} %select_n.157, bf16[4096,256]{1,0:T(8,128)(2,1)} %param.17, pred[]{:T(512)S(6)} %eq.50), kind=kLoop, calls=%fused_computation.16 | loop fusion | flops 524288 | bytes 3145733 | tf_op jit(solution)/shard_map/jit(_where)/select_n | solution.py:311
  30.2 1.1 collective-permute-start.27
  31.3 4.2 %collective-permute-done.4.refs_3_ = bf16[2,2,128,256]{3,2,1,0:T(8,128)(2,1)} collective-permute-done((bf16[2,2,128,256]{3,2,1,0:T(8,128)(2,1)}, bf16[2,2,128,256]{3,2,1,0:T(8,128)(2,1)}, u32[]{:S(2)}, u32[]{:S(2)}) %collective-permute-start.4) | collective-permute-done | bytes 262176 | tf_op jit(solution)/shard_map/ppermute | solution.py:35
  35.5 3.0 %collective-permute-start.26 = (bf16[128,512]{1,0:T(8,128)(2,1)S(1)}, bf16[128,512]{1,0:T(8,128)(2,1)S(1)}, u32[]{:S(2)}, u32[]{:S(2)}) collective-permute-start(bf16[128,512]{1,0:T(8,128)(2,1)S(1)} %copy-done.10), channel_id=1, source_target_pairs={{0,8},{4,12},{8,0},{12,4},{1,9},{5,13},{9,1},{13,5},{2,10},{6,14},... | collective-permute-start | bytes 393224 | tf_op jit(solution)/shard_map/ppermute | solution.py:35
  39.1 9.3 %collective-permute-done.8.refs_7_ = bf16[2,128,1024]{2,1,0:T(8,128)(2,1)} collective-permute-done((bf16[2,128,1024]{2,1,0:T(8,128)(2,1)}, bf16[2,128,1024]{2,1,0:T(8,128)(2,1)}, u32[]{:S(2)}, u32[]{:S(2)}) %collective-permute-start.8) | collective-permute-done | bytes 524320 | tf_op jit(solution)/shard_map/ppermute | solution.py:35
  48.3 10.8 %stats.1 = (f32[16,1024]{1,0:T(8,128)}, f32[16,1024]{1,0:T(8,128)}, f32[16,1024]{1,0:T(8,128)}, f32[16,1024]{1,0:T(8,128)}) custom-call(bf16[2,2,128,256]{3,2,1,0:T(8,128)(2,1)} %pad_maximum_fusion.2.refs_0_, bf16[2,2,128,256]{3,2,1,0:T(8,128)(2,1)} %copy-done.7, bf16[2,2,128,256]{3,2,1,0:T(8,128)(2,1)} %collective-permute-done.3.refs_2_, ...), custom_call_target="tpu_custom_call" | custom-call | flops 6000000000 | bytes 3000000 | tf_op jit(solution)/shard_map/stats/pallas_call | solution.py:178
  59.5 1.1 collective-permute-start.11
  61.3 0.7 collective-permute-start.28
  62.0 0.7 collective-permute-done.9.refs_11_
  62.7 1.4 collective-permute-done.10.refs_12_
  64.1 0.8 collective-permute-done.11.refs_13_
  64.9 17.9 %grads.1 = (bf16[4,2,128,256]{3,2,1,0:T(8,128)(2,1)}, bf16[2,2,128,256]{3,2,1,0:T(8,128)(2,1)}, bf16[2,2,128,256]{3,2,1,0:T(8,128)(2,1)}, f32[2,128,512]{2,1,0:T...) custom-call(bf16[2,2,128,256]{3,2,1,0:T(8,128)(2,1)} %pad_maximum_fusion.2.refs_0_, ...), custom_call_target="tpu_custom_call" | custom-call | flops 12000000000 | bytes 6000000 | tf_op jit(solution)/shard_map/grads/pallas_call | solution.py:191
  82.9 1.8 %collective-permute-start.14 = (bf16[2,128,512]{2,1,0:T(8,128)(2,1)}, bf16[2,128,512]{2,1,0:T(8,128)(2,1)S(1)}, u32[]{:S(2)}, u32[]{:S(2)}) collective-permute-start(bf16[2,128,512]{2,1,0:T(8,128)(2,1)} %get-tuple-element.71), channel_id=1, source_target_pairs={{0,96},{32,0},{64,32},{96,64},{1,97},{33,1},{65,33},{97,65},{2,98}... | collective-permute-start | bytes 786440 | tf_op jit(solution)/shard_map/ppermute | solution.py:35
  84.7 0.6 collective-permute-start.13
  85.3 2.7 %collective-permute-start.17 = (bf16[2,2,128,256]{3,2,1,0:T(8,128)(2,1)}, bf16[2,2,128,256]{3,2,1,0:T(8,128)(2,1)S(1)}, u32[]{:S(2)}, u32[]{:S(2)}) collective-permute-start(bf16[2,2,128,256]{3,2,1,0:T(8,128)(2,1)} %get-tuple-element.75), channel_id=1, source_target_pairs={{0,16},{16,0},{1,17},{17,1},{2,18},{18,2},{3,19},{19,3},{4,20},{20... | collective-permute-start | bytes 786440 | tf_op jit(solution)/shard_map/ppermute | solution.py:35
  88.3 1.3 maximum_select_fusion.1
  89.9 8.1 %collective-permute-done.16 = bf16[2,2,128,256]{3,2,1,0:T(8,128)(2,1)S(1)} collective-permute-done((bf16[2,2,128,256]{3,2,1,0:T(8,128)(2,1)}, bf16[2,2,128,256]{3,2,1,0:T(8,128)(2,1)S(1)}, u32[]{:S(2)}, u32[]{:S(2)}) %collective-permute-start.16) | collective-permute-done | bytes 262176 | tf_op jit(solution)/shard_map/ppermute | solution.py:35
  98.1 3.7 %collective-permute-start.29 = (bf16[4,128,1024]{2,1,0:T(8,128)(2,1)S(1)}, bf16[4,128,1024]{2,1,0:T(8,128)(2,1)S(1)}, u32[]{:S(2)}, u32[]{:S(2)}) collective-permute-start(bf16[4,128,1024]{2,1,0:T(8,128)(2,1)S(1)} %maximum_select_fusion.1), channel_id=1, source_target_pairs={{0,2},{2,0},{1,3},{3,1},{4,6},{6,4},{5,7},{7,5},{8,10},{10,8},{9,1... | collective-permute-start | bytes 3145736 | tf_op jit(solution)/shard_map/ppermute | solution.py:35
  102.0 2.7 %collective-permute-start.20 = (bf16[2,128,256]{2,1,0:T(8,128)(2,1)S(1)}, bf16[2,128,256]{2,1,0:T(8,128)(2,1)S(1)}, u32[]{:S(2)}, u32[]{:S(2)}) collective-permute-start(bf16[2,128,256]{2,1,0:T(8,128)(2,1)S(1)} %fusion.31), channel_id=1, source_target_pairs={{0,12},{4,0},{8,4},{12,8},{1,13},{5,1},{9,5},{13,9},{2,14},{6,2},{... | collective-permute-start | bytes 393224 | tf_op jit(solution)/shard_map/ppermute | solution.py:35
  105.2 3.3 %collective-permute-done.20 = bf16[2,128,256]{2,1,0:T(8,128)(2,1)S(1)} collective-permute-done((bf16[2,128,256]{2,1,0:T(8,128)(2,1)S(1)}, bf16[2,128,256]{2,1,0:T(8,128)(2,1)S(1)}, u32[]{:S(2)}, u32[]{:S(2)}) %collective-permute-start.20) | collective-permute-done | bytes 131104 | tf_op jit(solution)/shard_map/ppermute | solution.py:35
  108.5 1.5 %collective-permute-start.15 = (bf16[128,512]{1,0:T(8,128)(2,1)S(1)}, bf16[128,512]{1,0:T(8,128)(2,1)S(1)}, u32[]{:S(2)}, u32[]{:S(2)}) collective-permute-start(bf16[128,512]{1,0:T(8,128)(2,1)S(1)} %get-tuple-element.85), channel_id=1, source_target_pairs={{0,2},{2,0},{1,3},{3,1},{4,6},{6,4},{5,7},{7,5},{8,10},{10,8},{9,1... | collective-permute-start | bytes 393224 | tf_op jit(solution)/shard_map/ppermute | solution.py:35
  110.1 0.7 collective-permute-start.32
  110.8 3.7 %collective-permute-start.31 = (bf16[2,128,256]{2,1,0:T(8,128)(2,1)S(1)}, bf16[2,128,256]{2,1,0:T(8,128)(2,1)S(1)}, u32[]{:S(2)}, u32[]{:S(2)}) collective-permute-start(bf16[2,128,256]{2,1,0:T(8,128)(2,1)S(1)} %fusion.27), channel_id=1, source_target_pairs={{0,8},{4,12},{8,0},{12,4},{1,9},{5,13},{9,1},{13,5},{2,10},{6,14},... | collective-permute-start | bytes 393224 | tf_op jit(solution)/shard_map/ppermute | solution.py:35
  114.6 3.4 %collective-permute-start.21 = (bf16[128,256]{1,0:T(8,128)(2,1)S(1)}, bf16[128,256]{1,0:T(8,128)(2,1)S(1)}, u32[]{:S(2)}, u32[]{:S(2)}) collective-permute-start(bf16[128,256]{1,0:T(8,128)(2,1)S(1)} %slice_bitcast_fusion.2), channel_id=1, source_target_pairs={{0,2},{2,0},{1,3},{3,1},{4,6},{6,4},{5,7},{7,5},{8,10},{10,8},{9,1... | collective-permute-start | bytes 196616 | tf_op jit(solution)/shard_map/ppermute | solution.py:35
  118.0 0.8 maximum_select_fusion.2
  118.8 1.4 collective-permute-start.30
  122.1 2.3 %collective-permute-done.30 = bf16[2,128,256]{2,1,0:T(8,128)(2,1)S(1)} collective-permute-done((bf16[2,128,256]{2,1,0:T(8,128)(2,1)S(1)}, bf16[2,128,256]{2,1,0:T(8,128)(2,1)S(1)}, u32[]{:S(2)}, u32[]{:S(2)}) %collective-permute-start.30) | collective-permute-done | bytes 131104 | tf_op jit(solution)/shard_map/ppermute | solution.py:35
  124.4 1.6 %fusion.7 = bf16[1024,256]{1,0:T(8,128)(2,1)} fusion(bf16[1,2,128,256]{3,2,1,0:T(8,128)(2,1)S(1)} %bitcast.69, bf16[1,2,128,256]{3,2,1,0:T(8,128)(2,1)S(1)} %bitcast.70, bf16[1,2,128,256]{3,2,1,0:T(8,128)(2,1)S(1)} %bitcast.71, bf16[1,2,128,256]{3,2,1,0:T(8,128)(2,1)S(1)} %bitcast.64, bf16[4,1,128,1024]{3,2,0,1:T(8,128)(2,1)S(1)} %bitcast.68, ...), kind=kOutput, calls=%fused_computation.8 | convolution fusion | flops 538968064 | bytes 3145728 | tf_op jit(solution)/shard_map/dot_general | solution.py:346
  125.9 6.2 %all-to-all-start = ((bf16[16,64,256]{2,1,0:T(8,128)(2,1)}), bf16[16,64,256]{2,1,0:T(8,128)(2,1)}, u32[]{:S(2)}, u32[]{:S(2)}) async-start(bf16[16,64,256]{2,1,0:T(8,128)(2,1)} %bitcast.63), calls=%async_computation | async-start | bytes 1048576 | tf_op jit(solution)/shard_map/all_to_all | solution.py:353
  132.6 1.3 fusion.1
  133.9 9.5 %all-to-all-done.in_ref = bf16[16,64,256]{2,1,0:T(8,128)(2,1)} async-done(((bf16[16,64,256]{2,1,0:T(8,128)(2,1)}), bf16[16,64,256]{2,1,0:T(8,128)(2,1)}, u32[]{:S(2)}, u32[]{:S(2)}) %all-to-all-start) | async-done | bytes 524320 | tf_op jit(solution)/shard_map/all_to_all | solution.py:353
  143.4 1.7 %finish.1 = (f32[64,256]{1,0:T(8,128)}, f32[64,256]{1,0:T(8,128)}) custom-call(bf16[16,64,256]{2,1,0:T(8,128)(2,1)} %all-to-all-done.in_ref), custom_call_target="tpu_custom_call" | custom-call | tf_op jit(solution)/shard_map/finish/pallas_call | solution.py:263
  (100 shorter events, 7.9 us)
Async XLA Ops:
  0.6 27.8 %copy-start = (bf16[4096,256]{1,0:T(8,128)(2,1)S(1)}, bf16[4096,256]{1,0:T(8,128)(2,1)}, u32[]{:S(2)}) copy-start(bf16[4096,256]{1,0:T(8,128)(2,1)} %param.18) | copy-start | bytes 6291460
  3.3 2.5 %collective-permute-start = (bf16[128,256]{1,0:T(8,128)(2,1)}, bf16[128,256]{1,0:T(8,128)(2,1)S(1)}, u32[]{:S(2)}, u32[]{:S(2)}) collective-permute-start(bf16[128,256]{1,0:T(8,128)(2,1)} %get-tuple-element.55), channel_id=1, source_target_pairs={{0,2},{2,0},{1,3},{3,1},{4,6},{6,4},{5,7},{7,5},{8,10},{10,8},{9,1... | collective-permute-start | bytes 196616 | tf_op jit(solution)/shard_map/ppermute | solution.py:35
  4.7 13.3 %collective-permute-start.5 = (bf16[128,1024]{1,0:T(8,128)(2,1)}, bf16[128,1024]{1,0:T(8,128)(2,1)S(1)}, u32[]{:S(2)}, u32[]{:S(2)}) collective-permute-start(bf16[128,1024]{1,0:T(8,128)(2,1)} %get-tuple-element.57), channel_id=1, source_target_pairs={{0,2},{2,0},{1,3},{3,1},{4,6},{6,4},{5,7},{7,5},{8,10},{10,8},{9,1... | collective-permute-start | bytes 786440 | tf_op jit(solution)/shard_map/ppermute | solution.py:35
  6.4 7.4 %collective-permute-start.1 = (bf16[2,128,256]{2,1,0:T(8,128)(2,1)}, bf16[2,128,256]{2,1,0:T(8,128)(2,1)S(1)}, u32[]{:S(2)}, u32[]{:S(2)}) collective-permute-start(bf16[2,128,256]{2,1,0:T(8,128)(2,1)} %bitcast_dynamic-update-slice_fusion.1), channel_id=1, source_target_pairs={{0,16},{16,0},{1,17},{17,1},{2,18},{18,2},{3,19},{19,3},{4,20},{20... | collective-permute-start | bytes 393224 | tf_op jit(solution)/shard_map/ppermute | solution.py:35
  15.5 7.6 %collective-permute-start.2 = (bf16[2,2,128,256]{3,2,1,0:T(8,128)(2,1)}, bf16[2,2,128,256]{3,2,1,0:T(8,128)(2,1)S(1)}, u32[]{:S(2)}, u32[]{:S(2)}) collective-permute-start(bf16[2,2,128,256]{3,2,1,0:T(8,128)(2,1)} %pad_maximum_fusion.2.refs_0_), channel_id=1, source_target_pairs={{0,12},{4,0},{8,4},{12,8},{1,13},{5,1},{9,5},{13,9},{2,14},{6,2},{... | collective-permute-start | bytes 786440 | tf_op jit(solution)/shard_map/ppermute | solution.py:35
  18.7 19.8 %collective-permute-start.6 = (bf16[2,128,1024]{2,1,0:T(8,128)(2,1)}, bf16[2,128,1024]{2,1,0:T(8,128)(2,1)}, u32[]{:S(2)}, u32[]{:S(2)}) collective-permute-start(bf16[2,128,1024]{2,1,0:T(8,128)(2,1)} %bitcast_dynamic-update-slice_fusion.refs_4_), channel_id=1, source_target_pairs={{0,96},{32,0},{64,32},{96,64},{1,97},{33,1},{65,33},{97,65},{2,98}... | collective-permute-start | bytes 1572872 | tf_op jit(solution)/shard_map/ppermute | solution.py:35
  21.4 17.1 %collective-permute-start.7 = (bf16[2,128,1024]{2,1,0:T(8,128)(2,1)}, bf16[2,128,1024]{2,1,0:T(8,128)(2,1)}, u32[]{:S(2)}, u32[]{:S(2)}) collective-permute-start(bf16[2,128,1024]{2,1,0:T(8,128)(2,1)} %bitcast_dynamic-update-slice_fusion.refs_4_), channel_id=1, source_target_pairs={{0,64},{32,96},{64,0},{96,32},{1,65},{33,97},{65,1},{97,33},{2,66}... | collective-permute-start | bytes 1572872 | tf_op jit(solution)/shard_map/ppermute | solution.py:35
  21.8 26.6 %collective-permute-start.8 = (bf16[2,128,1024]{2,1,0:T(8,128)(2,1)}, bf16[2,128,1024]{2,1,0:T(8,128)(2,1)}, u32[]{:S(2)}, u32[]{:S(2)}) collective-permute-start(bf16[2,128,1024]{2,1,0:T(8,128)(2,1)} %bitcast_dynamic-update-slice_fusion.refs_4_), channel_id=1, source_target_pairs={{0,32},{32,64},{64,96},{96,0},{1,33},{33,65},{65,97},{97,1},{2,34}... | collective-permute-start | bytes 1572872 | tf_op jit(solution)/shard_map/ppermute | solution.py:35
  22.5 7.7 %collective-permute-start.3 = (bf16[2,2,128,256]{3,2,1,0:T(8,128)(2,1)}, bf16[2,2,128,256]{3,2,1,0:T(8,128)(2,1)}, u32[]{:S(2)}, u32[]{:S(2)}) collective-permute-start(bf16[2,2,128,256]{3,2,1,0:T(8,128)(2,1)} %pad_maximum_fusion.2.refs_0_), channel_id=1, source_target_pairs={{0,8},{4,12},{8,0},{12,4},{1,9},{5,13},{9,1},{13,5},{2,10},{6,14},... | collective-permute-start | bytes 786440 | tf_op jit(solution)/shard_map/ppermute | solution.py:35
  23.1 0.9 copy-start.7
  23.1 12.5 %collective-permute-start.4 = (bf16[2,2,128,256]{3,2,1,0:T(8,128)(2,1)}, bf16[2,2,128,256]{3,2,1,0:T(8,128)(2,1)}, u32[]{:S(2)}, u32[]{:S(2)}) collective-permute-start(bf16[2,2,128,256]{3,2,1,0:T(8,128)(2,1)} %pad_maximum_fusion.2.refs_0_), channel_id=1, source_target_pairs={{0,4},{4,8},{8,12},{12,0},{1,5},{5,9},{9,13},{13,1},{2,6},{6,10},{... | collective-permute-start | bytes 786440 | tf_op jit(solution)/shard_map/ppermute | solution.py:35
  28.4 1.8 %copy-start.11 = (bf16[128,512]{1,0:T(8,128)(2,1)S(1)}, bf16[128,512]{1,0:T(8,128)(2,1)}, u32[]{:S(2)}) copy-start(bf16[128,512]{1,0:T(8,128)(2,1)} %get-tuple-element.60) | copy-start | bytes 393220
  28.4 7.1 %copy-start.10 = (bf16[128,512]{1,0:T(8,128)(2,1)S(1)}, bf16[128,512]{1,0:T(8,128)(2,1)}, u32[]{:S(2)}) copy-start(bf16[128,512]{1,0:T(8,128)(2,1)} %get-tuple-element.61) | copy-start | bytes 393220
  28.4 10.1 %copy-start.9 = (bf16[128,512]{1,0:T(8,128)(2,1)S(1)}, bf16[128,512]{1,0:T(8,128)(2,1)}, u32[]{:S(2)}) copy-start(bf16[128,512]{1,0:T(8,128)(2,1)} %get-tuple-element.62) | copy-start | bytes 393220
  29.9 30.7 %copy-start.4 = (bf16[128,512]{1,0:T(8,128)(2,1)S(1)}, bf16[128,512]{1,0:T(8,128)(2,1)}, u32[]{:S(2)}) copy-start(bf16[128,512]{1,0:T(8,128)(2,1)} %get-tuple-element.59) | copy-start | bytes 393220
  30.2 28.9 %collective-permute-start.27 = (bf16[128,512]{1,0:T(8,128)(2,1)S(1)}, bf16[128,512]{1,0:T(8,128)(2,1)S(1)}, u32[]{:S(2)}, u32[]{:S(2)}) collective-permute-start(bf16[128,512]{1,0:T(8,128)(2,1)S(1)} %copy-done.11), channel_id=1, source_target_pairs={{0,4},{4,8},{8,12},{12,0},{1,5},{5,9},{9,13},{13,1},{2,6},{6,10},{... | collective-permute-start | bytes 393224 | tf_op jit(solution)/shard_map/ppermute | solution.py:35
  35.5 24.0 %collective-permute-start.26 = (bf16[128,512]{1,0:T(8,128)(2,1)S(1)}, bf16[128,512]{1,0:T(8,128)(2,1)S(1)}, u32[]{:S(2)}, u32[]{:S(2)}) collective-permute-start(bf16[128,512]{1,0:T(8,128)(2,1)S(1)} %copy-done.10), channel_id=1, source_target_pairs={{0,8},{4,12},{8,0},{12,4},{1,9},{5,13},{9,1},{13,5},{2,10},{6,14},... | collective-permute-start | bytes 393224 | tf_op jit(solution)/shard_map/ppermute | solution.py:35
  38.5 22.2 %collective-permute-start.25 = (bf16[128,512]{1,0:T(8,128)(2,1)S(1)}, bf16[128,512]{1,0:T(8,128)(2,1)S(1)}, u32[]{:S(2)}, u32[]{:S(2)}) collective-permute-start(bf16[128,512]{1,0:T(8,128)(2,1)S(1)} %copy-done.9), channel_id=1, source_target_pairs={{0,12},{4,0},{8,4},{12,8},{1,13},{5,1},{9,5},{13,9},{2,14},{6,2},{... | collective-permute-start | bytes 393224 | tf_op jit(solution)/shard_map/ppermute | solution.py:35
  38.5 80.3 %collective-permute-start.23 = (bf16[2048,256]{1,0:T(8,128)(2,1)S(1)}, bf16[2048,256]{1,0:T(8,128)(2,1)S(1)}, u32[]{:S(2)}, u32[]{:S(2)}) collective-permute-start(bf16[2048,256]{1,0:T(8,128)(2,1)S(1)} %dynamic-slice_select_fusion), channel_id=1, source_target_pairs={{0,1},{1,0},{2,3},{3,2},{4,5},{5,4},{6,7},{7,6},{8,9},{9,8},{10,11... | collective-permute-start | bytes 3145736 | tf_op jit(solution)/shard_map/ppermute | solution.py:35
  59.1 3.6 %collective-permute-start.9 = (f32[16,1024]{1,0:T(8,128)}, f32[16,1024]{1,0:T(8,128)}, u32[]{:S(2)}, u32[]{:S(2)}) collective-permute-start(f32[16,1024]{1,0:T(8,128)} %get-tuple-element.65), channel_id=1, source_target_pairs={{0,96},{32,0},{64,32},{96,64},{1,97},{33,1},{65,33},{97,65},{2,98}... | collective-permute-start | bytes 196616 | tf_op jit(solution)/shard_map/ppermute | solution.py:35
  59.1 5.0 %collective-permute-start.10 = (f32[16,1024]{1,0:T(8,128)}, f32[16,1024]{1,0:T(8,128)}, u32[]{:S(2)}, u32[]{:S(2)}) collective-permute-start(f32[16,1024]{1,0:T(8,128)} %get-tuple-element.66), channel_id=1, source_target_pairs={{0,64},{32,96},{64,0},{96,32},{1,65},{33,97},{65,1},{97,33},{2,66}... | collective-permute-start | bytes 196616 | tf_op jit(solution)/shard_map/ppermute | solution.py:35
  59.5 5.4 %collective-permute-start.11 = (f32[16,1024]{1,0:T(8,128)}, f32[16,1024]{1,0:T(8,128)}, u32[]{:S(2)}, u32[]{:S(2)}) collective-permute-start(f32[16,1024]{1,0:T(8,128)} %get-tuple-element.67), channel_id=1, source_target_pairs={{0,32},{32,64},{64,96},{96,0},{1,33},{33,65},{65,97},{97,1},{2,34}... | collective-permute-start | bytes 196616 | tf_op jit(solution)/shard_map/ppermute | solution.py:35
  60.6 0.7 copy-start.5
  61.3 26.7 %collective-permute-start.28 = (bf16[4,128,512]{2,1,0:T(8,128)(2,1)S(1)}, bf16[4,128,512]{2,1,0:T(8,128)(2,1)S(1)}, u32[]{:S(2)}, u32[]{:S(2)}) collective-permute-start(bf16[4,128,512]{2,1,0:T(8,128)(2,1)S(1)} %get-tuple-element.83), channel_id=1, source_target_pairs={{0,1},{1,0},{2,3},{3,2},{4,5},{5,4},{6,7},{7,6},{8,9},{9,8},{10,11... | collective-permute-start | bytes 1572872 | tf_op jit(solution)/shard_map/ppermute | solution.py:35
  82.9 19.0 %collective-permute-start.14 = (bf16[2,128,512]{2,1,0:T(8,128)(2,1)}, bf16[2,128,512]{2,1,0:T(8,128)(2,1)S(1)}, u32[]{:S(2)}, u32[]{:S(2)}) collective-permute-start(bf16[2,128,512]{2,1,0:T(8,128)(2,1)} %get-tuple-element.71), channel_id=1, source_target_pairs={{0,96},{32,0},{64,32},{96,64},{1,97},{33,1},{65,33},{97,65},{2,98}... | collective-permute-start | bytes 786440 | tf_op jit(solution)/shard_map/ppermute | solution.py:35
  84.7 17.3 %collective-permute-start.13 = (bf16[2,128,512]{2,1,0:T(8,128)(2,1)}, bf16[2,128,512]{2,1,0:T(8,128)(2,1)S(1)}, u32[]{:S(2)}, u32[]{:S(2)}) collective-permute-start(bf16[2,128,512]{2,1,0:T(8,128)(2,1)} %get-tuple-element.70), channel_id=1, source_target_pairs={{0,64},{32,96},{64,0},{96,32},{1,65},{33,97},{65,1},{97,33},{2,66}... | collective-permute-start | bytes 786440 | tf_op jit(solution)/shard_map/ppermute | solution.py:35
  85.3 12.8 %collective-permute-start.17 = (bf16[2,2,128,256]{3,2,1,0:T(8,128)(2,1)}, bf16[2,2,128,256]{3,2,1,0:T(8,128)(2,1)S(1)}, u32[]{:S(2)}, u32[]{:S(2)}) collective-permute-start(bf16[2,2,128,256]{3,2,1,0:T(8,128)(2,1)} %get-tuple-element.75), channel_id=1, source_target_pairs={{0,16},{16,0},{1,17},{17,1},{2,18},{18,2},{3,19},{19,3},{4,20},{20... | collective-permute-start | bytes 786440 | tf_op jit(solution)/shard_map/ppermute | solution.py:35
  88.0 10.0 %copy-start.8 = (bf16[2,128,512]{2,1,0:T(8,128)(2,1)S(1)}, bf16[2,128,512]{2,1,0:T(8,128)(2,1)}, u32[]{:S(2)}) copy-start(bf16[2,128,512]{2,1,0:T(8,128)(2,1)} %get-tuple-element.69) | copy-start | bytes 786436
  88.0 10.0 %copy-start.6 = (bf16[4,2,128,256]{3,2,1,0:T(8,128)(2,1)S(1)}, bf16[4,2,128,256]{3,2,1,0:T(8,128)(2,1)}, u32[]{:S(2)}) copy-start(bf16[4,2,128,256]{3,2,1,0:T(8,128)(2,1)} %get-tuple-element.74) | copy-start | bytes 1572868
  88.0 10.0 %collective-permute-start.16 = (bf16[2,2,128,256]{3,2,1,0:T(8,128)(2,1)}, bf16[2,2,128,256]{3,2,1,0:T(8,128)(2,1)S(1)}, u32[]{:S(2)}, u32[]{:S(2)}) collective-permute-start(bf16[2,2,128,256]{3,2,1,0:T(8,128)(2,1)} %get-tuple-element.73), channel_id=1, source_target_pairs={{0,16},{16,0},{1,17},{17,1},{2,18},{18,2},{3,19},{19,3},{4,20},{20... | collective-permute-start | bytes 786440 | tf_op jit(solution)/shard_map/ppermute | solution.py:35
  89.6 15.4 %copy-start.3 = (f32[2,128,512]{2,1,0:T(8,128)S(1)}, f32[2,128,512]{2,1,0:T(8,128)}, u32[]{:S(2)}) copy-start(f32[2,128,512]{2,1,0:T(8,128)} %get-tuple-element.68) | copy-start | bytes 1572868
  98.0 6.6 %collective-permute-start.12 = (bf16[2,128,512]{2,1,0:T(8,128)(2,1)S(1)}, bf16[2,128,512]{2,1,0:T(8,128)(2,1)S(1)}, u32[]{:S(2)}, u32[]{:S(2)}) collective-permute-start(bf16[2,128,512]{2,1,0:T(8,128)(2,1)S(1)} %copy-done.8), channel_id=1, source_target_pairs={{0,32},{32,64},{64,96},{96,0},{1,33},{33,65},{65,97},{97,1},{2,34}... | collective-permute-start | bytes 786440 | tf_op jit(solution)/shard_map/ppermute | solution.py:35
  98.1 26.3 %collective-permute-start.29 = (bf16[4,128,1024]{2,1,0:T(8,128)(2,1)S(1)}, bf16[4,128,1024]{2,1,0:T(8,128)(2,1)S(1)}, u32[]{:S(2)}, u32[]{:S(2)}) collective-permute-start(bf16[4,128,1024]{2,1,0:T(8,128)(2,1)S(1)} %maximum_select_fusion.1), channel_id=1, source_target_pairs={{0,2},{2,0},{1,3},{3,1},{4,6},{6,4},{5,7},{7,5},{8,10},{10,8},{9,1... | collective-permute-start | bytes 3145736 | tf_op jit(solution)/shard_map/ppermute | solution.py:35
  101.9 18.6 %copy-start.1 = (bf16[4096,256]{1,0:T(8,128)(2,1)S(1)}, bf16[4096,256]{1,0:T(8,128)(2,1)}, u32[]{:S(2)}) copy-start(bf16[4096,256]{1,0:T(8,128)(2,1)} %param.18) | copy-start | bytes 6291460
  101.9 8.1 %collective-permute-start.19 = (bf16[2,128,256]{2,1,0:T(8,128)(2,1)S(1)}, bf16[2,128,256]{2,1,0:T(8,128)(2,1)S(1)}, u32[]{:S(2)}, u32[]{:S(2)}) collective-permute-start(bf16[2,128,256]{2,1,0:T(8,128)(2,1)S(1)} %get-tuple-element.81), channel_id=1, source_target_pairs={{0,4},{4,8},{8,12},{12,0},{1,5},{5,9},{9,13},{13,1},{2,6},{6,10},{... | collective-permute-start | bytes 393224 | tf_op jit(solution)/shard_map/ppermute | solution.py:35
  102.0 6.5 %collective-permute-start.20 = (bf16[2,128,256]{2,1,0:T(8,128)(2,1)S(1)}, bf16[2,128,256]{2,1,0:T(8,128)(2,1)S(1)}, u32[]{:S(2)}, u32[]{:S(2)}) collective-permute-start(bf16[2,128,256]{2,1,0:T(8,128)(2,1)S(1)} %fusion.31), channel_id=1, source_target_pairs={{0,12},{4,0},{8,4},{12,8},{1,13},{5,1},{9,5},{13,9},{2,14},{6,2},{... | collective-permute-start | bytes 393224 | tf_op jit(solution)/shard_map/ppermute | solution.py:35
  104.7 5.4 %collective-permute-start.18 = (bf16[2,128,256]{2,1,0:T(8,128)(2,1)S(1)}, bf16[2,128,256]{2,1,0:T(8,128)(2,1)S(1)}, u32[]{:S(2)}, u32[]{:S(2)}) collective-permute-start(bf16[2,128,256]{2,1,0:T(8,128)(2,1)S(1)} %get-tuple-element.80), channel_id=1, source_target_pairs={{0,8},{4,12},{8,0},{12,4},{1,9},{5,13},{9,1},{13,5},{2,10},{6,14},... | collective-permute-start | bytes 393224 | tf_op jit(solution)/shard_map/ppermute | solution.py:35
  105.1 15.8 %copy-start.2 = (bf16[4096,256]{1,0:T(8,128)(2,1)S(1)}, bf16[4096,256]{1,0:T(8,128)(2,1)}, u32[]{:S(2)}) copy-start(bf16[4096,256]{1,0:T(8,128)(2,1)} %param.17) | copy-start | bytes 6291460
  108.5 6.1 %collective-permute-start.15 = (bf16[128,512]{1,0:T(8,128)(2,1)S(1)}, bf16[128,512]{1,0:T(8,128)(2,1)S(1)}, u32[]{:S(2)}, u32[]{:S(2)}) collective-permute-start(bf16[128,512]{1,0:T(8,128)(2,1)S(1)} %get-tuple-element.85), channel_id=1, source_target_pairs={{0,2},{2,0},{1,3},{3,1},{4,6},{6,4},{5,7},{7,5},{8,10},{10,8},{9,1... | collective-permute-start | bytes 393224 | tf_op jit(solution)/shard_map/ppermute | solution.py:35
  110.1 11.4 %collective-permute-start.32 = (bf16[2,128,256]{2,1,0:T(8,128)(2,1)S(1)}, bf16[2,128,256]{2,1,0:T(8,128)(2,1)S(1)}, u32[]{:S(2)}, u32[]{:S(2)}) collective-permute-start(bf16[2,128,256]{2,1,0:T(8,128)(2,1)S(1)} %fusion.27), channel_id=1, source_target_pairs={{0,4},{4,8},{8,12},{12,0},{1,5},{5,9},{9,13},{13,1},{2,6},{6,10},{... | collective-permute-start | bytes 393224 | tf_op jit(solution)/shard_map/ppermute | solution.py:35
  110.8 11.3 %collective-permute-start.31 = (bf16[2,128,256]{2,1,0:T(8,128)(2,1)S(1)}, bf16[2,128,256]{2,1,0:T(8,128)(2,1)S(1)}, u32[]{:S(2)}, u32[]{:S(2)}) collective-permute-start(bf16[2,128,256]{2,1,0:T(8,128)(2,1)S(1)} %fusion.27), channel_id=1, source_target_pairs={{0,8},{4,12},{8,0},{12,4},{1,9},{5,13},{9,1},{13,5},{2,10},{6,14},... | collective-permute-start | bytes 393224 | tf_op jit(solution)/shard_map/ppermute | solution.py:35
  114.6 5.6 %collective-permute-start.21 = (bf16[128,256]{1,0:T(8,128)(2,1)S(1)}, bf16[128,256]{1,0:T(8,128)(2,1)S(1)}, u32[]{:S(2)}, u32[]{:S(2)}) collective-permute-start(bf16[128,256]{1,0:T(8,128)(2,1)S(1)} %slice_bitcast_fusion.2), channel_id=1, source_target_pairs={{0,2},{2,0},{1,3},{3,1},{4,6},{6,4},{5,7},{7,5},{8,10},{10,8},{9,1... | collective-permute-start | bytes 196616 | tf_op jit(solution)/shard_map/ppermute | solution.py:35
  118.8 5.6 %collective-permute-start.30 = (bf16[2,128,256]{2,1,0:T(8,128)(2,1)S(1)}, bf16[2,128,256]{2,1,0:T(8,128)(2,1)S(1)}, u32[]{:S(2)}, u32[]{:S(2)}) collective-permute-start(bf16[2,128,256]{2,1,0:T(8,128)(2,1)S(1)} %fusion.27), channel_id=1, source_target_pairs={{0,12},{4,0},{8,4},{12,8},{1,13},{5,1},{9,5},{13,9},{2,14},{6,2},{... | collective-permute-start | bytes 393224 | tf_op jit(solution)/shard_map/ppermute | solution.py:35
  120.1 12.0 %collective-permute-start.24 = (bf16[2048,256]{1,0:T(8,128)(2,1)S(1)}, bf16[2048,256]{1,0:T(8,128)(2,1)S(1)}, u32[]{:S(2)}, u32[]{:S(2)}) collective-permute-start(bf16[2048,256]{1,0:T(8,128)(2,1)S(1)} %collective-permute-done.23), channel_id=1, source_target_pairs={{0,2},{2,0},{1,3},{3,1},{4,6},{6,4},{5,7},{7,5},{8,10},{10,8},{9,1... | collective-permute-start | bytes 3145736 | tf_op jit(solution)/shard_map/ppermute | solution.py:35
  121.5 10.6 %collective-permute-start.22 = (bf16[128,512]{1,0:T(8,128)(2,1)S(1)}, bf16[128,512]{1,0:T(8,128)(2,1)S(1)}, u32[]{:S(2)}, u32[]{:S(2)}) collective-permute-start(bf16[128,512]{1,0:T(8,128)(2,1)S(1)} %pad_maximum_fusion.3), channel_id=1, source_target_pairs={{0,1},{1,0},{2,3},{3,2},{4,5},{5,4},{6,7},{7,6},{8,9},{9,8},{10,11... | collective-permute-start | bytes 393224 | tf_op jit(solution)/shard_map/ppermute | solution.py:35
  125.9 17.5 %all-to-all-start = ((bf16[16,64,256]{2,1,0:T(8,128)(2,1)}), bf16[16,64,256]{2,1,0:T(8,128)(2,1)}, u32[]{:S(2)}, u32[]{:S(2)}) async-start(bf16[16,64,256]{2,1,0:T(8,128)(2,1)} %bitcast.63), calls=%async_computation | async-start | bytes 1048576 | tf_op jit(solution)/shard_map/all_to_all | solution.py:353

commit v3 on v2

--- a/solution.py
+++ b/solution.py
@@ -43,27 +43,39 @@
     return lax.dot_general(a, b, (((1,), (0,)), ((), ())), preferred_element_type=F32)
 
 
-def load_parts(kv_refs, qg_refs, kpos_ref, ks, vs, qs, gs, kposb):
+def part_copies(part, kv_refs, qg_refs, kv, qg, sem):
+    tok = pl.ds(part * T, T)
+    for b in range(4):
+        yield pltpu.make_async_copy(kv_refs[b].at[:, :, tok, :], kv.at[part, b], sem.at[part, b])
+    for s in range(4):
+        yield pltpu.make_async_copy(qg_refs[s].at[:, tok, :], qg.at[part, s], sem.at[part, 4 + s])
+
+
+def start_loads(kv_refs, qg_refs, kpos_ref, kv, qg, kposb, sem):
     for part in range(PARTS):
-        tok = slice(part * T, (part + 1) * T)
-        for b in range(4):
-            rows = slice(b * 4 * T, (b + 1) * 4 * T)
-            ks[part, rows, :] = kv_refs[b][:, :, tok, :HEAD].reshape(4 * T, HEAD)
-            vs[part, rows, :] = kv_refs[b][:, :, tok, HEAD:].reshape(4 * T, HEAD)
-        for h in range(GROUP):
-            for s in range(4):
-                row = (h * QSLOTS + s * 2) * T
-                qs[part, row : row + 2 * T, :] = qg_refs[s][:, tok, h * HEAD : (h + 1) * HEAD].reshape(2 * T, HEAD)
-                col = (GROUP + h) * HEAD
-                gs[part, row : row + 2 * T, :] = qg_refs[s][:, tok, col : col + HEAD].reshape(2 * T, HEAD)
+        for copy in part_copies(part, kv_refs, qg_refs, kv, qg, sem):
+            copy.start()
     for slot in range(KSLOTS):
         column = jnp.broadcast_to(kpos_ref[slot : slot + 1, :], (TOK, 128)).T
         for part in range(PARTS):
             kposb[part, slot * T : (slot + 1) * T, :] = column[part * T : (part + 1) * T, :]
 
 
-def masked_scores(delta, i, ip, ks, qs, kposb, qpos_ref):
-    s = nt(ks[ip], qs[i]) * SCORE2
+def keys_of(kv, ip):
+    return kv[ip, :, :, :, :, :HEAD].reshape(KR, HEAD)
+
+
+def values_of(kv, ip):
+    return kv[ip, :, :, :, :, HEAD:].reshape(KR, HEAD)
+
+
+def heads_of(qg, i, first):
+    cols = [(first + h) * HEAD for h in range(GROUP)]
+    return jnp.concatenate([qg[i, :, :, :, c : c + HEAD].reshape(QSLOTS * T, HEAD) for c in cols], axis=0)
+
+
+def masked_scores(delta, i, ip, k, q, kposb, qpos_ref):
+    s = nt(k, q) * SCORE2
     if delta == 0 or delta == SPAN:
         kp = jnp.concatenate([kposb[ip]] * (QR // 128), axis=1)
         qp = qpos_ref[i]
@@ -76,8 +88,8 @@
     kv_refs, qg_refs = refs[0:4], refs[4:8]
     kpos_ref, qpos_ref = refs[8:10]
     out_refs = refs[10:14]
-    ks, vs, qs, gs, kposb, ms, ls, ws = refs[14:]
-    load_parts(kv_refs, qg_refs, kpos_ref, ks, vs, qs, gs, kposb)
+    kv, qg, kposb, ms, ls, ws, sem = refs[14:]
+    start_loads(kv_refs, qg_refs, kpos_ref, kv, qg, kposb, sem)
     ms[...] = jnp.full(ms.shape, NEG, F32)
     ls[...] = jnp.zeros(ls.shape, F32)
     ws[...] = jnp.zeros(ws.shape, F32)
@@ -85,8 +97,12 @@
 
         def body(i, carry, delta=delta):
             ip = i - delta
-            s = masked_scores(delta, i, ip, ks, qs, kposb, qpos_ref).reshape(KR // 8, 8, QR)
-            dp = nt(vs[ip], gs[i]).reshape(KR // 8, 8, QR)
+            if delta == 0:
+                for copy in part_copies(i, kv_refs, qg_refs, kv, qg, sem):
+                    copy.wait()
+            s = masked_scores(delta, i, ip, keys_of(kv, ip), heads_of(qg, i, 0), kposb, qpos_ref)
+            s = s.reshape(KR // 8, 8, QR)
+            dp = nt(values_of(kv, ip), heads_of(qg, i, GROUP)).reshape(KR // 8, 8, QR)
             old = ms[i]
             new = jnp.maximum(old, jnp.max(s, axis=0))
             e = jnp.exp2(s - new[None])
@@ -119,26 +135,65 @@
     kpos_ref, qpos_ref = refs[8:10]
     st_refs = refs[10:14]
     dkv_near, dkv_first, dkv_last, dq_refs = refs[14], refs[15], refs[16], refs[17:21]
-    ks, vs, qs, gs, kposb, kt, dks, dvs, dqt, lse, mean = refs[21:]
-    far = (dkv_last.at[1], dkv_first.at[0], dkv_first.at[1], dkv_last.at[0])
-    load_parts(kv_refs, qg_refs, kpos_ref, ks, vs, qs, gs, kposb)
+    kv, qg, kposb, kt, qt, gt, dks, dvs, dqt, lse, mean, dkv_out, dq_wide, dq_out, sem, out_sem = refs[21:]
+    start_loads(kv_refs, qg_refs, kpos_ref, kv, qg, kposb, sem)
     for part in range(PARTS):
-        kt[part] = ks[part].T
         st = [r[part * 4 : part * 4 + 3, :] for r in st_refs]
         top = jnp.maximum(jnp.maximum(st[0][0:1], st[1][0:1]), jnp.maximum(st[2][0:1], st[3][0:1]))
         fade = [jnp.exp2(a[0:1] - top) for a in st]
         total = sum(a[1:2] * f for a, f in zip(st, fade))
         lse[part] = top + jnp.log2(total)
         mean[part] = sum(a[2:3] * f for a, f in zip(st, fade)) / total
+
+    def dkv_copies(part):
+        tok = slice(part * T, (part + 1) * T)
+        pairs = (
+            (dkv_out.at[part, 0], dkv_near.at[:, :, tok, :]),
+            (dkv_out.at[part, 1, 1:3], dkv_first.at[:, :, tok, :]),
+            (dkv_out.at[part, 1, 3], dkv_last.at[0, :, tok, :]),
+            (dkv_out.at[part, 1, 0], dkv_last.at[1, :, tok, :]),
+        )
+        return [pltpu.make_async_copy(a, b, out_sem.at[part, n]) for n, (a, b) in enumerate(pairs)]
+
+    def dq_copies(part):
+        tok = slice(part * T, (part + 1) * T)
+        pairs = [(dq_wide.at[part], dq_refs[0].at[:, tok, :])]
+        pairs += [(dq_out.at[part, s - 1], dq_refs[s].at[:, tok, :]) for s in (1, 2, 3)]
+        return [pltpu.make_async_copy(a, b, out_sem.at[part, 4 + n]) for n, (a, b) in enumerate(pairs)]
+
+    def emit_dkv(part):
+        dk = (dks[part] * SCALE).astype(BF).T.reshape(4, 2, 2, T, HEAD)
+        dv = dvs[part].astype(BF).T.reshape(4, 2, 2, T, HEAD)
+        for a in range(2):
+            dkv_out[part, a, :, :, :, :HEAD] = dk[:, a]
+            dkv_out[part, a, :, :, :, HEAD:] = dv[:, a]
+        for copy in dkv_copies(part):
+            copy.start()
+
+    def emit_dq(part):
+        dq = dqt[part].T * SCALE
+        for h in range(GROUP):
+            cols = slice(h * HEAD, (h + 1) * HEAD)
+            rows = dq[h * QSLOTS * T : (h + 1) * QSLOTS * T, :].reshape(4, 2, T, HEAD)
+            dq_wide[part, :, :, cols] = rows[0]
+            dq_out[part, :, :, :, cols] = rows[1:4].astype(BF)
+        for copy in dq_copies(part):
+            copy.start()
+
     for delta in range(SPAN + 1):
 
         def body(i, carry, delta=delta):
             ip = i - delta
-            q, g = qs[i], gs[i]
-            p = jnp.exp2(masked_scores(delta, i, ip, ks, qs, kposb, qpos_ref) - lse[i])
-            ds = (p * (nt(vs[ip], g) - mean[i])).astype(BF)
+            if delta == 0:
+                for copy in part_copies(i, kv_refs, qg_refs, kv, qg, sem):
+                    copy.wait()
+            k, q, g = keys_of(kv, ip), heads_of(qg, i, 0), heads_of(qg, i, GROUP)
+            if delta == 0:
+                kt[i], qt[i], gt[i] = k.T, q.T, g.T
+            p = jnp.exp2(masked_scores(delta, i, ip, k, q, kposb, qpos_ref) - lse[i])
+            ds = (p * (nt(values_of(kv, ip), g) - mean[i])).astype(BF)
             p = p.astype(BF)
-            dk, dv, dq = nn(ds, q), nn(p, g), nn(kt[ip], ds)
+            dk, dv, dq = nt(qt[i], ds), nt(gt[i], p), nn(kt[ip], ds)
             if delta == 0:
                 dks[ip], dvs[ip], dqt[i] = dk, dv, dq
             else:
@@ -148,37 +203,36 @@
             return carry
 
         lax.fori_loop(delta, PARTS, body, 0)
+        for part in range(PARTS):
+            if delta == min(SPAN, PARTS - 1 - part):
+                emit_dkv(part)
+            if delta == min(SPAN, part):
+                emit_dq(part)
     for part in range(PARTS):
-        tok = slice(part * T, (part + 1) * T)
-        for b in range(4):
-            for a in range(2):
-                rows = slice((b * 4 + a * 2) * T, (b * 4 + a * 2 + 2) * T)
-                ref = far[b] if a else dkv_near.at[b]
-                ref[:, tok, :HEAD] = (dks[part, rows, :] * SCALE).astype(BF).reshape(2, T, HEAD)
-                ref[:, tok, HEAD:] = dvs[part, rows, :].astype(BF).reshape(2, T, HEAD)
-        dq = dqt[part].T * SCALE
-        for h in range(GROUP):
-            for s in range(4):
-                row = (h * QSLOTS + s * 2) * T
-                piece = dq[row : row + 2 * T, :].reshape(2, T, HEAD)
-                dq_refs[s][:, tok, h * HEAD : (h + 1) * HEAD] = piece.astype(dq_refs[s].dtype)
+        for copy in dkv_copies(part) + dq_copies(part):
+            copy.wait()
 
 
 def common_scratch():
     return [
-        pltpu.VMEM((PARTS, KR, HEAD), BF),
-        pltpu.VMEM((PARTS, KR, HEAD), BF),
-        pltpu.VMEM((PARTS, QR, HEAD), BF),
-        pltpu.VMEM((PARTS, QR, HEAD), BF),
+        pltpu.VMEM((PARTS, 4, 2, 2, T, 2 * HEAD), BF),
+        pltpu.VMEM((PARTS, 4, 2, T, 2 * GROUP * HEAD), BF),
         pltpu.VMEM((PARTS, KR, 128), F32),
     ]
+
+
+def in_places(small):
+    return [pl.BlockSpec(memory_space=pl.ANY)] * 8 + [pl.BlockSpec(memory_space=pltpu.VMEM)] * small
 
 
 def run_stats(kvs, qgs, kpos, qpos):
     return pl.pallas_call(
         stats_kernel,
         out_shape=[jax.ShapeDtypeStruct((PARTS * 4, QR), F32)] * 4,
-        scratch_shapes=common_scratch() + [pltpu.VMEM((PARTS, 8, QR), F32)] * 3,
+        in_specs=in_places(2),
+        scratch_shapes=common_scratch()
+        + [pltpu.VMEM((PARTS, 8, QR), F32)] * 3
+        + [pltpu.SemaphoreType.DMA((PARTS, 8))],
         compiler_params=pltpu.CompilerParams(vmem_limit_bytes=VMEM_LIMIT),
         cost_estimate=pl.CostEstimate(flops=6_000_000_000, bytes_accessed=3_000_000, transcendentals=5_000_000),
         name="stats",
@@ -191,14 +245,23 @@
     out = pl.pallas_call(
         grads_kernel,
         out_shape=dkv + dq,
+        in_specs=in_places(6),
+        out_specs=[pl.BlockSpec(memory_space=pl.ANY)] * 7,
         scratch_shapes=common_scratch()
         + [
             pltpu.VMEM((PARTS, HEAD, KR), BF),
-            pltpu.VMEM((PARTS, KR, HEAD), F32),
-            pltpu.VMEM((PARTS, KR, HEAD), F32),
+            pltpu.VMEM((PARTS, HEAD, QR), BF),
+            pltpu.VMEM((PARTS, HEAD, QR), BF),
+            pltpu.VMEM((PARTS, HEAD, KR), F32),
+            pltpu.VMEM((PARTS, HEAD, KR), F32),
             pltpu.VMEM((PARTS, HEAD, QR), F32),
             pltpu.VMEM((PARTS, 1, QR), F32),
             pltpu.VMEM((PARTS, 1, QR), F32),
+            pltpu.VMEM((PARTS, 2, 4, 2, T, 2 * HEAD), BF),
+            pltpu.VMEM((PARTS, 2, T, GROUP * HEAD), F32),
+            pltpu.VMEM((PARTS, 3, 2, T, GROUP * HEAD), BF),
+            pltpu.SemaphoreType.DMA((PARTS, 8)),
+            pltpu.SemaphoreType.DMA((PARTS, 8)),
         ],
         compiler_params=pltpu.CompilerParams(vmem_limit_bytes=VMEM_LIMIT),
         cost_estimate=pl.CostEstimate(flops=12_000_000_000, bytes_accessed=6_000_000, transcendentals=5_000_000),
@@ -207,46 +270,62 @@
     return out[0], out[1:3], out[3:7]
 
 
-def pack_kernel(at_ref, q_ref, g_ref, k_ref, v_ref, kv_own, qg_own, kv_send, qg_send):
+def pack_kernel(at_ref, q_ref, g_ref, k_ref, v_ref, kv_own, qg_own, kv_send, qg_send, sem):
     wide = GROUP * HEAD
     mine = at_ref[0]
-    for which, kv, qg in ((mine, kv_own.at[0], qg_own.at[0]), (1 - mine, kv_send, qg_send)):
+    copies = []
+    for which, kv, qg in ((1 - mine, kv_send, qg_send), (mine, kv_own.at[0], qg_own.at[0])):
         cols = pl.ds(pl.multiple_of(which * wide, 128), wide)
         small = pl.ds(pl.multiple_of(which * HEAD, 128), HEAD)
-        kv[:, :HEAD] = k_ref[:, small]
-        kv[:, HEAD:] = v_ref[:, small]
-        qg[:, :wide] = q_ref[:, cols]
-        qg[:, wide:] = g_ref[:, cols]
-    kv_own[1] = kv_send[...]
-    qg_own[1] = qg_send[...]
+        for src, dst in (
+            (k_ref.at[:, small], kv.at[:, :HEAD]),
+            (v_ref.at[:, small], kv.at[:, HEAD:]),
+            (q_ref.at[:, cols], qg.at[:, :wide]),
+            (g_ref.at[:, cols], qg.at[:, wide:]),
+        ):
+            copies.append(pltpu.make_async_copy(src, dst, sem.at[len(copies)]))
+            copies[-1].start()
+    for copy in copies:
+        copy.wait()
 
 
 def run_pack(at, q, g, k, v):
     kv, qg = (TOK, 2 * HEAD), (TOK, 2 * GROUP * HEAD)
-    vmem = pl.BlockSpec(memory_space=pltpu.VMEM)
+    anywhere = pl.BlockSpec(memory_space=pl.ANY)
     return pl.pallas_call(
         pack_kernel,
         out_shape=[jax.ShapeDtypeStruct(a, BF) for a in ((2, *kv), (2, *qg), kv, qg)],
-        in_specs=[pl.BlockSpec(memory_space=pltpu.SMEM)] + [vmem] * 4,
+        in_specs=[pl.BlockSpec(memory_space=pltpu.SMEM)] + [anywhere] * 4,
+        out_specs=[anywhere] * 4,
+        scratch_shapes=[pltpu.SemaphoreType.DMA((8,))],
         name="pack",
     )(at, q, g, k, v)
 
 
-def columns_kernel(at_ref, in_ref, *out_refs):
-    for o in range(4):
-        target = (at_ref[1] + o) % 4
-        for n in range(4):
-            src = pl.ds(pl.multiple_of(n * 4 * HEAD + target * HEAD, 128), HEAD)
-            out_refs[o][:, n * HEAD : (n + 1) * HEAD] = in_ref[:, src]
-
-
-def run_columns(at, layer_input):
+def columns_kernel(at_ref, mine_ref, far_ref, out_0, out_1, out_2, out_3, sem):
+    copies = []
+    for ref, half in ((mine_ref, at_ref[2]), (far_ref, 1 - at_ref[2])):
+        for o, out in enumerate((out_0, out_1, out_2, out_3)):
+            target = (at_ref[1] + o) % 4
+            for n in range(4):
+                src = pl.ds(pl.multiple_of(n * 4 * HEAD + target * HEAD, 128), HEAD)
+                dst = pl.ds(pl.multiple_of(half * 4 * HEAD + n * HEAD, 128), HEAD)
+                copies.append(pltpu.make_async_copy(ref.at[:, src], out.at[:, dst], sem.at[len(copies)]))
+                copies[-1].start()
+    for copy in copies:
+        copy.wait()
+
+
+def run_columns(at, mine, far):
+    anywhere = pl.BlockSpec(memory_space=pl.ANY)
     return pl.pallas_call(
         columns_kernel,
-        out_shape=[jax.ShapeDtypeStruct((TOK, 4 * HEAD), BF)] * 4,
-        in_specs=[pl.BlockSpec(memory_space=pltpu.SMEM), pl.BlockSpec(memory_space=pltpu.VMEM)],
+        out_shape=[jax.ShapeDtypeStruct((TOK, 8 * HEAD), BF)] * 4,
+        in_specs=[pl.BlockSpec(memory_space=pltpu.SMEM), anywhere, anywhere],
+        out_specs=[anywhere] * 4,
+        scratch_shapes=[pltpu.SemaphoreType.DMA((32,))],
         name="columns",
-    )(at, layer_input)
+    )(at, mine, far)
 
 
 def finish_kernel(in_ref, k_ref, v_ref):
@@ -304,15 +383,13 @@
 
     half = key_matrix.shape[0] // 2
     cuts = [lax.dynamic_slice_in_dim(after(m, kv_both), (1 - t) * half, half, 0) for m in (key_matrix, value_matrix)]
-    x_pieces = run_columns(at, after(layer_input, kv_both))
-    x_half = jnp.stack([x_pieces[0]] + [moved(x_pieces[4 - o], "x", -o) for o in (1, 2, 3)])
-    x_other = moved(x_half, "tp", 1)
-    x_here = jnp.where(t == 0, jnp.concatenate([x_half, x_other], 2), jnp.concatenate([x_other, x_half], 2))
+    x_far = moved(layer_input, "tp", 1)
     m_far = moved(jnp.where(c == 0, *cuts), "tp", 1)
-    kpos = after(kpos, *x_pieces)
 
     sts = run_stats(kvs, qgs, kpos, qpos)
     sts = [sts[0]] + [moved(sts[o], "y", -o) for o in (1, 2, 3)]
+    x_pieces = run_columns(at, layer_input, after(x_far, sts[0]))
+    x_here = jnp.stack([x_pieces[0]] + [moved(x_pieces[4 - o], "x", -o) for o in (1, 2, 3)])
     dkv_near, dkv_sent, dqs = run_grads(kvs, qgs, kpos, qpos, sts)
 
     def total_of(own, arrived):

time: 146 us -> 221 us (1.51)
  Pallas kernels: 34.5 us -> 86.4 us
  waiting for transfers between devices: 44 us -> 65.2 us
  local copies, waits for them, and re-layouts: 4.04 us -> 6.33 us
    pallas_call x2, Pallas kernels: 19.9 us -> 52.5 us  [the longest x1 33.8 us: run_columns(): pl.pallas_call(columns_kernel, out_shape=[jax.ShapeDtypeStruct((TOK, 8 *...]
    ppermute x33, waiting for transfers between devices: 34.5 us -> 55.7 us  [moved(): return lax.ppermute(array, axis, [(i, (i + by) % n) for i in range(n)])]
    pallas_call x1, Pallas kernels: 2.08 us -> 21.7 us  [run_pack(): pl.pallas_call(pack_kernel, out_shape=[jax.ShapeDtypeStruct(a, BF) for a...]
    unnamed x24 -> x40, local copies, waits for them, and re-layouts: 0.61 us -> 2.9 us
    all_to_all x1, starting transfers between devices: 6.18 us -> 8.41 us  [step(): got = lax.all_to_all(pieces, ('y', 'z', 'c'), 0, 0, tiled=True)]
  transfers between devices with their start and end apart: 34 -> 34, of which waited for: 12 -> 11; matrix products, arithmetic and copies ran while one was open for 10% -> 6% of each run, Pallas kernels for 21% -> 29%
where the time goes in v3:
time: 221 us; the launch traced here: 220 us
  Pallas kernels  86.4 us (39%)
  waiting for transfers between devices  65.2 us (30%)
  starting transfers between devices  51.2 us (23%)
  local copies, waits for them, and re-layouts  6.33 us (3%)
  matrix products  5.39 us (2%)
  other arithmetic  4.5 us (2%)
    ppermute x33, waiting for transfers between devices, moved(): return lax.ppermute(array, axis, [(i, (i + by) % n) for i in range(n)])  55.7 us
    ppermute x33, starting transfers between devices, moved(): return lax.ppermute(array, axis, [(i, (i + by) % n) for i in range(n)])  42.8 us
    pallas_call x1, Pallas kernels, run_columns(): pl.pallas_call(columns_kernel, out_shape=[jax.ShapeDtypeStruct((TOK, 8 *...  33.8 us
    pallas_call x1, Pallas kernels, run_pack(): pl.pallas_call(pack_kernel, out_shape=[jax.ShapeDtypeStruct(a, BF) for a...  21.7 us
    pallas_call x1, Pallas kernels, run_grads(): pl.pallas_call(grads_kernel, out_shape=dkv + dq, in_specs=in_places(6), o...  18.7 us
    pallas_call x1, Pallas kernels, run_stats(): pl.pallas_call(stats_kernel, out_shape=[jax.ShapeDtypeStruct((PARTS * 4,...  10.5 us
    all_to_all x1, waiting for transfers between devices, step(): got = lax.all_to_all(pieces, ('y', 'z', 'c'), 0, 0, tiled=True)  9.5 us
    all_to_all x1, starting transfers between devices, step(): got = lax.all_to_all(pieces, ('y', 'z', 'c'), 0, 0, tiled=True)  8.41 us
  transfers between devices with their start and end apart: 34, of which 11 were waited for; matrix products, arithmetic and copies ran while one was open for 6% of the time, Pallas kernels for 29%

profile of v3, /device:TPU:1, one launch (start us, length us, event | category | flops | bytes accessed | tf_op | source)
XLA Modules:
  0.0 220.1 jit_solution(10990489650034963784)
XLA Ops:
  0.7 0.6 pad_add_fusion.at_ref
  1.3 21.7 %pack.1 = (bf16[2,128,256]{2,1,0:T(8,128)(2,1)}, bf16[2,128,1024]{2,1,0:T(8,128)(2,1)}, bf16[128,256]{1,0:T(8,128)(2,1)}, bf16[128,1024]{1,0:T(8,128)(2,1)}) custom-call(s32[3]{0:T(128)} %pad_add_fusion.at_ref, bf16[128,1024]{1,0:T(8,128)(2,1)} %q_ref.1, bf16[128,1024]{1,0:T(8,128)(2,1)} %g_ref.1, bf16[128,256]{1,0:T(8,128)(2,1)} %k_ref.1, ...), custom_call_target="tpu_custom_call" | custom-call | tf_op jit(solution)/shard_map/pack/pallas_call | solution.py:295
  23.0 1.5 collective-permute-start
  25.6 0.6 bitcast_dynamic-update-slice_fusion.1
  26.2 3.7 %collective-permute-start.1 = (bf16[2,128,256]{2,1,0:T(8,128)(2,1)}, bf16[2,128,256]{2,1,0:T(8,128)(2,1)S(1)}, u32[]{:S(2)}, u32[]{:S(2)}) collective-permute-start(bf16[2,128,256]{2,1,0:T(8,128)(2,1)} %bitcast_dynamic-update-slice_fusion.1), channel_id=1, source_target_pairs={{0,16},{16,0},{1,17},{17,1},{2,18},{18,2},{3,19},{19,3},{4,20},{20... | collective-permute-start | bytes 393224 | tf_op jit(solution)/shard_map/ppermute | solution.py:35
  30.2 3.5 %collective-permute-done.1 = bf16[2,128,256]{2,1,0:T(8,128)(2,1)S(1)} collective-permute-done((bf16[2,128,256]{2,1,0:T(8,128)(2,1)}, bf16[2,128,256]{2,1,0:T(8,128)(2,1)S(1)}, u32[]{:S(2)}, u32[]{:S(2)}) %collective-permute-start.1) | collective-permute-done | bytes 131104 | tf_op jit(solution)/shard_map/ppermute | solution.py:35
  33.6 0.9 pad_maximum_fusion.2.refs_0_
  34.6 2.5 %collective-permute-start.2 = (bf16[2,2,128,256]{3,2,1,0:T(8,128)(2,1)S(1)}, bf16[2,2,128,256]{3,2,1,0:T(8,128)(2,1)S(1)}, u32[]{:S(2)}, u32[]{:S(2)}) collective-permute-start(bf16[2,2,128,256]{3,2,1,0:T(8,128)(2,1)S(1)} %pad_maximum_fusion.2.refs_0_), channel_id=1, source_target_pairs={{0,12},{4,0},{8,4},{12,8},{1,13},{5,1},{9,5},{13,9},{2,14},{6,2},{... | collective-permute-start | bytes 786440 | tf_op jit(solution)/shard_map/ppermute | solution.py:35
  37.1 0.7 bitcast_dynamic-update-slice_fusion.refs_4_
  37.8 2.7 %collective-permute-start.6 = (bf16[2,128,1024]{2,1,0:T(8,128)(2,1)}, bf16[2,128,1024]{2,1,0:T(8,128)(2,1)S(1)}, u32[]{:S(2)}, u32[]{:S(2)}) collective-permute-start(bf16[2,128,1024]{2,1,0:T(8,128)(2,1)} %bitcast_dynamic-update-slice_fusion.refs_4_), channel_id=1, source_target_pairs={{0,96},{32,0},{64,32},{96,64},{1,97},{33,1},{65,33},{97,65},{2,98}... | collective-permute-start | bytes 1572872 | tf_op jit(solution)/shard_map/ppermute | solution.py:35
  40.9 0.7 collective-permute-start.8
  42.9 1.1 convolution_add_fusion.2
  44.8 0.6 broadcast_in_dim.61.refs_9_
  45.4 3.8 %collective-permute-done.3.refs_2_ = bf16[2,2,128,256]{3,2,1,0:T(8,128)(2,1)} collective-permute-done((bf16[2,2,128,256]{3,2,1,0:T(8,128)(2,1)S(1)}, bf16[2,2,128,256]{3,2,1,0:T(8,128)(2,1)}, u32[]{:S(2)}, u32[]{:S(2)}) %collective-permute-start.3) | collective-permute-done | bytes 262176 | tf_op jit(solution)/shard_map/ppermute | solution.py:35
  49.7 5.0 %collective-permute-done.4.refs_3_ = bf16[2,2,128,256]{3,2,1,0:T(8,128)(2,1)} collective-permute-done((bf16[2,2,128,256]{3,2,1,0:T(8,128)(2,1)S(1)}, bf16[2,2,128,256]{3,2,1,0:T(8,128)(2,1)}, u32[]{:S(2)}, u32[]{:S(2)}) %collective-permute-start.4) | collective-permute-done | bytes 262176 | tf_op jit(solution)/shard_map/ppermute | solution.py:35
  54.7 12.6 %collective-permute-done.8.refs_7_ = bf16[2,128,1024]{2,1,0:T(8,128)(2,1)S(1)} collective-permute-done((bf16[2,128,1024]{2,1,0:T(8,128)(2,1)}, bf16[2,128,1024]{2,1,0:T(8,128)(2,1)S(1)}, u32[]{:S(2)}, u32[]{:S(2)}) %collective-permute-start.8) | collective-permute-done | bytes 524320 | tf_op jit(solution)/shard_map/ppermute | solution.py:35
  67.4 0.8 copy-done.11
  68.2 10.5 %stats.1 = (f32[16,1024]{1,0:T(8,128)}, f32[16,1024]{1,0:T(8,128)}, f32[16,1024]{1,0:T(8,128)}, f32[16,1024]{1,0:T(8,128)}) custom-call(bf16[2,2,128,256]{3,2,1,0:T(8,128)(2,1)} %copy-done.8, bf16[2,2,128,256]{3,2,1,0:T(8,128)(2,1)} %copy-done.12, bf16[2,2,128,256]{3,2,1,0:T(8,128)(2,1)} %collective-permute-done.3.refs_2_, ...), custom_call_target="tpu_custom_call" | custom-call | flops 6000000000 | bytes 3000000 | tf_op jit(solution)/shard_map/stats/pallas_call | solution.py:229
  79.2 1.0 collective-permute-start.11
  80.2 0.8 copy-done.6
  81.0 33.8 %columns.1 = (bf16[128,1024]{1,0:T(8,128)(2,1)}, bf16[128,1024]{1,0:T(8,128)(2,1)}, bf16[128,1024]{1,0:T(8,128)(2,1)}, bf16[128,1024]{1,0:T(8,128)(2,1)}) custom-call(s32[3]{0:T(128)} %pad_add_fusion.at_ref, bf16[128,2048]{1,0:T(8,128)(2,1)} %mine_ref.1, bf16[128,2048]{1,0:T(8,128)(2,1)} %copy-done.6), custom_call_target="tpu_custom_call" | custom-call | tf_op jit(solution)/shard_map/columns/pallas_call | solution.py:321
  114.9 1.7 collective-permute-start.27
  116.7 1.2 collective-permute-start.26
  118.5 0.6 copy-done.19
  119.1 18.7 %grads.1 = (bf16[4,2,128,256]{3,2,1,0:T(8,128)(2,1)}, bf16[2,2,128,256]{3,2,1,0:T(8,128)(2,1)}, bf16[2,2,128,256]{3,2,1,0:T(8,128)(2,1)}, f32[2,128,512]{2,1,0:T...) custom-call(bf16[2,2,128,256]{3,2,1,0:T(8,128)(2,1)} %copy-done.8, ...), custom_call_target="tpu_custom_call" | custom-call | flops 12000000000 | bytes 6000000 | tf_op jit(solution)/shard_map/grads/pallas_call | solution.py:245
  137.8 2.8 %collective-permute-start.16 = (bf16[2,2,128,256]{3,2,1,0:T(8,128)(2,1)}, bf16[2,2,128,256]{3,2,1,0:T(8,128)(2,1)S(1)}, u32[]{:S(2)}, u32[]{:S(2)}) collective-permute-start(bf16[2,2,128,256]{3,2,1,0:T(8,128)(2,1)} %get-tuple-element.66), channel_id=1, source_target_pairs={{0,16},{16,0},{1,17},{17,1},{2,18},{18,2},{3,19},{19,3},{4,20},{20... | collective-permute-start | bytes 786440 | tf_op jit(solution)/shard_map/ppermute | solution.py:35
  140.6 1.5 dynamic-slice_select_fusion
  142.1 0.8 collective-permute-start.23
  142.9 2.4 %collective-permute-start.14 = (bf16[2,128,512]{2,1,0:T(8,128)(2,1)S(1)}, bf16[2,128,512]{2,1,0:T(8,128)(2,1)S(1)}, u32[]{:S(2)}, u32[]{:S(2)}) collective-permute-start(bf16[2,128,512]{2,1,0:T(8,128)(2,1)S(1)} %copy-done.15), channel_id=1, source_target_pairs={{0,96},{32,0},{64,32},{96,64},{1,97},{33,1},{65,33},{97,65},{2,98}... | collective-permute-start | bytes 786440 | tf_op jit(solution)/shard_map/ppermute | solution.py:35
  145.3 1.3 collective-permute-start.13
  146.6 0.9 collective-permute-start.17
  147.7 0.8 collective-permute-start.12
  148.6 25.2 %collective-permute-done.17 = bf16[2,2,128,256]{3,2,1,0:T(8,128)(2,1)S(1)} collective-permute-done((bf16[2,2,128,256]{3,2,1,0:T(8,128)(2,1)S(1)}, bf16[2,2,128,256]{3,2,1,0:T(8,128)(2,1)S(1)}, u32[]{:S(2)}, u32[]{:S(2)}) %collective-permute-start.17) | collective-permute-done | bytes 262176 | tf_op jit(solution)/shard_map/ppermute | solution.py:35
  173.8 2.6 %collective-permute-start.29 = (bf16[4,128,1024]{2,1,0:T(8,128)(2,1)S(1)}, bf16[4,128,1024]{2,1,0:T(8,128)(2,1)S(1)}, u32[]{:S(2)}, u32[]{:S(2)}) collective-permute-start(bf16[4,128,1024]{2,1,0:T(8,128)(2,1)S(1)} %get-tuple-element.79), channel_id=1, source_target_pairs={{0,2},{2,0},{1,3},{3,1},{4,6},{6,4},{5,7},{7,5},{8,10},{10,8},{9,1... | collective-permute-start | bytes 3145736 | tf_op jit(solution)/shard_map/ppermute | solution.py:35
  176.9 2.3 %collective-permute-start.20 = (bf16[2,128,256]{2,1,0:T(8,128)(2,1)S(1)}, bf16[2,128,256]{2,1,0:T(8,128)(2,1)S(1)}, u32[]{:S(2)}, u32[]{:S(2)}) collective-permute-start(bf16[2,128,256]{2,1,0:T(8,128)(2,1)S(1)} %fusion.31), channel_id=1, source_target_pairs={{0,12},{4,0},{8,4},{12,8},{1,13},{5,1},{9,5},{13,9},{2,14},{6,2},{... | collective-permute-start | bytes 393224 | tf_op jit(solution)/shard_map/ppermute | solution.py:35
  179.3 0.9 collective-permute-start.18
  180.3 2.1 collective-permute-done.20
  182.4 3.4 %collective-permute-start.15 = (bf16[128,512]{1,0:T(8,128)(2,1)S(1)}, bf16[128,512]{1,0:T(8,128)(2,1)S(1)}, u32[]{:S(2)}, u32[]{:S(2)}) collective-permute-start(bf16[128,512]{1,0:T(8,128)(2,1)S(1)} %get-tuple-element.83), channel_id=1, source_target_pairs={{0,2},{2,0},{1,3},{3,1},{4,6},{6,4},{5,7},{7,5},{8,10},{10,8},{9,1... | collective-permute-start | bytes 393224 | tf_op jit(solution)/shard_map/ppermute | solution.py:35
  186.4 4.1 %collective-permute-start.31 = (bf16[2,128,256]{2,1,0:T(8,128)(2,1)S(1)}, bf16[2,128,256]{2,1,0:T(8,128)(2,1)S(1)}, u32[]{:S(2)}, u32[]{:S(2)}) collective-permute-start(bf16[2,128,256]{2,1,0:T(8,128)(2,1)S(1)} %fusion.27), channel_id=1, source_target_pairs={{0,8},{4,12},{8,0},{12,4},{1,9},{5,13},{9,1},{13,5},{2,10},{6,14},... | collective-permute-start | bytes 393224 | tf_op jit(solution)/shard_map/ppermute | solution.py:35
  190.6 0.6 collective-permute-start.21
  191.2 0.8 maximum_select_fusion
  193.6 0.8 collective-permute-start.22
  194.4 2.6 %collective-permute-done.31 = bf16[2,128,256]{2,1,0:T(8,128)(2,1)S(1)} collective-permute-done((bf16[2,128,256]{2,1,0:T(8,128)(2,1)S(1)}, bf16[2,128,256]{2,1,0:T(8,128)(2,1)S(1)}, u32[]{:S(2)}, u32[]{:S(2)}) %collective-permute-start.31) | collective-permute-done | bytes 131104 | tf_op jit(solution)/shard_map/ppermute | solution.py:35
  197.0 1.6 fusion.7
  198.6 8.4 %all-to-all-start = ((bf16[16,64,256]{2,1,0:T(8,128)(2,1)}), bf16[16,64,256]{2,1,0:T(8,128)(2,1)}, u32[]{:S(2)}, u32[]{:S(2)}) async-start(bf16[16,64,256]{2,1,0:T(8,128)(2,1)} %bitcast.53), calls=%async_computation | async-start | bytes 1048576 | tf_op jit(solution)/shard_map/all_to_all | solution.py:430
  207.5 1.3 fusion.1
  208.8 9.5 %all-to-all-done.in_ref = bf16[16,64,256]{2,1,0:T(8,128)(2,1)} async-done(((bf16[16,64,256]{2,1,0:T(8,128)(2,1)}), bf16[16,64,256]{2,1,0:T(8,128)(2,1)}, u32[]{:S(2)}, u32[]{:S(2)}) %all-to-all-start) | async-done | bytes 524320 | tf_op jit(solution)/shard_map/all_to_all | solution.py:430
  218.3 1.7 finish.1
  (114 shorter events, 9.0 us)
Async XLA Ops:
  0.6 48.6 %copy-start.5 = (bf16[128,2048]{1,0:T(8,128)(2,1)S(1)}, bf16[128,2048]{1,0:T(8,128)(2,1)}, u32[]{:S(2)}) copy-start(bf16[128,2048]{1,0:T(8,128)(2,1)} %mine_ref.1) | copy-start | bytes 1572868
  23.0 2.6 %collective-permute-start = (bf16[128,256]{1,0:T(8,128)(2,1)}, bf16[128,256]{1,0:T(8,128)(2,1)S(1)}, u32[]{:S(2)}, u32[]{:S(2)}) collective-permute-start(bf16[128,256]{1,0:T(8,128)(2,1)} %get-tuple-element.54), channel_id=1, source_target_pairs={{0,2},{2,0},{1,3},{3,1},{4,6},{6,4},{5,7},{7,5},{8,10},{10,8},{9,1... | collective-permute-start | bytes 196616 | tf_op jit(solution)/shard_map/ppermute | solution.py:35
  24.5 12.7 %collective-permute-start.5 = (bf16[128,1024]{1,0:T(8,128)(2,1)}, bf16[128,1024]{1,0:T(8,128)(2,1)S(1)}, u32[]{:S(2)}, u32[]{:S(2)}) collective-permute-start(bf16[128,1024]{1,0:T(8,128)(2,1)} %get-tuple-element.56), channel_id=1, source_target_pairs={{0,2},{2,0},{1,3},{3,1},{4,6},{6,4},{5,7},{7,5},{8,10},{10,8},{9,1... | collective-permute-start | bytes 786440 | tf_op jit(solution)/shard_map/ppermute | solution.py:35
  26.2 7.4 %collective-permute-start.1 = (bf16[2,128,256]{2,1,0:T(8,128)(2,1)}, bf16[2,128,256]{2,1,0:T(8,128)(2,1)S(1)}, u32[]{:S(2)}, u32[]{:S(2)}) collective-permute-start(bf16[2,128,256]{2,1,0:T(8,128)(2,1)} %bitcast_dynamic-update-slice_fusion.1), channel_id=1, source_target_pairs={{0,16},{16,0},{1,17},{17,1},{2,18},{18,2},{3,19},{19,3},{4,20},{20... | collective-permute-start | bytes 393224 | tf_op jit(solution)/shard_map/ppermute | solution.py:35
  34.6 32.8 %copy-start.8 = (bf16[2,2,128,256]{3,2,1,0:T(8,128)(2,1)}, bf16[2,2,128,256]{3,2,1,0:T(8,128)(2,1)S(1)}, u32[]{:S(2)}) copy-start(bf16[2,2,128,256]{3,2,1,0:T(8,128)(2,1)S(1)} %pad_maximum_fusion.2.refs_0_) | copy-start | bytes 786436
  34.6 7.7 %collective-permute-start.2 = (bf16[2,2,128,256]{3,2,1,0:T(8,128)(2,1)S(1)}, bf16[2,2,128,256]{3,2,1,0:T(8,128)(2,1)S(1)}, u32[]{:S(2)}, u32[]{:S(2)}) collective-permute-start(bf16[2,2,128,256]{3,2,1,0:T(8,128)(2,1)S(1)} %pad_maximum_fusion.2.refs_0_), channel_id=1, source_target_pairs={{0,12},{4,0},{8,4},{12,8},{1,13},{5,1},{9,5},{13,9},{2,14},{6,2},{... | collective-permute-start | bytes 786440 | tf_op jit(solution)/shard_map/ppermute | solution.py:35
  37.8 16.9 %collective-permute-start.6 = (bf16[2,128,1024]{2,1,0:T(8,128)(2,1)}, bf16[2,128,1024]{2,1,0:T(8,128)(2,1)S(1)}, u32[]{:S(2)}, u32[]{:S(2)}) collective-permute-start(bf16[2,128,1024]{2,1,0:T(8,128)(2,1)} %bitcast_dynamic-update-slice_fusion.refs_4_), channel_id=1, source_target_pairs={{0,96},{32,0},{64,32},{96,64},{1,97},{33,1},{65,33},{97,65},{2,98}... | collective-permute-start | bytes 1572872 | tf_op jit(solution)/shard_map/ppermute | solution.py:35
  40.6 14.1 %collective-permute-start.7 = (bf16[2,128,1024]{2,1,0:T(8,128)(2,1)}, bf16[2,128,1024]{2,1,0:T(8,128)(2,1)S(1)}, u32[]{:S(2)}, u32[]{:S(2)}) collective-permute-start(bf16[2,128,1024]{2,1,0:T(8,128)(2,1)} %bitcast_dynamic-update-slice_fusion.refs_4_), channel_id=1, source_target_pairs={{0,64},{32,96},{64,0},{96,32},{1,65},{33,97},{65,1},{97,33},{2,66}... | collective-permute-start | bytes 1572872 | tf_op jit(solution)/shard_map/ppermute | solution.py:35
  40.9 26.4 %collective-permute-start.8 = (bf16[2,128,1024]{2,1,0:T(8,128)(2,1)}, bf16[2,128,1024]{2,1,0:T(8,128)(2,1)S(1)}, u32[]{:S(2)}, u32[]{:S(2)}) collective-permute-start(bf16[2,128,1024]{2,1,0:T(8,128)(2,1)} %bitcast_dynamic-update-slice_fusion.refs_4_), channel_id=1, source_target_pairs={{0,32},{32,64},{64,96},{96,0},{1,33},{33,65},{65,97},{97,1},{2,34}... | collective-permute-start | bytes 1572872 | tf_op jit(solution)/shard_map/ppermute | solution.py:35
  41.6 7.6 %collective-permute-start.3 = (bf16[2,2,128,256]{3,2,1,0:T(8,128)(2,1)S(1)}, bf16[2,2,128,256]{3,2,1,0:T(8,128)(2,1)}, u32[]{:S(2)}, u32[]{:S(2)}) collective-permute-start(bf16[2,2,128,256]{3,2,1,0:T(8,128)(2,1)S(1)} %pad_maximum_fusion.2.refs_0_), channel_id=1, source_target_pairs={{0,8},{4,12},{8,0},{12,4},{1,9},{5,13},{9,1},{13,5},{2,10},{6,14},... | collective-permute-start | bytes 786440 | tf_op jit(solution)/shard_map/ppermute | solution.py:35
  42.2 25.1 %copy-start.12 = (bf16[2,2,128,256]{3,2,1,0:T(8,128)(2,1)}, bf16[2,2,128,256]{3,2,1,0:T(8,128)(2,1)S(1)}, u32[]{:S(2)}) copy-start(bf16[2,2,128,256]{3,2,1,0:T(8,128)(2,1)S(1)} %collective-permute-done.2.refs_1_) | copy-start | bytes 786436
  42.2 12.5 %collective-permute-start.4 = (bf16[2,2,128,256]{3,2,1,0:T(8,128)(2,1)S(1)}, bf16[2,2,128,256]{3,2,1,0:T(8,128)(2,1)}, u32[]{:S(2)}, u32[]{:S(2)}) collective-permute-start(bf16[2,2,128,256]{3,2,1,0:T(8,128)(2,1)S(1)} %pad_maximum_fusion.2.refs_0_), channel_id=1, source_target_pairs={{0,4},{4,8},{8,12},{12,0},{1,5},{5,9},{9,13},{13,1},{2,6},{6,10},{... | collective-permute-start | bytes 786440 | tf_op jit(solution)/shard_map/ppermute | solution.py:35
  49.2 31.0 %collective-permute-start.25 = (bf16[128,2048]{1,0:T(8,128)(2,1)S(1)}, bf16[128,2048]{1,0:T(8,128)(2,1)S(1)}, u32[]{:S(2)}, u32[]{:S(2)}) collective-permute-start(bf16[128,2048]{1,0:T(8,128)(2,1)S(1)} %copy-done.5), channel_id=1, source_target_pairs={{0,1},{1,0},{2,3},{3,2},{4,5},{5,4},{6,7},{7,6},{8,9},{9,8},{10,11... | collective-permute-start | bytes 1572872 | tf_op jit(solution)/shard_map/ppermute | solution.py:35
  54.7 12.7 %copy-start.9 = (bf16[2,128,1024]{2,1,0:T(8,128)(2,1)}, bf16[2,128,1024]{2,1,0:T(8,128)(2,1)S(1)}, u32[]{:S(2)}) copy-start(bf16[2,128,1024]{2,1,0:T(8,128)(2,1)S(1)} %collective-permute-done.6.refs_5_) | copy-start | bytes 1572868
  54.7 12.7 %copy-start.10 = (bf16[2,128,1024]{2,1,0:T(8,128)(2,1)}, bf16[2,128,1024]{2,1,0:T(8,128)(2,1)S(1)}, u32[]{:S(2)}) copy-start(bf16[2,128,1024]{2,1,0:T(8,128)(2,1)S(1)} %collective-permute-done.7.refs_6_) | copy-start | bytes 1572868
  78.7 38.0 %collective-permute-start.9 = (f32[16,1024]{1,0:T(8,128)}, f32[16,1024]{1,0:T(8,128)S(1)}, u32[]{:S(2)}, u32[]{:S(2)}) collective-permute-start(f32[16,1024]{1,0:T(8,128)} %get-tuple-element.58), channel_id=1, source_target_pairs={{0,96},{32,0},{64,32},{96,64},{1,97},{33,1},{65,33},{97,65},{2,98}... | collective-permute-start | bytes 196616 | tf_op jit(solution)/shard_map/ppermute | solution.py:35
  78.8 39.1 %collective-permute-start.10 = (f32[16,1024]{1,0:T(8,128)}, f32[16,1024]{1,0:T(8,128)S(1)}, u32[]{:S(2)}, u32[]{:S(2)}) collective-permute-start(f32[16,1024]{1,0:T(8,128)} %get-tuple-element.59), channel_id=1, source_target_pairs={{0,64},{32,96},{64,0},{96,32},{1,65},{33,97},{65,1},{97,33},{2,66}... | collective-permute-start | bytes 196616 | tf_op jit(solution)/shard_map/ppermute | solution.py:35
  79.2 38.7 %collective-permute-start.11 = (f32[16,1024]{1,0:T(8,128)}, f32[16,1024]{1,0:T(8,128)S(1)}, u32[]{:S(2)}, u32[]{:S(2)}) collective-permute-start(f32[16,1024]{1,0:T(8,128)} %get-tuple-element.60), channel_id=1, source_target_pairs={{0,32},{32,64},{64,96},{96,0},{1,33},{33,65},{65,97},{97,1},{2,34}... | collective-permute-start | bytes 196616 | tf_op jit(solution)/shard_map/ppermute | solution.py:35
  114.8 28.1 %collective-permute-start.28 = (bf16[128,1024]{1,0:T(8,128)(2,1)}, bf16[128,1024]{1,0:T(8,128)(2,1)S(1)}, u32[]{:S(2)}, u32[]{:S(2)}) collective-permute-start(bf16[128,1024]{1,0:T(8,128)(2,1)} %get-tuple-element.75), channel_id=1, source_target_pairs={{0,4},{4,8},{8,12},{12,0},{1,5},{5,9},{9,13},{13,1},{2,6},{6,10},{... | collective-permute-start | bytes 786440 | tf_op jit(solution)/shard_map/ppermute | solution.py:35
  114.9 30.4 %collective-permute-start.27 = (bf16[128,1024]{1,0:T(8,128)(2,1)}, bf16[128,1024]{1,0:T(8,128)(2,1)S(1)}, u32[]{:S(2)}, u32[]{:S(2)}) collective-permute-start(bf16[128,1024]{1,0:T(8,128)(2,1)} %get-tuple-element.74), channel_id=1, source_target_pairs={{0,8},{4,12},{8,0},{12,4},{1,9},{5,13},{9,1},{13,5},{2,10},{6,14},... | collective-permute-start | bytes 786440 | tf_op jit(solution)/shard_map/ppermute | solution.py:35
  116.6 24.0 %copy-start = (bf16[4096,256]{1,0:T(8,128)(2,1)S(1)}, bf16[4096,256]{1,0:T(8,128)(2,1)}, u32[]{:S(2)}) copy-start(bf16[4096,256]{1,0:T(8,128)(2,1)} %param.18) | copy-start | bytes 6291460
  116.7 29.9 %collective-permute-start.26 = (bf16[128,1024]{1,0:T(8,128)(2,1)}, bf16[128,1024]{1,0:T(8,128)(2,1)S(1)}, u32[]{:S(2)}, u32[]{:S(2)}) collective-permute-start(bf16[128,1024]{1,0:T(8,128)(2,1)} %get-tuple-element.73), channel_id=1, source_target_pairs={{0,12},{4,0},{8,4},{12,8},{1,13},{5,1},{9,5},{13,9},{2,14},{6,2},{... | collective-permute-start | bytes 786440 | tf_op jit(solution)/shard_map/ppermute | solution.py:35
  137.8 7.5 %copy-start.14 = (bf16[2,128,512]{2,1,0:T(8,128)(2,1)S(1)}, bf16[2,128,512]{2,1,0:T(8,128)(2,1)}, u32[]{:S(2)}) copy-start(bf16[2,128,512]{2,1,0:T(8,128)(2,1)} %get-tuple-element.63) | copy-start | bytes 786436
  137.8 8.8 %copy-start.16 = (bf16[2,2,128,256]{3,2,1,0:T(8,128)(2,1)S(1)}, bf16[2,2,128,256]{3,2,1,0:T(8,128)(2,1)}, u32[]{:S(2)}) copy-start(bf16[2,2,128,256]{3,2,1,0:T(8,128)(2,1)} %get-tuple-element.68) | copy-start | bytes 786436
  137.8 9.7 %copy-start.7 = (bf16[128,1024]{1,0:T(8,128)(2,1)S(1)}, bf16[128,1024]{1,0:T(8,128)(2,1)}, u32[]{:S(2)}) copy-start(bf16[128,1024]{1,0:T(8,128)(2,1)} %get-tuple-element.72) | copy-start | bytes 786436
  137.8 9.8 %collective-permute-start.16 = (bf16[2,2,128,256]{3,2,1,0:T(8,128)(2,1)}, bf16[2,2,128,256]{3,2,1,0:T(8,128)(2,1)S(1)}, u32[]{:S(2)}, u32[]{:S(2)}) collective-permute-start(bf16[2,2,128,256]{3,2,1,0:T(8,128)(2,1)} %get-tuple-element.66), channel_id=1, source_target_pairs={{0,16},{16,0},{1,17},{17,1},{2,18},{18,2},{3,19},{19,3},{4,20},{20... | collective-permute-start | bytes 786440 | tf_op jit(solution)/shard_map/ppermute | solution.py:35
  142.1 5.6 %copy-start.13 = (bf16[2,128,512]{2,1,0:T(8,128)(2,1)S(1)}, bf16[2,128,512]{2,1,0:T(8,128)(2,1)}, u32[]{:S(2)}) copy-start(bf16[2,128,512]{2,1,0:T(8,128)(2,1)} %get-tuple-element.62) | copy-start | bytes 786436
  142.1 6.4 %copy-start.4 = (bf16[4,2,128,256]{3,2,1,0:T(8,128)(2,1)S(1)}, bf16[4,2,128,256]{3,2,1,0:T(8,128)(2,1)}, u32[]{:S(2)}) copy-start(bf16[4,2,128,256]{3,2,1,0:T(8,128)(2,1)} %get-tuple-element.67) | copy-start | bytes 1572868
  142.1 49.9 %collective-permute-start.23 = (bf16[2048,256]{1,0:T(8,128)(2,1)S(1)}, bf16[2048,256]{1,0:T(8,128)(2,1)S(1)}, u32[]{:S(2)}, u32[]{:S(2)}) collective-permute-start(bf16[2048,256]{1,0:T(8,128)(2,1)S(1)} %dynamic-slice_select_fusion), channel_id=1, source_target_pairs={{0,1},{1,0},{2,3},{3,2},{4,5},{5,4},{6,7},{7,6},{8,9},{9,8},{10,11... | collective-permute-start | bytes 3145736 | tf_op jit(solution)/shard_map/ppermute | solution.py:35
  142.9 33.6 %collective-permute-start.14 = (bf16[2,128,512]{2,1,0:T(8,128)(2,1)S(1)}, bf16[2,128,512]{2,1,0:T(8,128)(2,1)S(1)}, u32[]{:S(2)}, u32[]{:S(2)}) collective-permute-start(bf16[2,128,512]{2,1,0:T(8,128)(2,1)S(1)} %copy-done.15), channel_id=1, source_target_pairs={{0,96},{32,0},{64,32},{96,64},{1,97},{33,1},{65,33},{97,65},{2,98}... | collective-permute-start | bytes 786440 | tf_op jit(solution)/shard_map/ppermute | solution.py:35
  145.3 31.6 %collective-permute-start.13 = (bf16[2,128,512]{2,1,0:T(8,128)(2,1)S(1)}, bf16[2,128,512]{2,1,0:T(8,128)(2,1)S(1)}, u32[]{:S(2)}, u32[]{:S(2)}) collective-permute-start(bf16[2,128,512]{2,1,0:T(8,128)(2,1)S(1)} %copy-done.14), channel_id=1, source_target_pairs={{0,64},{32,96},{64,0},{96,32},{1,65},{33,97},{65,1},{97,33},{2,66}... | collective-permute-start | bytes 786440 | tf_op jit(solution)/shard_map/ppermute | solution.py:35
  146.6 27.2 %collective-permute-start.17 = (bf16[2,2,128,256]{3,2,1,0:T(8,128)(2,1)S(1)}, bf16[2,2,128,256]{3,2,1,0:T(8,128)(2,1)S(1)}, u32[]{:S(2)}, u32[]{:S(2)}) collective-permute-start(bf16[2,2,128,256]{3,2,1,0:T(8,128)(2,1)S(1)} %copy-done.16), channel_id=1, source_target_pairs={{0,16},{16,0},{1,17},{17,1},{2,18},{18,2},{3,19},{19,3},{4,20},{20... | collective-permute-start | bytes 786440 | tf_op jit(solution)/shard_map/ppermute | solution.py:35
  147.5 32.7 %copy-start.3 = (f32[2,128,512]{2,1,0:T(8,128)S(1)}, f32[2,128,512]{2,1,0:T(8,128)}, u32[]{:S(2)}) copy-start(f32[2,128,512]{2,1,0:T(8,128)} %get-tuple-element.61) | copy-start | bytes 1572868
  147.7 31.6 %collective-permute-start.12 = (bf16[2,128,512]{2,1,0:T(8,128)(2,1)S(1)}, bf16[2,128,512]{2,1,0:T(8,128)(2,1)S(1)}, u32[]{:S(2)}, u32[]{:S(2)}) collective-permute-start(bf16[2,128,512]{2,1,0:T(8,128)(2,1)S(1)} %copy-done.13), channel_id=1, source_target_pairs={{0,32},{32,64},{64,96},{96,0},{1,33},{33,65},{65,97},{97,1},{2,34}... | collective-permute-start | bytes 786440 | tf_op jit(solution)/shard_map/ppermute | solution.py:35
  173.8 23.2 %collective-permute-start.29 = (bf16[4,128,1024]{2,1,0:T(8,128)(2,1)S(1)}, bf16[4,128,1024]{2,1,0:T(8,128)(2,1)S(1)}, u32[]{:S(2)}, u32[]{:S(2)}) collective-permute-start(bf16[4,128,1024]{2,1,0:T(8,128)(2,1)S(1)} %get-tuple-element.79), channel_id=1, source_target_pairs={{0,2},{2,0},{1,3},{3,1},{4,6},{6,4},{5,7},{7,5},{8,10},{10,8},{9,1... | collective-permute-start | bytes 3145736 | tf_op jit(solution)/shard_map/ppermute | solution.py:35
  176.5 16.0 %copy-start.1 = (bf16[4096,256]{1,0:T(8,128)(2,1)S(1)}, bf16[4096,256]{1,0:T(8,128)(2,1)}, u32[]{:S(2)}) copy-start(bf16[4096,256]{1,0:T(8,128)(2,1)} %param.18) | copy-start | bytes 6291460
  176.5 9.3 %collective-permute-start.19 = (bf16[2,128,256]{2,1,0:T(8,128)(2,1)S(1)}, bf16[2,128,256]{2,1,0:T(8,128)(2,1)S(1)}, u32[]{:S(2)}, u32[]{:S(2)}) collective-permute-start(bf16[2,128,256]{2,1,0:T(8,128)(2,1)S(1)} %get-tuple-element.81), channel_id=1, source_target_pairs={{0,4},{4,8},{8,12},{12,0},{1,5},{5,9},{9,13},{13,1},{2,6},{6,10},{... | collective-permute-start | bytes 393224 | tf_op jit(solution)/shard_map/ppermute | solution.py:35
  176.9 5.5 %collective-permute-start.20 = (bf16[2,128,256]{2,1,0:T(8,128)(2,1)S(1)}, bf16[2,128,256]{2,1,0:T(8,128)(2,1)S(1)}, u32[]{:S(2)}, u32[]{:S(2)}) collective-permute-start(bf16[2,128,256]{2,1,0:T(8,128)(2,1)S(1)} %fusion.31), channel_id=1, source_target_pairs={{0,12},{4,0},{8,4},{12,8},{1,13},{5,1},{9,5},{13,9},{2,14},{6,2},{... | collective-permute-start | bytes 393224 | tf_op jit(solution)/shard_map/ppermute | solution.py:35
  179.3 6.6 %collective-permute-start.18 = (bf16[2,128,256]{2,1,0:T(8,128)(2,1)S(1)}, bf16[2,128,256]{2,1,0:T(8,128)(2,1)S(1)}, u32[]{:S(2)}, u32[]{:S(2)}) collective-permute-start(bf16[2,128,256]{2,1,0:T(8,128)(2,1)S(1)} %get-tuple-element.80), channel_id=1, source_target_pairs={{0,8},{4,12},{8,0},{12,4},{1,9},{5,13},{9,1},{13,5},{2,10},{6,14},... | collective-permute-start | bytes 393224 | tf_op jit(solution)/shard_map/ppermute | solution.py:35
  180.3 12.7 %copy-start.2 = (bf16[4096,256]{1,0:T(8,128)(2,1)S(1)}, bf16[4096,256]{1,0:T(8,128)(2,1)}, u32[]{:S(2)}) copy-start(bf16[4096,256]{1,0:T(8,128)(2,1)} %param.17) | copy-start | bytes 6291460
  182.4 8.1 %collective-permute-start.15 = (bf16[128,512]{1,0:T(8,128)(2,1)S(1)}, bf16[128,512]{1,0:T(8,128)(2,1)S(1)}, u32[]{:S(2)}, u32[]{:S(2)}) collective-permute-start(bf16[128,512]{1,0:T(8,128)(2,1)S(1)} %get-tuple-element.83), channel_id=1, source_target_pairs={{0,2},{2,0},{1,3},{3,1},{4,6},{6,4},{5,7},{7,5},{8,10},{10,8},{9,1... | collective-permute-start | bytes 393224 | tf_op jit(solution)/shard_map/ppermute | solution.py:35
  185.9 7.6 %collective-permute-start.32 = (bf16[2,128,256]{2,1,0:T(8,128)(2,1)S(1)}, bf16[2,128,256]{2,1,0:T(8,128)(2,1)S(1)}, u32[]{:S(2)}, u32[]{:S(2)}) collective-permute-start(bf16[2,128,256]{2,1,0:T(8,128)(2,1)S(1)} %fusion.27), channel_id=1, source_target_pairs={{0,4},{4,8},{8,12},{12,0},{1,5},{5,9},{9,13},{13,1},{2,6},{6,10},{... | collective-permute-start | bytes 393224 | tf_op jit(solution)/shard_map/ppermute | solution.py:35
  186.4 10.5 %collective-permute-start.31 = (bf16[2,128,256]{2,1,0:T(8,128)(2,1)S(1)}, bf16[2,128,256]{2,1,0:T(8,128)(2,1)S(1)}, u32[]{:S(2)}, u32[]{:S(2)}) collective-permute-start(bf16[2,128,256]{2,1,0:T(8,128)(2,1)S(1)} %fusion.27), channel_id=1, source_target_pairs={{0,8},{4,12},{8,0},{12,4},{1,9},{5,13},{9,1},{13,5},{2,10},{6,14},... | collective-permute-start | bytes 393224 | tf_op jit(solution)/shard_map/ppermute | solution.py:35
  190.6 1.6 collective-permute-start.21
  192.0 5.0 %collective-permute-start.30 = (bf16[2,128,256]{2,1,0:T(8,128)(2,1)S(1)}, bf16[2,128,256]{2,1,0:T(8,128)(2,1)S(1)}, u32[]{:S(2)}, u32[]{:S(2)}) collective-permute-start(bf16[2,128,256]{2,1,0:T(8,128)(2,1)S(1)} %fusion.27), channel_id=1, source_target_pairs={{0,12},{4,0},{8,4},{12,8},{1,13},{5,1},{9,5},{13,9},{2,14},{6,2},{... | collective-permute-start | bytes 393224 | tf_op jit(solution)/shard_map/ppermute | solution.py:35
  192.1 14.9 %collective-permute-start.24 = (bf16[2048,256]{1,0:T(8,128)(2,1)S(1)}, bf16[2048,256]{1,0:T(8,128)(2,1)S(1)}, u32[]{:S(2)}, u32[]{:S(2)}) collective-permute-start(bf16[2048,256]{1,0:T(8,128)(2,1)S(1)} %collective-permute-done.23), channel_id=1, source_target_pairs={{0,2},{2,0},{1,3},{3,1},{4,6},{6,4},{5,7},{7,5},{8,10},{10,8},{9,1... | collective-permute-start | bytes 3145736 | tf_op jit(solution)/shard_map/ppermute | solution.py:35
  193.6 13.5 %collective-permute-start.22 = (bf16[128,512]{1,0:T(8,128)(2,1)S(1)}, bf16[128,512]{1,0:T(8,128)(2,1)S(1)}, u32[]{:S(2)}, u32[]{:S(2)}) collective-permute-start(bf16[128,512]{1,0:T(8,128)(2,1)S(1)} %pad_maximum_fusion.3), channel_id=1, source_target_pairs={{0,1},{1,0},{2,3},{3,2},{4,5},{5,4},{6,7},{7,6},{8,9},{9,8},{10,11... | collective-permute-start | bytes 393224 | tf_op jit(solution)/shard_map/ppermute | solution.py:35
  198.6 19.7 %all-to-all-start = ((bf16[16,64,256]{2,1,0:T(8,128)(2,1)}), bf16[16,64,256]{2,1,0:T(8,128)(2,1)}, u32[]{:S(2)}, u32[]{:S(2)}) async-start(bf16[16,64,256]{2,1,0:T(8,128)(2,1)} %bitcast.53), calls=%async_computation | async-start | bytes 1048576 | tf_op jit(solution)/shard_map/all_to_all | solution.py:430
  (6 other events, 9.2 us)

commit v4 on v3

--- a/solution.py
+++ b/solution.py
@@ -135,7 +135,7 @@
     kpos_ref, qpos_ref = refs[8:10]
     st_refs = refs[10:14]
     dkv_near, dkv_first, dkv_last, dq_refs = refs[14], refs[15], refs[16], refs[17:21]
-    kv, qg, kposb, kt, qt, gt, dks, dvs, dqt, lse, mean, dkv_out, dq_wide, dq_out, sem, out_sem = refs[21:]
+    kv, qg, kposb, kt, dks, dvs, dqt, lse, mean, dkv_out, dq_wide, dq_out, sem, out_sem = refs[21:]
     start_loads(kv_refs, qg_refs, kpos_ref, kv, qg, kposb, sem)
     for part in range(PARTS):
         st = [r[part * 4 : part * 4 + 3, :] for r in st_refs]
@@ -162,8 +162,8 @@
         return [pltpu.make_async_copy(a, b, out_sem.at[part, 4 + n]) for n, (a, b) in enumerate(pairs)]
 
     def emit_dkv(part):
-        dk = (dks[part] * SCALE).astype(BF).T.reshape(4, 2, 2, T, HEAD)
-        dv = dvs[part].astype(BF).T.reshape(4, 2, 2, T, HEAD)
+        dk = (dks[part] * SCALE).astype(BF).reshape(4, 2, 2, T, HEAD)
+        dv = dvs[part].astype(BF).reshape(4, 2, 2, T, HEAD)
         for a in range(2):
             dkv_out[part, a, :, :, :, :HEAD] = dk[:, a]
             dkv_out[part, a, :, :, :, HEAD:] = dv[:, a]
@@ -189,11 +189,11 @@
                     copy.wait()
             k, q, g = keys_of(kv, ip), heads_of(qg, i, 0), heads_of(qg, i, GROUP)
             if delta == 0:
-                kt[i], qt[i], gt[i] = k.T, q.T, g.T
+                kt[i] = k.T
             p = jnp.exp2(masked_scores(delta, i, ip, k, q, kposb, qpos_ref) - lse[i])
             ds = (p * (nt(values_of(kv, ip), g) - mean[i])).astype(BF)
             p = p.astype(BF)
-            dk, dv, dq = nt(qt[i], ds), nt(gt[i], p), nn(kt[ip], ds)
+            dk, dv, dq = nn(ds, q), nn(p, g), nn(kt[ip], ds)
             if delta == 0:
                 dks[ip], dvs[ip], dqt[i] = dk, dv, dq
             else:
@@ -250,10 +250,8 @@
         scratch_shapes=common_scratch()
         + [
             pltpu.VMEM((PARTS, HEAD, KR), BF),
-            pltpu.VMEM((PARTS, HEAD, QR), BF),
-            pltpu.VMEM((PARTS, HEAD, QR), BF),
-            pltpu.VMEM((PARTS, HEAD, KR), F32),
-            pltpu.VMEM((PARTS, HEAD, KR), F32),
+            pltpu.VMEM((PARTS, KR, HEAD), F32),
+            pltpu.VMEM((PARTS, KR, HEAD), F32),
             pltpu.VMEM((PARTS, HEAD, QR), F32),
             pltpu.VMEM((PARTS, 1, QR), F32),
             pltpu.VMEM((PARTS, 1, QR), F32),
@@ -270,62 +268,46 @@
     return out[0], out[1:3], out[3:7]
 
 
-def pack_kernel(at_ref, q_ref, g_ref, k_ref, v_ref, kv_own, qg_own, kv_send, qg_send, sem):
+def pack_kernel(at_ref, q_ref, g_ref, k_ref, v_ref, kv_own, qg_own, kv_send, qg_send):
     wide = GROUP * HEAD
     mine = at_ref[0]
-    copies = []
-    for which, kv, qg in ((1 - mine, kv_send, qg_send), (mine, kv_own.at[0], qg_own.at[0])):
+    for which, kv, qg in ((mine, kv_own.at[0], qg_own.at[0]), (1 - mine, kv_send, qg_send)):
         cols = pl.ds(pl.multiple_of(which * wide, 128), wide)
         small = pl.ds(pl.multiple_of(which * HEAD, 128), HEAD)
-        for src, dst in (
-            (k_ref.at[:, small], kv.at[:, :HEAD]),
-            (v_ref.at[:, small], kv.at[:, HEAD:]),
-            (q_ref.at[:, cols], qg.at[:, :wide]),
-            (g_ref.at[:, cols], qg.at[:, wide:]),
-        ):
-            copies.append(pltpu.make_async_copy(src, dst, sem.at[len(copies)]))
-            copies[-1].start()
-    for copy in copies:
-        copy.wait()
+        kv[:, :HEAD] = k_ref[:, small]
+        kv[:, HEAD:] = v_ref[:, small]
+        qg[:, :wide] = q_ref[:, cols]
+        qg[:, wide:] = g_ref[:, cols]
+    kv_own[1] = kv_send[...]
+    qg_own[1] = qg_send[...]
 
 
 def run_pack(at, q, g, k, v):
     kv, qg = (TOK, 2 * HEAD), (TOK, 2 * GROUP * HEAD)
-    anywhere = pl.BlockSpec(memory_space=pl.ANY)
+    vmem = pl.BlockSpec(memory_space=pltpu.VMEM)
     return pl.pallas_call(
         pack_kernel,
         out_shape=[jax.ShapeDtypeStruct(a, BF) for a in ((2, *kv), (2, *qg), kv, qg)],
-        in_specs=[pl.BlockSpec(memory_space=pltpu.SMEM)] + [anywhere] * 4,
-        out_specs=[anywhere] * 4,
-        scratch_shapes=[pltpu.SemaphoreType.DMA((8,))],
+        in_specs=[pl.BlockSpec(memory_space=pltpu.SMEM)] + [vmem] * 4,
         name="pack",
     )(at, q, g, k, v)
 
 
-def columns_kernel(at_ref, mine_ref, far_ref, out_0, out_1, out_2, out_3, sem):
-    copies = []
-    for ref, half in ((mine_ref, at_ref[2]), (far_ref, 1 - at_ref[2])):
-        for o, out in enumerate((out_0, out_1, out_2, out_3)):
-            target = (at_ref[1] + o) % 4
-            for n in range(4):
-                src = pl.ds(pl.multiple_of(n * 4 * HEAD + target * HEAD, 128), HEAD)
-                dst = pl.ds(pl.multiple_of(half * 4 * HEAD + n * HEAD, 128), HEAD)
-                copies.append(pltpu.make_async_copy(ref.at[:, src], out.at[:, dst], sem.at[len(copies)]))
-                copies[-1].start()
-    for copy in copies:
-        copy.wait()
-
-
-def run_columns(at, mine, far):
-    anywhere = pl.BlockSpec(memory_space=pl.ANY)
+def columns_kernel(at_ref, in_ref, *out_refs):
+    for o in range(4):
+        target = (at_ref[1] + o) % 4
+        for n in range(4):
+            src = pl.ds(pl.multiple_of(n * 4 * HEAD + target * HEAD, 128), HEAD)
+            out_refs[o][:, n * HEAD : (n + 1) * HEAD] = in_ref[:, src]
+
+
+def run_columns(at, layer_input):
     return pl.pallas_call(
         columns_kernel,
-        out_shape=[jax.ShapeDtypeStruct((TOK, 8 * HEAD), BF)] * 4,
-        in_specs=[pl.BlockSpec(memory_space=pltpu.SMEM), anywhere, anywhere],
-        out_specs=[anywhere] * 4,
-        scratch_shapes=[pltpu.SemaphoreType.DMA((32,))],
+        out_shape=[jax.ShapeDtypeStruct((TOK, 4 * HEAD), BF)] * 4,
+        in_specs=[pl.BlockSpec(memory_space=pltpu.SMEM), pl.BlockSpec(memory_space=pltpu.VMEM)],
         name="columns",
-    )(at, mine, far)
+    )(at, layer_input)
 
 
 def finish_kernel(in_ref, k_ref, v_ref):
@@ -382,14 +364,16 @@
     kpos, qpos = positions(run_placement, y, z, x, c)
 
     half = key_matrix.shape[0] // 2
-    cuts = [lax.dynamic_slice_in_dim(after(m, kv_both), (1 - t) * half, half, 0) for m in (key_matrix, value_matrix)]
-    x_far = moved(layer_input, "tp", 1)
+    cuts = [lax.dynamic_slice_in_dim(after(m, kv_own), (1 - t) * half, half, 0) for m in (key_matrix, value_matrix)]
+    x_pieces = run_columns(at, after(layer_input, kv_both))
+    x_half = jnp.stack([x_pieces[0]] + [moved(x_pieces[4 - o], "x", -o) for o in (1, 2, 3)])
+    x_other = moved(x_half, "tp", 1)
+    x_here = jnp.where(t == 0, jnp.concatenate([x_half, x_other], 2), jnp.concatenate([x_other, x_half], 2))
     m_far = moved(jnp.where(c == 0, *cuts), "tp", 1)
+    kpos = after(kpos, *x_pieces)
 
     sts = run_stats(kvs, qgs, kpos, qpos)
     sts = [sts[0]] + [moved(sts[o], "y", -o) for o in (1, 2, 3)]
-    x_pieces = run_columns(at, layer_input, after(x_far, sts[0]))
-    x_here = jnp.stack([x_pieces[0]] + [moved(x_pieces[4 - o], "x", -o) for o in (1, 2, 3)])
     dkv_near, dkv_sent, dqs = run_grads(kvs, qgs, kpos, qpos, sts)
 
     def total_of(own, arrived):

time: 221 us -> 143 us (0.65)
  Pallas kernels: 86.4 us -> 34.4 us
  waiting for transfers between devices: 65.2 us -> 35.7 us
  starting transfers between devices: 51.2 us -> 55.5 us
  local copies, waits for them, and re-layouts: 6.33 us -> 4.03 us
    pallas_call x1, Pallas kernels: 33.8 us -> 1.98 us  [run_columns(): pl.pallas_call(columns_kernel, out_shape=[jax.ShapeDtypeStruct((TOK, 4 *...]
    ppermute x33, waiting for transfers between devices: 55.7 us -> 26.2 us  [moved(): return lax.ppermute(array, axis, [(i, (i + by) % n) for i in range(n)])]
    pallas_call x1, Pallas kernels: 21.7 us -> 2.05 us  [run_pack(): pl.pallas_call(pack_kernel, out_shape=[jax.ShapeDtypeStruct(a, BF) for a...]
    ppermute x33, starting transfers between devices: 42.8 us -> 49.1 us  [moved(): return lax.ppermute(array, axis, [(i, (i + by) % n) for i in range(n)])]
    unnamed x40 -> x20, local copies, waits for them, and re-layouts: 2.9 us -> 0.6 us
  transfers between devices with their start and end apart: 34 -> 34, of which waited for: 11 -> 14; matrix products, arithmetic and copies ran while one was open for 6% -> 10% of each run, Pallas kernels for 29% -> 22%
where the time goes in v4:
time: 143 us; the launch traced here: 142 us
  starting transfers between devices  55.5 us (39%)
  waiting for transfers between devices  35.7 us (25%)
  Pallas kernels  34.4 us (24%)
  other arithmetic  6.02 us (4%)
  matrix products  5.39 us (4%)
  local copies, waits for them, and re-layouts  4.03 us (3%)
    ppermute x33, starting transfers between devices, moved(): return lax.ppermute(array, axis, [(i, (i + by) % n) for i in range(n)])  49.1 us
    ppermute x33, waiting for transfers between devices, moved(): return lax.ppermute(array, axis, [(i, (i + by) % n) for i in range(n)])  26.2 us
    pallas_call x1, Pallas kernels, run_grads(): pl.pallas_call(grads_kernel, out_shape=dkv + dq, in_specs=in_places(6), o...  18.1 us
    pallas_call x1, Pallas kernels, run_stats(): pl.pallas_call(stats_kernel, out_shape=[jax.ShapeDtypeStruct((PARTS * 4,...  10.5 us
    all_to_all x1, waiting for transfers between devices, step(): got = lax.all_to_all(pieces, ('y', 'z', 'c'), 0, 0, tiled=True)  9.5 us
    all_to_all x1, starting transfers between devices, step(): got = lax.all_to_all(pieces, ('y', 'z', 'c'), 0, 0, tiled=True)  6.36 us
  transfers between devices with their start and end apart: 34, of which 14 were waited for; matrix products, arithmetic and copies ran while one was open for 10% of the time, Pallas kernels for 22%

profile of v4, /device:TPU:1, one launch (start us, length us, event | category | flops | bytes accessed | tf_op | source)
XLA Modules:
  0.0 142.0 jit_solution(4396196453615199769)
XLA Ops:
  1.3 2.1 %pack.1 = (bf16[2,128,256]{2,1,0:T(8,128)(2,1)}, bf16[2,128,1024]{2,1,0:T(8,128)(2,1)}, bf16[128,256]{1,0:T(8,128)(2,1)}, bf16[128,1024]{1,0:T(8,128)(2,1)}) custom-call(s32[3]{0:T(128)} %pad_add_fusion.at_ref, bf16[128,1024]{1,0:T(8,128)(2,1)} %q_ref.1, bf16[128,1024]{1,0:T(8,128)(2,1)} %g_ref.1, bf16[128,256]{1,0:T(8,128)(2,1)} %k_ref.1, ...), custom_call_target="tpu_custom_call" | custom-call | tf_op jit(solution)/shard_map/pack/pallas_call | solution.py:288
  3.3 1.4 collective-permute-start
  6.5 3.7 %collective-permute-start.1 = (bf16[2,128,256]{2,1,0:T(8,128)(2,1)}, bf16[2,128,256]{2,1,0:T(8,128)(2,1)S(1)}, u32[]{:S(2)}, u32[]{:S(2)}) collective-permute-start(bf16[2,128,256]{2,1,0:T(8,128)(2,1)} %bitcast_dynamic-update-slice_fusion.1), channel_id=1, source_target_pairs={{0,16},{16,0},{1,17},{17,1},{2,18},{18,2},{3,19},{19,3},{4,20},{20... | collective-permute-start | bytes 393224 | tf_op jit(solution)/shard_map/ppermute | solution.py:35
  10.2 3.7 %collective-permute-done.1 = bf16[2,128,256]{2,1,0:T(8,128)(2,1)S(1)} collective-permute-done((bf16[2,128,256]{2,1,0:T(8,128)(2,1)}, bf16[2,128,256]{2,1,0:T(8,128)(2,1)S(1)}, u32[]{:S(2)}, u32[]{:S(2)}) %collective-permute-start.1) | collective-permute-done | bytes 131104 | tf_op jit(solution)/shard_map/ppermute | solution.py:35
  13.9 0.9 pad_maximum_fusion.2.refs_0_
  14.9 1.3 collective-permute-start.4
  16.9 1.3 collective-permute-start.8
  18.2 2.6 %collective-permute-start.7 = (bf16[2,128,1024]{2,1,0:T(8,128)(2,1)}, bf16[2,128,1024]{2,1,0:T(8,128)(2,1)}, u32[]{:S(2)}, u32[]{:S(2)}) collective-permute-start(bf16[2,128,1024]{2,1,0:T(8,128)(2,1)} %bitcast_dynamic-update-slice_fusion.refs_4_), channel_id=1, source_target_pairs={{0,64},{32,96},{64,0},{96,32},{1,65},{33,97},{65,1},{97,33},{2,66}... | collective-permute-start | bytes 1572872 | tf_op jit(solution)/shard_map/ppermute | solution.py:35
  20.8 1.1 collective-permute-start.6
  21.9 2.5 %collective-permute-start.3 = (bf16[2,2,128,256]{3,2,1,0:T(8,128)(2,1)S(1)}, bf16[2,2,128,256]{3,2,1,0:T(8,128)(2,1)}, u32[]{:S(2)}, u32[]{:S(2)}) collective-permute-start(bf16[2,2,128,256]{3,2,1,0:T(8,128)(2,1)S(1)} %pad_maximum_fusion.2.refs_0_), channel_id=1, source_target_pairs={{0,8},{4,12},{8,0},{12,4},{1,9},{5,13},{9,1},{13,5},{2,10},{6,14},... | collective-permute-start | bytes 786440 | tf_op jit(solution)/shard_map/ppermute | solution.py:35
  24.4 1.2 collective-permute-start.2
  25.5 1.1 convolution_add_fusion.2
  28.0 1.5 %dynamic-slice_select_fusion = bf16[2048,256]{1,0:T(8,128)(2,1)S(1)} fusion(bf16[4096,256]{1,0:T(8,128)(2,1)S(1)} %copy-done, s32[]{:T(128)S(6)} %select_n.157, bf16[4096,256]{1,0:T(8,128)(2,1)} %param.17, pred[]{:T(512)S(6)} %eq.50), kind=kLoop, calls=%fused_computation.16 | loop fusion | flops 524288 | bytes 3145733 | tf_op jit(solution)/shard_map/jit(_where)/select_n | solution.py:372
  29.5 2.0 %columns.1 = (bf16[128,512]{1,0:T(8,128)(2,1)}, bf16[128,512]{1,0:T(8,128)(2,1)}, bf16[128,512]{1,0:T(8,128)(2,1)}, bf16[128,512]{1,0:T(8,128)(2,1)}) custom-call(s32[3]{0:T(128)} %pad_add_fusion.at_ref, bf16[128,2048]{1,0:T(8,128)(2,1)} %in_ref), custom_call_target="tpu_custom_call" | custom-call | tf_op jit(solution)/shard_map/columns/pallas_call | solution.py:305
  31.5 0.8 collective-permute-start.23
  32.3 2.4 %collective-permute-done.2.refs_1_ = bf16[2,2,128,256]{3,2,1,0:T(8,128)(2,1)} collective-permute-done((bf16[2,2,128,256]{3,2,1,0:T(8,128)(2,1)S(1)}, bf16[2,2,128,256]{3,2,1,0:T(8,128)(2,1)}, u32[]{:S(2)}, u32[]{:S(2)}) %collective-permute-start.2) | collective-permute-done | bytes 262176 | tf_op jit(solution)/shard_map/ppermute | solution.py:35
  34.7 2.6 %collective-permute-start.27 = (bf16[128,512]{1,0:T(8,128)(2,1)}, bf16[128,512]{1,0:T(8,128)(2,1)S(1)}, u32[]{:S(2)}, u32[]{:S(2)}) collective-permute-start(bf16[128,512]{1,0:T(8,128)(2,1)} %get-tuple-element.60), channel_id=1, source_target_pairs={{0,4},{4,8},{8,12},{12,0},{1,5},{5,9},{9,13},{13,1},{2,6},{6,10},{... | collective-permute-start | bytes 393224 | tf_op jit(solution)/shard_map/ppermute | solution.py:35
  37.3 2.1 %collective-permute-start.26 = (bf16[128,512]{1,0:T(8,128)(2,1)}, bf16[128,512]{1,0:T(8,128)(2,1)S(1)}, u32[]{:S(2)}, u32[]{:S(2)}) collective-permute-start(bf16[128,512]{1,0:T(8,128)(2,1)} %get-tuple-element.61), channel_id=1, source_target_pairs={{0,8},{4,12},{8,0},{12,4},{1,9},{5,13},{9,1},{13,5},{2,10},{6,14},... | collective-permute-start | bytes 393224 | tf_op jit(solution)/shard_map/ppermute | solution.py:35
  39.4 3.8 %collective-permute-done.7.refs_6_ = bf16[2,128,1024]{2,1,0:T(8,128)(2,1)} collective-permute-done((bf16[2,128,1024]{2,1,0:T(8,128)(2,1)}, bf16[2,128,1024]{2,1,0:T(8,128)(2,1)}, u32[]{:S(2)}, u32[]{:S(2)}) %collective-permute-start.7) | collective-permute-done | bytes 524320 | tf_op jit(solution)/shard_map/ppermute | solution.py:35
  43.1 1.5 %collective-permute-start.25 = (bf16[128,512]{1,0:T(8,128)(2,1)}, bf16[128,512]{1,0:T(8,128)(2,1)S(1)}, u32[]{:S(2)}, u32[]{:S(2)}) collective-permute-start(bf16[128,512]{1,0:T(8,128)(2,1)} %get-tuple-element.62), channel_id=1, source_target_pairs={{0,12},{4,0},{8,4},{12,8},{1,13},{5,1},{9,5},{13,9},{2,14},{6,2},{... | collective-permute-start | bytes 393224 | tf_op jit(solution)/shard_map/ppermute | solution.py:35
  44.6 10.5 %stats.1 = (f32[16,1024]{1,0:T(8,128)}, f32[16,1024]{1,0:T(8,128)}, f32[16,1024]{1,0:T(8,128)}, f32[16,1024]{1,0:T(8,128)}) custom-call(bf16[2,2,128,256]{3,2,1,0:T(8,128)(2,1)} %copy-done.7, bf16[2,2,128,256]{3,2,1,0:T(8,128)(2,1)} %collective-permute-done.2.refs_1_, bf16[2,2,128,256]{3,2,1,0:T(8,128)(2,1)} %collective-permute-done.3.refs_2_, ...), custom_call_target="tpu_custom_call" | custom-call | flops 6000000000 | bytes 3000000 | tf_op jit(solution)/shard_map/stats/pallas_call | solution.py:229
  55.1 2.0 %collective-permute-start.9 = (f32[16,1024]{1,0:T(8,128)}, f32[16,1024]{1,0:T(8,128)}, u32[]{:S(2)}, u32[]{:S(2)}) collective-permute-start(f32[16,1024]{1,0:T(8,128)} %get-tuple-element.65), channel_id=1, source_target_pairs={{0,96},{32,0},{64,32},{96,64},{1,97},{33,1},{65,33},{97,65},{2,98}... | collective-permute-start | bytes 196616 | tf_op jit(solution)/shard_map/ppermute | solution.py:35
  59.3 2.8 %collective-permute-done.10.refs_12_ = f32[16,1024]{1,0:T(8,128)} collective-permute-done((f32[16,1024]{1,0:T(8,128)}, f32[16,1024]{1,0:T(8,128)}, u32[]{:S(2)}, u32[]{:S(2)}) %collective-permute-start.10) | collective-permute-done | bytes 65568 | tf_op jit(solution)/shard_map/ppermute | solution.py:35
  62.5 18.1 %grads.1 = (bf16[4,2,128,256]{3,2,1,0:T(8,128)(2,1)}, bf16[2,2,128,256]{3,2,1,0:T(8,128)(2,1)}, bf16[2,2,128,256]{3,2,1,0:T(8,128)(2,1)}, f32[2,128,512]{2,1,0:T...) custom-call(bf16[2,2,128,256]{3,2,1,0:T(8,128)(2,1)} %copy-done.7, ...), custom_call_target="tpu_custom_call" | custom-call | flops 12000000000 | bytes 6000000 | tf_op jit(solution)/shard_map/grads/pallas_call | solution.py:245
  80.7 2.1 %collective-permute-start.13 = (bf16[2,128,512]{2,1,0:T(8,128)(2,1)}, bf16[2,128,512]{2,1,0:T(8,128)(2,1)S(1)}, u32[]{:S(2)}, u32[]{:S(2)}) collective-permute-start(bf16[2,128,512]{2,1,0:T(8,128)(2,1)} %get-tuple-element.70), channel_id=1, source_target_pairs={{0,64},{32,96},{64,0},{96,32},{1,65},{33,97},{65,1},{97,33},{2,66}... | collective-permute-start | bytes 786440 | tf_op jit(solution)/shard_map/ppermute | solution.py:35
  82.8 2.7 %collective-permute-start.16 = (bf16[2,2,128,256]{3,2,1,0:T(8,128)(2,1)}, bf16[2,2,128,256]{3,2,1,0:T(8,128)(2,1)S(1)}, u32[]{:S(2)}, u32[]{:S(2)}) collective-permute-start(bf16[2,2,128,256]{3,2,1,0:T(8,128)(2,1)} %get-tuple-element.73), channel_id=1, source_target_pairs={{0,16},{16,0},{1,17},{17,1},{2,18},{18,2},{3,19},{19,3},{4,20},{20... | collective-permute-start | bytes 786440 | tf_op jit(solution)/shard_map/ppermute | solution.py:35
  85.8 1.3 maximum_select_fusion.1
  87.4 2.3 %collective-permute-done.16 = bf16[2,2,128,256]{3,2,1,0:T(8,128)(2,1)S(1)} collective-permute-done((bf16[2,2,128,256]{3,2,1,0:T(8,128)(2,1)}, bf16[2,2,128,256]{3,2,1,0:T(8,128)(2,1)S(1)}, u32[]{:S(2)}, u32[]{:S(2)}) %collective-permute-start.16) | collective-permute-done | bytes 262176 | tf_op jit(solution)/shard_map/ppermute | solution.py:35
  89.7 1.0 collective-permute-start.14
  90.8 3.0 %collective-permute-done.17 = bf16[2,2,128,256]{3,2,1,0:T(8,128)(2,1)S(1)} collective-permute-done((bf16[2,2,128,256]{3,2,1,0:T(8,128)(2,1)}, bf16[2,2,128,256]{3,2,1,0:T(8,128)(2,1)S(1)}, u32[]{:S(2)}, u32[]{:S(2)}) %collective-permute-start.17) | collective-permute-done | bytes 262176 | tf_op jit(solution)/shard_map/ppermute | solution.py:35
  93.8 5.1 %collective-permute-start.29 = (bf16[4,128,1024]{2,1,0:T(8,128)(2,1)S(1)}, bf16[4,128,1024]{2,1,0:T(8,128)(2,1)S(1)}, u32[]{:S(2)}, u32[]{:S(2)}) collective-permute-start(bf16[4,128,1024]{2,1,0:T(8,128)(2,1)S(1)} %maximum_select_fusion.1), channel_id=1, source_target_pairs={{0,2},{2,0},{1,3},{3,1},{4,6},{6,4},{5,7},{7,5},{8,10},{10,8},{9,1... | collective-permute-start | bytes 3145736 | tf_op jit(solution)/shard_map/ppermute | solution.py:35
  98.9 1.3 collective-permute-start.19
  100.2 1.4 %collective-permute-start.18 = (bf16[2,128,256]{2,1,0:T(8,128)(2,1)S(1)}, bf16[2,128,256]{2,1,0:T(8,128)(2,1)S(1)}, u32[]{:S(2)}, u32[]{:S(2)}) collective-permute-start(bf16[2,128,256]{2,1,0:T(8,128)(2,1)S(1)} %get-tuple-element.80), channel_id=1, source_target_pairs={{0,8},{4,12},{8,0},{12,4},{1,9},{5,13},{9,1},{13,5},{2,10},{6,14},... | collective-permute-start | bytes 393224 | tf_op jit(solution)/shard_map/ppermute | solution.py:35
  101.6 1.9 %collective-permute-start.20 = (bf16[2,128,256]{2,1,0:T(8,128)(2,1)S(1)}, bf16[2,128,256]{2,1,0:T(8,128)(2,1)S(1)}, u32[]{:S(2)}, u32[]{:S(2)}) collective-permute-start(bf16[2,128,256]{2,1,0:T(8,128)(2,1)S(1)} %fusion.31), channel_id=1, source_target_pairs={{0,12},{4,0},{8,4},{12,8},{1,13},{5,1},{9,5},{13,9},{2,14},{6,2},{... | collective-permute-start | bytes 393224 | tf_op jit(solution)/shard_map/ppermute | solution.py:35
  103.8 0.9 collective-permute-start.15
  104.7 3.3 %collective-permute-done.18 = bf16[2,128,256]{2,1,0:T(8,128)(2,1)S(1)} collective-permute-done((bf16[2,128,256]{2,1,0:T(8,128)(2,1)S(1)}, bf16[2,128,256]{2,1,0:T(8,128)(2,1)S(1)}, u32[]{:S(2)}, u32[]{:S(2)}) %collective-permute-start.18) | collective-permute-done | bytes 131104 | tf_op jit(solution)/shard_map/ppermute | solution.py:35
  108.0 0.9 collective-permute-start.24
  109.0 2.1 %collective-permute-start.31 = (bf16[2,128,256]{2,1,0:T(8,128)(2,1)S(1)}, bf16[2,128,256]{2,1,0:T(8,128)(2,1)S(1)}, u32[]{:S(2)}, u32[]{:S(2)}) collective-permute-start(bf16[2,128,256]{2,1,0:T(8,128)(2,1)S(1)} %fusion.27), channel_id=1, source_target_pairs={{0,8},{4,12},{8,0},{12,4},{1,9},{5,13},{9,1},{13,5},{2,10},{6,14},... | collective-permute-start | bytes 393224 | tf_op jit(solution)/shard_map/ppermute | solution.py:35
  111.1 1.5 %collective-permute-start.30 = (bf16[2,128,256]{2,1,0:T(8,128)(2,1)S(1)}, bf16[2,128,256]{2,1,0:T(8,128)(2,1)S(1)}, u32[]{:S(2)}, u32[]{:S(2)}) collective-permute-start(bf16[2,128,256]{2,1,0:T(8,128)(2,1)S(1)} %fusion.27), channel_id=1, source_target_pairs={{0,12},{4,0},{8,4},{12,8},{1,13},{5,1},{9,5},{13,9},{2,14},{6,2},{... | collective-permute-start | bytes 393224 | tf_op jit(solution)/shard_map/ppermute | solution.py:35
  112.6 1.6 %collective-permute-start.21 = (bf16[128,256]{1,0:T(8,128)(2,1)S(1)}, bf16[128,256]{1,0:T(8,128)(2,1)S(1)}, u32[]{:S(2)}, u32[]{:S(2)}) collective-permute-start(bf16[128,256]{1,0:T(8,128)(2,1)S(1)} %slice_bitcast_fusion.2), channel_id=1, source_target_pairs={{0,2},{2,0},{1,3},{3,1},{4,6},{6,4},{5,7},{7,5},{8,10},{10,8},{9,1... | collective-permute-start | bytes 196616 | tf_op jit(solution)/shard_map/ppermute | solution.py:35
  114.2 0.8 maximum_select_fusion.2
  116.4 0.8 collective-permute-start.22
  117.7 3.3 %collective-permute-done.32 = bf16[2,128,256]{2,1,0:T(8,128)(2,1)S(1)} collective-permute-done((bf16[2,128,256]{2,1,0:T(8,128)(2,1)S(1)}, bf16[2,128,256]{2,1,0:T(8,128)(2,1)S(1)}, u32[]{:S(2)}, u32[]{:S(2)}) %collective-permute-start.32) | collective-permute-done | bytes 131104 | tf_op jit(solution)/shard_map/ppermute | solution.py:35
  121.0 1.6 %fusion.7 = bf16[1024,256]{1,0:T(8,128)(2,1)} fusion(bf16[1,2,128,256]{3,2,1,0:T(8,128)(2,1)S(1)} %bitcast.71, bf16[1,2,128,256]{3,2,1,0:T(8,128)(2,1)S(1)} %bitcast.69, bf16[1,2,128,256]{3,2,1,0:T(8,128)(2,1)S(1)} %bitcast.70, bf16[1,2,128,256]{3,2,1,0:T(8,128)(2,1)S(1)} %bitcast.64, bf16[4,1,128,1024]{3,2,0,1:T(8,128)(2,1)S(1)} %bitcast.68, ...), kind=kOutput, calls=%fused_computation.8 | convolution fusion | flops 538968064 | bytes 3145728 | tf_op jit(solution)/shard_map/dot_general | solution.py:407
  122.6 6.4 %all-to-all-start = ((bf16[16,64,256]{2,1,0:T(8,128)(2,1)}), bf16[16,64,256]{2,1,0:T(8,128)(2,1)}, u32[]{:S(2)}, u32[]{:S(2)}) async-start(bf16[16,64,256]{2,1,0:T(8,128)(2,1)} %bitcast.63), calls=%async_computation | async-start | bytes 1048576 | tf_op jit(solution)/shard_map/all_to_all | solution.py:414
  129.4 1.3 fusion.1
  130.8 9.5 %all-to-all-done.in_ref = bf16[16,64,256]{2,1,0:T(8,128)(2,1)} async-done(((bf16[16,64,256]{2,1,0:T(8,128)(2,1)}), bf16[16,64,256]{2,1,0:T(8,128)(2,1)}, u32[]{:S(2)}, u32[]{:S(2)}) %all-to-all-start) | async-done | bytes 524320 | tf_op jit(solution)/shard_map/all_to_all | solution.py:414
  140.3 1.7 %finish.1 = (f32[64,256]{1,0:T(8,128)}, f32[64,256]{1,0:T(8,128)}) custom-call(bf16[16,64,256]{2,1,0:T(8,128)(2,1)} %all-to-all-done.in_ref), custom_call_target="tpu_custom_call" | custom-call | tf_op jit(solution)/shard_map/finish/pallas_call | solution.py:324
  (96 shorter events, 10.7 us)
Async XLA Ops:
  0.6 27.4 %copy-start = (bf16[4096,256]{1,0:T(8,128)(2,1)S(1)}, bf16[4096,256]{1,0:T(8,128)(2,1)}, u32[]{:S(2)}) copy-start(bf16[4096,256]{1,0:T(8,128)(2,1)} %param.18) | copy-start | bytes 6291460
  3.3 2.5 %collective-permute-start = (bf16[128,256]{1,0:T(8,128)(2,1)}, bf16[128,256]{1,0:T(8,128)(2,1)S(1)}, u32[]{:S(2)}, u32[]{:S(2)}) collective-permute-start(bf16[128,256]{1,0:T(8,128)(2,1)} %get-tuple-element.55), channel_id=1, source_target_pairs={{0,2},{2,0},{1,3},{3,1},{4,6},{6,4},{5,7},{7,5},{8,10},{10,8},{9,1... | collective-permute-start | bytes 196616 | tf_op jit(solution)/shard_map/ppermute | solution.py:35
  4.7 11.4 %collective-permute-start.5 = (bf16[128,1024]{1,0:T(8,128)(2,1)}, bf16[128,1024]{1,0:T(8,128)(2,1)S(1)}, u32[]{:S(2)}, u32[]{:S(2)}) collective-permute-start(bf16[128,1024]{1,0:T(8,128)(2,1)} %get-tuple-element.57), channel_id=1, source_target_pairs={{0,2},{2,0},{1,3},{3,1},{4,6},{6,4},{5,7},{7,5},{8,10},{10,8},{9,1... | collective-permute-start | bytes 786440 | tf_op jit(solution)/shard_map/ppermute | solution.py:35
  6.5 7.4 %collective-permute-start.1 = (bf16[2,128,256]{2,1,0:T(8,128)(2,1)}, bf16[2,128,256]{2,1,0:T(8,128)(2,1)S(1)}, u32[]{:S(2)}, u32[]{:S(2)}) collective-permute-start(bf16[2,128,256]{2,1,0:T(8,128)(2,1)} %bitcast_dynamic-update-slice_fusion.1), channel_id=1, source_target_pairs={{0,16},{16,0},{1,17},{17,1},{2,18},{18,2},{3,19},{19,3},{4,20},{20... | collective-permute-start | bytes 393224 | tf_op jit(solution)/shard_map/ppermute | solution.py:35
  14.8 16.6 %copy-start.7 = (bf16[2,2,128,256]{3,2,1,0:T(8,128)(2,1)}, bf16[2,2,128,256]{3,2,1,0:T(8,128)(2,1)S(1)}, u32[]{:S(2)}) copy-start(bf16[2,2,128,256]{3,2,1,0:T(8,128)(2,1)S(1)} %pad_maximum_fusion.2.refs_0_) | copy-start | bytes 786436
  14.9 9.5 %collective-permute-start.4 = (bf16[2,2,128,256]{3,2,1,0:T(8,128)(2,1)S(1)}, bf16[2,2,128,256]{3,2,1,0:T(8,128)(2,1)S(1)}, u32[]{:S(2)}, u32[]{:S(2)}) collective-permute-start(bf16[2,2,128,256]{3,2,1,0:T(8,128)(2,1)S(1)} %pad_maximum_fusion.2.refs_0_), channel_id=1, source_target_pairs={{0,4},{4,8},{8,12},{12,0},{1,5},{5,9},{9,13},{13,1},{2,6},{6,10},{... | collective-permute-start | bytes 786440 | tf_op jit(solution)/shard_map/ppermute | solution.py:35
  16.9 20.4 %collective-permute-start.8 = (bf16[2,128,1024]{2,1,0:T(8,128)(2,1)}, bf16[2,128,1024]{2,1,0:T(8,128)(2,1)}, u32[]{:S(2)}, u32[]{:S(2)}) collective-permute-start(bf16[2,128,1024]{2,1,0:T(8,128)(2,1)} %bitcast_dynamic-update-slice_fusion.refs_4_), channel_id=1, source_target_pairs={{0,32},{32,64},{64,96},{96,0},{1,33},{33,65},{65,97},{97,1},{2,34}... | collective-permute-start | bytes 1572872 | tf_op jit(solution)/shard_map/ppermute | solution.py:35
  18.2 25.0 %collective-permute-start.7 = (bf16[2,128,1024]{2,1,0:T(8,128)(2,1)}, bf16[2,128,1024]{2,1,0:T(8,128)(2,1)}, u32[]{:S(2)}, u32[]{:S(2)}) collective-permute-start(bf16[2,128,1024]{2,1,0:T(8,128)(2,1)} %bitcast_dynamic-update-slice_fusion.refs_4_), channel_id=1, source_target_pairs={{0,64},{32,96},{64,0},{96,32},{1,65},{33,97},{65,1},{97,33},{2,66}... | collective-permute-start | bytes 1572872 | tf_op jit(solution)/shard_map/ppermute | solution.py:35
  20.8 23.8 %collective-permute-start.6 = (bf16[2,128,1024]{2,1,0:T(8,128)(2,1)}, bf16[2,128,1024]{2,1,0:T(8,128)(2,1)}, u32[]{:S(2)}, u32[]{:S(2)}) collective-permute-start(bf16[2,128,1024]{2,1,0:T(8,128)(2,1)} %bitcast_dynamic-update-slice_fusion.refs_4_), channel_id=1, source_target_pairs={{0,96},{32,0},{64,32},{96,64},{1,97},{33,1},{65,33},{97,65},{2,98}... | collective-permute-start | bytes 1572872 | tf_op jit(solution)/shard_map/ppermute | solution.py:35
  21.9 9.5 %collective-permute-start.3 = (bf16[2,2,128,256]{3,2,1,0:T(8,128)(2,1)S(1)}, bf16[2,2,128,256]{3,2,1,0:T(8,128)(2,1)}, u32[]{:S(2)}, u32[]{:S(2)}) collective-permute-start(bf16[2,2,128,256]{3,2,1,0:T(8,128)(2,1)S(1)} %pad_maximum_fusion.2.refs_0_), channel_id=1, source_target_pairs={{0,8},{4,12},{8,0},{12,4},{1,9},{5,13},{9,1},{13,5},{2,10},{6,14},... | collective-permute-start | bytes 786440 | tf_op jit(solution)/shard_map/ppermute | solution.py:35
  24.4 3.6 %copy-start.8 = (bf16[2,2,128,256]{3,2,1,0:T(8,128)(2,1)}, bf16[2,2,128,256]{3,2,1,0:T(8,128)(2,1)S(1)}, u32[]{:S(2)}) copy-start(bf16[2,2,128,256]{3,2,1,0:T(8,128)(2,1)S(1)} %collective-permute-done.4.refs_3_) | copy-start | bytes 786436
  24.4 10.3 %collective-permute-start.2 = (bf16[2,2,128,256]{3,2,1,0:T(8,128)(2,1)S(1)}, bf16[2,2,128,256]{3,2,1,0:T(8,128)(2,1)}, u32[]{:S(2)}, u32[]{:S(2)}) collective-permute-start(bf16[2,2,128,256]{3,2,1,0:T(8,128)(2,1)S(1)} %pad_maximum_fusion.2.refs_0_), channel_id=1, source_target_pairs={{0,12},{4,0},{8,4},{12,8},{1,13},{5,1},{9,5},{13,9},{2,14},{6,2},{... | collective-permute-start | bytes 786440 | tf_op jit(solution)/shard_map/ppermute | solution.py:35
  31.5 26.3 %copy-start.4 = (bf16[128,512]{1,0:T(8,128)(2,1)S(1)}, bf16[128,512]{1,0:T(8,128)(2,1)}, u32[]{:S(2)}) copy-start(bf16[128,512]{1,0:T(8,128)(2,1)} %get-tuple-element.59) | copy-start | bytes 393220
  31.5 72.3 %collective-permute-start.23 = (bf16[2048,256]{1,0:T(8,128)(2,1)S(1)}, bf16[2048,256]{1,0:T(8,128)(2,1)S(1)}, u32[]{:S(2)}, u32[]{:S(2)}) collective-permute-start(bf16[2048,256]{1,0:T(8,128)(2,1)S(1)} %dynamic-slice_select_fusion), channel_id=1, source_target_pairs={{0,1},{1,0},{2,3},{3,2},{4,5},{5,4},{6,7},{7,6},{8,9},{9,8},{10,11... | collective-permute-start | bytes 3145736 | tf_op jit(solution)/shard_map/ppermute | solution.py:35
  34.7 22.4 %collective-permute-start.27 = (bf16[128,512]{1,0:T(8,128)(2,1)}, bf16[128,512]{1,0:T(8,128)(2,1)S(1)}, u32[]{:S(2)}, u32[]{:S(2)}) collective-permute-start(bf16[128,512]{1,0:T(8,128)(2,1)} %get-tuple-element.60), channel_id=1, source_target_pairs={{0,4},{4,8},{8,12},{12,0},{1,5},{5,9},{9,13},{13,1},{2,6},{6,10},{... | collective-permute-start | bytes 393224 | tf_op jit(solution)/shard_map/ppermute | solution.py:35
  37.3 19.9 %collective-permute-start.26 = (bf16[128,512]{1,0:T(8,128)(2,1)}, bf16[128,512]{1,0:T(8,128)(2,1)S(1)}, u32[]{:S(2)}, u32[]{:S(2)}) collective-permute-start(bf16[128,512]{1,0:T(8,128)(2,1)} %get-tuple-element.61), channel_id=1, source_target_pairs={{0,8},{4,12},{8,0},{12,4},{1,9},{5,13},{9,1},{13,5},{2,10},{6,14},... | collective-permute-start | bytes 393224 | tf_op jit(solution)/shard_map/ppermute | solution.py:35
  43.1 14.6 %collective-permute-start.25 = (bf16[128,512]{1,0:T(8,128)(2,1)}, bf16[128,512]{1,0:T(8,128)(2,1)S(1)}, u32[]{:S(2)}, u32[]{:S(2)}) collective-permute-start(bf16[128,512]{1,0:T(8,128)(2,1)} %get-tuple-element.62), channel_id=1, source_target_pairs={{0,12},{4,0},{8,4},{12,8},{1,13},{5,1},{9,5},{13,9},{2,14},{6,2},{... | collective-permute-start | bytes 393224 | tf_op jit(solution)/shard_map/ppermute | solution.py:35
  55.1 4.3 %collective-permute-start.9 = (f32[16,1024]{1,0:T(8,128)}, f32[16,1024]{1,0:T(8,128)}, u32[]{:S(2)}, u32[]{:S(2)}) collective-permute-start(f32[16,1024]{1,0:T(8,128)} %get-tuple-element.65), channel_id=1, source_target_pairs={{0,96},{32,0},{64,32},{96,64},{1,97},{33,1},{65,33},{97,65},{2,98}... | collective-permute-start | bytes 196616 | tf_op jit(solution)/shard_map/ppermute | solution.py:35
  57.0 5.0 %collective-permute-start.10 = (f32[16,1024]{1,0:T(8,128)}, f32[16,1024]{1,0:T(8,128)}, u32[]{:S(2)}, u32[]{:S(2)}) collective-permute-start(f32[16,1024]{1,0:T(8,128)} %get-tuple-element.66), channel_id=1, source_target_pairs={{0,64},{32,96},{64,0},{96,32},{1,65},{33,97},{65,1},{97,33},{2,66}... | collective-permute-start | bytes 196616 | tf_op jit(solution)/shard_map/ppermute | solution.py:35
  57.1 5.3 %collective-permute-start.11 = (f32[16,1024]{1,0:T(8,128)}, f32[16,1024]{1,0:T(8,128)}, u32[]{:S(2)}, u32[]{:S(2)}) collective-permute-start(f32[16,1024]{1,0:T(8,128)} %get-tuple-element.67), channel_id=1, source_target_pairs={{0,32},{32,64},{64,96},{96,0},{1,33},{33,65},{65,97},{97,1},{2,34}... | collective-permute-start | bytes 196616 | tf_op jit(solution)/shard_map/ppermute | solution.py:35
  57.7 0.7 copy-start.5
  58.4 27.1 %collective-permute-start.28 = (bf16[4,128,512]{2,1,0:T(8,128)(2,1)S(1)}, bf16[4,128,512]{2,1,0:T(8,128)(2,1)S(1)}, u32[]{:S(2)}, u32[]{:S(2)}) collective-permute-start(bf16[4,128,512]{2,1,0:T(8,128)(2,1)S(1)} %get-tuple-element.83), channel_id=1, source_target_pairs={{0,1},{1,0},{2,3},{3,2},{4,5},{5,4},{6,7},{7,6},{8,9},{9,8},{10,11... | collective-permute-start | bytes 1572872 | tf_op jit(solution)/shard_map/ppermute | solution.py:35
  80.6 18.3 %collective-permute-start.12 = (bf16[2,128,512]{2,1,0:T(8,128)(2,1)}, bf16[2,128,512]{2,1,0:T(8,128)(2,1)S(1)}, u32[]{:S(2)}, u32[]{:S(2)}) collective-permute-start(bf16[2,128,512]{2,1,0:T(8,128)(2,1)} %get-tuple-element.69), channel_id=1, source_target_pairs={{0,32},{32,64},{64,96},{96,0},{1,33},{33,65},{65,97},{97,1},{2,34}... | collective-permute-start | bytes 786440 | tf_op jit(solution)/shard_map/ppermute | solution.py:35
  80.7 19.5 %collective-permute-start.13 = (bf16[2,128,512]{2,1,0:T(8,128)(2,1)}, bf16[2,128,512]{2,1,0:T(8,128)(2,1)S(1)}, u32[]{:S(2)}, u32[]{:S(2)}) collective-permute-start(bf16[2,128,512]{2,1,0:T(8,128)(2,1)} %get-tuple-element.70), channel_id=1, source_target_pairs={{0,64},{32,96},{64,0},{96,32},{1,65},{33,97},{65,1},{97,33},{2,66}... | collective-permute-start | bytes 786440 | tf_op jit(solution)/shard_map/ppermute | solution.py:35
  82.8 6.9 %collective-permute-start.16 = (bf16[2,2,128,256]{3,2,1,0:T(8,128)(2,1)}, bf16[2,2,128,256]{3,2,1,0:T(8,128)(2,1)S(1)}, u32[]{:S(2)}, u32[]{:S(2)}) collective-permute-start(bf16[2,2,128,256]{3,2,1,0:T(8,128)(2,1)} %get-tuple-element.73), channel_id=1, source_target_pairs={{0,16},{16,0},{1,17},{17,1},{2,18},{18,2},{3,19},{19,3},{4,20},{20... | collective-permute-start | bytes 786440 | tf_op jit(solution)/shard_map/ppermute | solution.py:35
  85.5 4.2 %copy-start.9 = (bf16[2,128,512]{2,1,0:T(8,128)(2,1)S(1)}, bf16[2,128,512]{2,1,0:T(8,128)(2,1)}, u32[]{:S(2)}) copy-start(bf16[2,128,512]{2,1,0:T(8,128)(2,1)} %get-tuple-element.71) | copy-start | bytes 786436
  85.5 5.2 %copy-start.6 = (bf16[4,2,128,256]{3,2,1,0:T(8,128)(2,1)S(1)}, bf16[4,2,128,256]{3,2,1,0:T(8,128)(2,1)}, u32[]{:S(2)}) copy-start(bf16[4,2,128,256]{3,2,1,0:T(8,128)(2,1)} %get-tuple-element.74) | copy-start | bytes 1572868
  85.5 8.3 %collective-permute-start.17 = (bf16[2,2,128,256]{3,2,1,0:T(8,128)(2,1)}, bf16[2,2,128,256]{3,2,1,0:T(8,128)(2,1)S(1)}, u32[]{:S(2)}, u32[]{:S(2)}) collective-permute-start(bf16[2,2,128,256]{3,2,1,0:T(8,128)(2,1)} %get-tuple-element.75), channel_id=1, source_target_pairs={{0,16},{16,0},{1,17},{17,1},{2,18},{18,2},{3,19},{19,3},{4,20},{20... | collective-permute-start | bytes 786440 | tf_op jit(solution)/shard_map/ppermute | solution.py:35
  87.1 16.5 %copy-start.3 = (f32[2,128,512]{2,1,0:T(8,128)S(1)}, f32[2,128,512]{2,1,0:T(8,128)}, u32[]{:S(2)}) copy-start(f32[2,128,512]{2,1,0:T(8,128)} %get-tuple-element.68) | copy-start | bytes 1572868
  89.7 11.9 %collective-permute-start.14 = (bf16[2,128,512]{2,1,0:T(8,128)(2,1)S(1)}, bf16[2,128,512]{2,1,0:T(8,128)(2,1)S(1)}, u32[]{:S(2)}, u32[]{:S(2)}) collective-permute-start(bf16[2,128,512]{2,1,0:T(8,128)(2,1)S(1)} %copy-done.9), channel_id=1, source_target_pairs={{0,96},{32,0},{64,32},{96,64},{1,97},{33,1},{65,33},{97,65},{2,98}... | collective-permute-start | bytes 786440 | tf_op jit(solution)/shard_map/ppermute | solution.py:35
  93.8 27.3 %collective-permute-start.29 = (bf16[4,128,1024]{2,1,0:T(8,128)(2,1)S(1)}, bf16[4,128,1024]{2,1,0:T(8,128)(2,1)S(1)}, u32[]{:S(2)}, u32[]{:S(2)}) collective-permute-start(bf16[4,128,1024]{2,1,0:T(8,128)(2,1)S(1)} %maximum_select_fusion.1), channel_id=1, source_target_pairs={{0,2},{2,0},{1,3},{3,1},{4,6},{6,4},{5,7},{7,5},{8,10},{10,8},{9,1... | collective-permute-start | bytes 3145736 | tf_op jit(solution)/shard_map/ppermute | solution.py:35
  98.9 16.4 %copy-start.1 = (bf16[4096,256]{1,0:T(8,128)(2,1)S(1)}, bf16[4096,256]{1,0:T(8,128)(2,1)}, u32[]{:S(2)}) copy-start(bf16[4096,256]{1,0:T(8,128)(2,1)} %param.18) | copy-start | bytes 6291460
  98.9 10.0 %collective-permute-start.19 = (bf16[2,128,256]{2,1,0:T(8,128)(2,1)S(1)}, bf16[2,128,256]{2,1,0:T(8,128)(2,1)S(1)}, u32[]{:S(2)}, u32[]{:S(2)}) collective-permute-start(bf16[2,128,256]{2,1,0:T(8,128)(2,1)S(1)} %get-tuple-element.81), channel_id=1, source_target_pairs={{0,4},{4,8},{8,12},{12,0},{1,5},{5,9},{9,13},{13,1},{2,6},{6,10},{... | collective-permute-start | bytes 393224 | tf_op jit(solution)/shard_map/ppermute | solution.py:35
  100.2 7.8 %collective-permute-start.18 = (bf16[2,128,256]{2,1,0:T(8,128)(2,1)S(1)}, bf16[2,128,256]{2,1,0:T(8,128)(2,1)S(1)}, u32[]{:S(2)}, u32[]{:S(2)}) collective-permute-start(bf16[2,128,256]{2,1,0:T(8,128)(2,1)S(1)} %get-tuple-element.80), channel_id=1, source_target_pairs={{0,8},{4,12},{8,0},{12,4},{1,9},{5,13},{9,1},{13,5},{2,10},{6,14},... | collective-permute-start | bytes 393224 | tf_op jit(solution)/shard_map/ppermute | solution.py:35
  101.6 7.3 %collective-permute-start.20 = (bf16[2,128,256]{2,1,0:T(8,128)(2,1)S(1)}, bf16[2,128,256]{2,1,0:T(8,128)(2,1)S(1)}, u32[]{:S(2)}, u32[]{:S(2)}) collective-permute-start(bf16[2,128,256]{2,1,0:T(8,128)(2,1)S(1)} %fusion.31), channel_id=1, source_target_pairs={{0,12},{4,0},{8,4},{12,8},{1,13},{5,1},{9,5},{13,9},{2,14},{6,2},{... | collective-permute-start | bytes 393224 | tf_op jit(solution)/shard_map/ppermute | solution.py:35
  103.7 12.1 %copy-start.2 = (bf16[4096,256]{1,0:T(8,128)(2,1)S(1)}, bf16[4096,256]{1,0:T(8,128)(2,1)}, u32[]{:S(2)}) copy-start(bf16[4096,256]{1,0:T(8,128)(2,1)} %param.17) | copy-start | bytes 6291460
  103.8 8.8 %collective-permute-start.15 = (bf16[128,512]{1,0:T(8,128)(2,1)S(1)}, bf16[128,512]{1,0:T(8,128)(2,1)S(1)}, u32[]{:S(2)}, u32[]{:S(2)}) collective-permute-start(bf16[128,512]{1,0:T(8,128)(2,1)S(1)} %get-tuple-element.85), channel_id=1, source_target_pairs={{0,2},{2,0},{1,3},{3,1},{4,6},{6,4},{5,7},{7,5},{8,10},{10,8},{9,1... | collective-permute-start | bytes 393224 | tf_op jit(solution)/shard_map/ppermute | solution.py:35
  108.0 20.9 %collective-permute-start.24 = (bf16[2048,256]{1,0:T(8,128)(2,1)S(1)}, bf16[2048,256]{1,0:T(8,128)(2,1)S(1)}, u32[]{:S(2)}, u32[]{:S(2)}) collective-permute-start(bf16[2048,256]{1,0:T(8,128)(2,1)S(1)} %collective-permute-done.23), channel_id=1, source_target_pairs={{0,2},{2,0},{1,3},{3,1},{4,6},{6,4},{5,7},{7,5},{8,10},{10,8},{9,1... | collective-permute-start | bytes 3145736 | tf_op jit(solution)/shard_map/ppermute | solution.py:35
  109.0 7.3 %collective-permute-start.31 = (bf16[2,128,256]{2,1,0:T(8,128)(2,1)S(1)}, bf16[2,128,256]{2,1,0:T(8,128)(2,1)S(1)}, u32[]{:S(2)}, u32[]{:S(2)}) collective-permute-start(bf16[2,128,256]{2,1,0:T(8,128)(2,1)S(1)} %fusion.27), channel_id=1, source_target_pairs={{0,8},{4,12},{8,0},{12,4},{1,9},{5,13},{9,1},{13,5},{2,10},{6,14},... | collective-permute-start | bytes 393224 | tf_op jit(solution)/shard_map/ppermute | solution.py:35
  111.1 6.6 %collective-permute-start.30 = (bf16[2,128,256]{2,1,0:T(8,128)(2,1)S(1)}, bf16[2,128,256]{2,1,0:T(8,128)(2,1)S(1)}, u32[]{:S(2)}, u32[]{:S(2)}) collective-permute-start(bf16[2,128,256]{2,1,0:T(8,128)(2,1)S(1)} %fusion.27), channel_id=1, source_target_pairs={{0,12},{4,0},{8,4},{12,8},{1,13},{5,1},{9,5},{13,9},{2,14},{6,2},{... | collective-permute-start | bytes 393224 | tf_op jit(solution)/shard_map/ppermute | solution.py:35
  112.6 2.5 %collective-permute-start.21 = (bf16[128,256]{1,0:T(8,128)(2,1)S(1)}, bf16[128,256]{1,0:T(8,128)(2,1)S(1)}, u32[]{:S(2)}, u32[]{:S(2)}) collective-permute-start(bf16[128,256]{1,0:T(8,128)(2,1)S(1)} %slice_bitcast_fusion.2), channel_id=1, source_target_pairs={{0,2},{2,0},{1,3},{3,1},{4,6},{6,4},{5,7},{7,5},{8,10},{10,8},{9,1... | collective-permute-start | bytes 196616 | tf_op jit(solution)/shard_map/ppermute | solution.py:35
  115.1 5.9 %collective-permute-start.32 = (bf16[2,128,256]{2,1,0:T(8,128)(2,1)S(1)}, bf16[2,128,256]{2,1,0:T(8,128)(2,1)S(1)}, u32[]{:S(2)}, u32[]{:S(2)}) collective-permute-start(bf16[2,128,256]{2,1,0:T(8,128)(2,1)S(1)} %fusion.27), channel_id=1, source_target_pairs={{0,4},{4,8},{8,12},{12,0},{1,5},{5,9},{9,13},{13,1},{2,6},{6,10},{... | collective-permute-start | bytes 393224 | tf_op jit(solution)/shard_map/ppermute | solution.py:35
  116.4 12.6 %collective-permute-start.22 = (bf16[128,512]{1,0:T(8,128)(2,1)S(1)}, bf16[128,512]{1,0:T(8,128)(2,1)S(1)}, u32[]{:S(2)}, u32[]{:S(2)}) collective-permute-start(bf16[128,512]{1,0:T(8,128)(2,1)S(1)} %pad_maximum_fusion.3), channel_id=1, source_target_pairs={{0,1},{1,0},{2,3},{3,2},{4,5},{5,4},{6,7},{7,6},{8,9},{9,8},{10,11... | collective-permute-start | bytes 393224 | tf_op jit(solution)/shard_map/ppermute | solution.py:35
  122.6 17.7 %all-to-all-start = ((bf16[16,64,256]{2,1,0:T(8,128)(2,1)}), bf16[16,64,256]{2,1,0:T(8,128)(2,1)}, u32[]{:S(2)}, u32[]{:S(2)}) async-start(bf16[16,64,256]{2,1,0:T(8,128)(2,1)} %bitcast.63), calls=%async_computation | async-start | bytes 1048576 | tf_op jit(solution)/shard_map/all_to_all | solution.py:414

commit v5 on v4

--- a/solution.py
+++ b/solution.py
@@ -18,7 +18,7 @@
 F32 = jnp.float32
 NEG = -1e30
 
-PARTS = 4
+PARTS = 8
 T = TOK // PARTS
 KSLOTS = 16
 QSLOTS = 8
@@ -61,12 +61,16 @@
             kposb[part, slot * T : (slot + 1) * T, :] = column[part * T : (part + 1) * T, :]
 
 
-def keys_of(kv, ip):
-    return kv[ip, :, :, :, :, :HEAD].reshape(KR, HEAD)
-
-
-def values_of(kv, ip):
-    return kv[ip, :, :, :, :, HEAD:].reshape(KR, HEAD)
+def lanes(first, count):
+    return pl.ds(pl.multiple_of(first * KR, 128), count * KR)
+
+
+def keys_of(kv, first, count):
+    return kv[pl.ds(first, count), :, :, :, :, :HEAD].reshape(count * KR, HEAD)
+
+
+def values_of(kv, first, count):
+    return kv[pl.ds(first, count), :, :, :, :, HEAD:].reshape(count * KR, HEAD)
 
 
 def heads_of(qg, i, first):
@@ -74,53 +78,51 @@
     return jnp.concatenate([qg[i, :, :, :, c : c + HEAD].reshape(QSLOTS * T, HEAD) for c in cols], axis=0)
 
 
-def masked_scores(delta, i, ip, k, q, kposb, qpos_ref):
+def masked_scores(i, count, k, q, kposb, qpos_ref):
     s = nt(k, q) * SCORE2
-    if delta == 0 or delta == SPAN:
-        kp = jnp.concatenate([kposb[ip]] * (QR // 128), axis=1)
-        qp = qpos_ref[i]
-        valid = (kp <= qp) if delta == 0 else (kp > qp - float(WINDOW))
-        s = jnp.where(valid, s, NEG)
-    return s
+    pieces = [s[n * KR : (n + 1) * KR] for n in range(count)]
+    qp = qpos_ref[i]
+    kp = jnp.concatenate([kposb[i]] * (QR // 128), axis=1)
+    pieces[-1] = jnp.where(kp <= qp, pieces[-1], NEG)
+    if count == SPAN + 1:
+        kp = jnp.concatenate([kposb[i - SPAN]] * (QR // 128), axis=1)
+        pieces[0] = jnp.where(kp > qp - float(WINDOW), pieces[0], NEG)
+    return jnp.concatenate(pieces, axis=0)
+
+
+def over_parts(body):
+    for i in range(SPAN):
+        body(i, i + 1)
+
+    def full(i, carry):
+        body(i, SPAN + 1)
+        return carry
+
+    lax.fori_loop(SPAN, PARTS, full, 0)
 
 
 def stats_kernel(*refs):
     kv_refs, qg_refs = refs[0:4], refs[4:8]
     kpos_ref, qpos_ref = refs[8:10]
     out_refs = refs[10:14]
-    kv, qg, kposb, ms, ls, ws, sem = refs[14:]
+    kv, qg, kposb, ms, sem = refs[14:]
     start_loads(kv_refs, qg_refs, kpos_ref, kv, qg, kposb, sem)
-    ms[...] = jnp.full(ms.shape, NEG, F32)
-    ls[...] = jnp.zeros(ls.shape, F32)
-    ws[...] = jnp.zeros(ws.shape, F32)
-    for delta in range(SPAN + 1):
-
-        def body(i, carry, delta=delta):
-            ip = i - delta
-            if delta == 0:
-                for copy in part_copies(i, kv_refs, qg_refs, kv, qg, sem):
-                    copy.wait()
-            s = masked_scores(delta, i, ip, keys_of(kv, ip), heads_of(qg, i, 0), kposb, qpos_ref)
-            s = s.reshape(KR // 8, 8, QR)
-            dp = nt(values_of(kv, ip), heads_of(qg, i, GROUP)).reshape(KR // 8, 8, QR)
-            old = ms[i]
-            new = jnp.maximum(old, jnp.max(s, axis=0))
-            e = jnp.exp2(s - new[None])
-            fade = jnp.exp2(old - new)
-            ls[i] = ls[i] * fade + jnp.sum(e, axis=0)
-            ws[i] = ws[i] * fade + jnp.sum(e * dp, axis=0)
-            ms[i] = new
-            return carry
-
-        lax.fori_loop(delta, PARTS, body, 0)
-    rows = []
-    for i in range(PARTS):
-        m8 = ms[i]
-        top = jnp.max(m8, axis=0, keepdims=True)
-        fade = jnp.exp2(m8 - top)
-        total = jnp.sum(ls[i] * fade, axis=0, keepdims=True)
-        weighted = jnp.sum(ws[i] * fade, axis=0, keepdims=True)
-        rows += [top, total, weighted, jnp.zeros((1, QR), F32)]
+
+    def body(i, count):
+        for copy in part_copies(i, kv_refs, qg_refs, kv, qg, sem):
+            copy.wait()
+        first, rows = i - count + 1, count * KR
+        s = masked_scores(i, count, keys_of(kv, first, count), heads_of(qg, i, 0), kposb, qpos_ref)
+        dp = nt(values_of(kv, first, count), heads_of(qg, i, GROUP)).reshape(rows // 8, 8, QR)
+        s = s.reshape(rows // 8, 8, QR)
+        top = jnp.max(jnp.max(s, axis=0), axis=0, keepdims=True)
+        e = jnp.exp2(s - top[None])
+        total = jnp.sum(jnp.sum(e, axis=0), axis=0, keepdims=True)
+        weighted = jnp.sum(jnp.sum(e * dp, axis=0), axis=0, keepdims=True)
+        ms[i] = jnp.concatenate([top, total, weighted, jnp.zeros((5, QR), F32)], axis=0)
+
+    over_parts(body)
+    rows = [ms[i][0:4] for i in range(PARTS)]
     stats = jnp.concatenate(rows, axis=0)
     per_head = QSLOTS * T
     for o in range(4):
@@ -180,34 +182,26 @@
         for copy in dq_copies(part):
             copy.start()
 
-    for delta in range(SPAN + 1):
-
-        def body(i, carry, delta=delta):
-            ip = i - delta
-            if delta == 0:
-                for copy in part_copies(i, kv_refs, qg_refs, kv, qg, sem):
-                    copy.wait()
-            k, q, g = keys_of(kv, ip), heads_of(qg, i, 0), heads_of(qg, i, GROUP)
-            if delta == 0:
-                kt[i] = k.T
-            p = jnp.exp2(masked_scores(delta, i, ip, k, q, kposb, qpos_ref) - lse[i])
-            ds = (p * (nt(values_of(kv, ip), g) - mean[i])).astype(BF)
-            p = p.astype(BF)
-            dk, dv, dq = nn(ds, q), nn(p, g), nn(kt[ip], ds)
-            if delta == 0:
-                dks[ip], dvs[ip], dqt[i] = dk, dv, dq
-            else:
-                dks[ip] += dk
-                dvs[ip] += dv
-                dqt[i] += dq
-            return carry
-
-        lax.fori_loop(delta, PARTS, body, 0)
-        for part in range(PARTS):
-            if delta == min(SPAN, PARTS - 1 - part):
-                emit_dkv(part)
-            if delta == min(SPAN, part):
-                emit_dq(part)
+    def body(i, count):
+        for copy in part_copies(i, kv_refs, qg_refs, kv, qg, sem):
+            copy.wait()
+        first = i - count + 1
+        k, q, g = keys_of(kv, first, count), heads_of(qg, i, 0), heads_of(qg, i, GROUP)
+        kt[:, lanes(i, 1)] = keys_of(kv, i, 1).T
+        p = jnp.exp2(masked_scores(i, count, k, q, kposb, qpos_ref) - lse[i])
+        ds = (p * (nt(values_of(kv, first, count), g) - mean[i])).astype(BF)
+        p = p.astype(BF)
+        dk, dv = nn(ds, q), nn(p, g)
+        dqt[i] = nn(kt[:, lanes(first, count)], ds)
+        for n in range(count - 1):
+            dks[first + n] += dk[n * KR : (n + 1) * KR]
+            dvs[first + n] += dv[n * KR : (n + 1) * KR]
+        dks[i], dvs[i] = dk[(count - 1) * KR :], dv[(count - 1) * KR :]
+
+    over_parts(body)
+    for part in range(PARTS):
+        emit_dkv(part)
+        emit_dq(part)
     for part in range(PARTS):
         for copy in dkv_copies(part) + dq_copies(part):
             copy.wait()
@@ -231,7 +225,7 @@
         out_shape=[jax.ShapeDtypeStruct((PARTS * 4, QR), F32)] * 4,
         in_specs=in_places(2),
         scratch_shapes=common_scratch()
-        + [pltpu.VMEM((PARTS, 8, QR), F32)] * 3
+        + [pltpu.VMEM((PARTS, 8, QR), F32)]
         + [pltpu.SemaphoreType.DMA((PARTS, 8))],
         compiler_params=pltpu.CompilerParams(vmem_limit_bytes=VMEM_LIMIT),
         cost_estimate=pl.CostEstimate(flops=6_000_000_000, bytes_accessed=3_000_000, transcendentals=5_000_000),
@@ -249,7 +243,7 @@
         out_specs=[pl.BlockSpec(memory_space=pl.ANY)] * 7,
         scratch_shapes=common_scratch()
         + [
-            pltpu.VMEM((PARTS, HEAD, KR), BF),
+            pltpu.VMEM((HEAD, PARTS * KR), BF),
             pltpu.VMEM((PARTS, KR, HEAD), F32),
             pltpu.VMEM((PARTS, KR, HEAD), F32),
             pltpu.VMEM((PARTS, HEAD, QR), F32),
@@ -268,9 +262,9 @@
     return out[0], out[1:3], out[3:7]
 
 
-def pack_kernel(at_ref, q_ref, g_ref, k_ref, v_ref, kv_own, qg_own, kv_send, qg_send):
+def pack_kernel(q_ref, g_ref, k_ref, v_ref, kv_own, qg_own, kv_send, qg_send):
     wide = GROUP * HEAD
-    mine = at_ref[0]
+    mine = lax.axis_index("c")
     for which, kv, qg in ((mine, kv_own.at[0], qg_own.at[0]), (1 - mine, kv_send, qg_send)):
         cols = pl.ds(pl.multiple_of(which * wide, 128), wide)
         small = pl.ds(pl.multiple_of(which * HEAD, 128), HEAD)
@@ -282,32 +276,35 @@
     qg_own[1] = qg_send[...]
 
 
-def run_pack(at, q, g, k, v):
+def run_pack(q, g, k, v):
     kv, qg = (TOK, 2 * HEAD), (TOK, 2 * GROUP * HEAD)
     vmem = pl.BlockSpec(memory_space=pltpu.VMEM)
     return pl.pallas_call(
         pack_kernel,
         out_shape=[jax.ShapeDtypeStruct(a, BF) for a in ((2, *kv), (2, *qg), kv, qg)],
-        in_specs=[pl.BlockSpec(memory_space=pltpu.SMEM)] + [vmem] * 4,
+        in_specs=[vmem] * 4,
         name="pack",
-    )(at, q, g, k, v)
-
-
-def columns_kernel(at_ref, in_ref, *out_refs):
-    for o in range(4):
-        target = (at_ref[1] + o) % 4
-        for n in range(4):
-            src = pl.ds(pl.multiple_of(n * 4 * HEAD + target * HEAD, 128), HEAD)
-            out_refs[o][:, n * HEAD : (n + 1) * HEAD] = in_ref[:, src]
-
-
-def run_columns(at, layer_input):
+    )(q, g, k, v)
+
+
+def columns_kernel(mine_ref, far_ref, *out_refs):
+    x, t = lax.axis_index("x"), lax.axis_index("tp")
+    for ref, half in ((mine_ref, t), (far_ref, 1 - t)):
+        for o in range(4):
+            target = (x + o) % 4
+            for n in range(4):
+                src = pl.ds(pl.multiple_of(n * 4 * HEAD + target * HEAD, 128), HEAD)
+                dst = pl.ds(pl.multiple_of(half * 4 * HEAD + n * HEAD, 128), HEAD)
+                out_refs[o][:, dst] = ref[:, src]
+
+
+def run_columns(mine, far):
     return pl.pallas_call(
         columns_kernel,
-        out_shape=[jax.ShapeDtypeStruct((TOK, 4 * HEAD), BF)] * 4,
-        in_specs=[pl.BlockSpec(memory_space=pltpu.SMEM), pl.BlockSpec(memory_space=pltpu.VMEM)],
+        out_shape=[jax.ShapeDtypeStruct((TOK, 8 * HEAD), BF)] * 4,
+        in_specs=[pl.BlockSpec(memory_space=pltpu.VMEM)] * 2,
         name="columns",
-    )(at, layer_input)
+    )(mine, far)
 
 
 def finish_kernel(in_ref, k_ref, v_ref):
@@ -354,8 +351,8 @@
 
 def step(query_rows, key_rows, value_rows, output_grad, layer_input, key_matrix, value_matrix, run_placement):
     y, z, x, c, t = (lax.axis_index(a) for a in ("y", "z", "x", "c", "tp"))
-    at = jnp.stack([c, x, t]).astype(jnp.int32)
-    kv_pair, qg_pair, kv_send, qg_send = run_pack(at, query_rows, output_grad, key_rows, value_rows)
+    x_far = moved(layer_input, "tp", 1)
+    kv_pair, qg_pair, kv_send, qg_send = run_pack(query_rows, output_grad, key_rows, value_rows)
     qg_own = qg_pair.at[1].set(moved(qg_send, "c", 1))
     kv_own = kv_pair.at[1].set(moved(kv_send, "c", 1))
     qgs = [qg_own] + [moved(qg_own, "y", -o) for o in (1, 2, 3)]
@@ -364,16 +361,13 @@
     kpos, qpos = positions(run_placement, y, z, x, c)
 
     half = key_matrix.shape[0] // 2
-    cuts = [lax.dynamic_slice_in_dim(after(m, kv_own), (1 - t) * half, half, 0) for m in (key_matrix, value_matrix)]
-    x_pieces = run_columns(at, after(layer_input, kv_both))
-    x_half = jnp.stack([x_pieces[0]] + [moved(x_pieces[4 - o], "x", -o) for o in (1, 2, 3)])
-    x_other = moved(x_half, "tp", 1)
-    x_here = jnp.where(t == 0, jnp.concatenate([x_half, x_other], 2), jnp.concatenate([x_other, x_half], 2))
+    cuts = [lax.dynamic_slice_in_dim(after(m, kv_both), (1 - t) * half, half, 0) for m in (key_matrix, value_matrix)]
+    x_pieces = run_columns(layer_input, x_far)
     m_far = moved(jnp.where(c == 0, *cuts), "tp", 1)
-    kpos = after(kpos, *x_pieces)
 
     sts = run_stats(kvs, qgs, kpos, qpos)
     sts = [sts[0]] + [moved(sts[o], "y", -o) for o in (1, 2, 3)]
+    x_here = jnp.stack([x_pieces[0]] + [moved(x_pieces[4 - o], "x", -o) for o in (1, 2, 3)])
     dkv_near, dkv_sent, dqs = run_grads(kvs, qgs, kpos, qpos, sts)
 
     def total_of(own, arrived):

time: 143 us -> 165 us (1.15)
  waiting for transfers between devices: 35.7 us -> 66 us
  starting transfers between devices: 55.5 us -> 50.9 us
  Pallas kernels: 34.4 us -> 31.8 us
  other arithmetic: 6.02 us -> 3.88 us
    ppermute x33, waiting for transfers between devices: 26.2 us -> 56.5 us  [moved(): return lax.ppermute(array, axis, [(i, (i + by) % n) for i in range(n)])]
    ppermute x33, starting transfers between devices: 49.1 us -> 42.5 us  [moved(): return lax.ppermute(array, axis, [(i, (i + by) % n) for i in range(n)])]
    pallas_call x1, Pallas kernels: 18.1 us -> 15.8 us  [run_grads(): pl.pallas_call(grads_kernel, out_shape=dkv + dq, in_specs=in_places(6), o...]
    all_to_all x1, starting transfers between devices: 6.36 us -> 8.41 us  [step(): got = lax.all_to_all(pieces, ('y', 'z', 'c'), 0, 0, tiled=True)]
  transfers between devices with their start and end apart: 34 -> 34, of which waited for: 14 -> 11; matrix products, arithmetic and copies ran while one was open for 10% -> 8% of each run, Pallas kernels for 22% -> 17%
where the time goes in v5:
time: 165 us; the launch traced here: 164 us
  waiting for transfers between devices  66 us (40%)
  starting transfers between devices  50.9 us (31%)
  Pallas kernels  31.8 us (19%)
  matrix products  5.37 us (3%)
  local copies, waits for them, and re-layouts  5.09 us (3%)
  other arithmetic  3.88 us (2%)
    ppermute x33, waiting for transfers between devices, moved(): return lax.ppermute(array, axis, [(i, (i + by) % n) for i in range(n)])  56.5 us
    ppermute x33, starting transfers between devices, moved(): return lax.ppermute(array, axis, [(i, (i + by) % n) for i in range(n)])  42.5 us
    pallas_call x1, Pallas kernels, run_grads(): pl.pallas_call(grads_kernel, out_shape=dkv + dq, in_specs=in_places(6), o...  15.8 us
    pallas_call x1, Pallas kernels, run_stats(): pl.pallas_call(stats_kernel, out_shape=[jax.ShapeDtypeStruct((PARTS * 4,...  9.75 us
    all_to_all x1, waiting for transfers between devices, step(): got = lax.all_to_all(pieces, ('y', 'z', 'c'), 0, 0, tiled=True)  9.5 us
    all_to_all x1, starting transfers between devices, step(): got = lax.all_to_all(pieces, ('y', 'z', 'c'), 0, 0, tiled=True)  8.41 us
  transfers between devices with their start and end apart: 34, of which 11 were waited for; matrix products, arithmetic and copies ran while one was open for 8% of the time, Pallas kernels for 17%

profile of v5, /device:TPU:1, one launch (start us, length us, event | category | flops | bytes accessed | tf_op | source)
XLA Modules:
  0.0 164.0 jit_solution(1552188827036794322)
XLA Ops:
  0.6 2.1 %pack.1 = (bf16[2,128,256]{2,1,0:T(8,128)(2,1)}, bf16[2,128,1024]{2,1,0:T(8,128)(2,1)}, bf16[128,256]{1,0:T(8,128)(2,1)}, bf16[128,1024]{1,0:T(8,128)(2,1)}) custom-call(bf16[128,1024]{1,0:T(8,128)(2,1)} %q_ref.1, bf16[128,1024]{1,0:T(8,128)(2,1)} %g_ref.1, bf16[128,256]{1,0:T(8,128)(2,1)} %k_ref.1, bf16[128,256]{1,0:T(8,128)(2,1)} %v_ref.1), custom_call_target="tpu_custom_call" | custom-call | tf_op jit(solution)/shard_map/pack/pallas_call | solution.py:282
  2.7 1.4 collective-permute-start
  5.2 0.6 bitcast_dynamic-update-slice_fusion.1
  5.8 3.7 %collective-permute-start.1 = (bf16[2,128,256]{2,1,0:T(8,128)(2,1)}, bf16[2,128,256]{2,1,0:T(8,128)(2,1)S(1)}, u32[]{:S(2)}, u32[]{:S(2)}) collective-permute-start(bf16[2,128,256]{2,1,0:T(8,128)(2,1)} %bitcast_dynamic-update-slice_fusion.1), channel_id=1, source_target_pairs={{0,16},{16,0},{1,17},{17,1},{2,18},{18,2},{3,19},{19,3},{4,20},{20... | collective-permute-start | bytes 393224 | tf_op jit(solution)/shard_map/ppermute | solution.py:35
  9.8 3.5 %collective-permute-done.1 = bf16[2,128,256]{2,1,0:T(8,128)(2,1)S(1)} collective-permute-done((bf16[2,128,256]{2,1,0:T(8,128)(2,1)}, bf16[2,128,256]{2,1,0:T(8,128)(2,1)S(1)}, u32[]{:S(2)}, u32[]{:S(2)}) %collective-permute-start.1) | collective-permute-done | bytes 131104 | tf_op jit(solution)/shard_map/ppermute | solution.py:35
  13.3 0.9 pad_maximum_fusion.2.refs_0_
  14.2 2.5 %collective-permute-start.2 = (bf16[2,2,128,256]{3,2,1,0:T(8,128)(2,1)S(1)}, bf16[2,2,128,256]{3,2,1,0:T(8,128)(2,1)S(1)}, u32[]{:S(2)}, u32[]{:S(2)}) collective-permute-start(bf16[2,2,128,256]{3,2,1,0:T(8,128)(2,1)S(1)} %pad_maximum_fusion.2.refs_0_), channel_id=1, source_target_pairs={{0,12},{4,0},{8,4},{12,8},{1,13},{5,1},{9,5},{13,9},{2,14},{6,2},{... | collective-permute-start | bytes 786440 | tf_op jit(solution)/shard_map/ppermute | solution.py:35
  16.8 0.7 bitcast_dynamic-update-slice_fusion.refs_4_
  17.5 2.7 %collective-permute-start.6 = (bf16[2,128,1024]{2,1,0:T(8,128)(2,1)}, bf16[2,128,1024]{2,1,0:T(8,128)(2,1)S(1)}, u32[]{:S(2)}, u32[]{:S(2)}) collective-permute-start(bf16[2,128,1024]{2,1,0:T(8,128)(2,1)} %bitcast_dynamic-update-slice_fusion.refs_4_), channel_id=1, source_target_pairs={{0,96},{32,0},{64,32},{96,64},{1,97},{33,1},{65,33},{97,65},{2,98}... | collective-permute-start | bytes 1572872 | tf_op jit(solution)/shard_map/ppermute | solution.py:35
  20.6 0.7 collective-permute-start.8
  21.3 0.6 collective-permute-start.3
  21.9 0.6 collective-permute-start.4
  22.6 1.1 convolution_add_fusion.2
  23.6 0.6 slice.116.refs_8_
  24.4 4.5 %collective-permute-done.3.refs_2_ = bf16[2,2,128,256]{3,2,1,0:T(8,128)(2,1)} collective-permute-done((bf16[2,2,128,256]{3,2,1,0:T(8,128)(2,1)S(1)}, bf16[2,2,128,256]{3,2,1,0:T(8,128)(2,1)}, u32[]{:S(2)}, u32[]{:S(2)}) %collective-permute-start.3) | collective-permute-done | bytes 262176 | tf_op jit(solution)/shard_map/ppermute | solution.py:35
  29.3 5.0 %collective-permute-done.4.refs_3_ = bf16[2,2,128,256]{3,2,1,0:T(8,128)(2,1)} collective-permute-done((bf16[2,2,128,256]{3,2,1,0:T(8,128)(2,1)S(1)}, bf16[2,2,128,256]{3,2,1,0:T(8,128)(2,1)}, u32[]{:S(2)}, u32[]{:S(2)}) %collective-permute-start.4) | collective-permute-done | bytes 262176 | tf_op jit(solution)/shard_map/ppermute | solution.py:35
  34.4 12.6 %collective-permute-done.8.refs_7_ = bf16[2,128,1024]{2,1,0:T(8,128)(2,1)S(1)} collective-permute-done((bf16[2,128,1024]{2,1,0:T(8,128)(2,1)}, bf16[2,128,1024]{2,1,0:T(8,128)(2,1)S(1)}, u32[]{:S(2)}, u32[]{:S(2)}) %collective-permute-start.8) | collective-permute-done | bytes 524320 | tf_op jit(solution)/shard_map/ppermute | solution.py:35
  47.0 0.7 broadcast_in_dim.60
  47.8 9.8 %stats.1 = (f32[32,512]{1,0:T(8,128)}, f32[32,512]{1,0:T(8,128)}, f32[32,512]{1,0:T(8,128)}, f32[32,512]{1,0:T(8,128)}) custom-call(bf16[2,2,128,256]{3,2,1,0:T(8,128)(2,1)} %copy-done.8, bf16[2,2,128,256]{3,2,1,0:T(8,128)(2,1)} %copy-done.12, bf16[2,2,128,256]{3,2,1,0:T(8,128)(2,1)} %collective-permute-done.3.refs_2_, ...), custom_call_target="tpu_custom_call" | custom-call | flops 6000000000 | bytes 3000000 | tf_op jit(solution)/shard_map/stats/pallas_call | solution.py:223
  58.1 1.0 collective-permute-start.11
  59.1 0.8 copy-done.6
  59.9 2.5 %columns.1 = (bf16[128,1024]{1,0:T(8,128)(2,1)}, bf16[128,1024]{1,0:T(8,128)(2,1)}, bf16[128,1024]{1,0:T(8,128)(2,1)}, bf16[128,1024]{1,0:T(8,128)(2,1)}) custom-call(bf16[128,2048]{1,0:T(8,128)(2,1)} %mine_ref.1, bf16[128,2048]{1,0:T(8,128)(2,1)} %copy-done.6), custom_call_target="tpu_custom_call" | custom-call | tf_op jit(solution)/shard_map/columns/pallas_call | solution.py:302
  62.4 1.7 %collective-permute-start.27 = (bf16[128,1024]{1,0:T(8,128)(2,1)}, bf16[128,1024]{1,0:T(8,128)(2,1)S(1)}, u32[]{:S(2)}, u32[]{:S(2)}) collective-permute-start(bf16[128,1024]{1,0:T(8,128)(2,1)} %get-tuple-element.72), channel_id=1, source_target_pairs={{0,8},{4,12},{8,0},{12,4},{1,9},{5,13},{9,1},{13,5},{2,10},{6,14},... | collective-permute-start | bytes 786440 | tf_op jit(solution)/shard_map/ppermute | solution.py:35
  64.1 1.2 collective-permute-start.26
  66.0 15.8 %grads.1 = (bf16[4,2,128,256]{3,2,1,0:T(8,128)(2,1)}, bf16[2,2,128,256]{3,2,1,0:T(8,128)(2,1)}, bf16[2,2,128,256]{3,2,1,0:T(8,128)(2,1)}, f32[2,128,512]{2,1,0:T...) custom-call(bf16[2,2,128,256]{3,2,1,0:T(8,128)(2,1)} %copy-done.8, ...), custom_call_target="tpu_custom_call" | custom-call | flops 12000000000 | bytes 6000000 | tf_op jit(solution)/shard_map/grads/pallas_call | solution.py:239
  81.8 2.8 %collective-permute-start.16 = (bf16[2,2,128,256]{3,2,1,0:T(8,128)(2,1)}, bf16[2,2,128,256]{3,2,1,0:T(8,128)(2,1)S(1)}, u32[]{:S(2)}, u32[]{:S(2)}) collective-permute-start(bf16[2,2,128,256]{3,2,1,0:T(8,128)(2,1)} %get-tuple-element.65), channel_id=1, source_target_pairs={{0,16},{16,0},{1,17},{17,1},{2,18},{18,2},{3,19},{19,3},{4,20},{20... | collective-permute-start | bytes 786440 | tf_op jit(solution)/shard_map/ppermute | solution.py:35
  84.6 1.5 dynamic-slice_select_fusion
  86.1 0.8 collective-permute-start.23
  86.9 0.9 collective-permute-start.17
  88.0 2.5 %collective-permute-start.14 = (bf16[2,128,512]{2,1,0:T(8,128)(2,1)S(1)}, bf16[2,128,512]{2,1,0:T(8,128)(2,1)S(1)}, u32[]{:S(2)}, u32[]{:S(2)}) collective-permute-start(bf16[2,128,512]{2,1,0:T(8,128)(2,1)S(1)} %copy-done.15), channel_id=1, source_target_pairs={{0,96},{32,0},{64,32},{96,64},{1,97},{33,1},{65,33},{97,65},{2,98}... | collective-permute-start | bytes 786440 | tf_op jit(solution)/shard_map/ppermute | solution.py:35
  90.4 1.3 collective-permute-start.13
  91.7 0.8 collective-permute-start.12
  92.6 25.3 %collective-permute-done.17 = bf16[2,2,128,256]{3,2,1,0:T(8,128)(2,1)S(1)} collective-permute-done((bf16[2,2,128,256]{3,2,1,0:T(8,128)(2,1)S(1)}, bf16[2,2,128,256]{3,2,1,0:T(8,128)(2,1)S(1)}, u32[]{:S(2)}, u32[]{:S(2)}) %collective-permute-start.17) | collective-permute-done | bytes 262176 | tf_op jit(solution)/shard_map/ppermute | solution.py:35
  117.9 2.5 %collective-permute-start.29 = (bf16[4,128,1024]{2,1,0:T(8,128)(2,1)S(1)}, bf16[4,128,1024]{2,1,0:T(8,128)(2,1)S(1)}, u32[]{:S(2)}, u32[]{:S(2)}) collective-permute-start(bf16[4,128,1024]{2,1,0:T(8,128)(2,1)S(1)} %get-tuple-element.77), channel_id=1, source_target_pairs={{0,2},{2,0},{1,3},{3,1},{4,6},{6,4},{5,7},{7,5},{8,10},{10,8},{9,1... | collective-permute-start | bytes 3145736 | tf_op jit(solution)/shard_map/ppermute | solution.py:35
  120.9 2.3 %collective-permute-start.20 = (bf16[2,128,256]{2,1,0:T(8,128)(2,1)S(1)}, bf16[2,128,256]{2,1,0:T(8,128)(2,1)S(1)}, u32[]{:S(2)}, u32[]{:S(2)}) collective-permute-start(bf16[2,128,256]{2,1,0:T(8,128)(2,1)S(1)} %fusion.31), channel_id=1, source_target_pairs={{0,12},{4,0},{8,4},{12,8},{1,13},{5,1},{9,5},{13,9},{2,14},{6,2},{... | collective-permute-start | bytes 393224 | tf_op jit(solution)/shard_map/ppermute | solution.py:35
  123.2 0.9 collective-permute-start.18
  124.3 2.1 %collective-permute-done.20 = bf16[2,128,256]{2,1,0:T(8,128)(2,1)S(1)} collective-permute-done((bf16[2,128,256]{2,1,0:T(8,128)(2,1)S(1)}, bf16[2,128,256]{2,1,0:T(8,128)(2,1)S(1)}, u32[]{:S(2)}, u32[]{:S(2)}) %collective-permute-start.20) | collective-permute-done | bytes 131104 | tf_op jit(solution)/shard_map/ppermute | solution.py:35
  126.4 3.4 %collective-permute-start.15 = (bf16[128,512]{1,0:T(8,128)(2,1)S(1)}, bf16[128,512]{1,0:T(8,128)(2,1)S(1)}, u32[]{:S(2)}, u32[]{:S(2)}) collective-permute-start(bf16[128,512]{1,0:T(8,128)(2,1)S(1)} %get-tuple-element.81), channel_id=1, source_target_pairs={{0,2},{2,0},{1,3},{3,1},{4,6},{6,4},{5,7},{7,5},{8,10},{10,8},{9,1... | collective-permute-start | bytes 393224 | tf_op jit(solution)/shard_map/ppermute | solution.py:35
  130.3 4.1 %collective-permute-start.31 = (bf16[2,128,256]{2,1,0:T(8,128)(2,1)S(1)}, bf16[2,128,256]{2,1,0:T(8,128)(2,1)S(1)}, u32[]{:S(2)}, u32[]{:S(2)}) collective-permute-start(bf16[2,128,256]{2,1,0:T(8,128)(2,1)S(1)} %fusion.27), channel_id=1, source_target_pairs={{0,8},{4,12},{8,0},{12,4},{1,9},{5,13},{9,1},{13,5},{2,10},{6,14},... | collective-permute-start | bytes 393224 | tf_op jit(solution)/shard_map/ppermute | solution.py:35
  134.5 0.6 collective-permute-start.21
  135.2 0.8 maximum_select_fusion
  137.5 0.8 collective-permute-start.22
  138.3 2.6 %collective-permute-done.31 = bf16[2,128,256]{2,1,0:T(8,128)(2,1)S(1)} collective-permute-done((bf16[2,128,256]{2,1,0:T(8,128)(2,1)S(1)}, bf16[2,128,256]{2,1,0:T(8,128)(2,1)S(1)}, u32[]{:S(2)}, u32[]{:S(2)}) %collective-permute-start.31) | collective-permute-done | bytes 131104 | tf_op jit(solution)/shard_map/ppermute | solution.py:35
  141.0 1.6 fusion.7
  142.6 8.4 %all-to-all-start = ((bf16[16,64,256]{2,1,0:T(8,128)(2,1)}), bf16[16,64,256]{2,1,0:T(8,128)(2,1)}, u32[]{:S(2)}, u32[]{:S(2)}) async-start(bf16[16,64,256]{2,1,0:T(8,128)(2,1)} %bitcast.51), calls=%async_computation | async-start | bytes 1048576 | tf_op jit(solution)/shard_map/all_to_all | solution.py:408
  151.5 1.3 fusion.1
  152.8 9.5 %all-to-all-done.in_ref = bf16[16,64,256]{2,1,0:T(8,128)(2,1)} async-done(((bf16[16,64,256]{2,1,0:T(8,128)(2,1)}), bf16[16,64,256]{2,1,0:T(8,128)(2,1)}, u32[]{:S(2)}, u32[]{:S(2)}) %all-to-all-start) | async-done | bytes 524320 | tf_op jit(solution)/shard_map/all_to_all | solution.py:408
  162.3 1.7 %finish.1 = (f32[64,256]{1,0:T(8,128)}, f32[64,256]{1,0:T(8,128)}) custom-call(bf16[16,64,256]{2,1,0:T(8,128)(2,1)} %all-to-all-done.in_ref), custom_call_target="tpu_custom_call" | custom-call | tf_op jit(solution)/shard_map/finish/pallas_call | solution.py:321
  (112 shorter events, 7.3 us)
Async XLA Ops:
  0.6 28.2 %copy-start.5 = (bf16[128,2048]{1,0:T(8,128)(2,1)S(1)}, bf16[128,2048]{1,0:T(8,128)(2,1)}, u32[]{:S(2)}) copy-start(bf16[128,2048]{1,0:T(8,128)(2,1)} %mine_ref.1) | copy-start | bytes 1572868
  2.7 2.5 %collective-permute-start = (bf16[128,256]{1,0:T(8,128)(2,1)}, bf16[128,256]{1,0:T(8,128)(2,1)S(1)}, u32[]{:S(2)}, u32[]{:S(2)}) collective-permute-start(bf16[128,256]{1,0:T(8,128)(2,1)} %get-tuple-element.53), channel_id=1, source_target_pairs={{0,2},{2,0},{1,3},{3,1},{4,6},{6,4},{5,7},{7,5},{8,10},{10,8},{9,1... | collective-permute-start | bytes 196616 | tf_op jit(solution)/shard_map/ppermute | solution.py:35
  4.1 12.7 %collective-permute-start.5 = (bf16[128,1024]{1,0:T(8,128)(2,1)}, bf16[128,1024]{1,0:T(8,128)(2,1)S(1)}, u32[]{:S(2)}, u32[]{:S(2)}) collective-permute-start(bf16[128,1024]{1,0:T(8,128)(2,1)} %get-tuple-element.55), channel_id=1, source_target_pairs={{0,2},{2,0},{1,3},{3,1},{4,6},{6,4},{5,7},{7,5},{8,10},{10,8},{9,1... | collective-permute-start | bytes 786440 | tf_op jit(solution)/shard_map/ppermute | solution.py:35
  5.8 7.4 %collective-permute-start.1 = (bf16[2,128,256]{2,1,0:T(8,128)(2,1)}, bf16[2,128,256]{2,1,0:T(8,128)(2,1)S(1)}, u32[]{:S(2)}, u32[]{:S(2)}) collective-permute-start(bf16[2,128,256]{2,1,0:T(8,128)(2,1)} %bitcast_dynamic-update-slice_fusion.1), channel_id=1, source_target_pairs={{0,16},{16,0},{1,17},{17,1},{2,18},{18,2},{3,19},{19,3},{4,20},{20... | collective-permute-start | bytes 393224 | tf_op jit(solution)/shard_map/ppermute | solution.py:35
  14.2 33.5 %copy-start.8 = (bf16[2,2,128,256]{3,2,1,0:T(8,128)(2,1)}, bf16[2,2,128,256]{3,2,1,0:T(8,128)(2,1)S(1)}, u32[]{:S(2)}) copy-start(bf16[2,2,128,256]{3,2,1,0:T(8,128)(2,1)S(1)} %pad_maximum_fusion.2.refs_0_) | copy-start | bytes 786436
  14.2 7.7 %collective-permute-start.2 = (bf16[2,2,128,256]{3,2,1,0:T(8,128)(2,1)S(1)}, bf16[2,2,128,256]{3,2,1,0:T(8,128)(2,1)S(1)}, u32[]{:S(2)}, u32[]{:S(2)}) collective-permute-start(bf16[2,2,128,256]{3,2,1,0:T(8,128)(2,1)S(1)} %pad_maximum_fusion.2.refs_0_), channel_id=1, source_target_pairs={{0,12},{4,0},{8,4},{12,8},{1,13},{5,1},{9,5},{13,9},{2,14},{6,2},{... | collective-permute-start | bytes 786440 | tf_op jit(solution)/shard_map/ppermute | solution.py:35
  17.5 16.9 %collective-permute-start.6 = (bf16[2,128,1024]{2,1,0:T(8,128)(2,1)}, bf16[2,128,1024]{2,1,0:T(8,128)(2,1)S(1)}, u32[]{:S(2)}, u32[]{:S(2)}) collective-permute-start(bf16[2,128,1024]{2,1,0:T(8,128)(2,1)} %bitcast_dynamic-update-slice_fusion.refs_4_), channel_id=1, source_target_pairs={{0,96},{32,0},{64,32},{96,64},{1,97},{33,1},{65,33},{97,65},{2,98}... | collective-permute-start | bytes 1572872 | tf_op jit(solution)/shard_map/ppermute | solution.py:35
  20.2 14.1 %collective-permute-start.7 = (bf16[2,128,1024]{2,1,0:T(8,128)(2,1)}, bf16[2,128,1024]{2,1,0:T(8,128)(2,1)S(1)}, u32[]{:S(2)}, u32[]{:S(2)}) collective-permute-start(bf16[2,128,1024]{2,1,0:T(8,128)(2,1)} %bitcast_dynamic-update-slice_fusion.refs_4_), channel_id=1, source_target_pairs={{0,64},{32,96},{64,0},{96,32},{1,65},{33,97},{65,1},{97,33},{2,66}... | collective-permute-start | bytes 1572872 | tf_op jit(solution)/shard_map/ppermute | solution.py:35
  20.6 26.4 %collective-permute-start.8 = (bf16[2,128,1024]{2,1,0:T(8,128)(2,1)}, bf16[2,128,1024]{2,1,0:T(8,128)(2,1)S(1)}, u32[]{:S(2)}, u32[]{:S(2)}) collective-permute-start(bf16[2,128,1024]{2,1,0:T(8,128)(2,1)} %bitcast_dynamic-update-slice_fusion.refs_4_), channel_id=1, source_target_pairs={{0,32},{32,64},{64,96},{96,0},{1,33},{33,65},{65,97},{97,1},{2,34}... | collective-permute-start | bytes 1572872 | tf_op jit(solution)/shard_map/ppermute | solution.py:35
  21.3 7.6 %collective-permute-start.3 = (bf16[2,2,128,256]{3,2,1,0:T(8,128)(2,1)S(1)}, bf16[2,2,128,256]{3,2,1,0:T(8,128)(2,1)}, u32[]{:S(2)}, u32[]{:S(2)}) collective-permute-start(bf16[2,2,128,256]{3,2,1,0:T(8,128)(2,1)S(1)} %pad_maximum_fusion.2.refs_0_), channel_id=1, source_target_pairs={{0,8},{4,12},{8,0},{12,4},{1,9},{5,13},{9,1},{13,5},{2,10},{6,14},... | collective-permute-start | bytes 786440 | tf_op jit(solution)/shard_map/ppermute | solution.py:35
  21.9 25.8 %copy-start.12 = (bf16[2,2,128,256]{3,2,1,0:T(8,128)(2,1)}, bf16[2,2,128,256]{3,2,1,0:T(8,128)(2,1)S(1)}, u32[]{:S(2)}) copy-start(bf16[2,2,128,256]{3,2,1,0:T(8,128)(2,1)S(1)} %collective-permute-done.2.refs_1_) | copy-start | bytes 786436
  21.9 12.5 %collective-permute-start.4 = (bf16[2,2,128,256]{3,2,1,0:T(8,128)(2,1)S(1)}, bf16[2,2,128,256]{3,2,1,0:T(8,128)(2,1)}, u32[]{:S(2)}, u32[]{:S(2)}) collective-permute-start(bf16[2,2,128,256]{3,2,1,0:T(8,128)(2,1)S(1)} %pad_maximum_fusion.2.refs_0_), channel_id=1, source_target_pairs={{0,4},{4,8},{8,12},{12,0},{1,5},{5,9},{9,13},{13,1},{2,6},{6,10},{... | collective-permute-start | bytes 786440 | tf_op jit(solution)/shard_map/ppermute | solution.py:35
  28.9 30.3 %collective-permute-start.25 = (bf16[128,2048]{1,0:T(8,128)(2,1)S(1)}, bf16[128,2048]{1,0:T(8,128)(2,1)S(1)}, u32[]{:S(2)}, u32[]{:S(2)}) collective-permute-start(bf16[128,2048]{1,0:T(8,128)(2,1)S(1)} %copy-done.5), channel_id=1, source_target_pairs={{0,1},{1,0},{2,3},{3,2},{4,5},{5,4},{6,7},{7,6},{8,9},{9,8},{10,11... | collective-permute-start | bytes 1572872 | tf_op jit(solution)/shard_map/ppermute | solution.py:35
  34.4 13.3 %copy-start.9 = (bf16[2,128,1024]{2,1,0:T(8,128)(2,1)}, bf16[2,128,1024]{2,1,0:T(8,128)(2,1)S(1)}, u32[]{:S(2)}) copy-start(bf16[2,128,1024]{2,1,0:T(8,128)(2,1)S(1)} %collective-permute-done.6.refs_5_) | copy-start | bytes 1572868
  34.4 13.3 %copy-start.10 = (bf16[2,128,1024]{2,1,0:T(8,128)(2,1)}, bf16[2,128,1024]{2,1,0:T(8,128)(2,1)S(1)}, u32[]{:S(2)}) copy-start(bf16[2,128,1024]{2,1,0:T(8,128)(2,1)S(1)} %collective-permute-done.7.refs_6_) | copy-start | bytes 1572868
  57.6 6.5 %collective-permute-start.9 = (f32[32,512]{1,0:T(8,128)}, f32[32,512]{1,0:T(8,128)S(1)}, u32[]{:S(2)}, u32[]{:S(2)}) collective-permute-start(f32[32,512]{1,0:T(8,128)} %get-tuple-element.57), channel_id=1, source_target_pairs={{0,96},{32,0},{64,32},{96,64},{1,97},{33,1},{65,33},{97,65},{2,98}... | collective-permute-start | bytes 196616 | tf_op jit(solution)/shard_map/ppermute | solution.py:35
  57.7 7.7 %collective-permute-start.10 = (f32[32,512]{1,0:T(8,128)}, f32[32,512]{1,0:T(8,128)S(1)}, u32[]{:S(2)}, u32[]{:S(2)}) collective-permute-start(f32[32,512]{1,0:T(8,128)} %get-tuple-element.58), channel_id=1, source_target_pairs={{0,64},{32,96},{64,0},{96,32},{1,65},{33,97},{65,1},{97,33},{2,66}... | collective-permute-start | bytes 196616 | tf_op jit(solution)/shard_map/ppermute | solution.py:35
  58.1 7.2 %collective-permute-start.11 = (f32[32,512]{1,0:T(8,128)}, f32[32,512]{1,0:T(8,128)S(1)}, u32[]{:S(2)}, u32[]{:S(2)}) collective-permute-start(f32[32,512]{1,0:T(8,128)} %get-tuple-element.59), channel_id=1, source_target_pairs={{0,32},{32,64},{64,96},{96,0},{1,33},{33,65},{65,97},{97,1},{2,34}... | collective-permute-start | bytes 196616 | tf_op jit(solution)/shard_map/ppermute | solution.py:35
  62.4 24.5 %collective-permute-start.28 = (bf16[128,1024]{1,0:T(8,128)(2,1)}, bf16[128,1024]{1,0:T(8,128)(2,1)S(1)}, u32[]{:S(2)}, u32[]{:S(2)}) collective-permute-start(bf16[128,1024]{1,0:T(8,128)(2,1)} %get-tuple-element.73), channel_id=1, source_target_pairs={{0,4},{4,8},{8,12},{12,0},{1,5},{5,9},{9,13},{13,1},{2,6},{6,10},{... | collective-permute-start | bytes 786440 | tf_op jit(solution)/shard_map/ppermute | solution.py:35
  62.4 25.4 %collective-permute-start.27 = (bf16[128,1024]{1,0:T(8,128)(2,1)}, bf16[128,1024]{1,0:T(8,128)(2,1)S(1)}, u32[]{:S(2)}, u32[]{:S(2)}) collective-permute-start(bf16[128,1024]{1,0:T(8,128)(2,1)} %get-tuple-element.72), channel_id=1, source_target_pairs={{0,8},{4,12},{8,0},{12,4},{1,9},{5,13},{9,1},{13,5},{2,10},{6,14},... | collective-permute-start | bytes 786440 | tf_op jit(solution)/shard_map/ppermute | solution.py:35
  64.1 23.6 %collective-permute-start.26 = (bf16[128,1024]{1,0:T(8,128)(2,1)}, bf16[128,1024]{1,0:T(8,128)(2,1)S(1)}, u32[]{:S(2)}, u32[]{:S(2)}) collective-permute-start(bf16[128,1024]{1,0:T(8,128)(2,1)} %get-tuple-element.71), channel_id=1, source_target_pairs={{0,12},{4,0},{8,4},{12,8},{1,13},{5,1},{9,5},{13,9},{2,14},{6,2},{... | collective-permute-start | bytes 786440 | tf_op jit(solution)/shard_map/ppermute | solution.py:35
  66.0 18.6 %copy-start = (bf16[4096,256]{1,0:T(8,128)(2,1)S(1)}, bf16[4096,256]{1,0:T(8,128)(2,1)}, u32[]{:S(2)}) copy-start(bf16[4096,256]{1,0:T(8,128)(2,1)} %param.18) | copy-start | bytes 6291460
  81.8 5.1 %copy-start.16 = (bf16[2,2,128,256]{3,2,1,0:T(8,128)(2,1)S(1)}, bf16[2,2,128,256]{3,2,1,0:T(8,128)(2,1)}, u32[]{:S(2)}) copy-start(bf16[2,2,128,256]{3,2,1,0:T(8,128)(2,1)} %get-tuple-element.67) | copy-start | bytes 786436
  81.8 6.0 %copy-start.7 = (bf16[128,1024]{1,0:T(8,128)(2,1)S(1)}, bf16[128,1024]{1,0:T(8,128)(2,1)}, u32[]{:S(2)}) copy-start(bf16[128,1024]{1,0:T(8,128)(2,1)} %get-tuple-element.70) | copy-start | bytes 786436
  81.8 9.9 %collective-permute-start.16 = (bf16[2,2,128,256]{3,2,1,0:T(8,128)(2,1)}, bf16[2,2,128,256]{3,2,1,0:T(8,128)(2,1)S(1)}, u32[]{:S(2)}, u32[]{:S(2)}) collective-permute-start(bf16[2,2,128,256]{3,2,1,0:T(8,128)(2,1)} %get-tuple-element.65), channel_id=1, source_target_pairs={{0,16},{16,0},{1,17},{17,1},{2,18},{18,2},{3,19},{19,3},{4,20},{20... | collective-permute-start | bytes 786440 | tf_op jit(solution)/shard_map/ppermute | solution.py:35
  86.0 4.4 %copy-start.14 = (bf16[2,128,512]{2,1,0:T(8,128)(2,1)S(1)}, bf16[2,128,512]{2,1,0:T(8,128)(2,1)}, u32[]{:S(2)}) copy-start(bf16[2,128,512]{2,1,0:T(8,128)(2,1)} %get-tuple-element.62) | copy-start | bytes 786436
  86.0 5.7 %copy-start.13 = (bf16[2,128,512]{2,1,0:T(8,128)(2,1)S(1)}, bf16[2,128,512]{2,1,0:T(8,128)(2,1)}, u32[]{:S(2)}) copy-start(bf16[2,128,512]{2,1,0:T(8,128)(2,1)} %get-tuple-element.61) | copy-start | bytes 786436
  86.1 6.4 %copy-start.4 = (bf16[4,2,128,256]{3,2,1,0:T(8,128)(2,1)S(1)}, bf16[4,2,128,256]{3,2,1,0:T(8,128)(2,1)}, u32[]{:S(2)}) copy-start(bf16[4,2,128,256]{3,2,1,0:T(8,128)(2,1)} %get-tuple-element.66) | copy-start | bytes 1572868
  86.1 49.9 %collective-permute-start.23 = (bf16[2048,256]{1,0:T(8,128)(2,1)S(1)}, bf16[2048,256]{1,0:T(8,128)(2,1)S(1)}, u32[]{:S(2)}, u32[]{:S(2)}) collective-permute-start(bf16[2048,256]{1,0:T(8,128)(2,1)S(1)} %dynamic-slice_select_fusion), channel_id=1, source_target_pairs={{0,1},{1,0},{2,3},{3,2},{4,5},{5,4},{6,7},{7,6},{8,9},{9,8},{10,11... | collective-permute-start | bytes 3145736 | tf_op jit(solution)/shard_map/ppermute | solution.py:35
  86.9 31.0 %collective-permute-start.17 = (bf16[2,2,128,256]{3,2,1,0:T(8,128)(2,1)S(1)}, bf16[2,2,128,256]{3,2,1,0:T(8,128)(2,1)S(1)}, u32[]{:S(2)}, u32[]{:S(2)}) collective-permute-start(bf16[2,2,128,256]{3,2,1,0:T(8,128)(2,1)S(1)} %copy-done.16), channel_id=1, source_target_pairs={{0,16},{16,0},{1,17},{17,1},{2,18},{18,2},{3,19},{19,3},{4,20},{20... | collective-permute-start | bytes 786440 | tf_op jit(solution)/shard_map/ppermute | solution.py:35
  87.8 36.3 %copy-start.3 = (f32[2,128,512]{2,1,0:T(8,128)S(1)}, f32[2,128,512]{2,1,0:T(8,128)}, u32[]{:S(2)}) copy-start(f32[2,128,512]{2,1,0:T(8,128)} %get-tuple-element.60) | copy-start | bytes 1572868
  88.0 32.5 %collective-permute-start.14 = (bf16[2,128,512]{2,1,0:T(8,128)(2,1)S(1)}, bf16[2,128,512]{2,1,0:T(8,128)(2,1)S(1)}, u32[]{:S(2)}, u32[]{:S(2)}) collective-permute-start(bf16[2,128,512]{2,1,0:T(8,128)(2,1)S(1)} %copy-done.15), channel_id=1, source_target_pairs={{0,96},{32,0},{64,32},{96,64},{1,97},{33,1},{65,33},{97,65},{2,98}... | collective-permute-start | bytes 786440 | tf_op jit(solution)/shard_map/ppermute | solution.py:35
  90.4 30.4 %collective-permute-start.13 = (bf16[2,128,512]{2,1,0:T(8,128)(2,1)S(1)}, bf16[2,128,512]{2,1,0:T(8,128)(2,1)S(1)}, u32[]{:S(2)}, u32[]{:S(2)}) collective-permute-start(bf16[2,128,512]{2,1,0:T(8,128)(2,1)S(1)} %copy-done.14), channel_id=1, source_target_pairs={{0,64},{32,96},{64,0},{96,32},{1,65},{33,97},{65,1},{97,33},{2,66}... | collective-permute-start | bytes 786440 | tf_op jit(solution)/shard_map/ppermute | solution.py:35
  91.7 31.5 %collective-permute-start.12 = (bf16[2,128,512]{2,1,0:T(8,128)(2,1)S(1)}, bf16[2,128,512]{2,1,0:T(8,128)(2,1)S(1)}, u32[]{:S(2)}, u32[]{:S(2)}) collective-permute-start(bf16[2,128,512]{2,1,0:T(8,128)(2,1)S(1)} %copy-done.13), channel_id=1, source_target_pairs={{0,32},{32,64},{64,96},{96,0},{1,33},{33,65},{65,97},{97,1},{2,34}... | collective-permute-start | bytes 786440 | tf_op jit(solution)/shard_map/ppermute | solution.py:35
  117.9 23.1 %collective-permute-start.29 = (bf16[4,128,1024]{2,1,0:T(8,128)(2,1)S(1)}, bf16[4,128,1024]{2,1,0:T(8,128)(2,1)S(1)}, u32[]{:S(2)}, u32[]{:S(2)}) collective-permute-start(bf16[4,128,1024]{2,1,0:T(8,128)(2,1)S(1)} %get-tuple-element.77), channel_id=1, source_target_pairs={{0,2},{2,0},{1,3},{3,1},{4,6},{6,4},{5,7},{7,5},{8,10},{10,8},{9,1... | collective-permute-start | bytes 3145736 | tf_op jit(solution)/shard_map/ppermute | solution.py:35
  120.4 16.0 %copy-start.1 = (bf16[4096,256]{1,0:T(8,128)(2,1)S(1)}, bf16[4096,256]{1,0:T(8,128)(2,1)}, u32[]{:S(2)}) copy-start(bf16[4096,256]{1,0:T(8,128)(2,1)} %param.18) | copy-start | bytes 6291460
  120.4 9.3 %collective-permute-start.19 = (bf16[2,128,256]{2,1,0:T(8,128)(2,1)S(1)}, bf16[2,128,256]{2,1,0:T(8,128)(2,1)S(1)}, u32[]{:S(2)}, u32[]{:S(2)}) collective-permute-start(bf16[2,128,256]{2,1,0:T(8,128)(2,1)S(1)} %get-tuple-element.79), channel_id=1, source_target_pairs={{0,4},{4,8},{8,12},{12,0},{1,5},{5,9},{9,13},{13,1},{2,6},{6,10},{... | collective-permute-start | bytes 393224 | tf_op jit(solution)/shard_map/ppermute | solution.py:35
  120.9 5.5 %collective-permute-start.20 = (bf16[2,128,256]{2,1,0:T(8,128)(2,1)S(1)}, bf16[2,128,256]{2,1,0:T(8,128)(2,1)S(1)}, u32[]{:S(2)}, u32[]{:S(2)}) collective-permute-start(bf16[2,128,256]{2,1,0:T(8,128)(2,1)S(1)} %fusion.31), channel_id=1, source_target_pairs={{0,12},{4,0},{8,4},{12,8},{1,13},{5,1},{9,5},{13,9},{2,14},{6,2},{... | collective-permute-start | bytes 393224 | tf_op jit(solution)/shard_map/ppermute | solution.py:35
  123.2 6.6 %collective-permute-start.18 = (bf16[2,128,256]{2,1,0:T(8,128)(2,1)S(1)}, bf16[2,128,256]{2,1,0:T(8,128)(2,1)S(1)}, u32[]{:S(2)}, u32[]{:S(2)}) collective-permute-start(bf16[2,128,256]{2,1,0:T(8,128)(2,1)S(1)} %get-tuple-element.78), channel_id=1, source_target_pairs={{0,8},{4,12},{8,0},{12,4},{1,9},{5,13},{9,1},{13,5},{2,10},{6,14},... | collective-permute-start | bytes 393224 | tf_op jit(solution)/shard_map/ppermute | solution.py:35
  124.3 12.7 %copy-start.2 = (bf16[4096,256]{1,0:T(8,128)(2,1)S(1)}, bf16[4096,256]{1,0:T(8,128)(2,1)}, u32[]{:S(2)}) copy-start(bf16[4096,256]{1,0:T(8,128)(2,1)} %param.17) | copy-start | bytes 6291460
  126.4 8.1 %collective-permute-start.15 = (bf16[128,512]{1,0:T(8,128)(2,1)S(1)}, bf16[128,512]{1,0:T(8,128)(2,1)S(1)}, u32[]{:S(2)}, u32[]{:S(2)}) collective-permute-start(bf16[128,512]{1,0:T(8,128)(2,1)S(1)} %get-tuple-element.81), channel_id=1, source_target_pairs={{0,2},{2,0},{1,3},{3,1},{4,6},{6,4},{5,7},{7,5},{8,10},{10,8},{9,1... | collective-permute-start | bytes 393224 | tf_op jit(solution)/shard_map/ppermute | solution.py:35
  129.9 7.6 %collective-permute-start.32 = (bf16[2,128,256]{2,1,0:T(8,128)(2,1)S(1)}, bf16[2,128,256]{2,1,0:T(8,128)(2,1)S(1)}, u32[]{:S(2)}, u32[]{:S(2)}) collective-permute-start(bf16[2,128,256]{2,1,0:T(8,128)(2,1)S(1)} %fusion.27), channel_id=1, source_target_pairs={{0,4},{4,8},{8,12},{12,0},{1,5},{5,9},{9,13},{13,1},{2,6},{6,10},{... | collective-permute-start | bytes 393224 | tf_op jit(solution)/shard_map/ppermute | solution.py:35
  130.3 10.5 %collective-permute-start.31 = (bf16[2,128,256]{2,1,0:T(8,128)(2,1)S(1)}, bf16[2,128,256]{2,1,0:T(8,128)(2,1)S(1)}, u32[]{:S(2)}, u32[]{:S(2)}) collective-permute-start(bf16[2,128,256]{2,1,0:T(8,128)(2,1)S(1)} %fusion.27), channel_id=1, source_target_pairs={{0,8},{4,12},{8,0},{12,4},{1,9},{5,13},{9,1},{13,5},{2,10},{6,14},... | collective-permute-start | bytes 393224 | tf_op jit(solution)/shard_map/ppermute | solution.py:35
  134.5 1.5 collective-permute-start.21
  135.9 5.0 %collective-permute-start.30 = (bf16[2,128,256]{2,1,0:T(8,128)(2,1)S(1)}, bf16[2,128,256]{2,1,0:T(8,128)(2,1)S(1)}, u32[]{:S(2)}, u32[]{:S(2)}) collective-permute-start(bf16[2,128,256]{2,1,0:T(8,128)(2,1)S(1)} %fusion.27), channel_id=1, source_target_pairs={{0,12},{4,0},{8,4},{12,8},{1,13},{5,1},{9,5},{13,9},{2,14},{6,2},{... | collective-permute-start | bytes 393224 | tf_op jit(solution)/shard_map/ppermute | solution.py:35
  136.1 14.9 %collective-permute-start.24 = (bf16[2048,256]{1,0:T(8,128)(2,1)S(1)}, bf16[2048,256]{1,0:T(8,128)(2,1)S(1)}, u32[]{:S(2)}, u32[]{:S(2)}) collective-permute-start(bf16[2048,256]{1,0:T(8,128)(2,1)S(1)} %collective-permute-done.23), channel_id=1, source_target_pairs={{0,2},{2,0},{1,3},{3,1},{4,6},{6,4},{5,7},{7,5},{8,10},{10,8},{9,1... | collective-permute-start | bytes 3145736 | tf_op jit(solution)/shard_map/ppermute | solution.py:35
  137.5 13.5 %collective-permute-start.22 = (bf16[128,512]{1,0:T(8,128)(2,1)S(1)}, bf16[128,512]{1,0:T(8,128)(2,1)S(1)}, u32[]{:S(2)}, u32[]{:S(2)}) collective-permute-start(bf16[128,512]{1,0:T(8,128)(2,1)S(1)} %pad_maximum_fusion.3), channel_id=1, source_target_pairs={{0,1},{1,0},{2,3},{3,2},{4,5},{5,4},{6,7},{7,6},{8,9},{9,8},{10,11... | collective-permute-start | bytes 393224 | tf_op jit(solution)/shard_map/ppermute | solution.py:35
  142.6 19.7 %all-to-all-start = ((bf16[16,64,256]{2,1,0:T(8,128)(2,1)}), bf16[16,64,256]{2,1,0:T(8,128)(2,1)}, u32[]{:S(2)}, u32[]{:S(2)}) async-start(bf16[16,64,256]{2,1,0:T(8,128)(2,1)} %bitcast.51), calls=%async_computation | async-start | bytes 1048576 | tf_op jit(solution)/shard_map/all_to_all | solution.py:408
  (6 other events, 6.1 us)

commit v6 on v5

--- a/solution.py
+++ b/solution.py
@@ -287,24 +287,22 @@
     )(q, g, k, v)
 
 
-def columns_kernel(mine_ref, far_ref, *out_refs):
-    x, t = lax.axis_index("x"), lax.axis_index("tp")
-    for ref, half in ((mine_ref, t), (far_ref, 1 - t)):
-        for o in range(4):
-            target = (x + o) % 4
-            for n in range(4):
-                src = pl.ds(pl.multiple_of(n * 4 * HEAD + target * HEAD, 128), HEAD)
-                dst = pl.ds(pl.multiple_of(half * 4 * HEAD + n * HEAD, 128), HEAD)
-                out_refs[o][:, dst] = ref[:, src]
-
-
-def run_columns(mine, far):
+def columns_kernel(in_ref, *out_refs):
+    x = lax.axis_index("x")
+    for o in range(4):
+        target = (x + o) % 4
+        for n in range(4):
+            src = pl.ds(pl.multiple_of(n * 4 * HEAD + target * HEAD, 128), HEAD)
+            out_refs[o][:, n * HEAD : (n + 1) * HEAD] = in_ref[:, src]
+
+
+def run_columns(layer_input):
     return pl.pallas_call(
         columns_kernel,
-        out_shape=[jax.ShapeDtypeStruct((TOK, 8 * HEAD), BF)] * 4,
-        in_specs=[pl.BlockSpec(memory_space=pltpu.VMEM)] * 2,
+        out_shape=[jax.ShapeDtypeStruct((TOK, 4 * HEAD), BF)] * 4,
+        in_specs=[pl.BlockSpec(memory_space=pltpu.VMEM)],
         name="columns",
-    )(mine, far)
+    )(layer_input)
 
 
 def finish_kernel(in_ref, k_ref, v_ref):
@@ -351,7 +349,6 @@
 
 def step(query_rows, key_rows, value_rows, output_grad, layer_input, key_matrix, value_matrix, run_placement):
     y, z, x, c, t = (lax.axis_index(a) for a in ("y", "z", "x", "c", "tp"))
-    x_far = moved(layer_input, "tp", 1)
     kv_pair, qg_pair, kv_send, qg_send = run_pack(query_rows, output_grad, key_rows, value_rows)
     qg_own = qg_pair.at[1].set(moved(qg_send, "c", 1))
     kv_own = kv_pair.at[1].set(moved(kv_send, "c", 1))
@@ -361,13 +358,16 @@
     kpos, qpos = positions(run_placement, y, z, x, c)
 
     half = key_matrix.shape[0] // 2
-    cuts = [lax.dynamic_slice_in_dim(after(m, kv_both), (1 - t) * half, half, 0) for m in (key_matrix, value_matrix)]
-    x_pieces = run_columns(layer_input, x_far)
+    cuts = [lax.dynamic_slice_in_dim(after(m, kv_own), (1 - t) * half, half, 0) for m in (key_matrix, value_matrix)]
+    x_pieces = run_columns(after(layer_input, kv_both, qpos))
+    x_half = jnp.stack([x_pieces[0]] + [moved(x_pieces[4 - o], "x", -o) for o in (1, 2, 3)])
+    x_other = moved(x_half, "tp", 1)
+    x_here = jnp.where(t == 0, jnp.concatenate([x_half, x_other], 2), jnp.concatenate([x_other, x_half], 2))
     m_far = moved(jnp.where(c == 0, *cuts), "tp", 1)
+    kpos = after(kpos, *x_pieces)
 
     sts = run_stats(kvs, qgs, kpos, qpos)
     sts = [sts[0]] + [moved(sts[o], "y", -o) for o in (1, 2, 3)]
-    x_here = jnp.stack([x_pieces[0]] + [moved(x_pieces[4 - o], "x", -o) for o in (1, 2, 3)])
     dkv_near, dkv_sent, dqs = run_grads(kvs, qgs, kpos, qpos, sts)
 
     def total_of(own, arrived):
@@ -387,7 +387,8 @@
     k_far = jnp.where(c == 0, m_far, m_core)
     v_far = jnp.where(c == 0, m_core, m_far)
 
-    dkv = total_of(row0, [moved(row, "x", o) for o, row in ((2, row2), (1, row1), (3, row3))])
+    got = [moved(row2, "x", 2), moved(row1, "x", 1)]
+    dkv = total_of(row0, got + [moved(row3, "x", 3)])
     dkv_all = jnp.stack([dkv] + [moved(dkv, "x", -o) for o in (1, 2, 3)])
     dkv_far = moved(dkv[1], "c", 1)
     k_here = own_first(c, dkv[0, :, :HEAD], dkv_far[:, :HEAD], 1)

time: 165 us -> 139 us (0.84)
  waiting for transfers between devices: 66 us -> 35.8 us
  starting transfers between devices: 50.9 us -> 55.5 us
    ppermute x33, waiting for transfers between devices: 56.5 us -> 26.4 us  [moved(): return lax.ppermute(array, axis, [(i, (i + by) % n) for i in range(n)])]
    ppermute x33, starting transfers between devices: 42.5 us -> 49.1 us  [moved(): return lax.ppermute(array, axis, [(i, (i + by) % n) for i in range(n)])]
    all_to_all x1, starting transfers between devices: 8.41 us -> 6.35 us  [step(): got = lax.all_to_all(pieces, ('y', 'z', 'c'), 0, 0, tiled=True)]
  transfers between devices with their start and end apart: 34 -> 34, of which waited for: 11 -> 14; matrix products, arithmetic and copies ran while one was open for 8% -> 10% of each run, Pallas kernels for 17% -> 20%
where the time goes in v6:
time: 139 us; the launch traced here: 138 us
  starting transfers between devices  55.5 us (40%)
  waiting for transfers between devices  35.8 us (26%)
  Pallas kernels  31.2 us (22%)
  matrix products  5.39 us (4%)
  other arithmetic  5.38 us (4%)
  local copies, waits for them, and re-layouts  3.98 us (3%)
    ppermute x33, starting transfers between devices, moved(): return lax.ppermute(array, axis, [(i, (i + by) % n) for i in range(n)])  49.1 us
    ppermute x33, waiting for transfers between devices, moved(): return lax.ppermute(array, axis, [(i, (i + by) % n) for i in range(n)])  26.4 us
    pallas_call x1, Pallas kernels, run_grads(): pl.pallas_call(grads_kernel, out_shape=dkv + dq, in_specs=in_places(6), o...  15.5 us
    pallas_call x1, Pallas kernels, run_stats(): pl.pallas_call(stats_kernel, out_shape=[jax.ShapeDtypeStruct((PARTS * 4,...  9.76 us
    all_to_all x1, waiting for transfers between devices, step(): got = lax.all_to_all(pieces, ('y', 'z', 'c'), 0, 0, tiled=True)  9.5 us
    all_to_all x1, starting transfers between devices, step(): got = lax.all_to_all(pieces, ('y', 'z', 'c'), 0, 0, tiled=True)  6.35 us
  transfers between devices with their start and end apart: 34, of which 14 were waited for; matrix products, arithmetic and copies ran while one was open for 10% of the time, Pallas kernels for 20%

profile of v6, /device:TPU:1, one launch (start us, length us, event | category | flops | bytes accessed | tf_op | source)
XLA Modules:
  0.0 138.2 jit_solution(1435247786165023454)
XLA Ops:
  0.6 2.2 %pack.1 = (bf16[2,128,256]{2,1,0:T(8,128)(2,1)}, bf16[2,128,1024]{2,1,0:T(8,128)(2,1)}, bf16[128,256]{1,0:T(8,128)(2,1)}, bf16[128,1024]{1,0:T(8,128)(2,1)}) custom-call(bf16[128,1024]{1,0:T(8,128)(2,1)} %q_ref.1, bf16[128,1024]{1,0:T(8,128)(2,1)} %g_ref.1, bf16[128,256]{1,0:T(8,128)(2,1)} %k_ref.1, bf16[128,256]{1,0:T(8,128)(2,1)} %v_ref.1), custom_call_target="tpu_custom_call" | custom-call | tf_op jit(solution)/shard_map/pack/pallas_call | solution.py:282
  2.8 1.4 collective-permute-start
  6.0 3.7 %collective-permute-start.1 = (bf16[2,128,256]{2,1,0:T(8,128)(2,1)}, bf16[2,128,256]{2,1,0:T(8,128)(2,1)S(1)}, u32[]{:S(2)}, u32[]{:S(2)}) collective-permute-start(bf16[2,128,256]{2,1,0:T(8,128)(2,1)} %bitcast_dynamic-update-slice_fusion.1), channel_id=1, source_target_pairs={{0,16},{16,0},{1,17},{17,1},{2,18},{18,2},{3,19},{19,3},{4,20},{20... | collective-permute-start | bytes 393224 | tf_op jit(solution)/shard_map/ppermute | solution.py:35
  9.7 3.7 %collective-permute-done.1 = bf16[2,128,256]{2,1,0:T(8,128)(2,1)S(1)} collective-permute-done((bf16[2,128,256]{2,1,0:T(8,128)(2,1)}, bf16[2,128,256]{2,1,0:T(8,128)(2,1)S(1)}, u32[]{:S(2)}, u32[]{:S(2)}) %collective-permute-start.1) | collective-permute-done | bytes 131104 | tf_op jit(solution)/shard_map/ppermute | solution.py:35
  13.4 0.9 pad_maximum_fusion.2.refs_0_
  14.3 1.3 collective-permute-start.4
  16.3 1.3 collective-permute-start.8
  17.6 2.6 %collective-permute-start.7 = (bf16[2,128,1024]{2,1,0:T(8,128)(2,1)}, bf16[2,128,1024]{2,1,0:T(8,128)(2,1)}, u32[]{:S(2)}, u32[]{:S(2)}) collective-permute-start(bf16[2,128,1024]{2,1,0:T(8,128)(2,1)} %bitcast_dynamic-update-slice_fusion.refs_4_), channel_id=1, source_target_pairs={{0,64},{32,96},{64,0},{96,32},{1,65},{33,97},{65,1},{97,33},{2,66}... | collective-permute-start | bytes 1572872 | tf_op jit(solution)/shard_map/ppermute | solution.py:35
  20.3 1.1 collective-permute-start.6
  21.4 2.5 %collective-permute-start.3 = (bf16[2,2,128,256]{3,2,1,0:T(8,128)(2,1)S(1)}, bf16[2,2,128,256]{3,2,1,0:T(8,128)(2,1)}, u32[]{:S(2)}, u32[]{:S(2)}) collective-permute-start(bf16[2,2,128,256]{3,2,1,0:T(8,128)(2,1)S(1)} %pad_maximum_fusion.2.refs_0_), channel_id=1, source_target_pairs={{0,8},{4,12},{8,0},{12,4},{1,9},{5,13},{9,1},{13,5},{2,10},{6,14},... | collective-permute-start | bytes 786440 | tf_op jit(solution)/shard_map/ppermute | solution.py:35
  23.9 1.2 collective-permute-start.2
  25.0 1.1 convolution_add_fusion.2
  26.8 1.5 %dynamic-slice_select_fusion = bf16[2048,256]{1,0:T(8,128)(2,1)S(1)} fusion(bf16[4096,256]{1,0:T(8,128)(2,1)S(1)} %copy-done, s32[]{:T(128)S(6)} %select_n.157, bf16[4096,256]{1,0:T(8,128)(2,1)} %param.17, pred[]{:T(512)S(6)} %eq.50), kind=kLoop, calls=%fused_computation.16 | loop fusion | flops 524288 | bytes 3145733 | tf_op jit(solution)/shard_map/jit(_where)/select_n | solution.py:366
  28.9 1.9 %columns.1 = (bf16[128,512]{1,0:T(8,128)(2,1)}, bf16[128,512]{1,0:T(8,128)(2,1)}, bf16[128,512]{1,0:T(8,128)(2,1)}, bf16[128,512]{1,0:T(8,128)(2,1)}) custom-call(bf16[128,2048]{1,0:T(8,128)(2,1)} %in_ref), custom_call_target="tpu_custom_call" | custom-call | tf_op jit(solution)/shard_map/columns/pallas_call | solution.py:300
  30.9 0.8 collective-permute-start.23
  31.7 2.5 %collective-permute-done.2.refs_1_ = bf16[2,2,128,256]{3,2,1,0:T(8,128)(2,1)} collective-permute-done((bf16[2,2,128,256]{3,2,1,0:T(8,128)(2,1)S(1)}, bf16[2,2,128,256]{3,2,1,0:T(8,128)(2,1)}, u32[]{:S(2)}, u32[]{:S(2)}) %collective-permute-start.2) | collective-permute-done | bytes 262176 | tf_op jit(solution)/shard_map/ppermute | solution.py:35
  34.2 2.6 %collective-permute-start.27 = (bf16[128,512]{1,0:T(8,128)(2,1)}, bf16[128,512]{1,0:T(8,128)(2,1)S(1)}, u32[]{:S(2)}, u32[]{:S(2)}) collective-permute-start(bf16[128,512]{1,0:T(8,128)(2,1)} %get-tuple-element.60), channel_id=1, source_target_pairs={{0,4},{4,8},{8,12},{12,0},{1,5},{5,9},{9,13},{13,1},{2,6},{6,10},{... | collective-permute-start | bytes 393224 | tf_op jit(solution)/shard_map/ppermute | solution.py:35
  36.8 2.1 %collective-permute-start.26 = (bf16[128,512]{1,0:T(8,128)(2,1)}, bf16[128,512]{1,0:T(8,128)(2,1)S(1)}, u32[]{:S(2)}, u32[]{:S(2)}) collective-permute-start(bf16[128,512]{1,0:T(8,128)(2,1)} %get-tuple-element.61), channel_id=1, source_target_pairs={{0,8},{4,12},{8,0},{12,4},{1,9},{5,13},{9,1},{13,5},{2,10},{6,14},... | collective-permute-start | bytes 393224 | tf_op jit(solution)/shard_map/ppermute | solution.py:35
  38.9 3.8 %collective-permute-done.7.refs_6_ = bf16[2,128,1024]{2,1,0:T(8,128)(2,1)} collective-permute-done((bf16[2,128,1024]{2,1,0:T(8,128)(2,1)}, bf16[2,128,1024]{2,1,0:T(8,128)(2,1)}, u32[]{:S(2)}, u32[]{:S(2)}) %collective-permute-start.7) | collective-permute-done | bytes 524320 | tf_op jit(solution)/shard_map/ppermute | solution.py:35
  42.6 1.5 %collective-permute-start.25 = (bf16[128,512]{1,0:T(8,128)(2,1)}, bf16[128,512]{1,0:T(8,128)(2,1)S(1)}, u32[]{:S(2)}, u32[]{:S(2)}) collective-permute-start(bf16[128,512]{1,0:T(8,128)(2,1)} %get-tuple-element.62), channel_id=1, source_target_pairs={{0,12},{4,0},{8,4},{12,8},{1,13},{5,1},{9,5},{13,9},{2,14},{6,2},{... | collective-permute-start | bytes 393224 | tf_op jit(solution)/shard_map/ppermute | solution.py:35
  44.1 9.8 %stats.1 = (f32[32,512]{1,0:T(8,128)}, f32[32,512]{1,0:T(8,128)}, f32[32,512]{1,0:T(8,128)}, f32[32,512]{1,0:T(8,128)}) custom-call(bf16[2,2,128,256]{3,2,1,0:T(8,128)(2,1)} %copy-done.7, bf16[2,2,128,256]{3,2,1,0:T(8,128)(2,1)} %collective-permute-done.2.refs_1_, bf16[2,2,128,256]{3,2,1,0:T(8,128)(2,1)} %collective-permute-done.3.refs_2_, ...), custom_call_target="tpu_custom_call" | custom-call | flops 6000000000 | bytes 3000000 | tf_op jit(solution)/shard_map/stats/pallas_call | solution.py:223
  53.9 2.0 %collective-permute-start.9 = (f32[32,512]{1,0:T(8,128)}, f32[32,512]{1,0:T(8,128)}, u32[]{:S(2)}, u32[]{:S(2)}) collective-permute-start(f32[32,512]{1,0:T(8,128)} %get-tuple-element.65), channel_id=1, source_target_pairs={{0,96},{32,0},{64,32},{96,64},{1,97},{33,1},{65,33},{97,65},{2,98}... | collective-permute-start | bytes 196616 | tf_op jit(solution)/shard_map/ppermute | solution.py:35
  58.1 2.8 %collective-permute-done.10.refs_12_ = f32[32,512]{1,0:T(8,128)} collective-permute-done((f32[32,512]{1,0:T(8,128)}, f32[32,512]{1,0:T(8,128)}, u32[]{:S(2)}, u32[]{:S(2)}) %collective-permute-start.10) | collective-permute-done | bytes 65568 | tf_op jit(solution)/shard_map/ppermute | solution.py:35
  61.3 15.5 %grads.1 = (bf16[4,2,128,256]{3,2,1,0:T(8,128)(2,1)}, bf16[2,2,128,256]{3,2,1,0:T(8,128)(2,1)}, bf16[2,2,128,256]{3,2,1,0:T(8,128)(2,1)}, f32[2,128,512]{2,1,0:T...) custom-call(bf16[2,2,128,256]{3,2,1,0:T(8,128)(2,1)} %copy-done.7, ...), custom_call_target="tpu_custom_call" | custom-call | flops 12000000000 | bytes 6000000 | tf_op jit(solution)/shard_map/grads/pallas_call | solution.py:239
  76.9 2.1 %collective-permute-start.13 = (bf16[2,128,512]{2,1,0:T(8,128)(2,1)}, bf16[2,128,512]{2,1,0:T(8,128)(2,1)S(1)}, u32[]{:S(2)}, u32[]{:S(2)}) collective-permute-start(bf16[2,128,512]{2,1,0:T(8,128)(2,1)} %get-tuple-element.70), channel_id=1, source_target_pairs={{0,64},{32,96},{64,0},{96,32},{1,65},{33,97},{65,1},{97,33},{2,66}... | collective-permute-start | bytes 786440 | tf_op jit(solution)/shard_map/ppermute | solution.py:35
  79.0 2.7 %collective-permute-start.16 = (bf16[2,2,128,256]{3,2,1,0:T(8,128)(2,1)}, bf16[2,2,128,256]{3,2,1,0:T(8,128)(2,1)S(1)}, u32[]{:S(2)}, u32[]{:S(2)}) collective-permute-start(bf16[2,2,128,256]{3,2,1,0:T(8,128)(2,1)} %get-tuple-element.73), channel_id=1, source_target_pairs={{0,16},{16,0},{1,17},{17,1},{2,18},{18,2},{3,19},{19,3},{4,20},{20... | collective-permute-start | bytes 786440 | tf_op jit(solution)/shard_map/ppermute | solution.py:35
  81.9 1.3 maximum_select_fusion.1
  83.6 2.3 %collective-permute-done.16 = bf16[2,2,128,256]{3,2,1,0:T(8,128)(2,1)S(1)} collective-permute-done((bf16[2,2,128,256]{3,2,1,0:T(8,128)(2,1)}, bf16[2,2,128,256]{3,2,1,0:T(8,128)(2,1)S(1)}, u32[]{:S(2)}, u32[]{:S(2)}) %collective-permute-start.16) | collective-permute-done | bytes 262176 | tf_op jit(solution)/shard_map/ppermute | solution.py:35
  85.9 1.0 collective-permute-start.14
  86.9 3.0 %collective-permute-done.17 = bf16[2,2,128,256]{3,2,1,0:T(8,128)(2,1)S(1)} collective-permute-done((bf16[2,2,128,256]{3,2,1,0:T(8,128)(2,1)}, bf16[2,2,128,256]{3,2,1,0:T(8,128)(2,1)S(1)}, u32[]{:S(2)}, u32[]{:S(2)}) %collective-permute-start.17) | collective-permute-done | bytes 262176 | tf_op jit(solution)/shard_map/ppermute | solution.py:35
  89.9 5.1 %collective-permute-start.29 = (bf16[4,128,1024]{2,1,0:T(8,128)(2,1)S(1)}, bf16[4,128,1024]{2,1,0:T(8,128)(2,1)S(1)}, u32[]{:S(2)}, u32[]{:S(2)}) collective-permute-start(bf16[4,128,1024]{2,1,0:T(8,128)(2,1)S(1)} %maximum_select_fusion.1), channel_id=1, source_target_pairs={{0,2},{2,0},{1,3},{3,1},{4,6},{6,4},{5,7},{7,5},{8,10},{10,8},{9,1... | collective-permute-start | bytes 3145736 | tf_op jit(solution)/shard_map/ppermute | solution.py:35
  95.1 1.3 collective-permute-start.19
  96.4 1.4 %collective-permute-start.18 = (bf16[2,128,256]{2,1,0:T(8,128)(2,1)S(1)}, bf16[2,128,256]{2,1,0:T(8,128)(2,1)S(1)}, u32[]{:S(2)}, u32[]{:S(2)}) collective-permute-start(bf16[2,128,256]{2,1,0:T(8,128)(2,1)S(1)} %get-tuple-element.80), channel_id=1, source_target_pairs={{0,8},{4,12},{8,0},{12,4},{1,9},{5,13},{9,1},{13,5},{2,10},{6,14},... | collective-permute-start | bytes 393224 | tf_op jit(solution)/shard_map/ppermute | solution.py:35
  97.8 1.9 %collective-permute-start.20 = (bf16[2,128,256]{2,1,0:T(8,128)(2,1)S(1)}, bf16[2,128,256]{2,1,0:T(8,128)(2,1)S(1)}, u32[]{:S(2)}, u32[]{:S(2)}) collective-permute-start(bf16[2,128,256]{2,1,0:T(8,128)(2,1)S(1)} %fusion.31), channel_id=1, source_target_pairs={{0,12},{4,0},{8,4},{12,8},{1,13},{5,1},{9,5},{13,9},{2,14},{6,2},{... | collective-permute-start | bytes 393224 | tf_op jit(solution)/shard_map/ppermute | solution.py:35
  99.9 0.9 collective-permute-start.15
  100.9 3.3 %collective-permute-done.18 = bf16[2,128,256]{2,1,0:T(8,128)(2,1)S(1)} collective-permute-done((bf16[2,128,256]{2,1,0:T(8,128)(2,1)S(1)}, bf16[2,128,256]{2,1,0:T(8,128)(2,1)S(1)}, u32[]{:S(2)}, u32[]{:S(2)}) %collective-permute-start.18) | collective-permute-done | bytes 131104 | tf_op jit(solution)/shard_map/ppermute | solution.py:35
  104.2 0.9 collective-permute-start.24
  105.2 2.1 %collective-permute-start.31 = (bf16[2,128,256]{2,1,0:T(8,128)(2,1)S(1)}, bf16[2,128,256]{2,1,0:T(8,128)(2,1)S(1)}, u32[]{:S(2)}, u32[]{:S(2)}) collective-permute-start(bf16[2,128,256]{2,1,0:T(8,128)(2,1)S(1)} %fusion.27), channel_id=1, source_target_pairs={{0,8},{4,12},{8,0},{12,4},{1,9},{5,13},{9,1},{13,5},{2,10},{6,14},... | collective-permute-start | bytes 393224 | tf_op jit(solution)/shard_map/ppermute | solution.py:35
  107.3 1.5 %collective-permute-start.30 = (bf16[2,128,256]{2,1,0:T(8,128)(2,1)S(1)}, bf16[2,128,256]{2,1,0:T(8,128)(2,1)S(1)}, u32[]{:S(2)}, u32[]{:S(2)}) collective-permute-start(bf16[2,128,256]{2,1,0:T(8,128)(2,1)S(1)} %fusion.27), channel_id=1, source_target_pairs={{0,12},{4,0},{8,4},{12,8},{1,13},{5,1},{9,5},{13,9},{2,14},{6,2},{... | collective-permute-start | bytes 393224 | tf_op jit(solution)/shard_map/ppermute | solution.py:35
  108.8 1.6 %collective-permute-start.21 = (bf16[128,256]{1,0:T(8,128)(2,1)S(1)}, bf16[128,256]{1,0:T(8,128)(2,1)S(1)}, u32[]{:S(2)}, u32[]{:S(2)}) collective-permute-start(bf16[128,256]{1,0:T(8,128)(2,1)S(1)} %slice_bitcast_fusion.2), channel_id=1, source_target_pairs={{0,2},{2,0},{1,3},{3,1},{4,6},{6,4},{5,7},{7,5},{8,10},{10,8},{9,1... | collective-permute-start | bytes 196616 | tf_op jit(solution)/shard_map/ppermute | solution.py:35
  110.4 0.8 maximum_select_fusion.2
  112.5 0.8 collective-permute-start.22
  113.8 3.3 %collective-permute-done.32 = bf16[2,128,256]{2,1,0:T(8,128)(2,1)S(1)} collective-permute-done((bf16[2,128,256]{2,1,0:T(8,128)(2,1)S(1)}, bf16[2,128,256]{2,1,0:T(8,128)(2,1)S(1)}, u32[]{:S(2)}, u32[]{:S(2)}) %collective-permute-start.32) | collective-permute-done | bytes 131104 | tf_op jit(solution)/shard_map/ppermute | solution.py:35
  117.2 1.6 %fusion.7 = bf16[1024,256]{1,0:T(8,128)(2,1)} fusion(bf16[1,2,128,256]{3,2,1,0:T(8,128)(2,1)S(1)} %bitcast.71, bf16[1,2,128,256]{3,2,1,0:T(8,128)(2,1)S(1)} %bitcast.69, bf16[1,2,128,256]{3,2,1,0:T(8,128)(2,1)S(1)} %bitcast.70, bf16[1,2,128,256]{3,2,1,0:T(8,128)(2,1)S(1)} %bitcast.62, bf16[4,1,128,1024]{3,2,0,1:T(8,128)(2,1)S(1)} %bitcast.68, ...), kind=kOutput, calls=%fused_computation.8 | convolution fusion | flops 538968064 | bytes 3145728 | tf_op jit(solution)/shard_map/dot_general | solution.py:402
  118.8 6.4 %all-to-all-start = ((bf16[16,64,256]{2,1,0:T(8,128)(2,1)}), bf16[16,64,256]{2,1,0:T(8,128)(2,1)}, u32[]{:S(2)}, u32[]{:S(2)}) async-start(bf16[16,64,256]{2,1,0:T(8,128)(2,1)} %bitcast.61), calls=%async_computation | async-start | bytes 1048576 | tf_op jit(solution)/shard_map/all_to_all | solution.py:409
  125.6 1.3 fusion.1
  126.9 9.5 %all-to-all-done.in_ref = bf16[16,64,256]{2,1,0:T(8,128)(2,1)} async-done(((bf16[16,64,256]{2,1,0:T(8,128)(2,1)}), bf16[16,64,256]{2,1,0:T(8,128)(2,1)}, u32[]{:S(2)}, u32[]{:S(2)}) %all-to-all-start) | async-done | bytes 524320 | tf_op jit(solution)/shard_map/all_to_all | solution.py:409
  136.4 1.7 %finish.1 = (f32[64,256]{1,0:T(8,128)}, f32[64,256]{1,0:T(8,128)}) custom-call(bf16[16,64,256]{2,1,0:T(8,128)(2,1)} %all-to-all-done.in_ref), custom_call_target="tpu_custom_call" | custom-call | tf_op jit(solution)/shard_map/finish/pallas_call | solution.py:319
  (94 shorter events, 10.0 us)
Async XLA Ops:
  0.6 26.2 %copy-start = (bf16[4096,256]{1,0:T(8,128)(2,1)S(1)}, bf16[4096,256]{1,0:T(8,128)(2,1)}, u32[]{:S(2)}) copy-start(bf16[4096,256]{1,0:T(8,128)(2,1)} %param.18) | copy-start | bytes 6291460
  2.8 2.5 %collective-permute-start = (bf16[128,256]{1,0:T(8,128)(2,1)}, bf16[128,256]{1,0:T(8,128)(2,1)S(1)}, u32[]{:S(2)}, u32[]{:S(2)}) collective-permute-start(bf16[128,256]{1,0:T(8,128)(2,1)} %get-tuple-element.55), channel_id=1, source_target_pairs={{0,2},{2,0},{1,3},{3,1},{4,6},{6,4},{5,7},{7,5},{8,10},{10,8},{9,1... | collective-permute-start | bytes 196616 | tf_op jit(solution)/shard_map/ppermute | solution.py:35
  4.2 11.4 %collective-permute-start.5 = (bf16[128,1024]{1,0:T(8,128)(2,1)}, bf16[128,1024]{1,0:T(8,128)(2,1)S(1)}, u32[]{:S(2)}, u32[]{:S(2)}) collective-permute-start(bf16[128,1024]{1,0:T(8,128)(2,1)} %get-tuple-element.57), channel_id=1, source_target_pairs={{0,2},{2,0},{1,3},{3,1},{4,6},{6,4},{5,7},{7,5},{8,10},{10,8},{9,1... | collective-permute-start | bytes 786440 | tf_op jit(solution)/shard_map/ppermute | solution.py:35
  6.0 7.4 %collective-permute-start.1 = (bf16[2,128,256]{2,1,0:T(8,128)(2,1)}, bf16[2,128,256]{2,1,0:T(8,128)(2,1)S(1)}, u32[]{:S(2)}, u32[]{:S(2)}) collective-permute-start(bf16[2,128,256]{2,1,0:T(8,128)(2,1)} %bitcast_dynamic-update-slice_fusion.1), channel_id=1, source_target_pairs={{0,16},{16,0},{1,17},{17,1},{2,18},{18,2},{3,19},{19,3},{4,20},{20... | collective-permute-start | bytes 393224 | tf_op jit(solution)/shard_map/ppermute | solution.py:35
  14.3 16.5 %copy-start.7 = (bf16[2,2,128,256]{3,2,1,0:T(8,128)(2,1)}, bf16[2,2,128,256]{3,2,1,0:T(8,128)(2,1)S(1)}, u32[]{:S(2)}) copy-start(bf16[2,2,128,256]{3,2,1,0:T(8,128)(2,1)S(1)} %pad_maximum_fusion.2.refs_0_) | copy-start | bytes 786436
  14.3 9.5 %collective-permute-start.4 = (bf16[2,2,128,256]{3,2,1,0:T(8,128)(2,1)S(1)}, bf16[2,2,128,256]{3,2,1,0:T(8,128)(2,1)S(1)}, u32[]{:S(2)}, u32[]{:S(2)}) collective-permute-start(bf16[2,2,128,256]{3,2,1,0:T(8,128)(2,1)S(1)} %pad_maximum_fusion.2.refs_0_), channel_id=1, source_target_pairs={{0,4},{4,8},{8,12},{12,0},{1,5},{5,9},{9,13},{13,1},{2,6},{6,10},{... | collective-permute-start | bytes 786440 | tf_op jit(solution)/shard_map/ppermute | solution.py:35
  16.3 20.4 %collective-permute-start.8 = (bf16[2,128,1024]{2,1,0:T(8,128)(2,1)}, bf16[2,128,1024]{2,1,0:T(8,128)(2,1)}, u32[]{:S(2)}, u32[]{:S(2)}) collective-permute-start(bf16[2,128,1024]{2,1,0:T(8,128)(2,1)} %bitcast_dynamic-update-slice_fusion.refs_4_), channel_id=1, source_target_pairs={{0,32},{32,64},{64,96},{96,0},{1,33},{33,65},{65,97},{97,1},{2,34}... | collective-permute-start | bytes 1572872 | tf_op jit(solution)/shard_map/ppermute | solution.py:35
  17.6 25.0 %collective-permute-start.7 = (bf16[2,128,1024]{2,1,0:T(8,128)(2,1)}, bf16[2,128,1024]{2,1,0:T(8,128)(2,1)}, u32[]{:S(2)}, u32[]{:S(2)}) collective-permute-start(bf16[2,128,1024]{2,1,0:T(8,128)(2,1)} %bitcast_dynamic-update-slice_fusion.refs_4_), channel_id=1, source_target_pairs={{0,64},{32,96},{64,0},{96,32},{1,65},{33,97},{65,1},{97,33},{2,66}... | collective-permute-start | bytes 1572872 | tf_op jit(solution)/shard_map/ppermute | solution.py:35
  20.3 23.8 %collective-permute-start.6 = (bf16[2,128,1024]{2,1,0:T(8,128)(2,1)}, bf16[2,128,1024]{2,1,0:T(8,128)(2,1)}, u32[]{:S(2)}, u32[]{:S(2)}) collective-permute-start(bf16[2,128,1024]{2,1,0:T(8,128)(2,1)} %bitcast_dynamic-update-slice_fusion.refs_4_), channel_id=1, source_target_pairs={{0,96},{32,0},{64,32},{96,64},{1,97},{33,1},{65,33},{97,65},{2,98}... | collective-permute-start | bytes 1572872 | tf_op jit(solution)/shard_map/ppermute | solution.py:35
  21.4 9.4 %collective-permute-start.3 = (bf16[2,2,128,256]{3,2,1,0:T(8,128)(2,1)S(1)}, bf16[2,2,128,256]{3,2,1,0:T(8,128)(2,1)}, u32[]{:S(2)}, u32[]{:S(2)}) collective-permute-start(bf16[2,2,128,256]{3,2,1,0:T(8,128)(2,1)S(1)} %pad_maximum_fusion.2.refs_0_), channel_id=1, source_target_pairs={{0,8},{4,12},{8,0},{12,4},{1,9},{5,13},{9,1},{13,5},{2,10},{6,14},... | collective-permute-start | bytes 786440 | tf_op jit(solution)/shard_map/ppermute | solution.py:35
  23.9 3.0 %copy-start.8 = (bf16[2,2,128,256]{3,2,1,0:T(8,128)(2,1)}, bf16[2,2,128,256]{3,2,1,0:T(8,128)(2,1)S(1)}, u32[]{:S(2)}) copy-start(bf16[2,2,128,256]{3,2,1,0:T(8,128)(2,1)S(1)} %collective-permute-done.4.refs_3_) | copy-start | bytes 786436
  23.9 10.3 %collective-permute-start.2 = (bf16[2,2,128,256]{3,2,1,0:T(8,128)(2,1)S(1)}, bf16[2,2,128,256]{3,2,1,0:T(8,128)(2,1)}, u32[]{:S(2)}, u32[]{:S(2)}) collective-permute-start(bf16[2,2,128,256]{3,2,1,0:T(8,128)(2,1)S(1)} %pad_maximum_fusion.2.refs_0_), channel_id=1, source_target_pairs={{0,12},{4,0},{8,4},{12,8},{1,13},{5,1},{9,5},{13,9},{2,14},{6,2},{... | collective-permute-start | bytes 786440 | tf_op jit(solution)/shard_map/ppermute | solution.py:35
  30.9 25.7 %copy-start.4 = (bf16[128,512]{1,0:T(8,128)(2,1)S(1)}, bf16[128,512]{1,0:T(8,128)(2,1)}, u32[]{:S(2)}) copy-start(bf16[128,512]{1,0:T(8,128)(2,1)} %get-tuple-element.59) | copy-start | bytes 393220
  30.9 69.1 %collective-permute-start.23 = (bf16[2048,256]{1,0:T(8,128)(2,1)S(1)}, bf16[2048,256]{1,0:T(8,128)(2,1)S(1)}, u32[]{:S(2)}, u32[]{:S(2)}) collective-permute-start(bf16[2048,256]{1,0:T(8,128)(2,1)S(1)} %dynamic-slice_select_fusion), channel_id=1, source_target_pairs={{0,1},{1,0},{2,3},{3,2},{4,5},{5,4},{6,7},{7,6},{8,9},{9,8},{10,11... | collective-permute-start | bytes 3145736 | tf_op jit(solution)/shard_map/ppermute | solution.py:35
  34.2 21.7 %collective-permute-start.27 = (bf16[128,512]{1,0:T(8,128)(2,1)}, bf16[128,512]{1,0:T(8,128)(2,1)S(1)}, u32[]{:S(2)}, u32[]{:S(2)}) collective-permute-start(bf16[128,512]{1,0:T(8,128)(2,1)} %get-tuple-element.60), channel_id=1, source_target_pairs={{0,4},{4,8},{8,12},{12,0},{1,5},{5,9},{9,13},{13,1},{2,6},{6,10},{... | collective-permute-start | bytes 393224 | tf_op jit(solution)/shard_map/ppermute | solution.py:35
  36.8 19.2 %collective-permute-start.26 = (bf16[128,512]{1,0:T(8,128)(2,1)}, bf16[128,512]{1,0:T(8,128)(2,1)S(1)}, u32[]{:S(2)}, u32[]{:S(2)}) collective-permute-start(bf16[128,512]{1,0:T(8,128)(2,1)} %get-tuple-element.61), channel_id=1, source_target_pairs={{0,8},{4,12},{8,0},{12,4},{1,9},{5,13},{9,1},{13,5},{2,10},{6,14},... | collective-permute-start | bytes 393224 | tf_op jit(solution)/shard_map/ppermute | solution.py:35
  42.6 13.9 %collective-permute-start.25 = (bf16[128,512]{1,0:T(8,128)(2,1)}, bf16[128,512]{1,0:T(8,128)(2,1)S(1)}, u32[]{:S(2)}, u32[]{:S(2)}) collective-permute-start(bf16[128,512]{1,0:T(8,128)(2,1)} %get-tuple-element.62), channel_id=1, source_target_pairs={{0,12},{4,0},{8,4},{12,8},{1,13},{5,1},{9,5},{13,9},{2,14},{6,2},{... | collective-permute-start | bytes 393224 | tf_op jit(solution)/shard_map/ppermute | solution.py:35
  53.9 4.3 %collective-permute-start.9 = (f32[32,512]{1,0:T(8,128)}, f32[32,512]{1,0:T(8,128)}, u32[]{:S(2)}, u32[]{:S(2)}) collective-permute-start(f32[32,512]{1,0:T(8,128)} %get-tuple-element.65), channel_id=1, source_target_pairs={{0,96},{32,0},{64,32},{96,64},{1,97},{33,1},{65,33},{97,65},{2,98}... | collective-permute-start | bytes 196616 | tf_op jit(solution)/shard_map/ppermute | solution.py:35
  55.8 5.0 %collective-permute-start.10 = (f32[32,512]{1,0:T(8,128)}, f32[32,512]{1,0:T(8,128)}, u32[]{:S(2)}, u32[]{:S(2)}) collective-permute-start(f32[32,512]{1,0:T(8,128)} %get-tuple-element.66), channel_id=1, source_target_pairs={{0,64},{32,96},{64,0},{96,32},{1,65},{33,97},{65,1},{97,33},{2,66}... | collective-permute-start | bytes 196616 | tf_op jit(solution)/shard_map/ppermute | solution.py:35
  55.9 5.3 %collective-permute-start.11 = (f32[32,512]{1,0:T(8,128)}, f32[32,512]{1,0:T(8,128)}, u32[]{:S(2)}, u32[]{:S(2)}) collective-permute-start(f32[32,512]{1,0:T(8,128)} %get-tuple-element.67), channel_id=1, source_target_pairs={{0,32},{32,64},{64,96},{96,0},{1,33},{33,65},{65,97},{97,1},{2,34}... | collective-permute-start | bytes 196616 | tf_op jit(solution)/shard_map/ppermute | solution.py:35
  56.5 0.7 copy-start.5
  57.2 24.5 %collective-permute-start.28 = (bf16[4,128,512]{2,1,0:T(8,128)(2,1)S(1)}, bf16[4,128,512]{2,1,0:T(8,128)(2,1)S(1)}, u32[]{:S(2)}, u32[]{:S(2)}) collective-permute-start(bf16[4,128,512]{2,1,0:T(8,128)(2,1)S(1)} %get-tuple-element.83), channel_id=1, source_target_pairs={{0,1},{1,0},{2,3},{3,2},{4,5},{5,4},{6,7},{7,6},{8,9},{9,8},{10,11... | collective-permute-start | bytes 1572872 | tf_op jit(solution)/shard_map/ppermute | solution.py:35
  76.8 18.3 %collective-permute-start.12 = (bf16[2,128,512]{2,1,0:T(8,128)(2,1)}, bf16[2,128,512]{2,1,0:T(8,128)(2,1)S(1)}, u32[]{:S(2)}, u32[]{:S(2)}) collective-permute-start(bf16[2,128,512]{2,1,0:T(8,128)(2,1)} %get-tuple-element.69), channel_id=1, source_target_pairs={{0,32},{32,64},{64,96},{96,0},{1,33},{33,65},{65,97},{97,1},{2,34}... | collective-permute-start | bytes 786440 | tf_op jit(solution)/shard_map/ppermute | solution.py:35
  76.9 19.5 %collective-permute-start.13 = (bf16[2,128,512]{2,1,0:T(8,128)(2,1)}, bf16[2,128,512]{2,1,0:T(8,128)(2,1)S(1)}, u32[]{:S(2)}, u32[]{:S(2)}) collective-permute-start(bf16[2,128,512]{2,1,0:T(8,128)(2,1)} %get-tuple-element.70), channel_id=1, source_target_pairs={{0,64},{32,96},{64,0},{96,32},{1,65},{33,97},{65,1},{97,33},{2,66}... | collective-permute-start | bytes 786440 | tf_op jit(solution)/shard_map/ppermute | solution.py:35
  79.0 6.9 %collective-permute-start.16 = (bf16[2,2,128,256]{3,2,1,0:T(8,128)(2,1)}, bf16[2,2,128,256]{3,2,1,0:T(8,128)(2,1)S(1)}, u32[]{:S(2)}, u32[]{:S(2)}) collective-permute-start(bf16[2,2,128,256]{3,2,1,0:T(8,128)(2,1)} %get-tuple-element.73), channel_id=1, source_target_pairs={{0,16},{16,0},{1,17},{17,1},{2,18},{18,2},{3,19},{19,3},{4,20},{20... | collective-permute-start | bytes 786440 | tf_op jit(solution)/shard_map/ppermute | solution.py:35
  81.7 4.2 %copy-start.9 = (bf16[2,128,512]{2,1,0:T(8,128)(2,1)S(1)}, bf16[2,128,512]{2,1,0:T(8,128)(2,1)}, u32[]{:S(2)}) copy-start(bf16[2,128,512]{2,1,0:T(8,128)(2,1)} %get-tuple-element.71) | copy-start | bytes 786436
  81.7 5.2 %copy-start.6 = (bf16[4,2,128,256]{3,2,1,0:T(8,128)(2,1)S(1)}, bf16[4,2,128,256]{3,2,1,0:T(8,128)(2,1)}, u32[]{:S(2)}) copy-start(bf16[4,2,128,256]{3,2,1,0:T(8,128)(2,1)} %get-tuple-element.74) | copy-start | bytes 1572868
  81.7 8.3 %collective-permute-start.17 = (bf16[2,2,128,256]{3,2,1,0:T(8,128)(2,1)}, bf16[2,2,128,256]{3,2,1,0:T(8,128)(2,1)S(1)}, u32[]{:S(2)}, u32[]{:S(2)}) collective-permute-start(bf16[2,2,128,256]{3,2,1,0:T(8,128)(2,1)} %get-tuple-element.75), channel_id=1, source_target_pairs={{0,16},{16,0},{1,17},{17,1},{2,18},{18,2},{3,19},{19,3},{4,20},{20... | collective-permute-start | bytes 786440 | tf_op jit(solution)/shard_map/ppermute | solution.py:35
  83.2 16.5 %copy-start.3 = (f32[2,128,512]{2,1,0:T(8,128)S(1)}, f32[2,128,512]{2,1,0:T(8,128)}, u32[]{:S(2)}) copy-start(f32[2,128,512]{2,1,0:T(8,128)} %get-tuple-element.68) | copy-start | bytes 1572868
  85.9 11.9 %collective-permute-start.14 = (bf16[2,128,512]{2,1,0:T(8,128)(2,1)S(1)}, bf16[2,128,512]{2,1,0:T(8,128)(2,1)S(1)}, u32[]{:S(2)}, u32[]{:S(2)}) collective-permute-start(bf16[2,128,512]{2,1,0:T(8,128)(2,1)S(1)} %copy-done.9), channel_id=1, source_target_pairs={{0,96},{32,0},{64,32},{96,64},{1,97},{33,1},{65,33},{97,65},{2,98}... | collective-permute-start | bytes 786440 | tf_op jit(solution)/shard_map/ppermute | solution.py:35
  89.9 27.2 %collective-permute-start.29 = (bf16[4,128,1024]{2,1,0:T(8,128)(2,1)S(1)}, bf16[4,128,1024]{2,1,0:T(8,128)(2,1)S(1)}, u32[]{:S(2)}, u32[]{:S(2)}) collective-permute-start(bf16[4,128,1024]{2,1,0:T(8,128)(2,1)S(1)} %maximum_select_fusion.1), channel_id=1, source_target_pairs={{0,2},{2,0},{1,3},{3,1},{4,6},{6,4},{5,7},{7,5},{8,10},{10,8},{9,1... | collective-permute-start | bytes 3145736 | tf_op jit(solution)/shard_map/ppermute | solution.py:35
  95.0 16.4 %copy-start.1 = (bf16[4096,256]{1,0:T(8,128)(2,1)S(1)}, bf16[4096,256]{1,0:T(8,128)(2,1)}, u32[]{:S(2)}) copy-start(bf16[4096,256]{1,0:T(8,128)(2,1)} %param.18) | copy-start | bytes 6291460
  95.1 10.0 %collective-permute-start.19 = (bf16[2,128,256]{2,1,0:T(8,128)(2,1)S(1)}, bf16[2,128,256]{2,1,0:T(8,128)(2,1)S(1)}, u32[]{:S(2)}, u32[]{:S(2)}) collective-permute-start(bf16[2,128,256]{2,1,0:T(8,128)(2,1)S(1)} %get-tuple-element.81), channel_id=1, source_target_pairs={{0,4},{4,8},{8,12},{12,0},{1,5},{5,9},{9,13},{13,1},{2,6},{6,10},{... | collective-permute-start | bytes 393224 | tf_op jit(solution)/shard_map/ppermute | solution.py:35
  96.4 7.8 %collective-permute-start.18 = (bf16[2,128,256]{2,1,0:T(8,128)(2,1)S(1)}, bf16[2,128,256]{2,1,0:T(8,128)(2,1)S(1)}, u32[]{:S(2)}, u32[]{:S(2)}) collective-permute-start(bf16[2,128,256]{2,1,0:T(8,128)(2,1)S(1)} %get-tuple-element.80), channel_id=1, source_target_pairs={{0,8},{4,12},{8,0},{12,4},{1,9},{5,13},{9,1},{13,5},{2,10},{6,14},... | collective-permute-start | bytes 393224 | tf_op jit(solution)/shard_map/ppermute | solution.py:35
  97.8 7.3 %collective-permute-start.20 = (bf16[2,128,256]{2,1,0:T(8,128)(2,1)S(1)}, bf16[2,128,256]{2,1,0:T(8,128)(2,1)S(1)}, u32[]{:S(2)}, u32[]{:S(2)}) collective-permute-start(bf16[2,128,256]{2,1,0:T(8,128)(2,1)S(1)} %fusion.31), channel_id=1, source_target_pairs={{0,12},{4,0},{8,4},{12,8},{1,13},{5,1},{9,5},{13,9},{2,14},{6,2},{... | collective-permute-start | bytes 393224 | tf_op jit(solution)/shard_map/ppermute | solution.py:35
  99.9 12.1 %copy-start.2 = (bf16[4096,256]{1,0:T(8,128)(2,1)S(1)}, bf16[4096,256]{1,0:T(8,128)(2,1)}, u32[]{:S(2)}) copy-start(bf16[4096,256]{1,0:T(8,128)(2,1)} %param.17) | copy-start | bytes 6291460
  99.9 8.9 %collective-permute-start.15 = (bf16[128,512]{1,0:T(8,128)(2,1)S(1)}, bf16[128,512]{1,0:T(8,128)(2,1)S(1)}, u32[]{:S(2)}, u32[]{:S(2)}) collective-permute-start(bf16[128,512]{1,0:T(8,128)(2,1)S(1)} %get-tuple-element.85), channel_id=1, source_target_pairs={{0,2},{2,0},{1,3},{3,1},{4,6},{6,4},{5,7},{7,5},{8,10},{10,8},{9,1... | collective-permute-start | bytes 393224 | tf_op jit(solution)/shard_map/ppermute | solution.py:35
  104.2 20.9 %collective-permute-start.24 = (bf16[2048,256]{1,0:T(8,128)(2,1)S(1)}, bf16[2048,256]{1,0:T(8,128)(2,1)S(1)}, u32[]{:S(2)}, u32[]{:S(2)}) collective-permute-start(bf16[2048,256]{1,0:T(8,128)(2,1)S(1)} %collective-permute-done.23), channel_id=1, source_target_pairs={{0,2},{2,0},{1,3},{3,1},{4,6},{6,4},{5,7},{7,5},{8,10},{10,8},{9,1... | collective-permute-start | bytes 3145736 | tf_op jit(solution)/shard_map/ppermute | solution.py:35
  105.2 7.3 %collective-permute-start.31 = (bf16[2,128,256]{2,1,0:T(8,128)(2,1)S(1)}, bf16[2,128,256]{2,1,0:T(8,128)(2,1)S(1)}, u32[]{:S(2)}, u32[]{:S(2)}) collective-permute-start(bf16[2,128,256]{2,1,0:T(8,128)(2,1)S(1)} %fusion.27), channel_id=1, source_target_pairs={{0,8},{4,12},{8,0},{12,4},{1,9},{5,13},{9,1},{13,5},{2,10},{6,14},... | collective-permute-start | bytes 393224 | tf_op jit(solution)/shard_map/ppermute | solution.py:35
  107.3 6.6 %collective-permute-start.30 = (bf16[2,128,256]{2,1,0:T(8,128)(2,1)S(1)}, bf16[2,128,256]{2,1,0:T(8,128)(2,1)S(1)}, u32[]{:S(2)}, u32[]{:S(2)}) collective-permute-start(bf16[2,128,256]{2,1,0:T(8,128)(2,1)S(1)} %fusion.27), channel_id=1, source_target_pairs={{0,12},{4,0},{8,4},{12,8},{1,13},{5,1},{9,5},{13,9},{2,14},{6,2},{... | collective-permute-start | bytes 393224 | tf_op jit(solution)/shard_map/ppermute | solution.py:35
  108.8 2.5 %collective-permute-start.21 = (bf16[128,256]{1,0:T(8,128)(2,1)S(1)}, bf16[128,256]{1,0:T(8,128)(2,1)S(1)}, u32[]{:S(2)}, u32[]{:S(2)}) collective-permute-start(bf16[128,256]{1,0:T(8,128)(2,1)S(1)} %slice_bitcast_fusion.2), channel_id=1, source_target_pairs={{0,2},{2,0},{1,3},{3,1},{4,6},{6,4},{5,7},{7,5},{8,10},{10,8},{9,1... | collective-permute-start | bytes 196616 | tf_op jit(solution)/shard_map/ppermute | solution.py:35
  111.3 5.9 %collective-permute-start.32 = (bf16[2,128,256]{2,1,0:T(8,128)(2,1)S(1)}, bf16[2,128,256]{2,1,0:T(8,128)(2,1)S(1)}, u32[]{:S(2)}, u32[]{:S(2)}) collective-permute-start(bf16[2,128,256]{2,1,0:T(8,128)(2,1)S(1)} %fusion.27), channel_id=1, source_target_pairs={{0,4},{4,8},{8,12},{12,0},{1,5},{5,9},{9,13},{13,1},{2,6},{6,10},{... | collective-permute-start | bytes 393224 | tf_op jit(solution)/shard_map/ppermute | solution.py:35
  112.5 12.6 %collective-permute-start.22 = (bf16[128,512]{1,0:T(8,128)(2,1)S(1)}, bf16[128,512]{1,0:T(8,128)(2,1)S(1)}, u32[]{:S(2)}, u32[]{:S(2)}) collective-permute-start(bf16[128,512]{1,0:T(8,128)(2,1)S(1)} %pad_maximum_fusion.3), channel_id=1, source_target_pairs={{0,1},{1,0},{2,3},{3,2},{4,5},{5,4},{6,7},{7,6},{8,9},{9,8},{10,11... | collective-permute-start | bytes 393224 | tf_op jit(solution)/shard_map/ppermute | solution.py:35
  118.8 17.7 %all-to-all-start = ((bf16[16,64,256]{2,1,0:T(8,128)(2,1)}), bf16[16,64,256]{2,1,0:T(8,128)(2,1)}, u32[]{:S(2)}, u32[]{:S(2)}) async-start(bf16[16,64,256]{2,1,0:T(8,128)(2,1)} %bitcast.61), calls=%async_computation | async-start | bytes 1048576 | tf_op jit(solution)/shard_map/all_to_all | solution.py:409

commit v7 on v6

--- a/solution.py
+++ b/solution.py
@@ -305,18 +305,29 @@
     )(layer_input)
 
 
-def finish_kernel(in_ref, k_ref, v_ref):
+def finish_kernel(in_ref, k_ref, v_ref, got, sem):
+    copies = [pltpu.make_async_copy(in_ref.at[n], got.at[n], sem.at[n]) for n in range(16)]
+    for copy in copies:
+        copy.start()
+    for copy in copies:
+        copy.wait()
     for h in range(2):
-        total = in_ref[h].astype(F32)
+        total = got[h].astype(F32)
         for n in range(1, 8):
-            total = total + in_ref[2 * n + h].astype(F32)
+            total = total + got[2 * n + h].astype(F32)
         k_ref[:, h * HEAD : (h + 1) * HEAD] = total[:, :HEAD]
         v_ref[:, h * HEAD : (h + 1) * HEAD] = total[:, HEAD:]
 
 
 def run_finish(got):
     out = jax.ShapeDtypeStruct((HEAD // 2, 2 * HEAD), F32)
-    return pl.pallas_call(finish_kernel, out_shape=[out, out], name="finish")(got)
+    return pl.pallas_call(
+        finish_kernel,
+        out_shape=[out, out],
+        in_specs=[pl.BlockSpec(memory_space=pl.ANY)],
+        scratch_shapes=[pltpu.VMEM((16, HEAD // 2, 2 * HEAD), BF), pltpu.SemaphoreType.DMA((16,))],
+        name="finish",
+    )(got)
 
 
 def positions(run_placement, y, z, x, c):

time: 139 us -> 139 us (level)
  no operation moved by 1% of the time
where the time goes in v7:
time: 139 us; the launch traced here: 138 us
  starting transfers between devices  55.5 us (40%)
  waiting for transfers between devices  35.8 us (26%)
  Pallas kernels  31.3 us (23%)
  matrix products  5.39 us (4%)
  other arithmetic  5.38 us (4%)
  local copies, waits for them, and re-layouts  3.98 us (3%)
    ppermute x33, starting transfers between devices, moved(): return lax.ppermute(array, axis, [(i, (i + by) % n) for i in range(n)])  49.1 us
    ppermute x33, waiting for transfers between devices, moved(): return lax.ppermute(array, axis, [(i, (i + by) % n) for i in range(n)])  26.4 us
    pallas_call x1, Pallas kernels, run_grads(): pl.pallas_call(grads_kernel, out_shape=dkv + dq, in_specs=in_places(6), o...  15.5 us
    pallas_call x1, Pallas kernels, run_stats(): pl.pallas_call(stats_kernel, out_shape=[jax.ShapeDtypeStruct((PARTS * 4,...  9.76 us
    all_to_all x1, waiting for transfers between devices, step(): got = lax.all_to_all(pieces, ('y', 'z', 'c'), 0, 0, tiled=True)  9.5 us
    all_to_all x1, starting transfers between devices, step(): got = lax.all_to_all(pieces, ('y', 'z', 'c'), 0, 0, tiled=True)  6.35 us
  transfers between devices with their start and end apart: 34, of which 14 were waited for; matrix products, arithmetic and copies ran while one was open for 10% of the time, Pallas kernels for 20%

profile of v7, /device:TPU:1, one launch (start us, length us, event | category | flops | bytes accessed | tf_op | source)
XLA Modules:
  0.0 138.4 jit_solution(11522985595396293505)
XLA Ops:
  0.6 2.2 %pack.1 = (bf16[2,128,256]{2,1,0:T(8,128)(2,1)}, bf16[2,128,1024]{2,1,0:T(8,128)(2,1)}, bf16[128,256]{1,0:T(8,128)(2,1)}, bf16[128,1024]{1,0:T(8,128)(2,1)}) custom-call(bf16[128,1024]{1,0:T(8,128)(2,1)} %q_ref.1, bf16[128,1024]{1,0:T(8,128)(2,1)} %g_ref.1, bf16[128,256]{1,0:T(8,128)(2,1)} %k_ref.1, bf16[128,256]{1,0:T(8,128)(2,1)} %v_ref.1), custom_call_target="tpu_custom_call" | custom-call | tf_op jit(solution)/shard_map/pack/pallas_call | solution.py:282
  2.8 1.4 collective-permute-start
  6.0 3.7 %collective-permute-start.1 = (bf16[2,128,256]{2,1,0:T(8,128)(2,1)}, bf16[2,128,256]{2,1,0:T(8,128)(2,1)S(1)}, u32[]{:S(2)}, u32[]{:S(2)}) collective-permute-start(bf16[2,128,256]{2,1,0:T(8,128)(2,1)} %bitcast_dynamic-update-slice_fusion.1), channel_id=1, source_target_pairs={{0,16},{16,0},{1,17},{17,1},{2,18},{18,2},{3,19},{19,3},{4,20},{20... | collective-permute-start | bytes 393224 | tf_op jit(solution)/shard_map/ppermute | solution.py:35
  9.7 3.7 %collective-permute-done.1 = bf16[2,128,256]{2,1,0:T(8,128)(2,1)S(1)} collective-permute-done((bf16[2,128,256]{2,1,0:T(8,128)(2,1)}, bf16[2,128,256]{2,1,0:T(8,128)(2,1)S(1)}, u32[]{:S(2)}, u32[]{:S(2)}) %collective-permute-start.1) | collective-permute-done | bytes 131104 | tf_op jit(solution)/shard_map/ppermute | solution.py:35
  13.4 0.9 pad_maximum_fusion.2.refs_0_
  14.3 1.3 collective-permute-start.4
  16.3 1.3 collective-permute-start.8
  17.6 2.6 %collective-permute-start.7 = (bf16[2,128,1024]{2,1,0:T(8,128)(2,1)}, bf16[2,128,1024]{2,1,0:T(8,128)(2,1)}, u32[]{:S(2)}, u32[]{:S(2)}) collective-permute-start(bf16[2,128,1024]{2,1,0:T(8,128)(2,1)} %bitcast_dynamic-update-slice_fusion.refs_4_), channel_id=1, source_target_pairs={{0,64},{32,96},{64,0},{96,32},{1,65},{33,97},{65,1},{97,33},{2,66}... | collective-permute-start | bytes 1572872 | tf_op jit(solution)/shard_map/ppermute | solution.py:35
  20.3 1.1 collective-permute-start.6
  21.4 2.5 %collective-permute-start.3 = (bf16[2,2,128,256]{3,2,1,0:T(8,128)(2,1)S(1)}, bf16[2,2,128,256]{3,2,1,0:T(8,128)(2,1)}, u32[]{:S(2)}, u32[]{:S(2)}) collective-permute-start(bf16[2,2,128,256]{3,2,1,0:T(8,128)(2,1)S(1)} %pad_maximum_fusion.2.refs_0_), channel_id=1, source_target_pairs={{0,8},{4,12},{8,0},{12,4},{1,9},{5,13},{9,1},{13,5},{2,10},{6,14},... | collective-permute-start | bytes 786440 | tf_op jit(solution)/shard_map/ppermute | solution.py:35
  23.9 1.2 collective-permute-start.2
  25.0 1.1 convolution_add_fusion.2
  26.8 1.5 %dynamic-slice_select_fusion = bf16[2048,256]{1,0:T(8,128)(2,1)S(1)} fusion(bf16[4096,256]{1,0:T(8,128)(2,1)S(1)} %copy-done, s32[]{:T(128)S(6)} %select_n.157, bf16[4096,256]{1,0:T(8,128)(2,1)} %param.17, pred[]{:T(512)S(6)} %eq.50), kind=kLoop, calls=%fused_computation.16 | loop fusion | flops 524288 | bytes 3145733 | tf_op jit(solution)/shard_map/jit(_where)/select_n | solution.py:377
  28.9 1.9 %columns.1 = (bf16[128,512]{1,0:T(8,128)(2,1)}, bf16[128,512]{1,0:T(8,128)(2,1)}, bf16[128,512]{1,0:T(8,128)(2,1)}, bf16[128,512]{1,0:T(8,128)(2,1)}) custom-call(bf16[128,2048]{1,0:T(8,128)(2,1)} %in_ref), custom_call_target="tpu_custom_call" | custom-call | tf_op jit(solution)/shard_map/columns/pallas_call | solution.py:300
  30.9 0.8 collective-permute-start.23
  31.7 2.5 %collective-permute-done.2.refs_1_ = bf16[2,2,128,256]{3,2,1,0:T(8,128)(2,1)} collective-permute-done((bf16[2,2,128,256]{3,2,1,0:T(8,128)(2,1)S(1)}, bf16[2,2,128,256]{3,2,1,0:T(8,128)(2,1)}, u32[]{:S(2)}, u32[]{:S(2)}) %collective-permute-start.2) | collective-permute-done | bytes 262176 | tf_op jit(solution)/shard_map/ppermute | solution.py:35
  34.2 2.6 %collective-permute-start.27 = (bf16[128,512]{1,0:T(8,128)(2,1)}, bf16[128,512]{1,0:T(8,128)(2,1)S(1)}, u32[]{:S(2)}, u32[]{:S(2)}) collective-permute-start(bf16[128,512]{1,0:T(8,128)(2,1)} %get-tuple-element.60), channel_id=1, source_target_pairs={{0,4},{4,8},{8,12},{12,0},{1,5},{5,9},{9,13},{13,1},{2,6},{6,10},{... | collective-permute-start | bytes 393224 | tf_op jit(solution)/shard_map/ppermute | solution.py:35
  36.8 2.1 %collective-permute-start.26 = (bf16[128,512]{1,0:T(8,128)(2,1)}, bf16[128,512]{1,0:T(8,128)(2,1)S(1)}, u32[]{:S(2)}, u32[]{:S(2)}) collective-permute-start(bf16[128,512]{1,0:T(8,128)(2,1)} %get-tuple-element.61), channel_id=1, source_target_pairs={{0,8},{4,12},{8,0},{12,4},{1,9},{5,13},{9,1},{13,5},{2,10},{6,14},... | collective-permute-start | bytes 393224 | tf_op jit(solution)/shard_map/ppermute | solution.py:35
  38.9 3.8 %collective-permute-done.7.refs_6_ = bf16[2,128,1024]{2,1,0:T(8,128)(2,1)} collective-permute-done((bf16[2,128,1024]{2,1,0:T(8,128)(2,1)}, bf16[2,128,1024]{2,1,0:T(8,128)(2,1)}, u32[]{:S(2)}, u32[]{:S(2)}) %collective-permute-start.7) | collective-permute-done | bytes 524320 | tf_op jit(solution)/shard_map/ppermute | solution.py:35
  42.6 1.5 %collective-permute-start.25 = (bf16[128,512]{1,0:T(8,128)(2,1)}, bf16[128,512]{1,0:T(8,128)(2,1)S(1)}, u32[]{:S(2)}, u32[]{:S(2)}) collective-permute-start(bf16[128,512]{1,0:T(8,128)(2,1)} %get-tuple-element.62), channel_id=1, source_target_pairs={{0,12},{4,0},{8,4},{12,8},{1,13},{5,1},{9,5},{13,9},{2,14},{6,2},{... | collective-permute-start | bytes 393224 | tf_op jit(solution)/shard_map/ppermute | solution.py:35
  44.1 9.8 %stats.1 = (f32[32,512]{1,0:T(8,128)}, f32[32,512]{1,0:T(8,128)}, f32[32,512]{1,0:T(8,128)}, f32[32,512]{1,0:T(8,128)}) custom-call(bf16[2,2,128,256]{3,2,1,0:T(8,128)(2,1)} %copy-done.7, bf16[2,2,128,256]{3,2,1,0:T(8,128)(2,1)} %collective-permute-done.2.refs_1_, bf16[2,2,128,256]{3,2,1,0:T(8,128)(2,1)} %collective-permute-done.3.refs_2_, ...), custom_call_target="tpu_custom_call" | custom-call | flops 6000000000 | bytes 3000000 | tf_op jit(solution)/shard_map/stats/pallas_call | solution.py:223
  53.9 2.0 %collective-permute-start.9 = (f32[32,512]{1,0:T(8,128)}, f32[32,512]{1,0:T(8,128)}, u32[]{:S(2)}, u32[]{:S(2)}) collective-permute-start(f32[32,512]{1,0:T(8,128)} %get-tuple-element.65), channel_id=1, source_target_pairs={{0,96},{32,0},{64,32},{96,64},{1,97},{33,1},{65,33},{97,65},{2,98}... | collective-permute-start | bytes 196616 | tf_op jit(solution)/shard_map/ppermute | solution.py:35
  58.1 2.8 %collective-permute-done.10.refs_12_ = f32[32,512]{1,0:T(8,128)} collective-permute-done((f32[32,512]{1,0:T(8,128)}, f32[32,512]{1,0:T(8,128)}, u32[]{:S(2)}, u32[]{:S(2)}) %collective-permute-start.10) | collective-permute-done | bytes 65568 | tf_op jit(solution)/shard_map/ppermute | solution.py:35
  61.3 15.5 %grads.1 = (bf16[4,2,128,256]{3,2,1,0:T(8,128)(2,1)}, bf16[2,2,128,256]{3,2,1,0:T(8,128)(2,1)}, bf16[2,2,128,256]{3,2,1,0:T(8,128)(2,1)}, f32[2,128,512]{2,1,0:T...) custom-call(bf16[2,2,128,256]{3,2,1,0:T(8,128)(2,1)} %copy-done.7, ...), custom_call_target="tpu_custom_call" | custom-call | flops 12000000000 | bytes 6000000 | tf_op jit(solution)/shard_map/grads/pallas_call | solution.py:239
  76.9 2.1 %collective-permute-start.13 = (bf16[2,128,512]{2,1,0:T(8,128)(2,1)}, bf16[2,128,512]{2,1,0:T(8,128)(2,1)S(1)}, u32[]{:S(2)}, u32[]{:S(2)}) collective-permute-start(bf16[2,128,512]{2,1,0:T(8,128)(2,1)} %get-tuple-element.70), channel_id=1, source_target_pairs={{0,64},{32,96},{64,0},{96,32},{1,65},{33,97},{65,1},{97,33},{2,66}... | collective-permute-start | bytes 786440 | tf_op jit(solution)/shard_map/ppermute | solution.py:35
  79.0 2.7 %collective-permute-start.16 = (bf16[2,2,128,256]{3,2,1,0:T(8,128)(2,1)}, bf16[2,2,128,256]{3,2,1,0:T(8,128)(2,1)S(1)}, u32[]{:S(2)}, u32[]{:S(2)}) collective-permute-start(bf16[2,2,128,256]{3,2,1,0:T(8,128)(2,1)} %get-tuple-element.73), channel_id=1, source_target_pairs={{0,16},{16,0},{1,17},{17,1},{2,18},{18,2},{3,19},{19,3},{4,20},{20... | collective-permute-start | bytes 786440 | tf_op jit(solution)/shard_map/ppermute | solution.py:35
  81.9 1.3 maximum_select_fusion.1
  83.6 2.3 %collective-permute-done.16 = bf16[2,2,128,256]{3,2,1,0:T(8,128)(2,1)S(1)} collective-permute-done((bf16[2,2,128,256]{3,2,1,0:T(8,128)(2,1)}, bf16[2,2,128,256]{3,2,1,0:T(8,128)(2,1)S(1)}, u32[]{:S(2)}, u32[]{:S(2)}) %collective-permute-start.16) | collective-permute-done | bytes 262176 | tf_op jit(solution)/shard_map/ppermute | solution.py:35
  85.9 1.0 collective-permute-start.14
  86.9 3.0 %collective-permute-done.17 = bf16[2,2,128,256]{3,2,1,0:T(8,128)(2,1)S(1)} collective-permute-done((bf16[2,2,128,256]{3,2,1,0:T(8,128)(2,1)}, bf16[2,2,128,256]{3,2,1,0:T(8,128)(2,1)S(1)}, u32[]{:S(2)}, u32[]{:S(2)}) %collective-permute-start.17) | collective-permute-done | bytes 262176 | tf_op jit(solution)/shard_map/ppermute | solution.py:35
  89.9 5.1 %collective-permute-start.29 = (bf16[4,128,1024]{2,1,0:T(8,128)(2,1)S(1)}, bf16[4,128,1024]{2,1,0:T(8,128)(2,1)S(1)}, u32[]{:S(2)}, u32[]{:S(2)}) collective-permute-start(bf16[4,128,1024]{2,1,0:T(8,128)(2,1)S(1)} %maximum_select_fusion.1), channel_id=1, source_target_pairs={{0,2},{2,0},{1,3},{3,1},{4,6},{6,4},{5,7},{7,5},{8,10},{10,8},{9,1... | collective-permute-start | bytes 3145736 | tf_op jit(solution)/shard_map/ppermute | solution.py:35
  95.1 1.3 collective-permute-start.19
  96.4 1.4 %collective-permute-start.18 = (bf16[2,128,256]{2,1,0:T(8,128)(2,1)S(1)}, bf16[2,128,256]{2,1,0:T(8,128)(2,1)S(1)}, u32[]{:S(2)}, u32[]{:S(2)}) collective-permute-start(bf16[2,128,256]{2,1,0:T(8,128)(2,1)S(1)} %get-tuple-element.80), channel_id=1, source_target_pairs={{0,8},{4,12},{8,0},{12,4},{1,9},{5,13},{9,1},{13,5},{2,10},{6,14},... | collective-permute-start | bytes 393224 | tf_op jit(solution)/shard_map/ppermute | solution.py:35
  97.8 1.9 %collective-permute-start.20 = (bf16[2,128,256]{2,1,0:T(8,128)(2,1)S(1)}, bf16[2,128,256]{2,1,0:T(8,128)(2,1)S(1)}, u32[]{:S(2)}, u32[]{:S(2)}) collective-permute-start(bf16[2,128,256]{2,1,0:T(8,128)(2,1)S(1)} %fusion.31), channel_id=1, source_target_pairs={{0,12},{4,0},{8,4},{12,8},{1,13},{5,1},{9,5},{13,9},{2,14},{6,2},{... | collective-permute-start | bytes 393224 | tf_op jit(solution)/shard_map/ppermute | solution.py:35
  99.9 0.9 collective-permute-start.15
  100.9 3.3 %collective-permute-done.18 = bf16[2,128,256]{2,1,0:T(8,128)(2,1)S(1)} collective-permute-done((bf16[2,128,256]{2,1,0:T(8,128)(2,1)S(1)}, bf16[2,128,256]{2,1,0:T(8,128)(2,1)S(1)}, u32[]{:S(2)}, u32[]{:S(2)}) %collective-permute-start.18) | collective-permute-done | bytes 131104 | tf_op jit(solution)/shard_map/ppermute | solution.py:35
  104.2 0.9 collective-permute-start.24
  105.2 2.1 %collective-permute-start.31 = (bf16[2,128,256]{2,1,0:T(8,128)(2,1)S(1)}, bf16[2,128,256]{2,1,0:T(8,128)(2,1)S(1)}, u32[]{:S(2)}, u32[]{:S(2)}) collective-permute-start(bf16[2,128,256]{2,1,0:T(8,128)(2,1)S(1)} %fusion.27), channel_id=1, source_target_pairs={{0,8},{4,12},{8,0},{12,4},{1,9},{5,13},{9,1},{13,5},{2,10},{6,14},... | collective-permute-start | bytes 393224 | tf_op jit(solution)/shard_map/ppermute | solution.py:35
  107.3 1.5 %collective-permute-start.30 = (bf16[2,128,256]{2,1,0:T(8,128)(2,1)S(1)}, bf16[2,128,256]{2,1,0:T(8,128)(2,1)S(1)}, u32[]{:S(2)}, u32[]{:S(2)}) collective-permute-start(bf16[2,128,256]{2,1,0:T(8,128)(2,1)S(1)} %fusion.27), channel_id=1, source_target_pairs={{0,12},{4,0},{8,4},{12,8},{1,13},{5,1},{9,5},{13,9},{2,14},{6,2},{... | collective-permute-start | bytes 393224 | tf_op jit(solution)/shard_map/ppermute | solution.py:35
  108.8 1.6 %collective-permute-start.21 = (bf16[128,256]{1,0:T(8,128)(2,1)S(1)}, bf16[128,256]{1,0:T(8,128)(2,1)S(1)}, u32[]{:S(2)}, u32[]{:S(2)}) collective-permute-start(bf16[128,256]{1,0:T(8,128)(2,1)S(1)} %slice_bitcast_fusion.2), channel_id=1, source_target_pairs={{0,2},{2,0},{1,3},{3,1},{4,6},{6,4},{5,7},{7,5},{8,10},{10,8},{9,1... | collective-permute-start | bytes 196616 | tf_op jit(solution)/shard_map/ppermute | solution.py:35
  110.4 0.8 maximum_select_fusion.2
  112.5 0.8 collective-permute-start.22
  113.8 3.3 %collective-permute-done.32 = bf16[2,128,256]{2,1,0:T(8,128)(2,1)S(1)} collective-permute-done((bf16[2,128,256]{2,1,0:T(8,128)(2,1)S(1)}, bf16[2,128,256]{2,1,0:T(8,128)(2,1)S(1)}, u32[]{:S(2)}, u32[]{:S(2)}) %collective-permute-start.32) | collective-permute-done | bytes 131104 | tf_op jit(solution)/shard_map/ppermute | solution.py:35
  117.2 1.6 %fusion.7 = bf16[1024,256]{1,0:T(8,128)(2,1)} fusion(bf16[1,2,128,256]{3,2,1,0:T(8,128)(2,1)S(1)} %bitcast.71, bf16[1,2,128,256]{3,2,1,0:T(8,128)(2,1)S(1)} %bitcast.69, bf16[1,2,128,256]{3,2,1,0:T(8,128)(2,1)S(1)} %bitcast.70, bf16[1,2,128,256]{3,2,1,0:T(8,128)(2,1)S(1)} %bitcast.62, bf16[4,1,128,1024]{3,2,0,1:T(8,128)(2,1)S(1)} %bitcast.68, ...), kind=kOutput, calls=%fused_computation.8 | convolution fusion | flops 538968064 | bytes 3145728 | tf_op jit(solution)/shard_map/dot_general | solution.py:413
  118.8 6.4 %all-to-all-start = ((bf16[16,64,256]{2,1,0:T(8,128)(2,1)}), bf16[16,64,256]{2,1,0:T(8,128)(2,1)}, u32[]{:S(2)}, u32[]{:S(2)}) async-start(bf16[16,64,256]{2,1,0:T(8,128)(2,1)} %bitcast.61), calls=%async_computation | async-start | bytes 1048576 | tf_op jit(solution)/shard_map/all_to_all | solution.py:420
  125.6 1.3 fusion.1
  126.9 9.5 %all-to-all-done.in_ref = bf16[16,64,256]{2,1,0:T(8,128)(2,1)} async-done(((bf16[16,64,256]{2,1,0:T(8,128)(2,1)}), bf16[16,64,256]{2,1,0:T(8,128)(2,1)}, u32[]{:S(2)}, u32[]{:S(2)}) %all-to-all-start) | async-done | bytes 524320 | tf_op jit(solution)/shard_map/all_to_all | solution.py:420
  136.4 1.8 %finish.1 = (f32[64,256]{1,0:T(8,128)}, f32[64,256]{1,0:T(8,128)}) custom-call(bf16[16,64,256]{2,1,0:T(8,128)(2,1)} %all-to-all-done.in_ref), custom_call_target="tpu_custom_call" | custom-call | tf_op jit(solution)/shard_map/finish/pallas_call | solution.py:324
  (94 shorter events, 10.0 us)
Async XLA Ops:
  0.6 26.2 %copy-start = (bf16[4096,256]{1,0:T(8,128)(2,1)S(1)}, bf16[4096,256]{1,0:T(8,128)(2,1)}, u32[]{:S(2)}) copy-start(bf16[4096,256]{1,0:T(8,128)(2,1)} %param.18) | copy-start | bytes 6291460
  2.8 2.5 %collective-permute-start = (bf16[128,256]{1,0:T(8,128)(2,1)}, bf16[128,256]{1,0:T(8,128)(2,1)S(1)}, u32[]{:S(2)}, u32[]{:S(2)}) collective-permute-start(bf16[128,256]{1,0:T(8,128)(2,1)} %get-tuple-element.55), channel_id=1, source_target_pairs={{0,2},{2,0},{1,3},{3,1},{4,6},{6,4},{5,7},{7,5},{8,10},{10,8},{9,1... | collective-permute-start | bytes 196616 | tf_op jit(solution)/shard_map/ppermute | solution.py:35
  4.2 11.4 %collective-permute-start.5 = (bf16[128,1024]{1,0:T(8,128)(2,1)}, bf16[128,1024]{1,0:T(8,128)(2,1)S(1)}, u32[]{:S(2)}, u32[]{:S(2)}) collective-permute-start(bf16[128,1024]{1,0:T(8,128)(2,1)} %get-tuple-element.57), channel_id=1, source_target_pairs={{0,2},{2,0},{1,3},{3,1},{4,6},{6,4},{5,7},{7,5},{8,10},{10,8},{9,1... | collective-permute-start | bytes 786440 | tf_op jit(solution)/shard_map/ppermute | solution.py:35
  6.0 7.4 %collective-permute-start.1 = (bf16[2,128,256]{2,1,0:T(8,128)(2,1)}, bf16[2,128,256]{2,1,0:T(8,128)(2,1)S(1)}, u32[]{:S(2)}, u32[]{:S(2)}) collective-permute-start(bf16[2,128,256]{2,1,0:T(8,128)(2,1)} %bitcast_dynamic-update-slice_fusion.1), channel_id=1, source_target_pairs={{0,16},{16,0},{1,17},{17,1},{2,18},{18,2},{3,19},{19,3},{4,20},{20... | collective-permute-start | bytes 393224 | tf_op jit(solution)/shard_map/ppermute | solution.py:35
  14.3 16.5 %copy-start.7 = (bf16[2,2,128,256]{3,2,1,0:T(8,128)(2,1)}, bf16[2,2,128,256]{3,2,1,0:T(8,128)(2,1)S(1)}, u32[]{:S(2)}) copy-start(bf16[2,2,128,256]{3,2,1,0:T(8,128)(2,1)S(1)} %pad_maximum_fusion.2.refs_0_) | copy-start | bytes 786436
  14.3 9.5 %collective-permute-start.4 = (bf16[2,2,128,256]{3,2,1,0:T(8,128)(2,1)S(1)}, bf16[2,2,128,256]{3,2,1,0:T(8,128)(2,1)S(1)}, u32[]{:S(2)}, u32[]{:S(2)}) collective-permute-start(bf16[2,2,128,256]{3,2,1,0:T(8,128)(2,1)S(1)} %pad_maximum_fusion.2.refs_0_), channel_id=1, source_target_pairs={{0,4},{4,8},{8,12},{12,0},{1,5},{5,9},{9,13},{13,1},{2,6},{6,10},{... | collective-permute-start | bytes 786440 | tf_op jit(solution)/shard_map/ppermute | solution.py:35
  16.3 20.4 %collective-permute-start.8 = (bf16[2,128,1024]{2,1,0:T(8,128)(2,1)}, bf16[2,128,1024]{2,1,0:T(8,128)(2,1)}, u32[]{:S(2)}, u32[]{:S(2)}) collective-permute-start(bf16[2,128,1024]{2,1,0:T(8,128)(2,1)} %bitcast_dynamic-update-slice_fusion.refs_4_), channel_id=1, source_target_pairs={{0,32},{32,64},{64,96},{96,0},{1,33},{33,65},{65,97},{97,1},{2,34}... | collective-permute-start | bytes 1572872 | tf_op jit(solution)/shard_map/ppermute | solution.py:35
  17.6 25.0 %collective-permute-start.7 = (bf16[2,128,1024]{2,1,0:T(8,128)(2,1)}, bf16[2,128,1024]{2,1,0:T(8,128)(2,1)}, u32[]{:S(2)}, u32[]{:S(2)}) collective-permute-start(bf16[2,128,1024]{2,1,0:T(8,128)(2,1)} %bitcast_dynamic-update-slice_fusion.refs_4_), channel_id=1, source_target_pairs={{0,64},{32,96},{64,0},{96,32},{1,65},{33,97},{65,1},{97,33},{2,66}... | collective-permute-start | bytes 1572872 | tf_op jit(solution)/shard_map/ppermute | solution.py:35
  20.3 23.8 %collective-permute-start.6 = (bf16[2,128,1024]{2,1,0:T(8,128)(2,1)}, bf16[2,128,1024]{2,1,0:T(8,128)(2,1)}, u32[]{:S(2)}, u32[]{:S(2)}) collective-permute-start(bf16[2,128,1024]{2,1,0:T(8,128)(2,1)} %bitcast_dynamic-update-slice_fusion.refs_4_), channel_id=1, source_target_pairs={{0,96},{32,0},{64,32},{96,64},{1,97},{33,1},{65,33},{97,65},{2,98}... | collective-permute-start | bytes 1572872 | tf_op jit(solution)/shard_map/ppermute | solution.py:35
  21.4 9.4 %collective-permute-start.3 = (bf16[2,2,128,256]{3,2,1,0:T(8,128)(2,1)S(1)}, bf16[2,2,128,256]{3,2,1,0:T(8,128)(2,1)}, u32[]{:S(2)}, u32[]{:S(2)}) collective-permute-start(bf16[2,2,128,256]{3,2,1,0:T(8,128)(2,1)S(1)} %pad_maximum_fusion.2.refs_0_), channel_id=1, source_target_pairs={{0,8},{4,12},{8,0},{12,4},{1,9},{5,13},{9,1},{13,5},{2,10},{6,14},... | collective-permute-start | bytes 786440 | tf_op jit(solution)/shard_map/ppermute | solution.py:35
  23.9 3.0 %copy-start.8 = (bf16[2,2,128,256]{3,2,1,0:T(8,128)(2,1)}, bf16[2,2,128,256]{3,2,1,0:T(8,128)(2,1)S(1)}, u32[]{:S(2)}) copy-start(bf16[2,2,128,256]{3,2,1,0:T(8,128)(2,1)S(1)} %collective-permute-done.4.refs_3_) | copy-start | bytes 786436
  23.9 10.3 %collective-permute-start.2 = (bf16[2,2,128,256]{3,2,1,0:T(8,128)(2,1)S(1)}, bf16[2,2,128,256]{3,2,1,0:T(8,128)(2,1)}, u32[]{:S(2)}, u32[]{:S(2)}) collective-permute-start(bf16[2,2,128,256]{3,2,1,0:T(8,128)(2,1)S(1)} %pad_maximum_fusion.2.refs_0_), channel_id=1, source_target_pairs={{0,12},{4,0},{8,4},{12,8},{1,13},{5,1},{9,5},{13,9},{2,14},{6,2},{... | collective-permute-start | bytes 786440 | tf_op jit(solution)/shard_map/ppermute | solution.py:35
  30.9 25.7 %copy-start.4 = (bf16[128,512]{1,0:T(8,128)(2,1)S(1)}, bf16[128,512]{1,0:T(8,128)(2,1)}, u32[]{:S(2)}) copy-start(bf16[128,512]{1,0:T(8,128)(2,1)} %get-tuple-element.59) | copy-start | bytes 393220
  30.9 69.1 %collective-permute-start.23 = (bf16[2048,256]{1,0:T(8,128)(2,1)S(1)}, bf16[2048,256]{1,0:T(8,128)(2,1)S(1)}, u32[]{:S(2)}, u32[]{:S(2)}) collective-permute-start(bf16[2048,256]{1,0:T(8,128)(2,1)S(1)} %dynamic-slice_select_fusion), channel_id=1, source_target_pairs={{0,1},{1,0},{2,3},{3,2},{4,5},{5,4},{6,7},{7,6},{8,9},{9,8},{10,11... | collective-permute-start | bytes 3145736 | tf_op jit(solution)/shard_map/ppermute | solution.py:35
  34.2 21.7 %collective-permute-start.27 = (bf16[128,512]{1,0:T(8,128)(2,1)}, bf16[128,512]{1,0:T(8,128)(2,1)S(1)}, u32[]{:S(2)}, u32[]{:S(2)}) collective-permute-start(bf16[128,512]{1,0:T(8,128)(2,1)} %get-tuple-element.60), channel_id=1, source_target_pairs={{0,4},{4,8},{8,12},{12,0},{1,5},{5,9},{9,13},{13,1},{2,6},{6,10},{... | collective-permute-start | bytes 393224 | tf_op jit(solution)/shard_map/ppermute | solution.py:35
  36.8 19.2 %collective-permute-start.26 = (bf16[128,512]{1,0:T(8,128)(2,1)}, bf16[128,512]{1,0:T(8,128)(2,1)S(1)}, u32[]{:S(2)}, u32[]{:S(2)}) collective-permute-start(bf16[128,512]{1,0:T(8,128)(2,1)} %get-tuple-element.61), channel_id=1, source_target_pairs={{0,8},{4,12},{8,0},{12,4},{1,9},{5,13},{9,1},{13,5},{2,10},{6,14},... | collective-permute-start | bytes 393224 | tf_op jit(solution)/shard_map/ppermute | solution.py:35
  42.6 13.9 %collective-permute-start.25 = (bf16[128,512]{1,0:T(8,128)(2,1)}, bf16[128,512]{1,0:T(8,128)(2,1)S(1)}, u32[]{:S(2)}, u32[]{:S(2)}) collective-permute-start(bf16[128,512]{1,0:T(8,128)(2,1)} %get-tuple-element.62), channel_id=1, source_target_pairs={{0,12},{4,0},{8,4},{12,8},{1,13},{5,1},{9,5},{13,9},{2,14},{6,2},{... | collective-permute-start | bytes 393224 | tf_op jit(solution)/shard_map/ppermute | solution.py:35
  53.9 4.3 %collective-permute-start.9 = (f32[32,512]{1,0:T(8,128)}, f32[32,512]{1,0:T(8,128)}, u32[]{:S(2)}, u32[]{:S(2)}) collective-permute-start(f32[32,512]{1,0:T(8,128)} %get-tuple-element.65), channel_id=1, source_target_pairs={{0,96},{32,0},{64,32},{96,64},{1,97},{33,1},{65,33},{97,65},{2,98}... | collective-permute-start | bytes 196616 | tf_op jit(solution)/shard_map/ppermute | solution.py:35
  55.8 5.0 %collective-permute-start.10 = (f32[32,512]{1,0:T(8,128)}, f32[32,512]{1,0:T(8,128)}, u32[]{:S(2)}, u32[]{:S(2)}) collective-permute-start(f32[32,512]{1,0:T(8,128)} %get-tuple-element.66), channel_id=1, source_target_pairs={{0,64},{32,96},{64,0},{96,32},{1,65},{33,97},{65,1},{97,33},{2,66}... | collective-permute-start | bytes 196616 | tf_op jit(solution)/shard_map/ppermute | solution.py:35
  55.9 5.3 %collective-permute-start.11 = (f32[32,512]{1,0:T(8,128)}, f32[32,512]{1,0:T(8,128)}, u32[]{:S(2)}, u32[]{:S(2)}) collective-permute-start(f32[32,512]{1,0:T(8,128)} %get-tuple-element.67), channel_id=1, source_target_pairs={{0,32},{32,64},{64,96},{96,0},{1,33},{33,65},{65,97},{97,1},{2,34}... | collective-permute-start | bytes 196616 | tf_op jit(solution)/shard_map/ppermute | solution.py:35
  56.5 0.7 copy-start.5
  57.2 24.5 %collective-permute-start.28 = (bf16[4,128,512]{2,1,0:T(8,128)(2,1)S(1)}, bf16[4,128,512]{2,1,0:T(8,128)(2,1)S(1)}, u32[]{:S(2)}, u32[]{:S(2)}) collective-permute-start(bf16[4,128,512]{2,1,0:T(8,128)(2,1)S(1)} %get-tuple-element.83), channel_id=1, source_target_pairs={{0,1},{1,0},{2,3},{3,2},{4,5},{5,4},{6,7},{7,6},{8,9},{9,8},{10,11... | collective-permute-start | bytes 1572872 | tf_op jit(solution)/shard_map/ppermute | solution.py:35
  76.8 18.3 %collective-permute-start.12 = (bf16[2,128,512]{2,1,0:T(8,128)(2,1)}, bf16[2,128,512]{2,1,0:T(8,128)(2,1)S(1)}, u32[]{:S(2)}, u32[]{:S(2)}) collective-permute-start(bf16[2,128,512]{2,1,0:T(8,128)(2,1)} %get-tuple-element.69), channel_id=1, source_target_pairs={{0,32},{32,64},{64,96},{96,0},{1,33},{33,65},{65,97},{97,1},{2,34}... | collective-permute-start | bytes 786440 | tf_op jit(solution)/shard_map/ppermute | solution.py:35
  76.9 19.5 %collective-permute-start.13 = (bf16[2,128,512]{2,1,0:T(8,128)(2,1)}, bf16[2,128,512]{2,1,0:T(8,128)(2,1)S(1)}, u32[]{:S(2)}, u32[]{:S(2)}) collective-permute-start(bf16[2,128,512]{2,1,0:T(8,128)(2,1)} %get-tuple-element.70), channel_id=1, source_target_pairs={{0,64},{32,96},{64,0},{96,32},{1,65},{33,97},{65,1},{97,33},{2,66}... | collective-permute-start | bytes 786440 | tf_op jit(solution)/shard_map/ppermute | solution.py:35
  79.0 6.9 %collective-permute-start.16 = (bf16[2,2,128,256]{3,2,1,0:T(8,128)(2,1)}, bf16[2,2,128,256]{3,2,1,0:T(8,128)(2,1)S(1)}, u32[]{:S(2)}, u32[]{:S(2)}) collective-permute-start(bf16[2,2,128,256]{3,2,1,0:T(8,128)(2,1)} %get-tuple-element.73), channel_id=1, source_target_pairs={{0,16},{16,0},{1,17},{17,1},{2,18},{18,2},{3,19},{19,3},{4,20},{20... | collective-permute-start | bytes 786440 | tf_op jit(solution)/shard_map/ppermute | solution.py:35
  81.7 4.2 %copy-start.9 = (bf16[2,128,512]{2,1,0:T(8,128)(2,1)S(1)}, bf16[2,128,512]{2,1,0:T(8,128)(2,1)}, u32[]{:S(2)}) copy-start(bf16[2,128,512]{2,1,0:T(8,128)(2,1)} %get-tuple-element.71) | copy-start | bytes 786436
  81.7 5.2 %copy-start.6 = (bf16[4,2,128,256]{3,2,1,0:T(8,128)(2,1)S(1)}, bf16[4,2,128,256]{3,2,1,0:T(8,128)(2,1)}, u32[]{:S(2)}) copy-start(bf16[4,2,128,256]{3,2,1,0:T(8,128)(2,1)} %get-tuple-element.74) | copy-start | bytes 1572868
  81.7 8.3 %collective-permute-start.17 = (bf16[2,2,128,256]{3,2,1,0:T(8,128)(2,1)}, bf16[2,2,128,256]{3,2,1,0:T(8,128)(2,1)S(1)}, u32[]{:S(2)}, u32[]{:S(2)}) collective-permute-start(bf16[2,2,128,256]{3,2,1,0:T(8,128)(2,1)} %get-tuple-element.75), channel_id=1, source_target_pairs={{0,16},{16,0},{1,17},{17,1},{2,18},{18,2},{3,19},{19,3},{4,20},{20... | collective-permute-start | bytes 786440 | tf_op jit(solution)/shard_map/ppermute | solution.py:35
  83.2 16.5 %copy-start.3 = (f32[2,128,512]{2,1,0:T(8,128)S(1)}, f32[2,128,512]{2,1,0:T(8,128)}, u32[]{:S(2)}) copy-start(f32[2,128,512]{2,1,0:T(8,128)} %get-tuple-element.68) | copy-start | bytes 1572868
  85.9 11.9 %collective-permute-start.14 = (bf16[2,128,512]{2,1,0:T(8,128)(2,1)S(1)}, bf16[2,128,512]{2,1,0:T(8,128)(2,1)S(1)}, u32[]{:S(2)}, u32[]{:S(2)}) collective-permute-start(bf16[2,128,512]{2,1,0:T(8,128)(2,1)S(1)} %copy-done.9), channel_id=1, source_target_pairs={{0,96},{32,0},{64,32},{96,64},{1,97},{33,1},{65,33},{97,65},{2,98}... | collective-permute-start | bytes 786440 | tf_op jit(solution)/shard_map/ppermute | solution.py:35
  89.9 27.2 %collective-permute-start.29 = (bf16[4,128,1024]{2,1,0:T(8,128)(2,1)S(1)}, bf16[4,128,1024]{2,1,0:T(8,128)(2,1)S(1)}, u32[]{:S(2)}, u32[]{:S(2)}) collective-permute-start(bf16[4,128,1024]{2,1,0:T(8,128)(2,1)S(1)} %maximum_select_fusion.1), channel_id=1, source_target_pairs={{0,2},{2,0},{1,3},{3,1},{4,6},{6,4},{5,7},{7,5},{8,10},{10,8},{9,1... | collective-permute-start | bytes 3145736 | tf_op jit(solution)/shard_map/ppermute | solution.py:35
  95.0 16.4 %copy-start.1 = (bf16[4096,256]{1,0:T(8,128)(2,1)S(1)}, bf16[4096,256]{1,0:T(8,128)(2,1)}, u32[]{:S(2)}) copy-start(bf16[4096,256]{1,0:T(8,128)(2,1)} %param.18) | copy-start | bytes 6291460
  95.1 10.0 %collective-permute-start.19 = (bf16[2,128,256]{2,1,0:T(8,128)(2,1)S(1)}, bf16[2,128,256]{2,1,0:T(8,128)(2,1)S(1)}, u32[]{:S(2)}, u32[]{:S(2)}) collective-permute-start(bf16[2,128,256]{2,1,0:T(8,128)(2,1)S(1)} %get-tuple-element.81), channel_id=1, source_target_pairs={{0,4},{4,8},{8,12},{12,0},{1,5},{5,9},{9,13},{13,1},{2,6},{6,10},{... | collective-permute-start | bytes 393224 | tf_op jit(solution)/shard_map/ppermute | solution.py:35
  96.4 7.8 %collective-permute-start.18 = (bf16[2,128,256]{2,1,0:T(8,128)(2,1)S(1)}, bf16[2,128,256]{2,1,0:T(8,128)(2,1)S(1)}, u32[]{:S(2)}, u32[]{:S(2)}) collective-permute-start(bf16[2,128,256]{2,1,0:T(8,128)(2,1)S(1)} %get-tuple-element.80), channel_id=1, source_target_pairs={{0,8},{4,12},{8,0},{12,4},{1,9},{5,13},{9,1},{13,5},{2,10},{6,14},... | collective-permute-start | bytes 393224 | tf_op jit(solution)/shard_map/ppermute | solution.py:35
  97.8 7.3 %collective-permute-start.20 = (bf16[2,128,256]{2,1,0:T(8,128)(2,1)S(1)}, bf16[2,128,256]{2,1,0:T(8,128)(2,1)S(1)}, u32[]{:S(2)}, u32[]{:S(2)}) collective-permute-start(bf16[2,128,256]{2,1,0:T(8,128)(2,1)S(1)} %fusion.31), channel_id=1, source_target_pairs={{0,12},{4,0},{8,4},{12,8},{1,13},{5,1},{9,5},{13,9},{2,14},{6,2},{... | collective-permute-start | bytes 393224 | tf_op jit(solution)/shard_map/ppermute | solution.py:35
  99.9 12.1 %copy-start.2 = (bf16[4096,256]{1,0:T(8,128)(2,1)S(1)}, bf16[4096,256]{1,0:T(8,128)(2,1)}, u32[]{:S(2)}) copy-start(bf16[4096,256]{1,0:T(8,128)(2,1)} %param.17) | copy-start | bytes 6291460
  99.9 8.9 %collective-permute-start.15 = (bf16[128,512]{1,0:T(8,128)(2,1)S(1)}, bf16[128,512]{1,0:T(8,128)(2,1)S(1)}, u32[]{:S(2)}, u32[]{:S(2)}) collective-permute-start(bf16[128,512]{1,0:T(8,128)(2,1)S(1)} %get-tuple-element.85), channel_id=1, source_target_pairs={{0,2},{2,0},{1,3},{3,1},{4,6},{6,4},{5,7},{7,5},{8,10},{10,8},{9,1... | collective-permute-start | bytes 393224 | tf_op jit(solution)/shard_map/ppermute | solution.py:35
  104.2 20.9 %collective-permute-start.24 = (bf16[2048,256]{1,0:T(8,128)(2,1)S(1)}, bf16[2048,256]{1,0:T(8,128)(2,1)S(1)}, u32[]{:S(2)}, u32[]{:S(2)}) collective-permute-start(bf16[2048,256]{1,0:T(8,128)(2,1)S(1)} %collective-permute-done.23), channel_id=1, source_target_pairs={{0,2},{2,0},{1,3},{3,1},{4,6},{6,4},{5,7},{7,5},{8,10},{10,8},{9,1... | collective-permute-start | bytes 3145736 | tf_op jit(solution)/shard_map/ppermute | solution.py:35
  105.2 7.3 %collective-permute-start.31 = (bf16[2,128,256]{2,1,0:T(8,128)(2,1)S(1)}, bf16[2,128,256]{2,1,0:T(8,128)(2,1)S(1)}, u32[]{:S(2)}, u32[]{:S(2)}) collective-permute-start(bf16[2,128,256]{2,1,0:T(8,128)(2,1)S(1)} %fusion.27), channel_id=1, source_target_pairs={{0,8},{4,12},{8,0},{12,4},{1,9},{5,13},{9,1},{13,5},{2,10},{6,14},... | collective-permute-start | bytes 393224 | tf_op jit(solution)/shard_map/ppermute | solution.py:35
  107.3 6.6 %collective-permute-start.30 = (bf16[2,128,256]{2,1,0:T(8,128)(2,1)S(1)}, bf16[2,128,256]{2,1,0:T(8,128)(2,1)S(1)}, u32[]{:S(2)}, u32[]{:S(2)}) collective-permute-start(bf16[2,128,256]{2,1,0:T(8,128)(2,1)S(1)} %fusion.27), channel_id=1, source_target_pairs={{0,12},{4,0},{8,4},{12,8},{1,13},{5,1},{9,5},{13,9},{2,14},{6,2},{... | collective-permute-start | bytes 393224 | tf_op jit(solution)/shard_map/ppermute | solution.py:35
  108.8 2.5 %collective-permute-start.21 = (bf16[128,256]{1,0:T(8,128)(2,1)S(1)}, bf16[128,256]{1,0:T(8,128)(2,1)S(1)}, u32[]{:S(2)}, u32[]{:S(2)}) collective-permute-start(bf16[128,256]{1,0:T(8,128)(2,1)S(1)} %slice_bitcast_fusion.2), channel_id=1, source_target_pairs={{0,2},{2,0},{1,3},{3,1},{4,6},{6,4},{5,7},{7,5},{8,10},{10,8},{9,1... | collective-permute-start | bytes 196616 | tf_op jit(solution)/shard_map/ppermute | solution.py:35
  111.3 5.9 %collective-permute-start.32 = (bf16[2,128,256]{2,1,0:T(8,128)(2,1)S(1)}, bf16[2,128,256]{2,1,0:T(8,128)(2,1)S(1)}, u32[]{:S(2)}, u32[]{:S(2)}) collective-permute-start(bf16[2,128,256]{2,1,0:T(8,128)(2,1)S(1)} %fusion.27), channel_id=1, source_target_pairs={{0,4},{4,8},{8,12},{12,0},{1,5},{5,9},{9,13},{13,1},{2,6},{6,10},{... | collective-permute-start | bytes 393224 | tf_op jit(solution)/shard_map/ppermute | solution.py:35
  112.5 12.6 %collective-permute-start.22 = (bf16[128,512]{1,0:T(8,128)(2,1)S(1)}, bf16[128,512]{1,0:T(8,128)(2,1)S(1)}, u32[]{:S(2)}, u32[]{:S(2)}) collective-permute-start(bf16[128,512]{1,0:T(8,128)(2,1)S(1)} %pad_maximum_fusion.3), channel_id=1, source_target_pairs={{0,1},{1,0},{2,3},{3,2},{4,5},{5,4},{6,7},{7,6},{8,9},{9,8},{10,11... | collective-permute-start | bytes 393224 | tf_op jit(solution)/shard_map/ppermute | solution.py:35
  118.8 17.7 %all-to-all-start = ((bf16[16,64,256]{2,1,0:T(8,128)(2,1)}), bf16[16,64,256]{2,1,0:T(8,128)(2,1)}, u32[]{:S(2)}, u32[]{:S(2)}) async-start(bf16[16,64,256]{2,1,0:T(8,128)(2,1)} %bitcast.61), calls=%async_computation | async-start | bytes 1048576 | tf_op jit(solution)/shard_map/all_to_all | solution.py:420

commit v8 on v7

--- a/solution.py
+++ b/solution.py
@@ -1,3 +1,4 @@
+import functools
 import math
 
 import jax
@@ -25,6 +26,7 @@
 KR = KSLOTS * T
 QR = QSLOTS * GROUP * T
 SPAN = PARTS // 2
+HALF = KR // 2
 SCALE = 1.0 / math.sqrt(HEAD)
 SCORE2 = SCALE * math.log2(math.e)
 VMEM_LIMIT = 60 * 1024 * 1024
@@ -62,7 +64,7 @@
 
 
 def lanes(first, count):
-    return pl.ds(pl.multiple_of(first * KR, 128), count * KR)
+    return pl.ds(pl.multiple_of(first * HALF, 128), count * HALF)
 
 
 def keys_of(kv, first, count):
@@ -78,9 +80,9 @@
     return jnp.concatenate([qg[i, :, :, :, c : c + HEAD].reshape(QSLOTS * T, HEAD) for c in cols], axis=0)
 
 
-def masked_scores(i, count, k, q, kposb, qpos_ref):
+def masked_scores(i, count, k, q, kposb, qpos_ref, size=KR):
     s = nt(k, q) * SCORE2
-    pieces = [s[n * KR : (n + 1) * KR] for n in range(count)]
+    pieces = [s[n * size : (n + 1) * size] for n in range(count)]
     qp = qpos_ref[i]
     kp = jnp.concatenate([kposb[i]] * (QR // 128), axis=1)
     pieces[-1] = jnp.where(kp <= qp, pieces[-1], NEG)
@@ -132,13 +134,48 @@
             out_refs[o][:, cols] = pltpu.roll(piece, o * 2 * T, 1) if o else piece
 
 
-def grads_kernel(*refs):
+def grads_kernel(near, *refs):
     kv_refs, qg_refs = refs[0:4], refs[4:8]
     kpos_ref, qpos_ref = refs[8:10]
     st_refs = refs[10:14]
-    dkv_near, dkv_first, dkv_last, dq_refs = refs[14], refs[15], refs[16], refs[17:21]
-    kv, qg, kposb, kt, dks, dvs, dqt, lse, mean, dkv_out, dq_wide, dq_out, sem, out_sem = refs[21:]
-    start_loads(kv_refs, qg_refs, kpos_ref, kv, qg, kposb, sem)
+    if near:
+        dq_in, dkv_ref, dq_refs = refs[14], refs[15], refs[16:20]
+        refs = refs[20:]
+    else:
+        dkv_ref, dq_part = refs[14:16]
+        refs = refs[16:]
+    kv, qg, kposb, kt, dks, dvs, dqt, lse, mean, dkv_out, dq_wide, dq_out, sem, out_sem = refs
+    side = 0 if near else 1
+
+    def loads(part):
+        tok = pl.ds(part * T, T)
+        for b in range(4):
+            yield pltpu.make_async_copy(kv_refs[b].at[side, :, tok, :], kv.at[part, b], sem.at[part, b])
+        for s in range(4):
+            yield pltpu.make_async_copy(qg_refs[s].at[:, tok, :], qg.at[part, s], sem.at[part, 4 + s])
+        if near:
+            yield pltpu.make_async_copy(dq_in.at[part], dqt.at[part], sem.at[part, 8])
+
+    def dkv_copy(part):
+        tok = slice(part * T, (part + 1) * T)
+        return pltpu.make_async_copy(dkv_out.at[part], dkv_ref.at[:, :, tok, :], out_sem.at[part, 0])
+
+    def dq_copies(part):
+        if not near:
+            return [pltpu.make_async_copy(dqt.at[part], dq_part.at[part], out_sem.at[part, 1])]
+        tok = slice(part * T, (part + 1) * T)
+        pairs = [(dq_wide.at[part], dq_refs[0].at[:, tok, :])]
+        pairs += [(dq_out.at[part, s - 1], dq_refs[s].at[:, tok, :]) for s in (1, 2, 3)]
+        return [pltpu.make_async_copy(a, b, out_sem.at[part, 1 + n]) for n, (a, b) in enumerate(pairs)]
+
+    for part in range(PARTS):
+        for copy in loads(part):
+            copy.start()
+    for n in range(KSLOTS // 2):
+        slot = (n // 2) * 4 + side * 2 + n % 2
+        column = jnp.broadcast_to(kpos_ref[slot : slot + 1, :], (TOK, 128)).T
+        for part in range(PARTS):
+            kposb[part, n * T : (n + 1) * T, :] = column[part * T : (part + 1) * T, :]
     for part in range(PARTS):
         st = [r[part * 4 : part * 4 + 3, :] for r in st_refs]
         top = jnp.maximum(jnp.maximum(st[0][0:1], st[1][0:1]), jnp.maximum(st[2][0:1], st[3][0:1]))
@@ -147,63 +184,41 @@
         lse[part] = top + jnp.log2(total)
         mean[part] = sum(a[2:3] * f for a, f in zip(st, fade)) / total
 
-    def dkv_copies(part):
-        tok = slice(part * T, (part + 1) * T)
-        pairs = (
-            (dkv_out.at[part, 0], dkv_near.at[:, :, tok, :]),
-            (dkv_out.at[part, 1, 1:3], dkv_first.at[:, :, tok, :]),
-            (dkv_out.at[part, 1, 3], dkv_last.at[0, :, tok, :]),
-            (dkv_out.at[part, 1, 0], dkv_last.at[1, :, tok, :]),
-        )
-        return [pltpu.make_async_copy(a, b, out_sem.at[part, n]) for n, (a, b) in enumerate(pairs)]
-
-    def dq_copies(part):
-        tok = slice(part * T, (part + 1) * T)
-        pairs = [(dq_wide.at[part], dq_refs[0].at[:, tok, :])]
-        pairs += [(dq_out.at[part, s - 1], dq_refs[s].at[:, tok, :]) for s in (1, 2, 3)]
-        return [pltpu.make_async_copy(a, b, out_sem.at[part, 4 + n]) for n, (a, b) in enumerate(pairs)]
-
-    def emit_dkv(part):
-        dk = (dks[part] * SCALE).astype(BF).reshape(4, 2, 2, T, HEAD)
-        dv = dvs[part].astype(BF).reshape(4, 2, 2, T, HEAD)
-        for a in range(2):
-            dkv_out[part, a, :, :, :, :HEAD] = dk[:, a]
-            dkv_out[part, a, :, :, :, HEAD:] = dv[:, a]
-        for copy in dkv_copies(part):
-            copy.start()
-
-    def emit_dq(part):
-        dq = dqt[part].T * SCALE
-        for h in range(GROUP):
-            cols = slice(h * HEAD, (h + 1) * HEAD)
-            rows = dq[h * QSLOTS * T : (h + 1) * QSLOTS * T, :].reshape(4, 2, T, HEAD)
-            dq_wide[part, :, :, cols] = rows[0]
-            dq_out[part, :, :, :, cols] = rows[1:4].astype(BF)
+    def body(i, count):
+        for copy in loads(i):
+            copy.wait()
+        first = i - count + 1
+        rows = count * HALF
+        k = kv[pl.ds(first, count), :, :, :, :HEAD].reshape(rows, HEAD)
+        v = kv[pl.ds(first, count), :, :, :, HEAD:].reshape(rows, HEAD)
+        q, g = heads_of(qg, i, 0), heads_of(qg, i, GROUP)
+        kt[:, lanes(i, 1)] = kv[i, :, :, :, :HEAD].reshape(HALF, HEAD).T
+        p = jnp.exp2(masked_scores(i, count, k, q, kposb, qpos_ref, HALF) - lse[i])
+        ds = (p * (nt(v, g) - mean[i])).astype(BF)
+        p = p.astype(BF)
+        dk, dv, dq = nn(ds, q), nn(p, g), nn(kt[:, lanes(first, count)], ds)
+        dqt[i] = dqt[i] + dq if near else dq
+        for n in range(count - 1):
+            dks[first + n] += dk[n * HALF : (n + 1) * HALF]
+            dvs[first + n] += dv[n * HALF : (n + 1) * HALF]
+        dks[i], dvs[i] = dk[rows - HALF :], dv[rows - HALF :]
+
+    over_parts(body)
+    for part in range(PARTS):
+        dkv_out[part, :, :, :, :HEAD] = (dks[part] * SCALE).astype(BF).reshape(4, 2, T, HEAD)
+        dkv_out[part, :, :, :, HEAD:] = dvs[part].astype(BF).reshape(4, 2, T, HEAD)
+        dkv_copy(part).start()
+        if near:
+            dq = dqt[part].T * SCALE
+            for h in range(GROUP):
+                cols = slice(h * HEAD, (h + 1) * HEAD)
+                rows = dq[h * QSLOTS * T : (h + 1) * QSLOTS * T, :].reshape(4, 2, T, HEAD)
+                dq_wide[part, :, :, cols] = rows[0]
+                dq_out[part, :, :, :, cols] = rows[1:4].astype(BF)
         for copy in dq_copies(part):
             copy.start()
-
-    def body(i, count):
-        for copy in part_copies(i, kv_refs, qg_refs, kv, qg, sem):
-            copy.wait()
-        first = i - count + 1
-        k, q, g = keys_of(kv, first, count), heads_of(qg, i, 0), heads_of(qg, i, GROUP)
-        kt[:, lanes(i, 1)] = keys_of(kv, i, 1).T
-        p = jnp.exp2(masked_scores(i, count, k, q, kposb, qpos_ref) - lse[i])
-        ds = (p * (nt(values_of(kv, first, count), g) - mean[i])).astype(BF)
-        p = p.astype(BF)
-        dk, dv = nn(ds, q), nn(p, g)
-        dqt[i] = nn(kt[:, lanes(first, count)], ds)
-        for n in range(count - 1):
-            dks[first + n] += dk[n * KR : (n + 1) * KR]
-            dvs[first + n] += dv[n * KR : (n + 1) * KR]
-        dks[i], dvs[i] = dk[(count - 1) * KR :], dv[(count - 1) * KR :]
-
-    over_parts(body)
     for part in range(PARTS):
-        emit_dkv(part)
-        emit_dq(part)
-    for part in range(PARTS):
-        for copy in dkv_copies(part) + dq_copies(part):
+        for copy in [dkv_copy(part)] + dq_copies(part):
             copy.wait()
 
 
@@ -233,33 +248,38 @@
     )(*kvs, *qgs, kpos, qpos)
 
 
-def run_grads(kvs, qgs, kpos, qpos, sts):
-    dkv = [jax.ShapeDtypeStruct((n, 2, TOK, 2 * HEAD), BF) for n in (4, 2, 2)]
-    dq = [jax.ShapeDtypeStruct((2, TOK, GROUP * HEAD), F32 if s == 0 else BF) for s in range(4)]
-    out = pl.pallas_call(
-        grads_kernel,
-        out_shape=dkv + dq,
-        in_specs=in_places(6),
-        out_specs=[pl.BlockSpec(memory_space=pl.ANY)] * 7,
-        scratch_shapes=common_scratch()
-        + [
-            pltpu.VMEM((HEAD, PARTS * KR), BF),
-            pltpu.VMEM((PARTS, KR, HEAD), F32),
-            pltpu.VMEM((PARTS, KR, HEAD), F32),
+def run_grads(near, kvs, qgs, kpos, qpos, sts, extra=()):
+    outs = [jax.ShapeDtypeStruct((4, 2, TOK, 2 * HEAD), BF)]
+    if near:
+        outs += [jax.ShapeDtypeStruct((2, TOK, GROUP * HEAD), F32 if s == 0 else BF) for s in range(4)]
+    else:
+        outs += [jax.ShapeDtypeStruct((PARTS, HEAD, QR), F32)]
+    anywhere = pl.BlockSpec(memory_space=pl.ANY)
+    return pl.pallas_call(
+        functools.partial(grads_kernel, near),
+        out_shape=outs,
+        in_specs=in_places(6) + [anywhere] * len(extra),
+        out_specs=[anywhere] * len(outs),
+        scratch_shapes=[
+            pltpu.VMEM((PARTS, 4, 2, T, 2 * HEAD), BF),
+            pltpu.VMEM((PARTS, 4, 2, T, 2 * GROUP * HEAD), BF),
+            pltpu.VMEM((PARTS, HALF, 128), F32),
+            pltpu.VMEM((HEAD, PARTS * HALF), BF),
+            pltpu.VMEM((PARTS, HALF, HEAD), F32),
+            pltpu.VMEM((PARTS, HALF, HEAD), F32),
             pltpu.VMEM((PARTS, HEAD, QR), F32),
             pltpu.VMEM((PARTS, 1, QR), F32),
             pltpu.VMEM((PARTS, 1, QR), F32),
-            pltpu.VMEM((PARTS, 2, 4, 2, T, 2 * HEAD), BF),
+            pltpu.VMEM((PARTS, 4, 2, T, 2 * HEAD), BF),
             pltpu.VMEM((PARTS, 2, T, GROUP * HEAD), F32),
             pltpu.VMEM((PARTS, 3, 2, T, GROUP * HEAD), BF),
-            pltpu.SemaphoreType.DMA((PARTS, 8)),
-            pltpu.SemaphoreType.DMA((PARTS, 8)),
+            pltpu.SemaphoreType.DMA((PARTS, 9)),
+            pltpu.SemaphoreType.DMA((PARTS, 5)),
         ],
         compiler_params=pltpu.CompilerParams(vmem_limit_bytes=VMEM_LIMIT),
-        cost_estimate=pl.CostEstimate(flops=12_000_000_000, bytes_accessed=6_000_000, transcendentals=5_000_000),
-        name="grads",
-    )(*kvs, *qgs, kpos, qpos, *sts)
-    return out[0], out[1:3], out[3:7]
+        cost_estimate=pl.CostEstimate(flops=6_000_000_000, bytes_accessed=6_000_000, transcendentals=2_500_000),
+        name="grads_near" if near else "grads_far",
+    )(*kvs, *qgs, kpos, qpos, *sts, *extra)
 
 
 def pack_kernel(q_ref, g_ref, k_ref, v_ref, kv_own, qg_own, kv_send, qg_send):
@@ -324,7 +344,7 @@
     return pl.pallas_call(
         finish_kernel,
         out_shape=[out, out],
-        in_specs=[pl.BlockSpec(memory_space=pl.ANY)],
+        in_specs=[pl.BlockSpec(memory_space=pltpu.HBM)],
         scratch_shapes=[pltpu.VMEM((16, HEAD // 2, 2 * HEAD), BF), pltpu.SemaphoreType.DMA((16,))],
         name="finish",
     )(got)
@@ -379,7 +399,9 @@
 
     sts = run_stats(kvs, qgs, kpos, qpos)
     sts = [sts[0]] + [moved(sts[o], "y", -o) for o in (1, 2, 3)]
-    dkv_near, dkv_sent, dqs = run_grads(kvs, qgs, kpos, qpos, sts)
+    dkv_sent, dq_part = run_grads(False, kvs, qgs, kpos, qpos, sts)
+    dkv_got = moved(dkv_sent, "z", 1)
+    dkv_near, *dqs = run_grads(True, kvs, qgs, kpos, qpos, sts, (dq_part,))
 
     def total_of(own, arrived):
         total = own.astype(F32)
@@ -387,19 +409,14 @@
             total = total + a.astype(F32)
         return total.astype(BF)
 
-    first = moved(dkv_sent[0], "z", 1)
-    row1, row2 = (total_of(dkv_near[o], [first[o - 1]]) for o in (1, 2))
-    last = moved(dkv_sent[1], "z", 1)
-    near = after(dkv_near, row1)
-    row3, row0 = (total_of(near[o], [last[n]]) for n, o in enumerate((3, 0)))
+    rows = [total_of(dkv_near[o], [dkv_got[o]]) for o in range(4)]
     dq = total_of(dqs[0], [moved(dqs[o], "y", o) for o in (1, 2, 3)])
     x_all = jnp.stack([x_here, moved(x_here, "c", 1)], axis=1)
     m_core = moved(m_far, "c", 1)
     k_far = jnp.where(c == 0, m_far, m_core)
     v_far = jnp.where(c == 0, m_core, m_far)
 
-    got = [moved(row2, "x", 2), moved(row1, "x", 1)]
-    dkv = total_of(row0, got + [moved(row3, "x", 3)])
+    dkv = total_of(rows[0], [moved(rows[o], "x", o) for o in (2, 1, 3)])
     dkv_all = jnp.stack([dkv] + [moved(dkv, "x", -o) for o in (1, 2, 3)])
     dkv_far = moved(dkv[1], "c", 1)
     k_here = own_first(c, dkv[0, :, :HEAD], dkv_far[:, :HEAD], 1)

time: 139 us -> 169 us (1.22)
  waiting for transfers between devices: 35.8 us -> 69.5 us
  starting transfers between devices: 55.5 us -> 45.3 us
  Pallas kernels: 31.3 us -> 37.4 us
    ppermute x33 -> x32, waiting for transfers between devices: 26.4 us -> 60 us  [moved(): return lax.ppermute(array, axis, [(i, (i + by) % n) for i in range(n)])]
    ppermute x33 -> x32, starting transfers between devices: 49.1 us -> 40.1 us  [moved(): return lax.ppermute(array, axis, [(i, (i + by) % n) for i in range(n)])]
    pallas_call x1 -> x2, Pallas kernels: 15.5 us -> 21.8 us  [run_grads(): pl.pallas_call(functools.partial(grads_kernel, near), out_shape=outs, in_...]
  transfers between devices with their start and end apart: 34 -> 33, of which waited for: 14 -> 14; matrix products, arithmetic and copies ran while one was open for 10% -> 8% of each run, Pallas kernels for 20% -> 20%
where the time goes in v8:
time: 169 us; the launch traced here: 168 us
  waiting for transfers between devices  69.5 us (41%)
  starting transfers between devices  45.3 us (27%)
  Pallas kernels  37.4 us (22%)
  matrix products  5.39 us (3%)
  local copies, waits for them, and re-layouts  4.88 us (3%)
  other arithmetic  4.72 us (3%)
    ppermute x32, waiting for transfers between devices, moved(): return lax.ppermute(array, axis, [(i, (i + by) % n) for i in range(n)])  60 us
    ppermute x32, starting transfers between devices, moved(): return lax.ppermute(array, axis, [(i, (i + by) % n) for i in range(n)])  40.1 us
    pallas_call x2, Pallas kernels, run_grads(): pl.pallas_call(functools.partial(grads_kernel, near), out_shape=outs, in_...  21.8 us
    pallas_call x1, Pallas kernels, run_stats(): pl.pallas_call(stats_kernel, out_shape=[jax.ShapeDtypeStruct((PARTS * 4,...  9.76 us
    all_to_all x1, waiting for transfers between devices, step(): got = lax.all_to_all(pieces, ('y', 'z', 'c'), 0, 0, tiled=True)  9.55 us
    all_to_all x1, starting transfers between devices, step(): got = lax.all_to_all(pieces, ('y', 'z', 'c'), 0, 0, tiled=True)  5.18 us
  transfers between devices with their start and end apart: 33, of which 14 were waited for; matrix products, arithmetic and copies ran while one was open for 8% of the time, Pallas kernels for 20%

profile of v8, /device:TPU:1, one launch (start us, length us, event | category | flops | bytes accessed | tf_op | source)
XLA Modules:
  0.0 168.4 jit_solution(14287355834931606061)
XLA Ops:
  0.6 2.0 %pack.1 = (bf16[2,128,256]{2,1,0:T(8,128)(2,1)}, bf16[2,128,1024]{2,1,0:T(8,128)(2,1)}, bf16[128,256]{1,0:T(8,128)(2,1)}, bf16[128,1024]{1,0:T(8,128)(2,1)}) custom-call(bf16[128,1024]{1,0:T(8,128)(2,1)} %q_ref.1, bf16[128,1024]{1,0:T(8,128)(2,1)} %g_ref.1, bf16[128,256]{1,0:T(8,128)(2,1)} %k_ref.1, bf16[128,256]{1,0:T(8,128)(2,1)} %v_ref.1), custom_call_target="tpu_custom_call" | custom-call | tf_op jit(solution)/shard_map/pack/pallas_call | solution.py:302
  2.7 1.4 collective-permute-start
  5.2 0.6 bitcast_dynamic-update-slice_fusion.1
  5.8 3.7 %collective-permute-start.1 = (bf16[2,128,256]{2,1,0:T(8,128)(2,1)}, bf16[2,128,256]{2,1,0:T(8,128)(2,1)S(1)}, u32[]{:S(2)}, u32[]{:S(2)}) collective-permute-start(bf16[2,128,256]{2,1,0:T(8,128)(2,1)} %bitcast_dynamic-update-slice_fusion.1), channel_id=1, source_target_pairs={{0,16},{16,0},{1,17},{17,1},{2,18},{18,2},{3,19},{19,3},{4,20},{20... | collective-permute-start | bytes 393224 | tf_op jit(solution)/shard_map/ppermute | solution.py:37
  9.8 3.5 %collective-permute-done.1 = bf16[2,128,256]{2,1,0:T(8,128)(2,1)S(1)} collective-permute-done((bf16[2,128,256]{2,1,0:T(8,128)(2,1)}, bf16[2,128,256]{2,1,0:T(8,128)(2,1)S(1)}, u32[]{:S(2)}, u32[]{:S(2)}) %collective-permute-start.1) | collective-permute-done | bytes 131104 | tf_op jit(solution)/shard_map/ppermute | solution.py:37
  13.2 0.9 pad_maximum_fusion.2.refs_0_
  14.2 2.5 %collective-permute-start.2 = (bf16[2,2,128,256]{3,2,1,0:T(8,128)(2,1)S(1)}, bf16[2,2,128,256]{3,2,1,0:T(8,128)(2,1)S(1)}, u32[]{:S(2)}, u32[]{:S(2)}) collective-permute-start(bf16[2,2,128,256]{3,2,1,0:T(8,128)(2,1)S(1)} %pad_maximum_fusion.2.refs_0_), channel_id=1, source_target_pairs={{0,12},{4,0},{8,4},{12,8},{1,13},{5,1},{9,5},{13,9},{2,14},{6,2},{... | collective-permute-start | bytes 786440 | tf_op jit(solution)/shard_map/ppermute | solution.py:37
  16.7 0.7 bitcast_dynamic-update-slice_fusion.refs_4_
  17.4 2.7 %collective-permute-start.6 = (bf16[2,128,1024]{2,1,0:T(8,128)(2,1)}, bf16[2,128,1024]{2,1,0:T(8,128)(2,1)S(1)}, u32[]{:S(2)}, u32[]{:S(2)}) collective-permute-start(bf16[2,128,1024]{2,1,0:T(8,128)(2,1)} %bitcast_dynamic-update-slice_fusion.refs_4_), channel_id=1, source_target_pairs={{0,96},{32,0},{64,32},{96,64},{1,97},{33,1},{65,33},{97,65},{2,98}... | collective-permute-start | bytes 1572872 | tf_op jit(solution)/shard_map/ppermute | solution.py:37
  20.5 0.7 collective-permute-start.8
  21.8 0.6 collective-permute-start.4
  22.5 1.1 convolution_add_fusion.2
  23.6 0.6 slice.116.refs_8_
  25.0 2.0 %columns.1 = (bf16[128,512]{1,0:T(8,128)(2,1)}, bf16[128,512]{1,0:T(8,128)(2,1)}, bf16[128,512]{1,0:T(8,128)(2,1)}, bf16[128,512]{1,0:T(8,128)(2,1)}) custom-call(bf16[128,2048]{1,0:T(8,128)(2,1)} %in_ref), custom_call_target="tpu_custom_call" | custom-call | tf_op jit(solution)/shard_map/columns/pallas_call | solution.py:320
  26.9 1.8 %collective-permute-done.3.refs_2_ = bf16[2,2,128,256]{3,2,1,0:T(8,128)(2,1)S(1)} collective-permute-done((bf16[2,2,128,256]{3,2,1,0:T(8,128)(2,1)S(1)}, bf16[2,2,128,256]{3,2,1,0:T(8,128)(2,1)S(1)}, u32[]{:S(2)}, u32[]{:S(2)}) %collective-permute-start.3) | collective-permute-done | bytes 262176 | tf_op jit(solution)/shard_map/ppermute | solution.py:37
  28.7 5.5 %collective-permute-done.4.refs_3_ = bf16[2,2,128,256]{3,2,1,0:T(8,128)(2,1)S(1)} collective-permute-done((bf16[2,2,128,256]{3,2,1,0:T(8,128)(2,1)S(1)}, bf16[2,2,128,256]{3,2,1,0:T(8,128)(2,1)S(1)}, u32[]{:S(2)}, u32[]{:S(2)}) %collective-permute-start.4) | collective-permute-done | bytes 262176 | tf_op jit(solution)/shard_map/ppermute | solution.py:37
  34.2 2.7 %collective-permute-start.25 = (bf16[128,512]{1,0:T(8,128)(2,1)}, bf16[128,512]{1,0:T(8,128)(2,1)S(1)}, u32[]{:S(2)}, u32[]{:S(2)}) collective-permute-start(bf16[128,512]{1,0:T(8,128)(2,1)} %get-tuple-element.60), channel_id=1, source_target_pairs={{0,8},{4,12},{8,0},{12,4},{1,9},{5,13},{9,1},{13,5},{2,10},{6,14},... | collective-permute-start | bytes 393224 | tf_op jit(solution)/shard_map/ppermute | solution.py:37
  37.0 10.0 %collective-permute-done.8.refs_7_ = bf16[2,128,1024]{2,1,0:T(8,128)(2,1)S(1)} collective-permute-done((bf16[2,128,1024]{2,1,0:T(8,128)(2,1)}, bf16[2,128,1024]{2,1,0:T(8,128)(2,1)S(1)}, u32[]{:S(2)}, u32[]{:S(2)}) %collective-permute-start.8) | collective-permute-done | bytes 524320 | tf_op jit(solution)/shard_map/ppermute | solution.py:37
  47.0 0.8 copy-done.8
  47.8 9.8 %stats.1 = (f32[32,512]{1,0:T(8,128)}, f32[32,512]{1,0:T(8,128)}, f32[32,512]{1,0:T(8,128)}, f32[32,512]{1,0:T(8,128)}) custom-call(bf16[2,2,128,256]{3,2,1,0:T(8,128)(2,1)} %copy-done.5, bf16[2,2,128,256]{3,2,1,0:T(8,128)(2,1)} %copy-done.10, bf16[2,2,128,256]{3,2,1,0:T(8,128)(2,1)} %copy-done.11, bf16[2,2,128,256]{3,2,1,0:T(8,128)(2,1)} %copy-done.12, ...), custom_call_target="tpu_custom_call" | custom-call | flops 6000000000 | bytes 3000000 | tf_op jit(solution)/shard_map/stats/pallas_call | solution.py:238
  58.1 1.0 collective-permute-start.11
  59.2 1.0 collective-permute-start.27
  60.2 0.8 collective-permute-done.9.refs_11_
  61.0 1.6 collective-permute-done.10.refs_12_
  62.6 0.8 collective-permute-done.11.refs_13_
  63.4 0.6 copy-done.15
  64.0 10.9 %grads_far.1 = (bf16[4,2,128,256]{3,2,1,0:T(8,128)(2,1)}, f32[8,128,512]{2,1,0:T(8,128)}) custom-call(bf16[2,2,128,256]{3,2,1,0:T(8,128)(2,1)} %copy-done.5, bf16[2,2,128,256]{3,2,1,0:T(8,128)(2,1)} %copy-done.10, bf16[2,2,128,256]{3,2,1,0:T(8,128)(2,1)} %copy-done.11, bf16[2,2,128,256]{3,2,1,0:T(8,128)(2,1)} %copy-done.12, ...), custom_call_target="tpu_custom_call" | custom-call | flops 6000000000 | bytes 6000000 | tf_op jit(solution)/shard_map/grads_far/pallas_call | solution.py:258
  74.9 10.9 %grads_near.1 = (bf16[4,2,128,256]{3,2,1,0:T(8,128)(2,1)}, f32[2,128,512]{2,1,0:T(8,128)}, bf16[2,128,512]{2,1,0:T(8,128)(2,1)}, bf16[2,128,512]{2,1,0:T(8,128)(2,1)}, bf16[2,128,512]{2,1,0:T(8,128)(2,1)}) custom-call(bf16[2,2,128,256]{3,2,1,0:T(8,128)(2,1)} %copy-done.5, bf16[2,2,128,256]{3,2,1,0:T(8,128)(2,1)} %copy-done.10, ...), custom_call_target="tpu_custom_call" | custom-call | flops 6000000000 | bytes 6000000 | tf_op jit(solution)/shard_map/grads_near/pallas_call | solution.py:258
  85.9 2.1 %collective-permute-start.14 = (bf16[2,128,512]{2,1,0:T(8,128)(2,1)}, bf16[2,128,512]{2,1,0:T(8,128)(2,1)S(1)}, u32[]{:S(2)}, u32[]{:S(2)}) collective-permute-start(bf16[2,128,512]{2,1,0:T(8,128)(2,1)} %get-tuple-element.71), channel_id=1, source_target_pairs={{0,96},{32,0},{64,32},{96,64},{1,97},{33,1},{65,33},{97,65},{2,98}... | collective-permute-start | bytes 786440 | tf_op jit(solution)/shard_map/ppermute | solution.py:37
  88.6 1.8 %dynamic-slice_select_fusion = bf16[2048,256]{1,0:T(8,128)(2,1)S(1)} fusion(bf16[4096,256]{1,0:T(8,128)(2,1)} %param.18, s32[]{:T(128)S(6)} %select_n.157, bf16[4096,256]{1,0:T(8,128)(2,1)} %param.17, pred[]{:T(512)S(6)} %eq.50), kind=kLoop, calls=%fused_computation.16 | loop fusion | flops 524288 | bytes 3145733 | tf_op jit(solution)/shard_map/jit(_where)/select_n | solution.py:397
  90.4 0.8 collective-permute-start.22
  91.2 3.4 %collective-permute-start.16 = (bf16[4,2,128,256]{3,2,1,0:T(8,128)(2,1)S(1)}, bf16[4,2,128,256]{3,2,1,0:T(8,128)(2,1)S(1)}, u32[]{:S(2)}, u32[]{:S(2)}) collective-permute-start(bf16[4,2,128,256]{3,2,1,0:T(8,128)(2,1)S(1)} %copy-done.9), channel_id=1, source_target_pairs={{0,16},{16,0},{1,17},{17,1},{2,18},{18,2},{3,19},{19,3},{4,20},{20... | collective-permute-start | bytes 1572872 | tf_op jit(solution)/shard_map/ppermute | solution.py:37
  94.9 0.8 collective-permute-done.13
  95.7 7.8 %collective-permute-done.12 = bf16[2,128,512]{2,1,0:T(8,128)(2,1)S(1)} collective-permute-done((bf16[2,128,512]{2,1,0:T(8,128)(2,1)}, bf16[2,128,512]{2,1,0:T(8,128)(2,1)S(1)}, u32[]{:S(2)}, u32[]{:S(2)}) %collective-permute-start.12) | collective-permute-done | bytes 262176 | tf_op jit(solution)/shard_map/ppermute | solution.py:37
  104.2 21.6 %collective-permute-done.16 = bf16[4,2,128,256]{3,2,1,0:T(8,128)(2,1)S(1)} collective-permute-done((bf16[4,2,128,256]{3,2,1,0:T(8,128)(2,1)S(1)}, bf16[4,2,128,256]{3,2,1,0:T(8,128)(2,1)S(1)}, u32[]{:S(2)}, u32[]{:S(2)}) %collective-permute-start.16) | collective-permute-done | bytes 524320 | tf_op jit(solution)/shard_map/ppermute | solution.py:37
  126.0 1.5 collective-permute-start.19
  127.5 1.4 collective-permute-start.17
  129.3 4.3 %collective-permute-start.28 = (bf16[4,128,1024]{2,1,0:T(8,128)(2,1)S(1)}, bf16[4,128,1024]{2,1,0:T(8,128)(2,1)S(1)}, u32[]{:S(2)}, u32[]{:S(2)}) collective-permute-start(bf16[4,128,1024]{2,1,0:T(8,128)(2,1)S(1)} %maximum_select_fusion.1), channel_id=1, source_target_pairs={{0,2},{2,0},{1,3},{3,1},{4,6},{6,4},{5,7},{7,5},{8,10},{10,8},{9,1... | collective-permute-start | bytes 3145736 | tf_op jit(solution)/shard_map/ppermute | solution.py:37
  133.9 0.8 maximum_select_fusion.2
  134.8 4.1 %collective-permute-start.20 = (bf16[128,256]{1,0:T(8,128)(2,1)S(1)}, bf16[128,256]{1,0:T(8,128)(2,1)S(1)}, u32[]{:S(2)}, u32[]{:S(2)}) collective-permute-start(bf16[128,256]{1,0:T(8,128)(2,1)S(1)} %slice_bitcast_fusion.2), channel_id=1, source_target_pairs={{0,2},{2,0},{1,3},{3,1},{4,6},{6,4},{5,7},{7,5},{8,10},{10,8},{9,1... | collective-permute-start | bytes 196616 | tf_op jit(solution)/shard_map/ppermute | solution.py:37
  138.9 3.0 %collective-permute-start.30 = (bf16[2,128,256]{2,1,0:T(8,128)(2,1)S(1)}, bf16[2,128,256]{2,1,0:T(8,128)(2,1)S(1)}, u32[]{:S(2)}, u32[]{:S(2)}) collective-permute-start(bf16[2,128,256]{2,1,0:T(8,128)(2,1)S(1)} %fusion.27), channel_id=1, source_target_pairs={{0,8},{4,12},{8,0},{12,4},{1,9},{5,13},{9,1},{13,5},{2,10},{6,14},... | collective-permute-start | bytes 393224 | tf_op jit(solution)/shard_map/ppermute | solution.py:37
  143.0 2.1 %collective-permute-done.31 = bf16[2,128,256]{2,1,0:T(8,128)(2,1)S(1)} collective-permute-done((bf16[2,128,256]{2,1,0:T(8,128)(2,1)S(1)}, bf16[2,128,256]{2,1,0:T(8,128)(2,1)S(1)}, u32[]{:S(2)}, u32[]{:S(2)}) %collective-permute-start.31) | collective-permute-done | bytes 131104 | tf_op jit(solution)/shard_map/ppermute | solution.py:37
  145.1 3.2 %collective-permute-done.30 = bf16[2,128,256]{2,1,0:T(8,128)(2,1)S(1)} collective-permute-done((bf16[2,128,256]{2,1,0:T(8,128)(2,1)S(1)}, bf16[2,128,256]{2,1,0:T(8,128)(2,1)S(1)}, u32[]{:S(2)}, u32[]{:S(2)}) %collective-permute-start.30) | collective-permute-done | bytes 131104 | tf_op jit(solution)/shard_map/ppermute | solution.py:37
  148.3 1.6 fusion.7
  149.9 5.2 %all-to-all-start = ((bf16[16,64,256]{2,1,0:T(8,128)(2,1)}), bf16[16,64,256]{2,1,0:T(8,128)(2,1)}, u32[]{:S(2)}, u32[]{:S(2)}) async-start(bf16[16,64,256]{2,1,0:T(8,128)(2,1)} %bitcast.61), calls=%async_computation | async-start | bytes 1048576 | tf_op jit(solution)/shard_map/all_to_all | solution.py:437
  155.5 1.3 fusion.1
  156.8 9.6 %all-to-all-done.in_ref = bf16[16,64,256]{2,1,0:T(8,128)(2,1)} async-done(((bf16[16,64,256]{2,1,0:T(8,128)(2,1)}), bf16[16,64,256]{2,1,0:T(8,128)(2,1)}, u32[]{:S(2)}, u32[]{:S(2)}) %all-to-all-start) | async-done | bytes 524320 | tf_op jit(solution)/shard_map/all_to_all | solution.py:437
  166.4 1.8 %finish.1 = (f32[64,256]{1,0:T(8,128)}, f32[64,256]{1,0:T(8,128)}) custom-call(bf16[16,64,256]{2,1,0:T(8,128)(2,1)} %all-to-all-done.in_ref), custom_call_target="tpu_custom_call" | custom-call | tf_op jit(solution)/shard_map/finish/pallas_call | solution.py:344
  (104 shorter events, 8.0 us)
Async XLA Ops:
  2.7 2.5 %collective-permute-start = (bf16[128,256]{1,0:T(8,128)(2,1)}, bf16[128,256]{1,0:T(8,128)(2,1)S(1)}, u32[]{:S(2)}, u32[]{:S(2)}) collective-permute-start(bf16[128,256]{1,0:T(8,128)(2,1)} %get-tuple-element.54), channel_id=1, source_target_pairs={{0,2},{2,0},{1,3},{3,1},{4,6},{6,4},{5,7},{7,5},{8,10},{10,8},{9,1... | collective-permute-start | bytes 196616 | tf_op jit(solution)/shard_map/ppermute | solution.py:37
  4.0 12.7 %collective-permute-start.5 = (bf16[128,1024]{1,0:T(8,128)(2,1)}, bf16[128,1024]{1,0:T(8,128)(2,1)S(1)}, u32[]{:S(2)}, u32[]{:S(2)}) collective-permute-start(bf16[128,1024]{1,0:T(8,128)(2,1)} %get-tuple-element.56), channel_id=1, source_target_pairs={{0,2},{2,0},{1,3},{3,1},{4,6},{6,4},{5,7},{7,5},{8,10},{10,8},{9,1... | collective-permute-start | bytes 786440 | tf_op jit(solution)/shard_map/ppermute | solution.py:37
  5.8 7.4 %collective-permute-start.1 = (bf16[2,128,256]{2,1,0:T(8,128)(2,1)}, bf16[2,128,256]{2,1,0:T(8,128)(2,1)S(1)}, u32[]{:S(2)}, u32[]{:S(2)}) collective-permute-start(bf16[2,128,256]{2,1,0:T(8,128)(2,1)} %bitcast_dynamic-update-slice_fusion.1), channel_id=1, source_target_pairs={{0,16},{16,0},{1,17},{17,1},{2,18},{18,2},{3,19},{19,3},{4,20},{20... | collective-permute-start | bytes 393224 | tf_op jit(solution)/shard_map/ppermute | solution.py:37
  14.2 32.8 %copy-start.5 = (bf16[2,2,128,256]{3,2,1,0:T(8,128)(2,1)}, bf16[2,2,128,256]{3,2,1,0:T(8,128)(2,1)S(1)}, u32[]{:S(2)}) copy-start(bf16[2,2,128,256]{3,2,1,0:T(8,128)(2,1)S(1)} %pad_maximum_fusion.2.refs_0_) | copy-start | bytes 786436
  14.2 7.7 %collective-permute-start.2 = (bf16[2,2,128,256]{3,2,1,0:T(8,128)(2,1)S(1)}, bf16[2,2,128,256]{3,2,1,0:T(8,128)(2,1)S(1)}, u32[]{:S(2)}, u32[]{:S(2)}) collective-permute-start(bf16[2,2,128,256]{3,2,1,0:T(8,128)(2,1)S(1)} %pad_maximum_fusion.2.refs_0_), channel_id=1, source_target_pairs={{0,12},{4,0},{8,4},{12,8},{1,13},{5,1},{9,5},{13,9},{2,14},{6,2},{... | collective-permute-start | bytes 786440 | tf_op jit(solution)/shard_map/ppermute | solution.py:37
  17.4 19.5 %collective-permute-start.6 = (bf16[2,128,1024]{2,1,0:T(8,128)(2,1)}, bf16[2,128,1024]{2,1,0:T(8,128)(2,1)S(1)}, u32[]{:S(2)}, u32[]{:S(2)}) collective-permute-start(bf16[2,128,1024]{2,1,0:T(8,128)(2,1)} %bitcast_dynamic-update-slice_fusion.refs_4_), channel_id=1, source_target_pairs={{0,96},{32,0},{64,32},{96,64},{1,97},{33,1},{65,33},{97,65},{2,98}... | collective-permute-start | bytes 1572872 | tf_op jit(solution)/shard_map/ppermute | solution.py:37
  20.2 16.8 %collective-permute-start.7 = (bf16[2,128,1024]{2,1,0:T(8,128)(2,1)}, bf16[2,128,1024]{2,1,0:T(8,128)(2,1)S(1)}, u32[]{:S(2)}, u32[]{:S(2)}) collective-permute-start(bf16[2,128,1024]{2,1,0:T(8,128)(2,1)} %bitcast_dynamic-update-slice_fusion.refs_4_), channel_id=1, source_target_pairs={{0,64},{32,96},{64,0},{96,32},{1,65},{33,97},{65,1},{97,33},{2,66}... | collective-permute-start | bytes 1572872 | tf_op jit(solution)/shard_map/ppermute | solution.py:37
  20.5 26.4 %collective-permute-start.8 = (bf16[2,128,1024]{2,1,0:T(8,128)(2,1)}, bf16[2,128,1024]{2,1,0:T(8,128)(2,1)S(1)}, u32[]{:S(2)}, u32[]{:S(2)}) collective-permute-start(bf16[2,128,1024]{2,1,0:T(8,128)(2,1)} %bitcast_dynamic-update-slice_fusion.refs_4_), channel_id=1, source_target_pairs={{0,32},{32,64},{64,96},{96,0},{1,33},{33,65},{65,97},{97,1},{2,34}... | collective-permute-start | bytes 1572872 | tf_op jit(solution)/shard_map/ppermute | solution.py:37
  21.2 7.5 %collective-permute-start.3 = (bf16[2,2,128,256]{3,2,1,0:T(8,128)(2,1)S(1)}, bf16[2,2,128,256]{3,2,1,0:T(8,128)(2,1)S(1)}, u32[]{:S(2)}, u32[]{:S(2)}) collective-permute-start(bf16[2,2,128,256]{3,2,1,0:T(8,128)(2,1)S(1)} %pad_maximum_fusion.2.refs_0_), channel_id=1, source_target_pairs={{0,8},{4,12},{8,0},{12,4},{1,9},{5,13},{9,1},{13,5},{2,10},{6,14},... | collective-permute-start | bytes 786440 | tf_op jit(solution)/shard_map/ppermute | solution.py:37
  21.8 25.1 %copy-start.10 = (bf16[2,2,128,256]{3,2,1,0:T(8,128)(2,1)}, bf16[2,2,128,256]{3,2,1,0:T(8,128)(2,1)S(1)}, u32[]{:S(2)}) copy-start(bf16[2,2,128,256]{3,2,1,0:T(8,128)(2,1)S(1)} %collective-permute-done.2.refs_1_) | copy-start | bytes 786436
  21.8 12.4 %collective-permute-start.4 = (bf16[2,2,128,256]{3,2,1,0:T(8,128)(2,1)S(1)}, bf16[2,2,128,256]{3,2,1,0:T(8,128)(2,1)S(1)}, u32[]{:S(2)}, u32[]{:S(2)}) collective-permute-start(bf16[2,2,128,256]{3,2,1,0:T(8,128)(2,1)S(1)} %pad_maximum_fusion.2.refs_0_), channel_id=1, source_target_pairs={{0,4},{4,8},{8,12},{12,0},{1,5},{5,9},{9,13},{13,1},{2,6},{6,10},{... | collective-permute-start | bytes 786440 | tf_op jit(solution)/shard_map/ppermute | solution.py:37
  26.9 32.2 %copy-start.3 = (bf16[128,512]{1,0:T(8,128)(2,1)S(1)}, bf16[128,512]{1,0:T(8,128)(2,1)}, u32[]{:S(2)}) copy-start(bf16[128,512]{1,0:T(8,128)(2,1)} %get-tuple-element.58) | copy-start | bytes 393220
  28.7 18.3 %copy-start.11 = (bf16[2,2,128,256]{3,2,1,0:T(8,128)(2,1)}, bf16[2,2,128,256]{3,2,1,0:T(8,128)(2,1)S(1)}, u32[]{:S(2)}) copy-start(bf16[2,2,128,256]{3,2,1,0:T(8,128)(2,1)S(1)} %collective-permute-done.3.refs_2_) | copy-start | bytes 786436
  28.7 29.4 %collective-permute-start.26 = (bf16[128,512]{1,0:T(8,128)(2,1)}, bf16[128,512]{1,0:T(8,128)(2,1)S(1)}, u32[]{:S(2)}, u32[]{:S(2)}) collective-permute-start(bf16[128,512]{1,0:T(8,128)(2,1)} %get-tuple-element.59), channel_id=1, source_target_pairs={{0,4},{4,8},{8,12},{12,0},{1,5},{5,9},{9,13},{13,1},{2,6},{6,10},{... | collective-permute-start | bytes 393224 | tf_op jit(solution)/shard_map/ppermute | solution.py:37
  34.2 12.8 %copy-start.12 = (bf16[2,2,128,256]{3,2,1,0:T(8,128)(2,1)}, bf16[2,2,128,256]{3,2,1,0:T(8,128)(2,1)S(1)}, u32[]{:S(2)}) copy-start(bf16[2,2,128,256]{3,2,1,0:T(8,128)(2,1)S(1)} %collective-permute-done.4.refs_3_) | copy-start | bytes 786436
  34.2 24.9 %collective-permute-start.25 = (bf16[128,512]{1,0:T(8,128)(2,1)}, bf16[128,512]{1,0:T(8,128)(2,1)S(1)}, u32[]{:S(2)}, u32[]{:S(2)}) collective-permute-start(bf16[128,512]{1,0:T(8,128)(2,1)} %get-tuple-element.60), channel_id=1, source_target_pairs={{0,8},{4,12},{8,0},{12,4},{1,9},{5,13},{9,1},{13,5},{2,10},{6,14},... | collective-permute-start | bytes 393224 | tf_op jit(solution)/shard_map/ppermute | solution.py:37
  37.0 10.0 %copy-start.6 = (bf16[2,128,1024]{2,1,0:T(8,128)(2,1)}, bf16[2,128,1024]{2,1,0:T(8,128)(2,1)S(1)}, u32[]{:S(2)}) copy-start(bf16[2,128,1024]{2,1,0:T(8,128)(2,1)S(1)} %collective-permute-done.6.refs_5_) | copy-start | bytes 1572868
  37.0 22.2 %collective-permute-start.24 = (bf16[128,512]{1,0:T(8,128)(2,1)}, bf16[128,512]{1,0:T(8,128)(2,1)S(1)}, u32[]{:S(2)}, u32[]{:S(2)}) collective-permute-start(bf16[128,512]{1,0:T(8,128)(2,1)} %get-tuple-element.61), channel_id=1, source_target_pairs={{0,12},{4,0},{8,4},{12,8},{1,13},{5,1},{9,5},{13,9},{2,14},{6,2},{... | collective-permute-start | bytes 393224 | tf_op jit(solution)/shard_map/ppermute | solution.py:37
  37.0 10.0 %copy-start.7 = (bf16[2,128,1024]{2,1,0:T(8,128)(2,1)}, bf16[2,128,1024]{2,1,0:T(8,128)(2,1)S(1)}, u32[]{:S(2)}) copy-start(bf16[2,128,1024]{2,1,0:T(8,128)(2,1)S(1)} %collective-permute-done.7.refs_6_) | copy-start | bytes 1572868
  47.0 0.8 copy-start.8
  57.6 3.4 %collective-permute-start.9 = (f32[32,512]{1,0:T(8,128)}, f32[32,512]{1,0:T(8,128)S(1)}, u32[]{:S(2)}, u32[]{:S(2)}) collective-permute-start(f32[32,512]{1,0:T(8,128)} %get-tuple-element.64), channel_id=1, source_target_pairs={{0,96},{32,0},{64,32},{96,64},{1,97},{33,1},{65,33},{97,65},{2,98}... | collective-permute-start | bytes 196616 | tf_op jit(solution)/shard_map/ppermute | solution.py:37
  57.7 4.9 %collective-permute-start.10 = (f32[32,512]{1,0:T(8,128)}, f32[32,512]{1,0:T(8,128)S(1)}, u32[]{:S(2)}, u32[]{:S(2)}) collective-permute-start(f32[32,512]{1,0:T(8,128)} %get-tuple-element.65), channel_id=1, source_target_pairs={{0,64},{32,96},{64,0},{96,32},{1,65},{33,97},{65,1},{97,33},{2,66}... | collective-permute-start | bytes 196616 | tf_op jit(solution)/shard_map/ppermute | solution.py:37
  58.1 5.3 %collective-permute-start.11 = (f32[32,512]{1,0:T(8,128)}, f32[32,512]{1,0:T(8,128)S(1)}, u32[]{:S(2)}, u32[]{:S(2)}) collective-permute-start(f32[32,512]{1,0:T(8,128)} %get-tuple-element.66), channel_id=1, source_target_pairs={{0,32},{32,64},{64,96},{96,0},{1,33},{33,65},{65,97},{97,1},{2,34}... | collective-permute-start | bytes 196616 | tf_op jit(solution)/shard_map/ppermute | solution.py:37
  59.2 32.0 %collective-permute-start.27 = (bf16[4,128,512]{2,1,0:T(8,128)(2,1)S(1)}, bf16[4,128,512]{2,1,0:T(8,128)(2,1)S(1)}, u32[]{:S(2)}, u32[]{:S(2)}) collective-permute-start(bf16[4,128,512]{2,1,0:T(8,128)(2,1)S(1)} %get-tuple-element.82), channel_id=1, source_target_pairs={{0,1},{1,0},{2,3},{3,2},{4,5},{5,4},{6,7},{7,6},{8,9},{9,8},{10,11... | collective-permute-start | bytes 1572872 | tf_op jit(solution)/shard_map/ppermute | solution.py:37
  61.0 2.4 %copy-start.13 = (f32[32,512]{1,0:T(8,128)}, f32[32,512]{1,0:T(8,128)S(1)}, u32[]{:S(2)}) copy-start(f32[32,512]{1,0:T(8,128)S(1)} %collective-permute-done.9.refs_11_) | copy-start | bytes 196612
  62.6 0.8 copy-start.14
  85.9 5.3 %copy-start.9 = (bf16[4,2,128,256]{3,2,1,0:T(8,128)(2,1)S(1)}, bf16[4,2,128,256]{3,2,1,0:T(8,128)(2,1)}, u32[]{:S(2)}) copy-start(bf16[4,2,128,256]{3,2,1,0:T(8,128)(2,1)} %get-tuple-element.73) | copy-start | bytes 1572868
  85.9 9.0 %collective-permute-start.14 = (bf16[2,128,512]{2,1,0:T(8,128)(2,1)}, bf16[2,128,512]{2,1,0:T(8,128)(2,1)S(1)}, u32[]{:S(2)}, u32[]{:S(2)}) collective-permute-start(bf16[2,128,512]{2,1,0:T(8,128)(2,1)} %get-tuple-element.71), channel_id=1, source_target_pairs={{0,96},{32,0},{64,32},{96,64},{1,97},{33,1},{65,33},{97,65},{2,98}... | collective-permute-start | bytes 786440 | tf_op jit(solution)/shard_map/ppermute | solution.py:37
  87.9 7.7 %collective-permute-start.13 = (bf16[2,128,512]{2,1,0:T(8,128)(2,1)}, bf16[2,128,512]{2,1,0:T(8,128)(2,1)S(1)}, u32[]{:S(2)}, u32[]{:S(2)}) collective-permute-start(bf16[2,128,512]{2,1,0:T(8,128)(2,1)} %get-tuple-element.70), channel_id=1, source_target_pairs={{0,64},{32,96},{64,0},{96,32},{1,65},{33,97},{65,1},{97,33},{2,66}... | collective-permute-start | bytes 786440 | tf_op jit(solution)/shard_map/ppermute | solution.py:37
  88.3 15.2 %copy-start.2 = (f32[2,128,512]{2,1,0:T(8,128)S(1)}, f32[2,128,512]{2,1,0:T(8,128)}, u32[]{:S(2)}) copy-start(f32[2,128,512]{2,1,0:T(8,128)} %get-tuple-element.68) | copy-start | bytes 1572868
  88.3 15.2 %collective-permute-start.12 = (bf16[2,128,512]{2,1,0:T(8,128)(2,1)}, bf16[2,128,512]{2,1,0:T(8,128)(2,1)S(1)}, u32[]{:S(2)}, u32[]{:S(2)}) collective-permute-start(bf16[2,128,512]{2,1,0:T(8,128)(2,1)} %get-tuple-element.69), channel_id=1, source_target_pairs={{0,32},{32,64},{64,96},{96,0},{1,33},{33,65},{65,97},{97,1},{2,34}... | collective-permute-start | bytes 786440 | tf_op jit(solution)/shard_map/ppermute | solution.py:37
  90.4 38.9 %collective-permute-start.22 = (bf16[2048,256]{1,0:T(8,128)(2,1)S(1)}, bf16[2048,256]{1,0:T(8,128)(2,1)S(1)}, u32[]{:S(2)}, u32[]{:S(2)}) collective-permute-start(bf16[2048,256]{1,0:T(8,128)(2,1)S(1)} %dynamic-slice_select_fusion), channel_id=1, source_target_pairs={{0,1},{1,0},{2,3},{3,2},{4,5},{5,4},{6,7},{7,6},{8,9},{9,8},{10,11... | collective-permute-start | bytes 3145736 | tf_op jit(solution)/shard_map/ppermute | solution.py:37
  91.2 34.7 %copy-start.4 = (bf16[4,2,128,256]{3,2,1,0:T(8,128)(2,1)S(1)}, bf16[4,2,128,256]{3,2,1,0:T(8,128)(2,1)}, u32[]{:S(2)}) copy-start(bf16[4,2,128,256]{3,2,1,0:T(8,128)(2,1)} %get-tuple-element.72) | copy-start | bytes 1572868
  91.2 34.7 %collective-permute-start.16 = (bf16[4,2,128,256]{3,2,1,0:T(8,128)(2,1)S(1)}, bf16[4,2,128,256]{3,2,1,0:T(8,128)(2,1)S(1)}, u32[]{:S(2)}, u32[]{:S(2)}) collective-permute-start(bf16[4,2,128,256]{3,2,1,0:T(8,128)(2,1)S(1)} %copy-done.9), channel_id=1, source_target_pairs={{0,16},{16,0},{1,17},{17,1},{2,18},{18,2},{3,19},{19,3},{4,20},{20... | collective-permute-start | bytes 1572872 | tf_op jit(solution)/shard_map/ppermute | solution.py:37
  103.7 29.9 %collective-permute-start.15 = (bf16[128,512]{1,0:T(8,128)(2,1)S(1)}, bf16[128,512]{1,0:T(8,128)(2,1)S(1)}, u32[]{:S(2)}, u32[]{:S(2)}) collective-permute-start(bf16[128,512]{1,0:T(8,128)(2,1)S(1)} %get-tuple-element.84), channel_id=1, source_target_pairs={{0,2},{2,0},{1,3},{3,1},{4,6},{6,4},{5,7},{7,5},{8,10},{10,8},{9,1... | collective-permute-start | bytes 393224 | tf_op jit(solution)/shard_map/ppermute | solution.py:37
  126.0 16.0 %copy-start = (bf16[4096,256]{1,0:T(8,128)(2,1)S(1)}, bf16[4096,256]{1,0:T(8,128)(2,1)}, u32[]{:S(2)}) copy-start(bf16[4096,256]{1,0:T(8,128)(2,1)} %param.18) | copy-start | bytes 6291460
  126.0 8.7 %collective-permute-start.19 = (bf16[2,128,256]{2,1,0:T(8,128)(2,1)S(1)}, bf16[2,128,256]{2,1,0:T(8,128)(2,1)S(1)}, u32[]{:S(2)}, u32[]{:S(2)}) collective-permute-start(bf16[2,128,256]{2,1,0:T(8,128)(2,1)S(1)} %get-tuple-element.79), channel_id=1, source_target_pairs={{0,12},{4,0},{8,4},{12,8},{1,13},{5,1},{9,5},{13,9},{2,14},{6,2},{... | collective-permute-start | bytes 393224 | tf_op jit(solution)/shard_map/ppermute | solution.py:37
  127.5 7.2 %collective-permute-start.18 = (bf16[2,128,256]{2,1,0:T(8,128)(2,1)S(1)}, bf16[2,128,256]{2,1,0:T(8,128)(2,1)S(1)}, u32[]{:S(2)}, u32[]{:S(2)}) collective-permute-start(bf16[2,128,256]{2,1,0:T(8,128)(2,1)S(1)} %get-tuple-element.80), channel_id=1, source_target_pairs={{0,4},{4,8},{8,12},{12,0},{1,5},{5,9},{9,13},{13,1},{2,6},{6,10},{... | collective-permute-start | bytes 393224 | tf_op jit(solution)/shard_map/ppermute | solution.py:37
  127.5 7.2 %collective-permute-start.17 = (bf16[2,128,256]{2,1,0:T(8,128)(2,1)S(1)}, bf16[2,128,256]{2,1,0:T(8,128)(2,1)S(1)}, u32[]{:S(2)}, u32[]{:S(2)}) collective-permute-start(bf16[2,128,256]{2,1,0:T(8,128)(2,1)S(1)} %get-tuple-element.78), channel_id=1, source_target_pairs={{0,8},{4,12},{8,0},{12,4},{1,9},{5,13},{9,1},{13,5},{2,10},{6,14},... | collective-permute-start | bytes 393224 | tf_op jit(solution)/shard_map/ppermute | solution.py:37
  129.2 13.3 %copy-start.1 = (bf16[4096,256]{1,0:T(8,128)(2,1)S(1)}, bf16[4096,256]{1,0:T(8,128)(2,1)}, u32[]{:S(2)}) copy-start(bf16[4096,256]{1,0:T(8,128)(2,1)} %param.17) | copy-start | bytes 6291460
  129.3 19.0 %collective-permute-start.28 = (bf16[4,128,1024]{2,1,0:T(8,128)(2,1)S(1)}, bf16[4,128,1024]{2,1,0:T(8,128)(2,1)S(1)}, u32[]{:S(2)}, u32[]{:S(2)}) collective-permute-start(bf16[4,128,1024]{2,1,0:T(8,128)(2,1)S(1)} %maximum_select_fusion.1), channel_id=1, source_target_pairs={{0,2},{2,0},{1,3},{3,1},{4,6},{6,4},{5,7},{7,5},{8,10},{10,8},{9,1... | collective-permute-start | bytes 3145736 | tf_op jit(solution)/shard_map/ppermute | solution.py:37
  133.6 21.5 %collective-permute-start.23 = (bf16[2048,256]{1,0:T(8,128)(2,1)S(1)}, bf16[2048,256]{1,0:T(8,128)(2,1)S(1)}, u32[]{:S(2)}, u32[]{:S(2)}) collective-permute-start(bf16[2048,256]{1,0:T(8,128)(2,1)S(1)} %collective-permute-done.22), channel_id=1, source_target_pairs={{0,2},{2,0},{1,3},{3,1},{4,6},{6,4},{5,7},{7,5},{8,10},{10,8},{9,1... | collective-permute-start | bytes 3145736 | tf_op jit(solution)/shard_map/ppermute | solution.py:37
  134.8 7.1 %collective-permute-start.20 = (bf16[128,256]{1,0:T(8,128)(2,1)S(1)}, bf16[128,256]{1,0:T(8,128)(2,1)S(1)}, u32[]{:S(2)}, u32[]{:S(2)}) collective-permute-start(bf16[128,256]{1,0:T(8,128)(2,1)S(1)} %slice_bitcast_fusion.2), channel_id=1, source_target_pairs={{0,2},{2,0},{1,3},{3,1},{4,6},{6,4},{5,7},{7,5},{8,10},{10,8},{9,1... | collective-permute-start | bytes 196616 | tf_op jit(solution)/shard_map/ppermute | solution.py:37
  138.9 6.2 %collective-permute-start.31 = (bf16[2,128,256]{2,1,0:T(8,128)(2,1)S(1)}, bf16[2,128,256]{2,1,0:T(8,128)(2,1)S(1)}, u32[]{:S(2)}, u32[]{:S(2)}) collective-permute-start(bf16[2,128,256]{2,1,0:T(8,128)(2,1)S(1)} %fusion.27), channel_id=1, source_target_pairs={{0,4},{4,8},{8,12},{12,0},{1,5},{5,9},{9,13},{13,1},{2,6},{6,10},{... | collective-permute-start | bytes 393224 | tf_op jit(solution)/shard_map/ppermute | solution.py:37
  138.9 9.3 %collective-permute-start.30 = (bf16[2,128,256]{2,1,0:T(8,128)(2,1)S(1)}, bf16[2,128,256]{2,1,0:T(8,128)(2,1)S(1)}, u32[]{:S(2)}, u32[]{:S(2)}) collective-permute-start(bf16[2,128,256]{2,1,0:T(8,128)(2,1)S(1)} %fusion.27), channel_id=1, source_target_pairs={{0,8},{4,12},{8,0},{12,4},{1,9},{5,13},{9,1},{13,5},{2,10},{6,14},... | collective-permute-start | bytes 393224 | tf_op jit(solution)/shard_map/ppermute | solution.py:37
  142.0 6.3 %collective-permute-start.29 = (bf16[2,128,256]{2,1,0:T(8,128)(2,1)S(1)}, bf16[2,128,256]{2,1,0:T(8,128)(2,1)S(1)}, u32[]{:S(2)}, u32[]{:S(2)}) collective-permute-start(bf16[2,128,256]{2,1,0:T(8,128)(2,1)S(1)} %fusion.27), channel_id=1, source_target_pairs={{0,12},{4,0},{8,4},{12,8},{1,13},{5,1},{9,5},{13,9},{2,14},{6,2},{... | collective-permute-start | bytes 393224 | tf_op jit(solution)/shard_map/ppermute | solution.py:37
  145.1 9.9 %collective-permute-start.21 = (bf16[128,512]{1,0:T(8,128)(2,1)S(1)}, bf16[128,512]{1,0:T(8,128)(2,1)S(1)}, u32[]{:S(2)}, u32[]{:S(2)}) collective-permute-start(bf16[128,512]{1,0:T(8,128)(2,1)S(1)} %pad_maximum_fusion.3), channel_id=1, source_target_pairs={{0,1},{1,0},{2,3},{3,2},{4,5},{5,4},{6,7},{7,6},{8,9},{9,8},{10,11... | collective-permute-start | bytes 393224 | tf_op jit(solution)/shard_map/ppermute | solution.py:37
  149.9 16.5 %all-to-all-start = ((bf16[16,64,256]{2,1,0:T(8,128)(2,1)}), bf16[16,64,256]{2,1,0:T(8,128)(2,1)}, u32[]{:S(2)}, u32[]{:S(2)}) async-start(bf16[16,64,256]{2,1,0:T(8,128)(2,1)} %bitcast.61), calls=%async_computation | async-start | bytes 1048576 | tf_op jit(solution)/shard_map/all_to_all | solution.py:437
  (1 other events, 0.6 us)

commit v9 on v7

--- a/solution.py
+++ b/solution.py
@@ -1,3 +1,4 @@
+import functools
 import math
 
 import jax
@@ -122,8 +123,7 @@
         ms[i] = jnp.concatenate([top, total, weighted, jnp.zeros((5, QR), F32)], axis=0)
 
     over_parts(body)
-    rows = [ms[i][0:4] for i in range(PARTS)]
-    stats = jnp.concatenate(rows, axis=0)
+    stats = jnp.concatenate([ms[i][n : n + 1] for n in range(3) for i in range(PARTS)], axis=0)
     per_head = QSLOTS * T
     for o in range(4):
         for h in range(GROUP):
@@ -139,13 +139,15 @@
     dkv_near, dkv_first, dkv_last, dq_refs = refs[14], refs[15], refs[16], refs[17:21]
     kv, qg, kposb, kt, dks, dvs, dqt, lse, mean, dkv_out, dq_wide, dq_out, sem, out_sem = refs[21:]
     start_loads(kv_refs, qg_refs, kpos_ref, kv, qg, kposb, sem)
+    kinds = [[r[n * PARTS : (n + 1) * PARTS, :] for r in st_refs] for n in range(3)]
+    top = functools.reduce(jnp.maximum, kinds[0])
+    fade = [jnp.exp2(a - top) for a in kinds[0]]
+    total = sum(a * f for a, f in zip(kinds[1], fade))
+    merged = top + jnp.log2(total)
+    means = sum(a * f for a, f in zip(kinds[2], fade)) / total
     for part in range(PARTS):
-        st = [r[part * 4 : part * 4 + 3, :] for r in st_refs]
-        top = jnp.maximum(jnp.maximum(st[0][0:1], st[1][0:1]), jnp.maximum(st[2][0:1], st[3][0:1]))
-        fade = [jnp.exp2(a[0:1] - top) for a in st]
-        total = sum(a[1:2] * f for a, f in zip(st, fade))
-        lse[part] = top + jnp.log2(total)
-        mean[part] = sum(a[2:3] * f for a, f in zip(st, fade)) / total
+        lse[part] = merged[part : part + 1]
+        mean[part] = means[part : part + 1]
 
     def dkv_copies(part):
         tok = slice(part * T, (part + 1) * T)
@@ -222,7 +224,7 @@
 def run_stats(kvs, qgs, kpos, qpos):
     return pl.pallas_call(
         stats_kernel,
-        out_shape=[jax.ShapeDtypeStruct((PARTS * 4, QR), F32)] * 4,
+        out_shape=[jax.ShapeDtypeStruct((PARTS * 3, QR), F32)] * 4,
         in_specs=in_places(2),
         scratch_shapes=common_scratch()
         + [pltpu.VMEM((PARTS, 8, QR), F32)]
@@ -272,8 +274,6 @@
         kv[:, HEAD:] = v_ref[:, small]
         qg[:, :wide] = q_ref[:, cols]
         qg[:, wide:] = g_ref[:, cols]
-    kv_own[1] = kv_send[...]
-    qg_own[1] = qg_send[...]
 
 
 def run_pack(q, g, k, v):
@@ -363,7 +363,9 @@
     kv_pair, qg_pair, kv_send, qg_send = run_pack(query_rows, output_grad, key_rows, value_rows)
     qg_own = qg_pair.at[1].set(moved(qg_send, "c", 1))
     kv_own = kv_pair.at[1].set(moved(kv_send, "c", 1))
-    qgs = [qg_own] + [moved(qg_own, "y", -o) for o in (1, 2, 3)]
+    q_next = moved(qg_own, "y", -1)
+    q_rest = [moved(qg_own, "y", -o) for o in (2, 3)]
+    qgs = [qg_own, q_next] + q_rest
     kv_both = jnp.stack([kv_own, moved(kv_own, "z", 1)])
     kvs = [kv_both] + [moved(kv_both, "x", -o) for o in (1, 2, 3)]
     kpos, qpos = positions(run_placement, y, z, x, c)

time: 139 us -> 139 us (level)
  transfers between devices with their start and end apart: 34 -> 34, of which waited for: 14 -> 13; matrix products, arithmetic and copies ran while one was open for 10% -> 10% of each run, Pallas kernels for 20% -> 20%
where the time goes in v9:
time: 139 us; the launch traced here: 138 us
  starting transfers between devices  55.9 us (40%)
  waiting for transfers between devices  34.9 us (25%)
  Pallas kernels  31.2 us (22%)
  other arithmetic  5.38 us (4%)
  matrix products  5.38 us (4%)
  local copies, waits for them, and re-layouts  4.01 us (3%)
    ppermute x33, starting transfers between devices, moved(): return lax.ppermute(array, axis, [(i, (i + by) % n) for i in range(n)])  49.4 us
    ppermute x33, waiting for transfers between devices, moved(): return lax.ppermute(array, axis, [(i, (i + by) % n) for i in range(n)])  25.4 us
    pallas_call x1, Pallas kernels, run_grads(): pl.pallas_call(grads_kernel, out_shape=dkv + dq, in_specs=in_places(6), o...  15.5 us
    pallas_call x1, Pallas kernels, run_stats(): pl.pallas_call(stats_kernel, out_shape=[jax.ShapeDtypeStruct((PARTS * 3,...  9.75 us
    all_to_all x1, waiting for transfers between devices, step(): got = lax.all_to_all(pieces, ('y', 'z', 'c'), 0, 0, tiled=True)  9.5 us
    all_to_all x1, starting transfers between devices, step(): got = lax.all_to_all(pieces, ('y', 'z', 'c'), 0, 0, tiled=True)  6.52 us
  transfers between devices with their start and end apart: 34, of which 13 were waited for; matrix products, arithmetic and copies ran while one was open for 10% of the time, Pallas kernels for 20%

profile of v9, /device:TPU:1, one launch (start us, length us, event | category | flops | bytes accessed | tf_op | source)
XLA Modules:
  0.0 138.0 jit_solution(17796389172782594689)
XLA Ops:
  0.6 2.2 %pack.1 = (bf16[2,128,256]{2,1,0:T(8,128)(2,1)}, bf16[2,128,1024]{2,1,0:T(8,128)(2,1)}, bf16[128,256]{1,0:T(8,128)(2,1)}, bf16[128,1024]{1,0:T(8,128)(2,1)}) custom-call(bf16[128,1024]{1,0:T(8,128)(2,1)} %q_ref.1, bf16[128,1024]{1,0:T(8,128)(2,1)} %g_ref.1, bf16[128,256]{1,0:T(8,128)(2,1)} %k_ref.1, bf16[128,256]{1,0:T(8,128)(2,1)} %v_ref.1), custom_call_target="tpu_custom_call" | custom-call | tf_op jit(solution)/shard_map/pack/pallas_call | solution.py:282
  2.8 1.4 %collective-permute-start = (bf16[128,256]{1,0:T(8,128)(2,1)}, bf16[128,256]{1,0:T(8,128)(2,1)S(1)}, u32[]{:S(2)}, u32[]{:S(2)}) collective-permute-start(bf16[128,256]{1,0:T(8,128)(2,1)} %get-tuple-element.55), channel_id=1, source_target_pairs={{0,2},{2,0},{1,3},{3,1},{4,6},{6,4},{5,7},{7,5},{8,10},{10,8},{9,1... | collective-permute-start | bytes 196616 | tf_op jit(solution)/shard_map/ppermute | solution.py:36
  6.0 3.7 %collective-permute-start.1 = (bf16[2,128,256]{2,1,0:T(8,128)(2,1)}, bf16[2,128,256]{2,1,0:T(8,128)(2,1)S(1)}, u32[]{:S(2)}, u32[]{:S(2)}) collective-permute-start(bf16[2,128,256]{2,1,0:T(8,128)(2,1)} %bitcast_dynamic-update-slice_fusion.1), channel_id=1, source_target_pairs={{0,16},{16,0},{1,17},{17,1},{2,18},{18,2},{3,19},{19,3},{4,20},{20... | collective-permute-start | bytes 393224 | tf_op jit(solution)/shard_map/ppermute | solution.py:36
  9.7 3.7 %collective-permute-done.1 = bf16[2,128,256]{2,1,0:T(8,128)(2,1)S(1)} collective-permute-done((bf16[2,128,256]{2,1,0:T(8,128)(2,1)}, bf16[2,128,256]{2,1,0:T(8,128)(2,1)S(1)}, u32[]{:S(2)}, u32[]{:S(2)}) %collective-permute-start.1) | collective-permute-done | bytes 131104 | tf_op jit(solution)/shard_map/ppermute | solution.py:36
  13.4 0.9 pad_maximum_fusion.2.refs_0_
  14.3 1.3 collective-permute-start.4
  16.3 1.3 collective-permute-start.8
  17.6 2.6 %collective-permute-start.7 = (bf16[2,128,1024]{2,1,0:T(8,128)(2,1)}, bf16[2,128,1024]{2,1,0:T(8,128)(2,1)}, u32[]{:S(2)}, u32[]{:S(2)}) collective-permute-start(bf16[2,128,1024]{2,1,0:T(8,128)(2,1)} %bitcast_dynamic-update-slice_fusion.refs_4_), channel_id=1, source_target_pairs={{0,64},{32,96},{64,0},{96,32},{1,65},{33,97},{65,1},{97,33},{2,66}... | collective-permute-start | bytes 1572872 | tf_op jit(solution)/shard_map/ppermute | solution.py:36
  20.3 1.1 collective-permute-start.6
  21.4 2.5 %collective-permute-start.3 = (bf16[2,2,128,256]{3,2,1,0:T(8,128)(2,1)S(1)}, bf16[2,2,128,256]{3,2,1,0:T(8,128)(2,1)}, u32[]{:S(2)}, u32[]{:S(2)}) collective-permute-start(bf16[2,2,128,256]{3,2,1,0:T(8,128)(2,1)S(1)} %pad_maximum_fusion.2.refs_0_), channel_id=1, source_target_pairs={{0,8},{4,12},{8,0},{12,4},{1,9},{5,13},{9,1},{13,5},{2,10},{6,14},... | collective-permute-start | bytes 786440 | tf_op jit(solution)/shard_map/ppermute | solution.py:36
  23.9 1.2 collective-permute-start.2
  25.0 1.1 convolution_add_fusion.2
  26.9 1.5 %dynamic-slice_select_fusion = bf16[2048,256]{1,0:T(8,128)(2,1)S(1)} fusion(bf16[4096,256]{1,0:T(8,128)(2,1)S(1)} %copy-done, s32[]{:T(128)S(6)} %select_n.157, bf16[4096,256]{1,0:T(8,128)(2,1)} %param.17, pred[]{:T(512)S(6)} %eq.50), kind=kLoop, calls=%fused_computation.16 | loop fusion | flops 524288 | bytes 3145733 | tf_op jit(solution)/shard_map/jit(_where)/select_n | solution.py:379
  28.9 1.9 %columns.1 = (bf16[128,512]{1,0:T(8,128)(2,1)}, bf16[128,512]{1,0:T(8,128)(2,1)}, bf16[128,512]{1,0:T(8,128)(2,1)}, bf16[128,512]{1,0:T(8,128)(2,1)}) custom-call(bf16[128,2048]{1,0:T(8,128)(2,1)} %in_ref), custom_call_target="tpu_custom_call" | custom-call | tf_op jit(solution)/shard_map/columns/pallas_call | solution.py:300
  30.9 0.8 collective-permute-start.23
  31.7 2.4 %collective-permute-done.2.refs_1_ = bf16[2,2,128,256]{3,2,1,0:T(8,128)(2,1)} collective-permute-done((bf16[2,2,128,256]{3,2,1,0:T(8,128)(2,1)S(1)}, bf16[2,2,128,256]{3,2,1,0:T(8,128)(2,1)}, u32[]{:S(2)}, u32[]{:S(2)}) %collective-permute-start.2) | collective-permute-done | bytes 262176 | tf_op jit(solution)/shard_map/ppermute | solution.py:36
  34.1 2.6 %collective-permute-start.27 = (bf16[128,512]{1,0:T(8,128)(2,1)}, bf16[128,512]{1,0:T(8,128)(2,1)S(1)}, u32[]{:S(2)}, u32[]{:S(2)}) collective-permute-start(bf16[128,512]{1,0:T(8,128)(2,1)} %get-tuple-element.60), channel_id=1, source_target_pairs={{0,4},{4,8},{8,12},{12,0},{1,5},{5,9},{9,13},{13,1},{2,6},{6,10},{... | collective-permute-start | bytes 393224 | tf_op jit(solution)/shard_map/ppermute | solution.py:36
  36.7 2.1 %collective-permute-start.26 = (bf16[128,512]{1,0:T(8,128)(2,1)}, bf16[128,512]{1,0:T(8,128)(2,1)S(1)}, u32[]{:S(2)}, u32[]{:S(2)}) collective-permute-start(bf16[128,512]{1,0:T(8,128)(2,1)} %get-tuple-element.61), channel_id=1, source_target_pairs={{0,8},{4,12},{8,0},{12,4},{1,9},{5,13},{9,1},{13,5},{2,10},{6,14},... | collective-permute-start | bytes 393224 | tf_op jit(solution)/shard_map/ppermute | solution.py:36
  38.8 3.8 %collective-permute-done.7.refs_6_ = bf16[2,128,1024]{2,1,0:T(8,128)(2,1)} collective-permute-done((bf16[2,128,1024]{2,1,0:T(8,128)(2,1)}, bf16[2,128,1024]{2,1,0:T(8,128)(2,1)}, u32[]{:S(2)}, u32[]{:S(2)}) %collective-permute-start.7) | collective-permute-done | bytes 524320 | tf_op jit(solution)/shard_map/ppermute | solution.py:36
  42.6 1.5 %collective-permute-start.25 = (bf16[128,512]{1,0:T(8,128)(2,1)}, bf16[128,512]{1,0:T(8,128)(2,1)S(1)}, u32[]{:S(2)}, u32[]{:S(2)}) collective-permute-start(bf16[128,512]{1,0:T(8,128)(2,1)} %get-tuple-element.62), channel_id=1, source_target_pairs={{0,12},{4,0},{8,4},{12,8},{1,13},{5,1},{9,5},{13,9},{2,14},{6,2},{... | collective-permute-start | bytes 393224 | tf_op jit(solution)/shard_map/ppermute | solution.py:36
  44.1 9.7 %stats.1 = (f32[24,512]{1,0:T(8,128)}, f32[24,512]{1,0:T(8,128)}, f32[24,512]{1,0:T(8,128)}, f32[24,512]{1,0:T(8,128)}) custom-call(bf16[2,2,128,256]{3,2,1,0:T(8,128)(2,1)} %copy-done.7, bf16[2,2,128,256]{3,2,1,0:T(8,128)(2,1)} %collective-permute-done.2.refs_1_, bf16[2,2,128,256]{3,2,1,0:T(8,128)(2,1)} %collective-permute-done.3.refs_2_, ...), custom_call_target="tpu_custom_call" | custom-call | flops 6000000000 | bytes 3000000 | tf_op jit(solution)/shard_map/stats/pallas_call | solution.py:225
  53.8 2.0 %collective-permute-start.9 = (f32[24,512]{1,0:T(8,128)}, f32[24,512]{1,0:T(8,128)S(1)}, u32[]{:S(2)}, u32[]{:S(2)}) collective-permute-start(f32[24,512]{1,0:T(8,128)} %get-tuple-element.65), channel_id=1, source_target_pairs={{0,96},{32,0},{64,32},{96,64},{1,97},{33,1},{65,33},{97,65},{2,98}... | collective-permute-start | bytes 147464 | tf_op jit(solution)/shard_map/ppermute | solution.py:36
  57.9 2.8 %collective-permute-done.10.refs_12_ = f32[24,512]{1,0:T(8,128)} collective-permute-done((f32[24,512]{1,0:T(8,128)}, f32[24,512]{1,0:T(8,128)}, u32[]{:S(2)}, u32[]{:S(2)}) %collective-permute-start.10) | collective-permute-done | bytes 49184 | tf_op jit(solution)/shard_map/ppermute | solution.py:36
  60.9 15.5 %grads.1 = (bf16[4,2,128,256]{3,2,1,0:T(8,128)(2,1)}, bf16[2,2,128,256]{3,2,1,0:T(8,128)(2,1)}, bf16[2,2,128,256]{3,2,1,0:T(8,128)(2,1)}, f32[2,128,512]{2,1,0:T...) custom-call(bf16[2,2,128,256]{3,2,1,0:T(8,128)(2,1)} %copy-done.7, ...), custom_call_target="tpu_custom_call" | custom-call | flops 12000000000 | bytes 6000000 | tf_op jit(solution)/shard_map/grads/pallas_call | solution.py:241
  76.5 1.9 %collective-permute-start.13 = (bf16[2,128,512]{2,1,0:T(8,128)(2,1)}, bf16[2,128,512]{2,1,0:T(8,128)(2,1)S(1)}, u32[]{:S(2)}, u32[]{:S(2)}) collective-permute-start(bf16[2,128,512]{2,1,0:T(8,128)(2,1)} %get-tuple-element.70), channel_id=1, source_target_pairs={{0,64},{32,96},{64,0},{96,32},{1,65},{33,97},{65,1},{97,33},{2,66}... | collective-permute-start | bytes 786440 | tf_op jit(solution)/shard_map/ppermute | solution.py:36
  78.4 2.7 %collective-permute-start.16 = (bf16[2,2,128,256]{3,2,1,0:T(8,128)(2,1)}, bf16[2,2,128,256]{3,2,1,0:T(8,128)(2,1)S(1)}, u32[]{:S(2)}, u32[]{:S(2)}) collective-permute-start(bf16[2,2,128,256]{3,2,1,0:T(8,128)(2,1)} %get-tuple-element.73), channel_id=1, source_target_pairs={{0,16},{16,0},{1,17},{17,1},{2,18},{18,2},{3,19},{19,3},{4,20},{20... | collective-permute-start | bytes 786440 | tf_op jit(solution)/shard_map/ppermute | solution.py:36
  81.4 1.3 maximum_select_fusion.1
  83.0 2.3 %collective-permute-done.16 = bf16[2,2,128,256]{3,2,1,0:T(8,128)(2,1)S(1)} collective-permute-done((bf16[2,2,128,256]{3,2,1,0:T(8,128)(2,1)}, bf16[2,2,128,256]{3,2,1,0:T(8,128)(2,1)S(1)}, u32[]{:S(2)}, u32[]{:S(2)}) %collective-permute-start.16) | collective-permute-done | bytes 262176 | tf_op jit(solution)/shard_map/ppermute | solution.py:36
  85.3 1.3 collective-permute-start.14
  86.7 2.3 %collective-permute-done.17 = bf16[2,2,128,256]{3,2,1,0:T(8,128)(2,1)S(1)} collective-permute-done((bf16[2,2,128,256]{3,2,1,0:T(8,128)(2,1)}, bf16[2,2,128,256]{3,2,1,0:T(8,128)(2,1)S(1)}, u32[]{:S(2)}, u32[]{:S(2)}) %collective-permute-start.17) | collective-permute-done | bytes 262176 | tf_op jit(solution)/shard_map/ppermute | solution.py:36
  89.0 5.4 %collective-permute-start.29 = (bf16[4,128,1024]{2,1,0:T(8,128)(2,1)S(1)}, bf16[4,128,1024]{2,1,0:T(8,128)(2,1)S(1)}, u32[]{:S(2)}, u32[]{:S(2)}) collective-permute-start(bf16[4,128,1024]{2,1,0:T(8,128)(2,1)S(1)} %maximum_select_fusion.1), channel_id=1, source_target_pairs={{0,2},{2,0},{1,3},{3,1},{4,6},{6,4},{5,7},{7,5},{8,10},{10,8},{9,1... | collective-permute-start | bytes 3145736 | tf_op jit(solution)/shard_map/ppermute | solution.py:36
  94.5 1.3 collective-permute-start.19
  95.8 1.4 %collective-permute-start.18 = (bf16[2,128,256]{2,1,0:T(8,128)(2,1)S(1)}, bf16[2,128,256]{2,1,0:T(8,128)(2,1)S(1)}, u32[]{:S(2)}, u32[]{:S(2)}) collective-permute-start(bf16[2,128,256]{2,1,0:T(8,128)(2,1)S(1)} %get-tuple-element.80), channel_id=1, source_target_pairs={{0,8},{4,12},{8,0},{12,4},{1,9},{5,13},{9,1},{13,5},{2,10},{6,14},... | collective-permute-start | bytes 393224 | tf_op jit(solution)/shard_map/ppermute | solution.py:36
  97.2 1.9 %collective-permute-start.20 = (bf16[2,128,256]{2,1,0:T(8,128)(2,1)S(1)}, bf16[2,128,256]{2,1,0:T(8,128)(2,1)S(1)}, u32[]{:S(2)}, u32[]{:S(2)}) collective-permute-start(bf16[2,128,256]{2,1,0:T(8,128)(2,1)S(1)} %fusion.31), channel_id=1, source_target_pairs={{0,12},{4,0},{8,4},{12,8},{1,13},{5,1},{9,5},{13,9},{2,14},{6,2},{... | collective-permute-start | bytes 393224 | tf_op jit(solution)/shard_map/ppermute | solution.py:36
  99.3 0.9 collective-permute-start.15
  100.2 3.4 %collective-permute-done.18 = bf16[2,128,256]{2,1,0:T(8,128)(2,1)S(1)} collective-permute-done((bf16[2,128,256]{2,1,0:T(8,128)(2,1)S(1)}, bf16[2,128,256]{2,1,0:T(8,128)(2,1)S(1)}, u32[]{:S(2)}, u32[]{:S(2)}) %collective-permute-start.18) | collective-permute-done | bytes 131104 | tf_op jit(solution)/shard_map/ppermute | solution.py:36
  103.6 0.9 collective-permute-start.24
  104.6 2.0 %collective-permute-start.31 = (bf16[2,128,256]{2,1,0:T(8,128)(2,1)S(1)}, bf16[2,128,256]{2,1,0:T(8,128)(2,1)S(1)}, u32[]{:S(2)}, u32[]{:S(2)}) collective-permute-start(bf16[2,128,256]{2,1,0:T(8,128)(2,1)S(1)} %fusion.27), channel_id=1, source_target_pairs={{0,8},{4,12},{8,0},{12,4},{1,9},{5,13},{9,1},{13,5},{2,10},{6,14},... | collective-permute-start | bytes 393224 | tf_op jit(solution)/shard_map/ppermute | solution.py:36
  106.6 1.6 %collective-permute-start.30 = (bf16[2,128,256]{2,1,0:T(8,128)(2,1)S(1)}, bf16[2,128,256]{2,1,0:T(8,128)(2,1)S(1)}, u32[]{:S(2)}, u32[]{:S(2)}) collective-permute-start(bf16[2,128,256]{2,1,0:T(8,128)(2,1)S(1)} %fusion.27), channel_id=1, source_target_pairs={{0,12},{4,0},{8,4},{12,8},{1,13},{5,1},{9,5},{13,9},{2,14},{6,2},{... | collective-permute-start | bytes 393224 | tf_op jit(solution)/shard_map/ppermute | solution.py:36
  108.3 1.5 %collective-permute-start.21 = (bf16[128,256]{1,0:T(8,128)(2,1)S(1)}, bf16[128,256]{1,0:T(8,128)(2,1)S(1)}, u32[]{:S(2)}, u32[]{:S(2)}) collective-permute-start(bf16[128,256]{1,0:T(8,128)(2,1)S(1)} %slice_bitcast_fusion.2), channel_id=1, source_target_pairs={{0,2},{2,0},{1,3},{3,1},{4,6},{6,4},{5,7},{7,5},{8,10},{10,8},{9,1... | collective-permute-start | bytes 196616 | tf_op jit(solution)/shard_map/ppermute | solution.py:36
  109.8 0.8 maximum_select_fusion.2
  111.9 0.8 collective-permute-start.22
  113.3 3.3 %collective-permute-done.32 = bf16[2,128,256]{2,1,0:T(8,128)(2,1)S(1)} collective-permute-done((bf16[2,128,256]{2,1,0:T(8,128)(2,1)S(1)}, bf16[2,128,256]{2,1,0:T(8,128)(2,1)S(1)}, u32[]{:S(2)}, u32[]{:S(2)}) %collective-permute-start.32) | collective-permute-done | bytes 131104 | tf_op jit(solution)/shard_map/ppermute | solution.py:36
  116.6 1.6 %fusion.7 = bf16[1024,256]{1,0:T(8,128)(2,1)} fusion(bf16[1,2,128,256]{3,2,1,0:T(8,128)(2,1)S(1)} %bitcast.71, bf16[1,2,128,256]{3,2,1,0:T(8,128)(2,1)S(1)} %bitcast.69, bf16[1,2,128,256]{3,2,1,0:T(8,128)(2,1)S(1)} %bitcast.70, bf16[1,2,128,256]{3,2,1,0:T(8,128)(2,1)S(1)} %bitcast.62, bf16[4,1,128,1024]{3,2,0,1:T(8,128)(2,1)S(1)} %bitcast.68, ...), kind=kOutput, calls=%fused_computation.8 | convolution fusion | flops 538968064 | bytes 3145728 | tf_op jit(solution)/shard_map/dot_general | solution.py:415
  118.1 6.5 %all-to-all-start = ((bf16[16,64,256]{2,1,0:T(8,128)(2,1)}), bf16[16,64,256]{2,1,0:T(8,128)(2,1)}, u32[]{:S(2)}, u32[]{:S(2)}) async-start(bf16[16,64,256]{2,1,0:T(8,128)(2,1)} %bitcast.61), calls=%async_computation | async-start | bytes 1048576 | tf_op jit(solution)/shard_map/all_to_all | solution.py:422
  125.2 1.3 fusion.1
  126.5 9.5 %all-to-all-done.in_ref = bf16[16,64,256]{2,1,0:T(8,128)(2,1)} async-done(((bf16[16,64,256]{2,1,0:T(8,128)(2,1)}), bf16[16,64,256]{2,1,0:T(8,128)(2,1)}, u32[]{:S(2)}, u32[]{:S(2)}) %all-to-all-start) | async-done | bytes 524320 | tf_op jit(solution)/shard_map/all_to_all | solution.py:422
  136.0 1.8 %finish.1 = (f32[64,256]{1,0:T(8,128)}, f32[64,256]{1,0:T(8,128)}) custom-call(bf16[16,64,256]{2,1,0:T(8,128)(2,1)} %all-to-all-done.in_ref), custom_call_target="tpu_custom_call" | custom-call | tf_op jit(solution)/shard_map/finish/pallas_call | solution.py:324
  (96 shorter events, 9.6 us)
Async XLA Ops:
  0.6 26.2 %copy-start = (bf16[4096,256]{1,0:T(8,128)(2,1)S(1)}, bf16[4096,256]{1,0:T(8,128)(2,1)}, u32[]{:S(2)}) copy-start(bf16[4096,256]{1,0:T(8,128)(2,1)} %param.18) | copy-start | bytes 6291460
  2.8 2.5 %collective-permute-start = (bf16[128,256]{1,0:T(8,128)(2,1)}, bf16[128,256]{1,0:T(8,128)(2,1)S(1)}, u32[]{:S(2)}, u32[]{:S(2)}) collective-permute-start(bf16[128,256]{1,0:T(8,128)(2,1)} %get-tuple-element.55), channel_id=1, source_target_pairs={{0,2},{2,0},{1,3},{3,1},{4,6},{6,4},{5,7},{7,5},{8,10},{10,8},{9,1... | collective-permute-start | bytes 196616 | tf_op jit(solution)/shard_map/ppermute | solution.py:36
  4.2 11.4 %collective-permute-start.5 = (bf16[128,1024]{1,0:T(8,128)(2,1)}, bf16[128,1024]{1,0:T(8,128)(2,1)S(1)}, u32[]{:S(2)}, u32[]{:S(2)}) collective-permute-start(bf16[128,1024]{1,0:T(8,128)(2,1)} %get-tuple-element.57), channel_id=1, source_target_pairs={{0,2},{2,0},{1,3},{3,1},{4,6},{6,4},{5,7},{7,5},{8,10},{10,8},{9,1... | collective-permute-start | bytes 786440 | tf_op jit(solution)/shard_map/ppermute | solution.py:36
  6.0 7.4 %collective-permute-start.1 = (bf16[2,128,256]{2,1,0:T(8,128)(2,1)}, bf16[2,128,256]{2,1,0:T(8,128)(2,1)S(1)}, u32[]{:S(2)}, u32[]{:S(2)}) collective-permute-start(bf16[2,128,256]{2,1,0:T(8,128)(2,1)} %bitcast_dynamic-update-slice_fusion.1), channel_id=1, source_target_pairs={{0,16},{16,0},{1,17},{17,1},{2,18},{18,2},{3,19},{19,3},{4,20},{20... | collective-permute-start | bytes 393224 | tf_op jit(solution)/shard_map/ppermute | solution.py:36
  14.3 16.6 %copy-start.7 = (bf16[2,2,128,256]{3,2,1,0:T(8,128)(2,1)}, bf16[2,2,128,256]{3,2,1,0:T(8,128)(2,1)S(1)}, u32[]{:S(2)}) copy-start(bf16[2,2,128,256]{3,2,1,0:T(8,128)(2,1)S(1)} %pad_maximum_fusion.2.refs_0_) | copy-start | bytes 786436
  14.3 9.5 %collective-permute-start.4 = (bf16[2,2,128,256]{3,2,1,0:T(8,128)(2,1)S(1)}, bf16[2,2,128,256]{3,2,1,0:T(8,128)(2,1)S(1)}, u32[]{:S(2)}, u32[]{:S(2)}) collective-permute-start(bf16[2,2,128,256]{3,2,1,0:T(8,128)(2,1)S(1)} %pad_maximum_fusion.2.refs_0_), channel_id=1, source_target_pairs={{0,4},{4,8},{8,12},{12,0},{1,5},{5,9},{9,13},{13,1},{2,6},{6,10},{... | collective-permute-start | bytes 786440 | tf_op jit(solution)/shard_map/ppermute | solution.py:36
  16.3 20.4 %collective-permute-start.8 = (bf16[2,128,1024]{2,1,0:T(8,128)(2,1)}, bf16[2,128,1024]{2,1,0:T(8,128)(2,1)}, u32[]{:S(2)}, u32[]{:S(2)}) collective-permute-start(bf16[2,128,1024]{2,1,0:T(8,128)(2,1)} %bitcast_dynamic-update-slice_fusion.refs_4_), channel_id=1, source_target_pairs={{0,32},{32,64},{64,96},{96,0},{1,33},{33,65},{65,97},{97,1},{2,34}... | collective-permute-start | bytes 1572872 | tf_op jit(solution)/shard_map/ppermute | solution.py:36
  17.6 25.0 %collective-permute-start.7 = (bf16[2,128,1024]{2,1,0:T(8,128)(2,1)}, bf16[2,128,1024]{2,1,0:T(8,128)(2,1)}, u32[]{:S(2)}, u32[]{:S(2)}) collective-permute-start(bf16[2,128,1024]{2,1,0:T(8,128)(2,1)} %bitcast_dynamic-update-slice_fusion.refs_4_), channel_id=1, source_target_pairs={{0,64},{32,96},{64,0},{96,32},{1,65},{33,97},{65,1},{97,33},{2,66}... | collective-permute-start | bytes 1572872 | tf_op jit(solution)/shard_map/ppermute | solution.py:36
  20.3 23.8 %collective-permute-start.6 = (bf16[2,128,1024]{2,1,0:T(8,128)(2,1)}, bf16[2,128,1024]{2,1,0:T(8,128)(2,1)}, u32[]{:S(2)}, u32[]{:S(2)}) collective-permute-start(bf16[2,128,1024]{2,1,0:T(8,128)(2,1)} %bitcast_dynamic-update-slice_fusion.refs_4_), channel_id=1, source_target_pairs={{0,96},{32,0},{64,32},{96,64},{1,97},{33,1},{65,33},{97,65},{2,98}... | collective-permute-start | bytes 1572872 | tf_op jit(solution)/shard_map/ppermute | solution.py:36
  21.4 9.5 %collective-permute-start.3 = (bf16[2,2,128,256]{3,2,1,0:T(8,128)(2,1)S(1)}, bf16[2,2,128,256]{3,2,1,0:T(8,128)(2,1)}, u32[]{:S(2)}, u32[]{:S(2)}) collective-permute-start(bf16[2,2,128,256]{3,2,1,0:T(8,128)(2,1)S(1)} %pad_maximum_fusion.2.refs_0_), channel_id=1, source_target_pairs={{0,8},{4,12},{8,0},{12,4},{1,9},{5,13},{9,1},{13,5},{2,10},{6,14},... | collective-permute-start | bytes 786440 | tf_op jit(solution)/shard_map/ppermute | solution.py:36
  23.9 3.0 %copy-start.8 = (bf16[2,2,128,256]{3,2,1,0:T(8,128)(2,1)}, bf16[2,2,128,256]{3,2,1,0:T(8,128)(2,1)S(1)}, u32[]{:S(2)}) copy-start(bf16[2,2,128,256]{3,2,1,0:T(8,128)(2,1)S(1)} %collective-permute-done.4.refs_3_) | copy-start | bytes 786436
  23.9 10.3 %collective-permute-start.2 = (bf16[2,2,128,256]{3,2,1,0:T(8,128)(2,1)S(1)}, bf16[2,2,128,256]{3,2,1,0:T(8,128)(2,1)}, u32[]{:S(2)}, u32[]{:S(2)}) collective-permute-start(bf16[2,2,128,256]{3,2,1,0:T(8,128)(2,1)S(1)} %pad_maximum_fusion.2.refs_0_), channel_id=1, source_target_pairs={{0,12},{4,0},{8,4},{12,8},{1,13},{5,1},{9,5},{13,9},{2,14},{6,2},{... | collective-permute-start | bytes 786440 | tf_op jit(solution)/shard_map/ppermute | solution.py:36
  30.9 25.6 %copy-start.4 = (bf16[128,512]{1,0:T(8,128)(2,1)S(1)}, bf16[128,512]{1,0:T(8,128)(2,1)}, u32[]{:S(2)}) copy-start(bf16[128,512]{1,0:T(8,128)(2,1)} %get-tuple-element.59) | copy-start | bytes 393220
  30.9 68.4 %collective-permute-start.23 = (bf16[2048,256]{1,0:T(8,128)(2,1)S(1)}, bf16[2048,256]{1,0:T(8,128)(2,1)S(1)}, u32[]{:S(2)}, u32[]{:S(2)}) collective-permute-start(bf16[2048,256]{1,0:T(8,128)(2,1)S(1)} %dynamic-slice_select_fusion), channel_id=1, source_target_pairs={{0,1},{1,0},{2,3},{3,2},{4,5},{5,4},{6,7},{7,6},{8,9},{9,8},{10,11... | collective-permute-start | bytes 3145736 | tf_op jit(solution)/shard_map/ppermute | solution.py:36
  34.1 21.7 %collective-permute-start.27 = (bf16[128,512]{1,0:T(8,128)(2,1)}, bf16[128,512]{1,0:T(8,128)(2,1)S(1)}, u32[]{:S(2)}, u32[]{:S(2)}) collective-permute-start(bf16[128,512]{1,0:T(8,128)(2,1)} %get-tuple-element.60), channel_id=1, source_target_pairs={{0,4},{4,8},{8,12},{12,0},{1,5},{5,9},{9,13},{13,1},{2,6},{6,10},{... | collective-permute-start | bytes 393224 | tf_op jit(solution)/shard_map/ppermute | solution.py:36
  36.7 19.1 %collective-permute-start.26 = (bf16[128,512]{1,0:T(8,128)(2,1)}, bf16[128,512]{1,0:T(8,128)(2,1)S(1)}, u32[]{:S(2)}, u32[]{:S(2)}) collective-permute-start(bf16[128,512]{1,0:T(8,128)(2,1)} %get-tuple-element.61), channel_id=1, source_target_pairs={{0,8},{4,12},{8,0},{12,4},{1,9},{5,13},{9,1},{13,5},{2,10},{6,14},... | collective-permute-start | bytes 393224 | tf_op jit(solution)/shard_map/ppermute | solution.py:36
  42.6 13.9 %collective-permute-start.25 = (bf16[128,512]{1,0:T(8,128)(2,1)}, bf16[128,512]{1,0:T(8,128)(2,1)S(1)}, u32[]{:S(2)}, u32[]{:S(2)}) collective-permute-start(bf16[128,512]{1,0:T(8,128)(2,1)} %get-tuple-element.62), channel_id=1, source_target_pairs={{0,12},{4,0},{8,4},{12,8},{1,13},{5,1},{9,5},{13,9},{2,14},{6,2},{... | collective-permute-start | bytes 393224 | tf_op jit(solution)/shard_map/ppermute | solution.py:36
  53.8 4.0 %collective-permute-start.9 = (f32[24,512]{1,0:T(8,128)}, f32[24,512]{1,0:T(8,128)S(1)}, u32[]{:S(2)}, u32[]{:S(2)}) collective-permute-start(f32[24,512]{1,0:T(8,128)} %get-tuple-element.65), channel_id=1, source_target_pairs={{0,96},{32,0},{64,32},{96,64},{1,97},{33,1},{65,33},{97,65},{2,98}... | collective-permute-start | bytes 147464 | tf_op jit(solution)/shard_map/ppermute | solution.py:36
  55.8 4.9 %collective-permute-start.10 = (f32[24,512]{1,0:T(8,128)}, f32[24,512]{1,0:T(8,128)}, u32[]{:S(2)}, u32[]{:S(2)}) collective-permute-start(f32[24,512]{1,0:T(8,128)} %get-tuple-element.66), channel_id=1, source_target_pairs={{0,64},{32,96},{64,0},{96,32},{1,65},{33,97},{65,1},{97,33},{2,66}... | collective-permute-start | bytes 147464 | tf_op jit(solution)/shard_map/ppermute | solution.py:36
  55.9 5.0 %collective-permute-start.11 = (f32[24,512]{1,0:T(8,128)}, f32[24,512]{1,0:T(8,128)}, u32[]{:S(2)}, u32[]{:S(2)}) collective-permute-start(f32[24,512]{1,0:T(8,128)} %get-tuple-element.67), channel_id=1, source_target_pairs={{0,32},{32,64},{64,96},{96,0},{1,33},{33,65},{65,97},{97,1},{2,34}... | collective-permute-start | bytes 147464 | tf_op jit(solution)/shard_map/ppermute | solution.py:36
  56.5 0.7 copy-start.5
  57.1 23.9 %collective-permute-start.28 = (bf16[4,128,512]{2,1,0:T(8,128)(2,1)S(1)}, bf16[4,128,512]{2,1,0:T(8,128)(2,1)S(1)}, u32[]{:S(2)}, u32[]{:S(2)}) collective-permute-start(bf16[4,128,512]{2,1,0:T(8,128)(2,1)S(1)} %get-tuple-element.83), channel_id=1, source_target_pairs={{0,1},{1,0},{2,3},{3,2},{4,5},{5,4},{6,7},{7,6},{8,9},{9,8},{10,11... | collective-permute-start | bytes 1572872 | tf_op jit(solution)/shard_map/ppermute | solution.py:36
  57.9 3.0 %copy-start.10 = (f32[24,512]{1,0:T(8,128)}, f32[24,512]{1,0:T(8,128)S(1)}, u32[]{:S(2)}) copy-start(f32[24,512]{1,0:T(8,128)S(1)} %collective-permute-done.9.refs_11_) | copy-start | bytes 147460
  76.4 18.1 %collective-permute-start.12 = (bf16[2,128,512]{2,1,0:T(8,128)(2,1)}, bf16[2,128,512]{2,1,0:T(8,128)(2,1)S(1)}, u32[]{:S(2)}, u32[]{:S(2)}) collective-permute-start(bf16[2,128,512]{2,1,0:T(8,128)(2,1)} %get-tuple-element.69), channel_id=1, source_target_pairs={{0,32},{32,64},{64,96},{96,0},{1,33},{33,65},{65,97},{97,1},{2,34}... | collective-permute-start | bytes 786440 | tf_op jit(solution)/shard_map/ppermute | solution.py:36
  76.5 19.3 %collective-permute-start.13 = (bf16[2,128,512]{2,1,0:T(8,128)(2,1)}, bf16[2,128,512]{2,1,0:T(8,128)(2,1)S(1)}, u32[]{:S(2)}, u32[]{:S(2)}) collective-permute-start(bf16[2,128,512]{2,1,0:T(8,128)(2,1)} %get-tuple-element.70), channel_id=1, source_target_pairs={{0,64},{32,96},{64,0},{96,32},{1,65},{33,97},{65,1},{97,33},{2,66}... | collective-permute-start | bytes 786440 | tf_op jit(solution)/shard_map/ppermute | solution.py:36
  78.4 6.9 %collective-permute-start.16 = (bf16[2,2,128,256]{3,2,1,0:T(8,128)(2,1)}, bf16[2,2,128,256]{3,2,1,0:T(8,128)(2,1)S(1)}, u32[]{:S(2)}, u32[]{:S(2)}) collective-permute-start(bf16[2,2,128,256]{3,2,1,0:T(8,128)(2,1)} %get-tuple-element.73), channel_id=1, source_target_pairs={{0,16},{16,0},{1,17},{17,1},{2,18},{18,2},{3,19},{19,3},{4,20},{20... | collective-permute-start | bytes 786440 | tf_op jit(solution)/shard_map/ppermute | solution.py:36
  81.1 4.2 %copy-start.9 = (bf16[2,128,512]{2,1,0:T(8,128)(2,1)S(1)}, bf16[2,128,512]{2,1,0:T(8,128)(2,1)}, u32[]{:S(2)}) copy-start(bf16[2,128,512]{2,1,0:T(8,128)(2,1)} %get-tuple-element.71) | copy-start | bytes 786436
  81.1 5.5 %copy-start.6 = (bf16[4,2,128,256]{3,2,1,0:T(8,128)(2,1)S(1)}, bf16[4,2,128,256]{3,2,1,0:T(8,128)(2,1)}, u32[]{:S(2)}) copy-start(bf16[4,2,128,256]{3,2,1,0:T(8,128)(2,1)} %get-tuple-element.74) | copy-start | bytes 1572868
  81.1 7.9 %collective-permute-start.17 = (bf16[2,2,128,256]{3,2,1,0:T(8,128)(2,1)}, bf16[2,2,128,256]{3,2,1,0:T(8,128)(2,1)S(1)}, u32[]{:S(2)}, u32[]{:S(2)}) collective-permute-start(bf16[2,2,128,256]{3,2,1,0:T(8,128)(2,1)} %get-tuple-element.75), channel_id=1, source_target_pairs={{0,16},{16,0},{1,17},{17,1},{2,18},{18,2},{3,19},{19,3},{4,20},{20... | collective-permute-start | bytes 786440 | tf_op jit(solution)/shard_map/ppermute | solution.py:36
  82.7 16.4 %copy-start.3 = (f32[2,128,512]{2,1,0:T(8,128)S(1)}, f32[2,128,512]{2,1,0:T(8,128)}, u32[]{:S(2)}) copy-start(f32[2,128,512]{2,1,0:T(8,128)} %get-tuple-element.68) | copy-start | bytes 1572868
  85.3 11.9 %collective-permute-start.14 = (bf16[2,128,512]{2,1,0:T(8,128)(2,1)S(1)}, bf16[2,128,512]{2,1,0:T(8,128)(2,1)S(1)}, u32[]{:S(2)}, u32[]{:S(2)}) collective-permute-start(bf16[2,128,512]{2,1,0:T(8,128)(2,1)S(1)} %copy-done.9), channel_id=1, source_target_pairs={{0,96},{32,0},{64,32},{96,64},{1,97},{33,1},{65,33},{97,65},{2,98}... | collective-permute-start | bytes 786440 | tf_op jit(solution)/shard_map/ppermute | solution.py:36
  89.0 27.6 %collective-permute-start.29 = (bf16[4,128,1024]{2,1,0:T(8,128)(2,1)S(1)}, bf16[4,128,1024]{2,1,0:T(8,128)(2,1)S(1)}, u32[]{:S(2)}, u32[]{:S(2)}) collective-permute-start(bf16[4,128,1024]{2,1,0:T(8,128)(2,1)S(1)} %maximum_select_fusion.1), channel_id=1, source_target_pairs={{0,2},{2,0},{1,3},{3,1},{4,6},{6,4},{5,7},{7,5},{8,10},{10,8},{9,1... | collective-permute-start | bytes 3145736 | tf_op jit(solution)/shard_map/ppermute | solution.py:36
  94.5 16.4 %copy-start.1 = (bf16[4096,256]{1,0:T(8,128)(2,1)S(1)}, bf16[4096,256]{1,0:T(8,128)(2,1)}, u32[]{:S(2)}) copy-start(bf16[4096,256]{1,0:T(8,128)(2,1)} %param.18) | copy-start | bytes 6291460
  94.5 10.0 %collective-permute-start.19 = (bf16[2,128,256]{2,1,0:T(8,128)(2,1)S(1)}, bf16[2,128,256]{2,1,0:T(8,128)(2,1)S(1)}, u32[]{:S(2)}, u32[]{:S(2)}) collective-permute-start(bf16[2,128,256]{2,1,0:T(8,128)(2,1)S(1)} %get-tuple-element.81), channel_id=1, source_target_pairs={{0,4},{4,8},{8,12},{12,0},{1,5},{5,9},{9,13},{13,1},{2,6},{6,10},{... | collective-permute-start | bytes 393224 | tf_op jit(solution)/shard_map/ppermute | solution.py:36
  95.8 7.8 %collective-permute-start.18 = (bf16[2,128,256]{2,1,0:T(8,128)(2,1)S(1)}, bf16[2,128,256]{2,1,0:T(8,128)(2,1)S(1)}, u32[]{:S(2)}, u32[]{:S(2)}) collective-permute-start(bf16[2,128,256]{2,1,0:T(8,128)(2,1)S(1)} %get-tuple-element.80), channel_id=1, source_target_pairs={{0,8},{4,12},{8,0},{12,4},{1,9},{5,13},{9,1},{13,5},{2,10},{6,14},... | collective-permute-start | bytes 393224 | tf_op jit(solution)/shard_map/ppermute | solution.py:36
  97.2 7.3 %collective-permute-start.20 = (bf16[2,128,256]{2,1,0:T(8,128)(2,1)S(1)}, bf16[2,128,256]{2,1,0:T(8,128)(2,1)S(1)}, u32[]{:S(2)}, u32[]{:S(2)}) collective-permute-start(bf16[2,128,256]{2,1,0:T(8,128)(2,1)S(1)} %fusion.31), channel_id=1, source_target_pairs={{0,12},{4,0},{8,4},{12,8},{1,13},{5,1},{9,5},{13,9},{2,14},{6,2},{... | collective-permute-start | bytes 393224 | tf_op jit(solution)/shard_map/ppermute | solution.py:36
  99.3 12.1 %copy-start.2 = (bf16[4096,256]{1,0:T(8,128)(2,1)S(1)}, bf16[4096,256]{1,0:T(8,128)(2,1)}, u32[]{:S(2)}) copy-start(bf16[4096,256]{1,0:T(8,128)(2,1)} %param.17) | copy-start | bytes 6291460
  99.3 9.0 %collective-permute-start.15 = (bf16[128,512]{1,0:T(8,128)(2,1)S(1)}, bf16[128,512]{1,0:T(8,128)(2,1)S(1)}, u32[]{:S(2)}, u32[]{:S(2)}) collective-permute-start(bf16[128,512]{1,0:T(8,128)(2,1)S(1)} %get-tuple-element.85), channel_id=1, source_target_pairs={{0,2},{2,0},{1,3},{3,1},{4,6},{6,4},{5,7},{7,5},{8,10},{10,8},{9,1... | collective-permute-start | bytes 393224 | tf_op jit(solution)/shard_map/ppermute | solution.py:36
  103.6 21.1 %collective-permute-start.24 = (bf16[2048,256]{1,0:T(8,128)(2,1)S(1)}, bf16[2048,256]{1,0:T(8,128)(2,1)S(1)}, u32[]{:S(2)}, u32[]{:S(2)}) collective-permute-start(bf16[2048,256]{1,0:T(8,128)(2,1)S(1)} %collective-permute-done.23), channel_id=1, source_target_pairs={{0,2},{2,0},{1,3},{3,1},{4,6},{6,4},{5,7},{7,5},{8,10},{10,8},{9,1... | collective-permute-start | bytes 3145736 | tf_op jit(solution)/shard_map/ppermute | solution.py:36
  104.6 7.2 %collective-permute-start.31 = (bf16[2,128,256]{2,1,0:T(8,128)(2,1)S(1)}, bf16[2,128,256]{2,1,0:T(8,128)(2,1)S(1)}, u32[]{:S(2)}, u32[]{:S(2)}) collective-permute-start(bf16[2,128,256]{2,1,0:T(8,128)(2,1)S(1)} %fusion.27), channel_id=1, source_target_pairs={{0,8},{4,12},{8,0},{12,4},{1,9},{5,13},{9,1},{13,5},{2,10},{6,14},... | collective-permute-start | bytes 393224 | tf_op jit(solution)/shard_map/ppermute | solution.py:36
  106.6 6.7 %collective-permute-start.30 = (bf16[2,128,256]{2,1,0:T(8,128)(2,1)S(1)}, bf16[2,128,256]{2,1,0:T(8,128)(2,1)S(1)}, u32[]{:S(2)}, u32[]{:S(2)}) collective-permute-start(bf16[2,128,256]{2,1,0:T(8,128)(2,1)S(1)} %fusion.27), channel_id=1, source_target_pairs={{0,12},{4,0},{8,4},{12,8},{1,13},{5,1},{9,5},{13,9},{2,14},{6,2},{... | collective-permute-start | bytes 393224 | tf_op jit(solution)/shard_map/ppermute | solution.py:36
  108.3 2.4 %collective-permute-start.21 = (bf16[128,256]{1,0:T(8,128)(2,1)S(1)}, bf16[128,256]{1,0:T(8,128)(2,1)S(1)}, u32[]{:S(2)}, u32[]{:S(2)}) collective-permute-start(bf16[128,256]{1,0:T(8,128)(2,1)S(1)} %slice_bitcast_fusion.2), channel_id=1, source_target_pairs={{0,2},{2,0},{1,3},{3,1},{4,6},{6,4},{5,7},{7,5},{8,10},{10,8},{9,1... | collective-permute-start | bytes 196616 | tf_op jit(solution)/shard_map/ppermute | solution.py:36
  110.7 5.9 %collective-permute-start.32 = (bf16[2,128,256]{2,1,0:T(8,128)(2,1)S(1)}, bf16[2,128,256]{2,1,0:T(8,128)(2,1)S(1)}, u32[]{:S(2)}, u32[]{:S(2)}) collective-permute-start(bf16[2,128,256]{2,1,0:T(8,128)(2,1)S(1)} %fusion.27), channel_id=1, source_target_pairs={{0,4},{4,8},{8,12},{12,0},{1,5},{5,9},{9,13},{13,1},{2,6},{6,10},{... | collective-permute-start | bytes 393224 | tf_op jit(solution)/shard_map/ppermute | solution.py:36
  111.9 12.8 %collective-permute-start.22 = (bf16[128,512]{1,0:T(8,128)(2,1)S(1)}, bf16[128,512]{1,0:T(8,128)(2,1)S(1)}, u32[]{:S(2)}, u32[]{:S(2)}) collective-permute-start(bf16[128,512]{1,0:T(8,128)(2,1)S(1)} %pad_maximum_fusion.3), channel_id=1, source_target_pairs={{0,1},{1,0},{2,3},{3,2},{4,5},{5,4},{6,7},{7,6},{8,9},{9,8},{10,11... | collective-permute-start | bytes 393224 | tf_op jit(solution)/shard_map/ppermute | solution.py:36
  118.1 17.8 %all-to-all-start = ((bf16[16,64,256]{2,1,0:T(8,128)(2,1)}), bf16[16,64,256]{2,1,0:T(8,128)(2,1)}, u32[]{:S(2)}, u32[]{:S(2)}) async-start(bf16[16,64,256]{2,1,0:T(8,128)(2,1)} %bitcast.61), calls=%async_computation | async-start | bytes 1048576 | tf_op jit(solution)/shard_map/all_to_all | solution.py:422
